TPU v7x, 32 devices: a whole 2x2x4 slice. The times are simulated.
32 devices in a mesh: lat: 8 (over y, x, core), lon: 4 (over z).
Axes of the slice: x: 2, y: 2, z: 4, core: 2. Of those that a mesh axis runs over, the one named last changes fastest.
Arguments:
- tokens: bfloat16 [2, 48, 48, 1024], P(None, 'lat', 'lon'), may hold values from -6 to 6
- layer_norm_gain: float32 [1024], replicated, may hold values from 0.5 to 1.5
- layer_norm_bias: float32 [1024], replicated, may hold values from -3 to 3
- w_qkv: bfloat16 [1024, 1536], replicated, may hold values from -2 to 2
- w_out: bfloat16 [512, 1024], replicated, may hold values from -0.25 to 0.25
- output_cotangent: bfloat16 [2, 48, 48, 1024], P(None, 'lat', 'lon'), may hold values from -6 to 6
Outputs:
- output: bfloat16 [2, 48, 48, 1024], P(None, 'lat', 'lon')
- token_gradient: bfloat16 [2, 48, 48, 1024], P(None, 'lat', 'lon')
- d_qkv: float32 [1024, 1536], P(('lat', 'lon'))
- d_out: float32 [512, 1024], P(None, ('lat', 'lon'))
- gain_gradient_scaled: float32 [1024], P(('lat', 'lon'))
- d_bias: float32 [1024], P(('lat', 'lon'))
All inputs are finite; a program needn't handle non-finite values.
Results may differ from a plain program's by a relative error of at most 0.0093.
Values may be sent and summed in bfloat16 or wider, within the bound.
No kernel may reach another device: no remote copies, remote signals or barrier semaphores. Data moves between devices by JAX's collectives and lax.ppermute only.
A program may use at most 64 MiB of HBM per device.

v0:
```python
import math

import jax
import jax.numpy as jnp
from jax import lax
from jax.sharding import PartitionSpec as P

HDIM = 64
WLAT = 6
WLON = 12


def padded(cells, sides, width):
    for axis, dim in sides:
        count = lax.axis_size(axis)
        ends = count - 1
        head = lax.slice_in_dim(cells, 0, width, axis=dim)
        tail = lax.slice_in_dim(cells, cells.shape[dim] - width, cells.shape[dim], axis=dim)
        cells = jnp.concatenate(
            [
                lax.ppermute(tail, axis, [(i, (i + 1) % count) for i in range(ends)]),
                cells,
                lax.ppermute(head, axis, [((i + 1) % count, i) for i in range(ends)]),
            ],
            axis=dim,
        )
    return cells


def windows(grid_data, win_rows):
    levels, row_total, col_total, channels = grid_data.shape
    grid_data = grid_data.reshape(
        levels, row_total // win_rows, win_rows, col_total // WLON, WLON, channels
    )
    grid_data = grid_data.transpose(1, 3, 0, 2, 4, 5)
    return grid_data.reshape(-1, levels * win_rows * WLON, channels)


def from_windows(win_data, levels, row_total, col_total, win_rows):
    channels = win_data.shape[-1]
    grid_data = win_data.reshape(
        row_total // win_rows, col_total // WLON, levels, win_rows, WLON, channels
    )
    grid_data = grid_data.transpose(2, 0, 3, 1, 4, 5)
    return grid_data.reshape(levels, row_total, col_total, channels)


def attend(queries, key_part, value_part, grad_att, key_valid):
    score_scale = queries.shape[-1] ** (-0.5)
    scores = (
        jnp.einsum("nqhd,nkhd->nhqk", queries, key_part, preferred_element_type=jnp.float32)
        * score_scale
    )
    scores = jnp.where(key_valid[:, None, None, :], scores, -1e30)
    row_max = jnp.max(scores, axis=-1, keepdims=True)
    exp_scores = jnp.exp(scores - row_max)
    probabilities = exp_scores / jnp.sum(exp_scores, axis=-1, keepdims=True)
    probs_low = probabilities.astype(jnp.bfloat16)
    attended = jnp.einsum(
        "nhqk,nkhd->nqhd", probs_low, value_part, preferred_element_type=jnp.float32
    ).astype(jnp.bfloat16)
    grad_prob = jnp.einsum(
        "nqhd,nkhd->nhqk", grad_att, value_part, preferred_element_type=jnp.float32
    )
    row_inner = jnp.sum(probabilities * grad_prob, axis=-1, keepdims=True)
    grad_score = (probabilities * (grad_prob - row_inner)).astype(jnp.bfloat16)
    grad_query = (
        jnp.einsum("nhqk,nkhd->nqhd", grad_score, key_part, preferred_element_type=jnp.float32)
        * score_scale
    ).astype(jnp.bfloat16)
    grad_key = (
        jnp.einsum("nhqk,nqhd->nkhd", grad_score, queries, preferred_element_type=jnp.float32)
        * score_scale
    )
    grad_value = jnp.einsum(
        "nhqk,nqhd->nkhd", probs_low, grad_att, preferred_element_type=jnp.float32
    )
    return (attended, grad_query, grad_key, grad_value)


def run_windows(per_query, per_key, query_rows, key_valid):
    levels, query_total, col_total, channels = per_query.shape
    key_total = per_key.shape[1]
    inner_width = channels // 2
    head_dim = HDIM
    head_count = inner_width // head_dim
    query_win = windows(per_query, query_rows)
    key_win = windows(per_key, WLAT)
    win_count, query_len, _ = query_win.shape
    key_len = key_win.shape[1]
    attended, grad_query, grad_key, grad_value = attend(
        query_win[..., :inner_width].reshape(win_count, query_len, head_count, head_dim),
        key_win[..., :inner_width].reshape(win_count, key_len, head_count, head_dim),
        key_win[..., inner_width:].reshape(win_count, key_len, head_count, head_dim),
        query_win[..., inner_width:].reshape(win_count, query_len, head_count, head_dim),
        key_valid,
    )
    query_out = jnp.concatenate(
        [
            attended.reshape(win_count, query_len, inner_width),
            grad_query.reshape(win_count, query_len, inner_width),
        ],
        axis=-1,
    )
    key_out = jnp.concatenate(
        [
            grad_key.reshape(win_count, key_len, inner_width),
            grad_value.reshape(win_count, key_len, inner_width),
        ],
        axis=-1,
    )
    return (
        from_windows(query_out, levels, query_total, col_total, query_rows),
        from_windows(key_out, levels, key_total, col_total, WLAT),
    )


def on_device(tokens, layer_norm_gain, layer_norm_bias, w_qkv, w_out, output_cotangent):
    levels, lat_rows, lon_cols, model_width = tokens.shape
    inner_width = w_out.shape[0]
    half_lat = WLAT // 2
    half_lon = WLON // 2
    lat_count = lax.axis_size("lat")
    lat_place = lax.axis_index("lat")
    lon_count = lax.axis_size("lon")
    lon_place = lax.axis_index("lon")
    norm_factor = 1.0 / math.sqrt(levels * lat_rows * lon_cols * lat_count * lon_count)
    tokens_wide = tokens.astype(jnp.float32)
    average = jnp.mean(tokens_wide, axis=-1, keepdims=True)
    centered_input = tokens_wide - average
    inverse_deviation = lax.rsqrt(
        jnp.mean(centered_input * centered_input, axis=-1, keepdims=True) + 1e-05
    )
    standardized_input = centered_input * inverse_deviation
    normalized_tokens = (standardized_input * layer_norm_gain + layer_norm_bias).astype(
        jnp.bfloat16
    )
    flat_normed = normalized_tokens.reshape(-1, model_width)
    projected = jnp.dot(flat_normed, w_qkv, preferred_element_type=jnp.float32).astype(jnp.bfloat16)
    projected = projected.reshape(levels, lat_rows, lon_cols, 3 * inner_width)
    key_pairs = projected[..., inner_width:]
    grad_flat = output_cotangent.reshape(-1, model_width)
    grad_att = jnp.einsum("td,hd->th", grad_flat, w_out, preferred_element_type=jnp.float32).astype(
        jnp.bfloat16
    )
    grad_att = grad_att.reshape(levels, lat_rows, lon_cols, inner_width)
    widened = padded(key_pairs, (("lon", 2),), half_lon)
    extended = padded(widened, (("lat", 1),), half_lat)
    col_total = lon_cols + WLON
    query_side = jnp.concatenate([projected[..., :inner_width], grad_att], axis=-1)
    query_side = jnp.pad(query_side, ((0, 0), (0, 0), (half_lon, half_lon), (0, 0)))
    col_ids = jnp.arange(col_total)
    left_ok = jnp.logical_or(lon_place > 0, col_ids >= half_lon)
    right_ok = jnp.logical_or(lon_place < lon_count - 1, col_ids < lon_cols + half_lon)
    col_ok = jnp.logical_and(left_ok, right_ok).astype(jnp.float32).reshape(1, 1, col_total, 1)
    row_ids = jnp.arange(WLAT)
    top_ok = jnp.logical_or(lat_place > 0, row_ids >= half_lat)
    bottom_ok = jnp.logical_or(lat_place < lat_count - 1, row_ids < half_lat)
    edge_rows = jnp.concatenate([top_ok, bottom_ok]).astype(jnp.float32)
    mask_grid = jnp.broadcast_to(
        edge_rows.reshape(1, 2 * WLAT, 1, 1) * col_ok, (levels, 2 * WLAT, col_total, 1)
    )
    edge_valid = windows(mask_grid, WLAT)[..., 0] > 0.5
    edge_query = jnp.concatenate(
        [query_side[:, :half_lat], query_side[:, lat_rows - half_lat :]], axis=1
    )
    edge_key = jnp.concatenate([extended[:, :WLAT], extended[:, lat_rows:]], axis=1)
    edge_out, edge_grads = run_windows(edge_query, edge_key, half_lat, edge_valid)
    query_results = edge_out
    query_results = query_results[:, :, half_lon : half_lon + lon_cols]
    attended = query_results[..., :inner_width]
    grad_query = query_results[..., inner_width:]
    rim_rows = jnp.concatenate(
        [edge_grads[:, :half_lat], edge_grads[:, lat_rows + half_lat :]], axis=1
    )
    received = padded(rim_rows.astype(jnp.bfloat16), (("lat", 1),), half_lat).astype(rim_rows.dtype)
    owned = edge_grads[:, half_lat : lat_rows + half_lat]
    owned = owned + jnp.pad(
        received[:, :half_lat], ((0, 0), (0, lat_rows - half_lat), (0, 0), (0, 0))
    )
    owned = owned + jnp.pad(
        received[:, 3 * half_lat :], ((0, 0), (lat_rows - half_lat, 0), (0, 0), (0, 0))
    )
    rim_cols = jnp.concatenate([owned[:, :, :half_lon], owned[:, :, lon_cols + half_lon :]], axis=2)
    received_cols = padded(rim_cols, (("lon", 2),), half_lon)
    centre = owned[:, :, half_lon : lon_cols + half_lon]
    centre = centre + jnp.pad(
        received_cols[:, :, :half_lon], ((0, 0), (0, 0), (0, lon_cols - half_lon), (0, 0))
    )
    centre = centre + jnp.pad(
        received_cols[:, :, 3 * half_lon :], ((0, 0), (0, 0), (lon_cols - half_lon, 0), (0, 0))
    )
    key_value_grads = centre.astype(jnp.bfloat16)
    grad_proj = jnp.concatenate([grad_query, key_value_grads], axis=-1).reshape(-1, 3 * inner_width)
    attended_flat = attended.reshape(-1, inner_width)
    mixed = jnp.dot(attended_flat, w_out, preferred_element_type=jnp.float32).reshape(
        tokens_wide.shape
    )
    y_out = (tokens_wide + mixed).astype(jnp.bfloat16)
    term_out = jnp.einsum("ti,td->id", attended_flat, grad_flat, preferred_element_type=jnp.float32)
    term_qkv = jnp.einsum("td,tj->dj", flat_normed, grad_proj, preferred_element_type=jnp.float32)
    gradient_of_normalized = jnp.einsum(
        "tj,dj->td", grad_proj, w_qkv, preferred_element_type=jnp.float32
    ).reshape(tokens_wide.shape)
    gain_term_value = jnp.sum(gradient_of_normalized * standardized_input, axis=(0, 1, 2))
    term_bias = jnp.sum(gradient_of_normalized, axis=(0, 1, 2))
    partial_sums = (
        lax.psum_scatter(term_qkv, "lat", scatter_dimension=0, tiled=True),
        lax.psum_scatter(term_out, "lat", scatter_dimension=1, tiled=True),
        lax.psum_scatter(gain_term_value, "lat", scatter_dimension=0, tiled=True),
        lax.psum_scatter(term_bias, "lat", scatter_dimension=0, tiled=True),
    )
    totals = (
        lax.psum_scatter(partial_sums[0], "lon", scatter_dimension=0, tiled=True),
        lax.psum_scatter(partial_sums[1], "lon", scatter_dimension=1, tiled=True),
        lax.psum_scatter(partial_sums[2], "lon", scatter_dimension=0, tiled=True),
        lax.psum_scatter(partial_sums[3], "lon", scatter_dimension=0, tiled=True),
    )
    d_qkv = totals[0] * norm_factor
    d_out = totals[1] * norm_factor
    gain_gradient_scaled = totals[2] * norm_factor
    d_bias = totals[3] * norm_factor
    gradient_of_standardized = gradient_of_normalized * layer_norm_gain
    first_moment_term = jnp.mean(gradient_of_standardized, axis=-1, keepdims=True)
    second_moment_term = jnp.mean(
        gradient_of_standardized * standardized_input, axis=-1, keepdims=True
    )
    token_gradient = (
        output_cotangent.astype(jnp.float32)
        + (gradient_of_standardized - first_moment_term - standardized_input * second_moment_term)
        * inverse_deviation
    ).astype(jnp.bfloat16)
    return (y_out, token_gradient, d_qkv, d_out, gain_gradient_scaled, d_bias)


def solution(mesh):
    in_specs = (P(None, "lat", "lon", None), P(), P(), P(), P(), P(None, "lat", "lon", None))
    out_specs = (
        P(None, "lat", "lon", None),
        P(None, "lat", "lon", None),
        P(("lat", "lon"), None),
        P(None, ("lat", "lon")),
        P(("lat", "lon")),
        P(("lat", "lon")),
    )
    return jax.shard_map(
        on_device, mesh=mesh, in_specs=in_specs, out_specs=out_specs, check_vma=False
    )
```

profile of v0, /device:TPU:0, one launch (start us, length us, event | category | flops | bytes accessed | tf_op | source)
XLA Modules:
  0.0 276.7 jit_solution(8413669356450958406)
XLA Ops:
  11.8 2.3 convolution_convert_fusion
  14.1 1.9 reshape.180
  16.0 1.9 fusion.62
  19.2 6.3 %collective-permute-start = (bf16[2,6,6,1024]{3,2,1,0:T(8,128)(2,1)}, bf16[2,6,6,1024]{3,2,1,0:T(8,128)(2,1)}, u32[]{:S(2)}, u32[]{:S(2)}) collective-permute-start(bf16[2,6,6,1024]{3,2,1,0:T(8,128)(2,1)} %get-tuple-element.45), channel_id=1, source_target_pairs={{0,1},{1,2},{2,3},{4,5},{5,6},{6,7},{8,9},{9,10},{10,11},{12,13},{... | collective-permute-start | bytes 442376 | tf_op jit(solution)/shard_map/ppermute | solution.py:21
  25.5 1.8 slice.104
  29.8 2.5 convolution_convert_fusion.2
  36.9 2.2 collective-permute-start.2
  45.6 2.8 %reshape.187 = bf16[4,72,1024]{2,0,1:T(4,128)(2,1)} reshape(bf16[2,2,2,3,12,1024]{5,1,0,4,3,2:T(2,128)(2,1)} %copy.53) | data formatting | bytes 1179648 | tf_op jit(solution)/shard_map/reshape | solution.py:36
  48.4 2.1 fusion.60
  50.5 2.1 copy.54
  52.6 2.1 copy.57
  57.4 2.2 copy.49
  59.7 4.0 %reshape.182 = bf16[4,144,1024]{2,0,1:T(4,128)(2,1)} reshape(bf16[2,2,2,6,12,1024]{5,1,0,4,3,2:T(2,128)(2,1)} %copy.49) | data formatting | bytes 2359296 | tf_op jit(solution)/shard_map/reshape | solution.py:36
  63.6 2.7 fusion.58
  66.3 2.3 copy.50
  68.6 2.3 copy.55
  70.8 3.6 %fusion.63 = (f32[4,8,72]{2,1,0:T(8,128)S(1)}, f32[4,8,72,144]{3,2,1,0:T(8,128)}) fusion(pred[4,144]{1,0:T(4,128)(4,1)S(1)} %copy-done.17, bf16[4,72,8,64]{1,3,2,0:T(8,128)(2,1)} %bitcast.92, bf16[4,144,8,64]{1,3,2,0:T(8,128)(2,1)} %bitcast.89), kind=kOutput, calls=%fused_computation.104 | convolution fusion | flops 43794576 | bytes 2221632 | tf_op jit(solution)/shard_map/sub | solution.py:56
  74.4 3.5 %fusion.12 = bf16[4,72,8,64]{1,3,2,0:T(8,128)(2,1)} fusion(bf16[4,144,8,64]{1,3,2,0:T(8,128)(2,1)} %bitcast.95, f32[4,8,72,144]{3,2,1,0:T(8,128)} %get-tuple-element.47, f32[4,8,72]{2,1,0:T(8,128)S(1)} %get-tuple-element.46), kind=kOutput, calls=%fused_computation.27 | convolution fusion | flops 43278336 | bytes 2221056 | tf_op jit(solution)/shard_map/nhqk,nkhd->nqhd/dot_general | solution.py:59
  77.9 2.4 multiply_reduce_fusion
  80.3 2.0 convolution_bitcast_fusion.2
  82.3 2.7 copy.56
  85.0 2.1 concatenate.55
  87.1 3.0 %multiply_convert_fusion = bf16[4,8,72,144]{3,2,1,0:T(8,128)(2,1)S(1)} fusion(f32[4,8,72,144]{3,2,1,0:T(8,128)} %get-tuple-element.49, f32[4,8,72]{2,1,0:T(8,128)S(1)} %get-tuple-element.48, f32[4,8,72,144]{3,2,1,0:T(8,128)} %get-tuple-element.47, f32[4,8,72]{2,1,0:T(8,128)S(1)} %get-tuple-element.46), kind=kLoop, calls=%fused_computation.14 | loop fusion | flops 1327104 | bytes 3336192 | tf_op jit(solution)/shard_map/convert_element_type | solution.py:66
  92.4 2.7 copy.58
  95.1 2.1 concatenate.56
  100.9 1.9 convolution_bitcast_fusion.1
  102.9 3.2 %multiply_bitcast_fusion = f32[4,144,8,64]{1,3,2,0:T(8,128)} fusion(bf16[4,72,8,64]{1,3,2,0:T(8,128)(2,1)} %bitcast.93, bf16[4,8,72,144]{3,2,1,0:T(8,128)(2,1)} %copy-done.1), kind=kOutput, calls=%fused_computation.18 | convolution fusion | flops 42762240 | bytes 2138112 | tf_op jit(solution)/shard_map/nhqk,nqhd->nkhd/dot_general | solution.py:72
  106.0 3.5 %copy.64 = f32[4,144,8,64]{3,2,0,1:T(8,128)} copy(f32[4,144,8,64]{1,3,2,0:T(8,128)} %convolution_bitcast_fusion.2) | data formatting | bytes 2359296 | tf_op jit(solution)/shard_map/nhqk,nqhd->nkhd/transpose | solution.py:75
  109.5 3.2 %concatenate.59 = f32[2,2,2,6,12,512]{5,1,0,4,3,2:T(2,128)} reshape(f32[4,144,8,64]{3,2,0,1:T(8,128)} %copy.64) | data formatting | bytes 2359296 | tf_op jit(solution)/shard_map/concatenate | solution.py:105
  112.7 3.6 %copy.63 = f32[4,144,8,64]{3,2,0,1:T(8,128)} copy(f32[4,144,8,64]{1,3,2,0:T(8,128)} %multiply_bitcast_fusion) | data formatting | bytes 2359296 | tf_op jit(solution)/shard_map/mul | solution.py:72
  116.3 3.2 %concatenate.58 = f32[2,2,2,6,12,512]{5,1,0,4,3,2:T(2,128)} reshape(f32[4,144,8,64]{3,2,0,1:T(8,128)} %copy.63) | data formatting | bytes 2359296 | tf_op jit(solution)/shard_map/concatenate | solution.py:105
  119.5 2.9 %maximum_bitcast_fusion = f32[2,2,6,2,12,1024]{5,3,1,4,2,0:T(2,128)S(1)} fusion(f32[2,2,2,6,12,512]{5,1,0,4,3,2:T(2,128)} %concatenate.59, f32[2,2,2,6,12,512]{5,1,0,4,3,2:T(2,128)} %concatenate.58), kind=kLoop, calls=%fused_computation.13 | loop fusion | flops 589824 | bytes 4718592 | tf_op jit(solution)/shard_map/transpose | solution.py:44
  122.4 1.8 copy.65
  125.0 4.4 %collective-permute-start.4 = (bf16[2,3,24,1024]{3,2,1,0:T(8,128)(2,1)S(1)}, bf16[2,3,24,1024]{3,2,1,0:T(8,128)(2,1)S(1)}, u32[]{:S(2)}, u32[]{:S(2)}) collective-permute-start(bf16[2,3,24,1024]{3,2,1,0:T(8,128)(2,1)S(1)} %get-tuple-element.34), channel_id=1, source_target_pairs={{0,4},{4,8},{8,12},{12,16},{16,20},{20,24},{24,28},{1,5},{5,9},{9,... | collective-permute-start | bytes 884744 | tf_op jit(solution)/shard_map/ppermute | solution.py:21
  131.7 2.4 collective-permute-done.5
  135.2 2.9 %collective-permute-start.6 = (f32[2,6,6,1024]{3,2,1,0:T(8,128)S(1)}, f32[2,6,6,1024]{3,2,1,0:T(8,128)S(1)}, u32[]{:S(2)}, u32[]{:S(2)}) collective-permute-start(f32[2,6,6,1024]{3,2,1,0:T(8,128)S(1)} %get-tuple-element.32), channel_id=1, source_target_pairs={{0,1},{1,2},{2,3},{4,5},{5,6},{6,7},{8,9},{9,10},{10,11},{12,13},{... | collective-permute-start | bytes 884744 | tf_op jit(solution)/shard_map/ppermute | solution.py:21
  139.5 3.9 %collective-permute-done.6 = f32[2,6,6,1024]{3,2,1,0:T(8,128)S(1)} collective-permute-done((f32[2,6,6,1024]{3,2,1,0:T(8,128)S(1)}, f32[2,6,6,1024]{3,2,1,0:T(8,128)S(1)}, u32[]{:S(2)}, u32[]{:S(2)}) %collective-permute-start.6) | collective-permute-done | bytes 294944 | tf_op jit(solution)/shard_map/ppermute | solution.py:21
  143.4 4.7 %collective-permute-done.7 = f32[2,6,6,1024]{3,2,1,0:T(8,128)S(1)} collective-permute-done((f32[2,6,6,1024]{3,2,1,0:T(8,128)S(1)}, f32[2,6,6,1024]{3,2,1,0:T(8,128)S(1)}, u32[]{:S(2)}, u32[]{:S(2)}) %collective-permute-start.7) | collective-permute-done | bytes 294944 | tf_op jit(solution)/shard_map/ppermute | solution.py:23
  149.1 3.8 %convolution_bitcast_fusion = f32[1024,1536]{1,0:T(8,128)} fusion(bf16[2,6,12,1024]{3,2,1,0:T(8,128)(2,1)S(1)} %fusion.43, bf16[2,6,12,512]{3,2,1,0:T(8,128)(2,1)S(1)} %copy.79, bf16[2,6,12,1024]{3,0,2,1:T(2,128)(2,1)S(1)} %copy-done.2, f32[1024]{0:T(1024)S(1)} %copy-done.16, f32[1024]{0:T(1024)S(1)} %copy-done.15, f32[2,6,12]{2,1,0:T(8,128)S(1)} %add_rsqrt_fusion, ...), kind=kOutput, calls=%fused_computation.1 | convolution fusion | flops 454754304 | bytes 7038080 | tf_op jit(solution)/shard_map/td,tj->dj/dot_general | solution.py:201
  153.0 1.8 copy.76
  157.3 65.3 %reduce-scatter.7.cloned.1.call-done = f32[128,1536]{1,0:T(8,128)} async-done(((f32[1024,1536]{1,0:T(8,128)}), f32[128,1536]{1,0:T(8,128)}) %reduce-scatter.7.cloned.1.call-update) | async-done | bytes 786448 | tf_op jit(solution)/shard_map/reduce_scatter | solution.py:208
  222.7 1.7 fusion.11
  225.5 2.2 fusion.40
  227.7 12.7 %all-reduce.8 = (f32[1024]{0:T(1024)S(1)}, f32[1024]{0:T(1024)S(1)}) all-reduce(f32[1024]{0:T(1024)S(1)} %get-tuple-element.24, f32[1024]{0:T(1024)S(1)} %get-tuple-element.27), channel_id=6, replica_groups=mesh['lat'=8,'lon'=4] {'lat'}, use_global_device_ids=true, to_apply=%region_12.13.clone | all-reduce | flops 2048 | bytes 16384
  243.2 11.8 %all-reduce.9 = (f32[128]{0:T(128)S(1)}, f32[128]{0:T(128)S(1)}) all-reduce(f32[128]{0:T(128)S(1)} %dynamic-slice.1, f32[128]{0:T(128)S(1)} %dynamic-slice.5), channel_id=7, replica_groups=mesh['lat'=8,'lon'=4] {'lon'}, use_global_device_ids=true, to_apply=%region_13.14.clone | all-reduce | flops 256 | bytes 2048
  257.8 1.7 copy.71
  259.5 9.1 %reduce-scatter.9.cloned.1.call-done = f32[32,1536]{1,0:T(8,128)} async-done(((f32[128,1536]{1,0:T(8,128)}), f32[32,1536]{1,0:T(8,128)}) %reduce-scatter.9.cloned.1.call-update) | async-done | bytes 196624 | tf_op jit(solution)/shard_map/reduce_scatter | solution.py:214
  268.6 1.6 broadcast_multiply_fusion.1
  (113 shorter events, 42.6 us)
Async XLA Ops:
  7.2 4.6 %copy-start = (bf16[1024,1536]{1,0:T(8,128)(2,1)S(1)}, bf16[1024,1536]{1,0:T(8,128)(2,1)}, u32[]{:S(2)}) copy-start(bf16[1024,1536]{1,0:T(8,128)(2,1)} %param.9) | copy-start | bytes 9437188
  7.2 145.8 %reduce-scatter.11.cloned.1.call-start = ((), (), s32[]{:S(2)}) async-start(), calls=%async_computation.6 | async-start | bytes 2359296 | tf_op jit(solution)/shard_map/reduce_scatter | solution.py:209
  17.9 16.7 %collective-permute-start.1 = (bf16[2,6,6,1024]{3,2,1,0:T(8,128)(2,1)}, bf16[2,6,6,1024]{3,2,1,0:T(8,128)(2,1)}, u32[]{:S(2)}, u32[]{:S(2)}) collective-permute-start(bf16[2,6,6,1024]{3,2,1,0:T(8,128)(2,1)} %get-tuple-element.44), channel_id=1, source_target_pairs={{1,0},{2,1},{3,2},{5,4},{6,5},{7,6},{9,8},{10,9},{11,10},{13,12},{... | collective-permute-start | bytes 442376 | tf_op jit(solution)/shard_map/ppermute | solution.py:23
  19.2 15.4 %collective-permute-start = (bf16[2,6,6,1024]{3,2,1,0:T(8,128)(2,1)}, bf16[2,6,6,1024]{3,2,1,0:T(8,128)(2,1)}, u32[]{:S(2)}, u32[]{:S(2)}) collective-permute-start(bf16[2,6,6,1024]{3,2,1,0:T(8,128)(2,1)} %get-tuple-element.45), channel_id=1, source_target_pairs={{0,1},{1,2},{2,3},{4,5},{5,6},{6,7},{8,9},{9,10},{10,11},{12,13},{... | collective-permute-start | bytes 442376 | tf_op jit(solution)/shard_map/ppermute | solution.py:21
  29.8 10.6 %slice-start = ((bf16[2,6,12,1536]{3,2,1,0:T(8,128)(2,1)}), bf16[2,6,12,512]{3,2,1,0:T(8,128)(2,1)S(1)}, s32[]{:S(2)}) async-start(bf16[2,6,12,1536]{3,2,1,0:T(8,128)(2,1)} %reshape.180), calls=%async_computation.8 | async-start | bytes 393216 | tf_op jit(solution)/shard_map/slice | solution.py:150
  36.9 17.7 %collective-permute-start.2 = (bf16[2,3,24,1024]{3,2,1,0:T(8,128)(2,1)}, bf16[2,3,24,1024]{3,2,1,0:T(8,128)(2,1)}, u32[]{:S(2)}, u32[]{:S(2)}) collective-permute-start(bf16[2,3,24,1024]{3,2,1,0:T(8,128)(2,1)} %get-tuple-element.42), channel_id=1, source_target_pairs={{0,4},{4,8},{8,12},{12,16},{16,20},{20,24},{24,28},{1,5},{5,9},{9,... | collective-permute-start | bytes 884744 | tf_op jit(solution)/shard_map/ppermute | solution.py:21
  39.1 15.6 %collective-permute-start.3 = (bf16[2,3,24,1024]{3,2,1,0:T(8,128)(2,1)}, bf16[2,3,24,1024]{3,2,1,0:T(8,128)(2,1)}, u32[]{:S(2)}, u32[]{:S(2)}) collective-permute-start(bf16[2,3,24,1024]{3,2,1,0:T(8,128)(2,1)} %get-tuple-element.43), channel_id=1, source_target_pairs={{4,0},{8,4},{12,8},{16,12},{20,16},{24,20},{28,24},{5,1},{9,5},{13... | collective-permute-start | bytes 884744 | tf_op jit(solution)/shard_map/ppermute | solution.py:23
  45.6 9.0 %copy-start.4 = (bf16[2,6,12,1024]{3,2,1,0:T(8,128)(2,1)S(1)}, bf16[2,6,12,1024]{3,2,1,0:T(8,128)(2,1)}, u32[]{:S(2)}) copy-start(bf16[2,6,12,1024]{3,2,1,0:T(8,128)(2,1)} %slice.104) | copy-start | bytes 884740
  66.3 4.5 %copy-start.17 = (pred[4,144]{1,0:T(4,128)(4,1)S(1)}, pred[4,144]{1,0:T(4,128)(4,1)}, u32[]{:S(2)}) copy-start(pred[4,144]{1,0:T(4,128)(4,1)} %gt.28) | copy-start | bytes 1732
  74.4 3.5 %copy-start.5 = (f32[4,8,72,144]{3,2,1,0:T(8,128)S(1)}, f32[4,8,72,144]{3,2,1,0:T(8,128)}, u32[]{:S(2)}) copy-start(f32[4,8,72,144]{3,2,1,0:T(8,128)} %get-tuple-element.47) | copy-start | bytes 3981316
  74.4 3.5 %copy-start.7 = (bf16[4,144,512]{1,2,0:T(8,128)(2,1)S(1)}, bf16[4,144,512]{1,2,0:T(8,128)(2,1)}, u32[]{:S(2)}) copy-start(bf16[4,144,512]{1,2,0:T(8,128)(2,1)} %copy.50) | copy-start | bytes 1769476
  74.4 3.5 %copy-start.10 = (bf16[4,72,512]{1,2,0:T(8,128)(2,1)S(1)}, bf16[4,72,512]{1,2,0:T(8,128)(2,1)}, u32[]{:S(2)}) copy-start(bf16[4,72,512]{1,2,0:T(8,128)(2,1)} %copy.57) | copy-start | bytes 884740
  87.1 4.1 %copy-start.3 = (bf16[4,144,512]{1,2,0:T(8,128)(2,1)S(1)}, bf16[4,144,512]{1,2,0:T(8,128)(2,1)}, u32[]{:S(2)}) copy-start(bf16[4,144,512]{1,2,0:T(8,128)(2,1)} %copy.55) | copy-start | bytes 1769476
  90.1 1.0 copy-start.1
  95.1 5.9 %copy-start.6 = (bf16[2,6,12,1024]{3,0,2,1:T(2,128)(2,1)S(1)}, bf16[2,6,12,1024]{3,0,2,1:T(2,128)(2,1)}, u32[]{:S(2)}) copy-start(bf16[2,6,12,1024]{3,0,2,1:T(2,128)(2,1)} %param.11) | copy-start | bytes 884740
  100.3 0.7 copy-start.8
  102.8 119.8 %reduce-scatter.7.cloned.1.call-start = ((), (), s32[]{:S(2)}) async-start(), calls=%async_computation.4 | async-start | bytes 7077888 | tf_op jit(solution)/shard_map/reduce_scatter | solution.py:208
  125.0 6.7 %collective-permute-start.4 = (bf16[2,3,24,1024]{3,2,1,0:T(8,128)(2,1)S(1)}, bf16[2,3,24,1024]{3,2,1,0:T(8,128)(2,1)S(1)}, u32[]{:S(2)}, u32[]{:S(2)}) collective-permute-start(bf16[2,3,24,1024]{3,2,1,0:T(8,128)(2,1)S(1)} %get-tuple-element.34), channel_id=1, source_target_pairs={{0,4},{4,8},{8,12},{12,16},{16,20},{20,24},{24,28},{1,5},{5,9},{9,... | collective-permute-start | bytes 884744 | tf_op jit(solution)/shard_map/ppermute | solution.py:21
  129.4 4.7 %collective-permute-start.5 = (bf16[2,3,24,1024]{3,2,1,0:T(8,128)(2,1)S(1)}, bf16[2,3,24,1024]{3,2,1,0:T(8,128)(2,1)S(1)}, u32[]{:S(2)}, u32[]{:S(2)}) collective-permute-start(bf16[2,3,24,1024]{3,2,1,0:T(8,128)(2,1)S(1)} %get-tuple-element.35), channel_id=1, source_target_pairs={{4,0},{8,4},{12,8},{16,12},{20,16},{24,20},{28,24},{5,1},{9,5},{13... | collective-permute-start | bytes 884744 | tf_op jit(solution)/shard_map/ppermute | solution.py:23
  134.1 0.7 copy-start.18
  134.8 4.7 %copy-start.9 = (bf16[2,6,12,512]{3,0,2,1:T(2,128)(2,1)S(1)}, bf16[2,6,12,512]{3,0,2,1:T(2,128)(2,1)}, u32[]{:S(2)}) copy-start(bf16[2,6,12,512]{3,0,2,1:T(2,128)(2,1)} %get-tuple-element.38) | copy-start | bytes 442372
  135.1 14.0 %copy-start.2 = (bf16[2,6,12,1024]{3,0,2,1:T(2,128)(2,1)S(1)}, bf16[2,6,12,1024]{3,0,2,1:T(2,128)(2,1)}, u32[]{:S(2)}) copy-start(bf16[2,6,12,1024]{3,0,2,1:T(2,128)(2,1)} %param.6) | copy-start | bytes 884740
  135.1 14.0 %copy-start.15 = (f32[1024]{0:T(1024)S(1)}, f32[1024]{0:T(1024)}, u32[]{:S(2)}) copy-start(f32[1024]{0:T(1024)} %param.7) | copy-start | bytes 12292
  135.1 14.0 %copy-start.16 = (f32[1024]{0:T(1024)S(1)}, f32[1024]{0:T(1024)}, u32[]{:S(2)}) copy-start(f32[1024]{0:T(1024)} %param.8) | copy-start | bytes 12292
  135.2 8.2 %collective-permute-start.6 = (f32[2,6,6,1024]{3,2,1,0:T(8,128)S(1)}, f32[2,6,6,1024]{3,2,1,0:T(8,128)S(1)}, u32[]{:S(2)}, u32[]{:S(2)}) collective-permute-start(f32[2,6,6,1024]{3,2,1,0:T(8,128)S(1)} %get-tuple-element.32), channel_id=1, source_target_pairs={{0,1},{1,2},{2,3},{4,5},{5,6},{6,7},{8,9},{9,10},{10,11},{12,13},{... | collective-permute-start | bytes 884744 | tf_op jit(solution)/shard_map/ppermute | solution.py:21
  138.1 9.9 %collective-permute-start.7 = (f32[2,6,6,1024]{3,2,1,0:T(8,128)S(1)}, f32[2,6,6,1024]{3,2,1,0:T(8,128)S(1)}, u32[]{:S(2)}, u32[]{:S(2)}) collective-permute-start(f32[2,6,6,1024]{3,2,1,0:T(8,128)S(1)} %get-tuple-element.33), channel_id=1, source_target_pairs={{1,0},{2,1},{3,2},{5,4},{6,5},{7,6},{9,8},{10,9},{11,10},{13,12},{... | collective-permute-start | bytes 884744 | tf_op jit(solution)/shard_map/ppermute | solution.py:23
  139.5 8.8 %copy-start.13 = (bf16[2,6,12,512]{3,2,1,0:T(8,128)(2,1)}, bf16[2,6,12,512]{3,2,1,0:T(8,128)(2,1)S(1)}, u32[]{:S(2)}) copy-start(bf16[2,6,12,512]{3,2,1,0:T(8,128)(2,1)S(1)} %copy.79) | copy-start | bytes 442372
  148.3 0.8 copy-start.11
  152.9 2.0 copy-start.20
  152.9 3.2 %copy-start.19 = (u32[32]{0:T(128)S(1)}, u32[32]{0:T(128)}, u32[]{:S(2)}) copy-start(u32[32]{0:T(128)} %constant.64) | copy-start | bytes 388
  152.9 103.2 %reduce-scatter.13.cloned.1.call-start = ((), (), s32[]{:S(2)}) async-start(), calls=%async_computation.7 | async-start | bytes 327680
  154.8 113.8 %reduce-scatter.9.cloned.1.call-start = ((), (), s32[]{:S(2)}) async-start(), calls=%async_computation.5 | async-start | bytes 983040 | tf_op jit(solution)/shard_map/reduce_scatter | solution.py:214
  222.7 2.8 %copy-start.12 = (bf16[2,6,12,1024]{3,2,1,0:T(8,128)(2,1)S(1)}, bf16[2,6,12,1024]{3,2,1,0:T(8,128)(2,1)}, u32[]{:S(2)}) copy-start(bf16[2,6,12,1024]{3,2,1,0:T(8,128)(2,1)} %copy-done.11) | copy-start | bytes 884740
  222.7 2.8 %copy-start.14 = (bf16[2,6,12,512]{3,2,1,0:T(8,128)(2,1)S(1)}, bf16[2,6,12,512]{3,2,1,0:T(8,128)(2,1)}, u32[]{:S(2)}) copy-start(bf16[2,6,12,512]{3,2,1,0:T(8,128)(2,1)} %copy-done.13) | copy-start | bytes 442372
Sparse Core Ops, SparseCore 0:
  103.0 45.4 reduce-scatter.10
  153.0 69.6 reduce-scatter.6
  224.9 19.9 reduce-scatter.12
  247.1 21.3 reduce-scatter.8
where the time goes:
time: 278 us; the launch traced here: 277 us
  waiting for transfers between devices  85.4 us (31%)
  local copies, waits for them, and re-layouts  78 us (28%)
  matrix products  30.3 us (11%)
  blocking collectives  24.5 us (9%)
  other arithmetic  21.7 us (8%)
  starting transfers between devices  21.3 us (8%)
  between operations  15.5 us (6%)
    reduce_scatter x1, waiting for transfers between devices, on_device(): lax.psum_scatter(term_qkv, 'lat', scatter_dimension=0, tiled=True)  65.3 us
    unnamed x2, blocking collectives  24.5 us
    ppermute x4, starting transfers between devices, padded(): lax.ppermute(tail, axis, [(i, (i + 1) % count) for i in range(ends)])  15.7 us
    unnamed x54, local copies, waits for them, and re-layouts  13.1 us
    reduce_scatter x1, waiting for transfers between devices, on_device(): lax.psum_scatter(partial_sums[0], 'lon', scatter_dimension=0, tiled=True)  9.08 us
    ppermute x4, waiting for transfers between devices, padded(): lax.ppermute(head, axis, [((i + 1) % count, i) for i in range(ends)])  7.03 us
    reshape x2, local copies, waits for them, and re-layouts, windows(): return grid_data.reshape(-1, levels * win_rows * WLON, channels)  6.75 us
    concatenate x2, local copies, waits for them, and re-layouts, run_windows(): jnp.concatenate([grad_key.reshape(win_count, key_len, inner_width), grad_...  6.4 us
  transfers between devices with their start and end apart: 12, of which 5 were waited for; matrix products, arithmetic and copies ran while one was open for 24% of the time, Pallas kernels for 0%

commit v1 on v0

v1 whole, which is shorter than its diff:
```python
import functools
import math

import jax
import jax.numpy as jnp
from jax import lax
from jax.experimental import pallas as pl
from jax.experimental.pallas import tpu as pltpu
from jax.sharding import PartitionSpec as P

HDIM = 64
WLAT = 6
WLON = 12
F32 = jnp.float32
BF16 = jnp.bfloat16
LANES = 128

VMEM_SPEC = pl.BlockSpec(memory_space=pltpu.VMEM)
SMEM_SPEC = pl.BlockSpec(memory_space=pltpu.SMEM)


def dot(a, b, contract):
    return lax.dot_general(a, b, ((contract[0], contract[1]), ((), ())), preferred_element_type=F32)


def call(body, name, outs, args, scratch=(), smem=0, cost=None):
    specs = [SMEM_SPEC] * smem + [VMEM_SPEC] * (len(args) - smem)
    return pl.pallas_call(
        body,
        name=name,
        out_shape=[jax.ShapeDtypeStruct(s, d) for s, d in outs],
        in_specs=specs,
        out_specs=[VMEM_SPEC] * len(outs),
        scratch_shapes=list(scratch),
        cost_estimate=cost,
    )(*args)


def corners(rows, cols):
    return ((rows // 2, cols // 2), (rows // 2, 0), (0, cols // 2), (0, 0))


def pack_body(tok_ref, cot_ref, *refs):
    outs, wide = refs[:4], refs[4]
    levels, rows, cols, width = tok_ref.shape
    half_rows, half_cols = rows // 2, cols // 2
    for out_ref, (row0, col0) in zip(outs, corners(rows, cols)):
        for part, ref in enumerate((tok_ref, cot_ref)):
            for level in range(levels):
                for row in range(half_rows):
                    at = (level * half_rows + row) * half_cols
                    line = ref[level, row0 + row].astype(F32)
                    wide[at : at + half_cols, :] = line[col0 : col0 + half_cols]
            out_ref[:, part * width : (part + 1) * width] = wide[...].astype(BF16)


def gather_tokens(quads, part, wide):
    count, width = quads[0].shape[0], wide.shape[1]
    for place, quad in enumerate(quads):
        wide[place * count : (place + 1) * count, :] = quad[
            :, part * width : (part + 1) * width
        ].astype(F32)
    return wide[...]


def normalize(tokens_wide):
    average = jnp.mean(tokens_wide, axis=-1, keepdims=True)
    centered = tokens_wide - average
    inverse = lax.rsqrt(jnp.mean(centered * centered, axis=-1, keepdims=True) + 1e-05)
    return centered * inverse, inverse


def reorder(order_ref, source, target, group):
    for place in range(source.shape[0] // group):
        start = pl.multiple_of(order_ref[place] * group, group)
        target[place * group : (place + 1) * group, :] = source[pl.ds(start, group), :]


def attention_body(
    group, order_ref, edge_ref, q0, q1, q2, q3, gain_ref, bias_ref, w_qkv_ref, w_out_ref,
    keep_ref, send_ref, y_ref, gproj_ref, normed_t_ref,
    wide, att, side, turned,
):
    quads = (q0, q1, q2, q3)
    count = q0.shape[0]
    inner = w_out_ref.shape[0]
    heads = inner // HDIM
    scale = HDIM ** (-0.5)
    grad = gather_tokens(quads, 1, wide).astype(BF16)
    side[...] = wide[...].T.astype(BF16)
    reorder(order_ref, side, turned, group)
    tokens_wide = gather_tokens(quads, 0, wide)
    standard, _ = normalize(tokens_wide)
    normed = standard * gain_ref[...] + bias_ref[...]
    side[...] = normed.T.astype(BF16)
    reorder(order_ref, side, normed_t_ref, group)
    projected = dot(normed.astype(BF16), w_qkv_ref[...], ((1,), (0,))).astype(BF16)
    grad_att = dot(grad, w_out_ref[...], ((1,), (1,))).astype(BF16)
    total = 4 * count
    row_id = lax.broadcasted_iota(jnp.int32, (total, total), 0) // count
    col_id = lax.broadcasted_iota(jnp.int32, (total, total), 1) // count
    apart = jnp.where((row_id >= 2) != (col_id >= 2), edge_ref[0], 0) + jnp.where(
        (row_id % 2) != (col_id % 2), edge_ref[1], 0
    )
    blocked = apart > 0
    for head in range(heads):
        at = slice(head * HDIM, (head + 1) * HDIM)
        query = projected[:, at]
        key = projected[:, inner + head * HDIM : inner + (head + 1) * HDIM]
        value = projected[:, 2 * inner + head * HDIM : 2 * inner + (head + 1) * HDIM]
        grad_head = grad_att[:, at]
        scores = dot(query, key, ((1,), (1,))) * scale
        scores = jnp.where(blocked, -1e30, scores)
        exps = jnp.exp(scores - jnp.max(scores, axis=-1, keepdims=True))
        probs = exps / jnp.sum(exps, axis=-1, keepdims=True)
        low = probs.astype(BF16)
        att[:, at] = dot(low, value, ((1,), (0,))).astype(BF16)
        grad_prob = dot(grad_head, value, ((1,), (1,)))
        inner_sum = jnp.sum(probs * grad_prob, axis=-1, keepdims=True)
        grad_score = probs * (grad_prob - inner_sum)
        score_low = grad_score.astype(BF16)
        gproj_ref[:, at] = (dot(score_low, key, ((1,), (0,))) * scale).astype(BF16)
        gproj_ref[:, inner + head * HDIM : inner + (head + 1) * HDIM] = (
            dot(score_low, query, ((0,), (0,))) * scale
        ).astype(BF16)
        gproj_ref[:, 2 * inner + head * HDIM : 2 * inner + (head + 1) * HDIM] = dot(
            low, grad_head, ((0,), (0,))
        ).astype(BF16)
    half = keep_ref.shape[0]
    for ref, rows in ((keep_ref, slice(0, half)), (send_ref, slice(half, 2 * half))):
        ref[:, :inner] = dot(turned[rows, :], att[...], ((1,), (0,))).astype(BF16)
        ref[:, inner:] = dot(
            normed_t_ref[rows, :], gproj_ref[:, 2 * inner :], ((1,), (0,))
        ).astype(BF16)
    wide[...] = wide[...] + dot(att[...], w_out_ref[...], ((1,), (0,)))
    for place in range(4):
        y_ref[place] = wide[place * count : (place + 1) * count, :].astype(BF16)


def gradient_body(
    group, order_ref, q0, q1, q2, q3, y_ref, gproj_ref, normed_t_ref, gain_ref, w_qkv_ref,
    keep_ref, send_ref, o0, o1, o2, o3,
    wide, flat, turned,
):
    quads = (q0, q1, q2, q3)
    count = q0.shape[0]
    width = wide.shape[1]
    standard, inverse = normalize(gather_tokens(quads, 0, wide))
    grad_normed = dot(gproj_ref[...], w_qkv_ref[...], ((1,), (1,)))
    sums = [
        jnp.sum(grad_normed * standard, axis=0, keepdims=True),
        jnp.sum(grad_normed, axis=0, keepdims=True),
    ]
    line = lax.broadcasted_iota(jnp.int32, (LANES, width), 0)
    block = jnp.where(line == 0, sums[0], jnp.where(line == 1, sums[1], 0.0))
    flat[...] = block.T
    reorder(order_ref, flat, turned, group)
    grad_hat = grad_normed * gain_ref[...]
    first = jnp.mean(grad_hat, axis=-1, keepdims=True)
    second = jnp.mean(grad_hat * standard, axis=-1, keepdims=True)
    change = (grad_hat - first - standard * second) * inverse
    wide[...] = gather_tokens(quads, 1, wide) + change
    for place, out in enumerate((o0, o1, o2, o3)):
        out[:, :width] = y_ref[place]
        out[:, width:] = wide[place * count : (place + 1) * count, :].astype(BF16)
    half, cols = keep_ref.shape
    cols = cols - LANES
    for ref, rows in ((keep_ref, slice(0, half)), (send_ref, slice(half, 2 * half))):
        ref[:, :cols] = dot(normed_t_ref[rows, :], gproj_ref[:, :cols], ((1,), (0,))).astype(BF16)
        ref[:, cols:] = turned[rows, :].astype(BF16)


def unpack_body(q0, q1, q2, q3, y_ref, grad_ref, wide, lines):
    levels, rows, cols, width = y_ref.shape
    half_rows, half_cols = rows // 2, cols // 2
    for part, out in enumerate((y_ref, grad_ref)):
        for quad, (row0, col0) in zip((q0, q1, q2, q3), corners(rows, cols)):
            wide[...] = quad[:, part * width : (part + 1) * width].astype(F32)
            for level in range(levels):
                for row in range(half_rows):
                    at = (level * half_rows + row) * half_cols
                    lines[level, row0 + row, col0 : col0 + half_cols, :] = wide[
                        at : at + half_cols, :
                    ]
        out[...] = lines[...].astype(BF16)


def first_body(keep, got, both, send_a, send_b):
    quarter = send_a.shape[0]
    for out, to, start in (
        (both, 0, 0), (send_a, 0, quarter), (both, quarter, 2 * quarter), (send_b, 0, 3 * quarter),
    ):
        out[to : to + quarter, :] = (
            keep[start : start + quarter, :].astype(F32) + got[start : start + quarter, :].astype(F32)
        ).astype(BF16)


def second_body(keep, got_a, got_b, both, send_a, send_b):
    part = send_a.shape[0]
    for side, (got, send) in enumerate(((got_a, send_a), (got_b, send_b))):
        base = 2 * part * side
        for out, to, start in ((both, part * side, 0), (send, 0, part)):
            out[to : to + part, :] = (
                keep[base + start : base + start + part, :].astype(F32)
                + got[start : start + part, :].astype(F32)
            ).astype(BF16)


def third_body(keep, got_a, got_b, *outs):
    part = got_a.shape[0]
    size = outs[0].shape[0]
    for place, out in enumerate(outs):
        start = place * size
        got = got_a if start < part else got_b
        within = start % part
        out[...] = (
            keep[start : start + size, :].astype(F32) + got[within : within + size, :].astype(F32)
        ).astype(BF16)


def xor_pairs(count, bit):
    return [(i, i ^ bit) for i in range(count)]


def scatter_sum(keep, send, lon_count):
    lat_count = lax.axis_size("lat")
    rows, cols = keep.shape
    got = lax.ppermute(send, "lat", xor_pairs(lat_count, 1))
    quarter = rows // 4
    shape = lambda n: ((n, cols), BF16)
    both, send_a, send_b = call(
        first_body, "sum_first", [shape(2 * quarter), shape(quarter), shape(quarter)], (keep, got)
    )
    got_a = lax.ppermute(send_a, "lat", xor_pairs(lat_count, 2))
    got_b = lax.ppermute(send_b, "lat", xor_pairs(lat_count, 4))
    part = quarter // 2
    both, send_a, send_b = call(
        second_body, "sum_second", [shape(2 * part), shape(part), shape(part)], (both, got_a, got_b)
    )
    got_a = lax.ppermute(send_a, "lat", xor_pairs(lat_count, 4))
    got_b = lax.ppermute(send_b, "lat", xor_pairs(lat_count, 2))
    size = 2 * part // lon_count
    pieces = call(third_body, "sum_third", [shape(size)] * lon_count, (both, got_a, got_b))
    total = pieces[0].astype(F32)
    arrived = [
        lax.ppermute(pieces[k], "lon", [(i, (i + k) % lon_count) for i in range(lon_count)])
        for k in range(1, lon_count)
    ]
    for item in arrived:
        total = total + item.astype(F32)
    return total


def on_device(tokens, layer_norm_gain, layer_norm_bias, w_qkv, w_out, output_cotangent):
    levels, lat_rows, lon_cols, width = tokens.shape
    inner = w_out.shape[0]
    lat_count, lon_count = lax.axis_size("lat"), lax.axis_size("lon")
    lat_place, lon_place = lax.axis_index("lat"), lax.axis_index("lon")
    cells = levels * lat_rows * lon_cols
    count = cells // 4
    norm_factor = 1.0 / math.sqrt(cells * lat_count * lon_count)

    def moved(lat_step, lon_step):
        pairs = []
        for i in range(lat_count):
            for j in range(lon_count):
                to = ((i + lat_step) % lat_count) * lon_count + (j + lon_step) % lon_count
                pairs.append((i * lon_count + j, to))
        return pairs

    steps = ((0, 1), (1, 0), (1, 1))

    own, *sends = call(
        pack_body, "pack", [((count, 2 * width), BF16)] * 4, (tokens, output_cotangent),
        scratch=[pltpu.VMEM((count, width), F32)],
    )
    quads = [own] + [
        lax.ppermute(item, ("lat", "lon"), moved(-a, -b)) for item, (a, b) in zip(sends, steps)
    ]

    share = width // (lat_count * lon_count)
    hyper = lat_count == 8 and lon_count % 2 == 0 and share % 16 == 0
    if hyper:
        group = share
        order = []
        half_lon = lon_count // 2
        for core in range(2):
            for side in range(2):
                for outer in range(2):
                    for nested in range(2):
                        x_bit, y_bit = (outer, nested) if side == 0 else (nested, outer)
                        block = lat_place ^ (core + 2 * x_bit + 4 * y_bit)
                        for k in range(half_lon):
                            step = (lon_place + side * half_lon + k) % lon_count
                            order.append(block * lon_count + step)
        order = jnp.stack(order).astype(jnp.int32)
    else:
        group = 16
        order = jnp.arange(width // group, dtype=jnp.int32)
    edges = jnp.stack([lat_place == lat_count - 1, lon_place == lon_count - 1]).astype(jnp.int32)

    gain_row = layer_norm_gain.reshape(1, width)
    bias_row = layer_norm_bias.reshape(1, width)
    early, early_send, y_part, grad_proj, normed_t = call(
        functools.partial(attention_body, group),
        "attention",
        [
            ((width // 2, 2 * inner), BF16),
            ((width // 2, 2 * inner), BF16),
            ((4, count, width), BF16),
            ((cells, 3 * inner), BF16),
            ((width, cells), BF16),
        ],
        (order, edges, *quads, gain_row, bias_row, w_qkv, w_out),
        scratch=[
            pltpu.VMEM((cells, width), F32),
            pltpu.VMEM((cells, inner), BF16),
            pltpu.VMEM((width, cells), BF16),
            pltpu.VMEM((width, cells), BF16),
        ],
        smem=2,
    )
    late, late_send, *returns = call(
        functools.partial(gradient_body, group),
        "gradient",
        [((width // 2, 2 * inner + LANES), BF16)] * 2 + [((count, 2 * width), BF16)] * 4,
        (order, *quads, y_part, grad_proj, normed_t, gain_row, w_qkv),
        scratch=[
            pltpu.VMEM((cells, width), F32),
            pltpu.VMEM((width, LANES), F32),
            pltpu.VMEM((width, LANES), F32),
        ],
        smem=1,
    )
    if hyper:
        early_total = scatter_sum(early, early_send, lon_count)
        late_total = scatter_sum(late, late_send, lon_count)
    else:
        def natural(a, b):
            whole = jnp.concatenate([a, b], axis=0).astype(F32)
            whole = lax.psum_scatter(whole, "lat", scatter_dimension=0, tiled=True)
            return lax.psum_scatter(whole, "lon", scatter_dimension=0, tiled=True)

        early_total = natural(early, early_send)
        late_total = natural(late, late_send)
    back = [returns[0]] + [
        lax.ppermute(item, ("lat", "lon"), moved(a, b)) for item, (a, b) in zip(returns[1:], steps)
    ]
    y_out, token_gradient = call(
        unpack_body, "unpack", [(tokens.shape, BF16)] * 2, tuple(back),
        scratch=[pltpu.VMEM((count, width), F32), pltpu.VMEM(tokens.shape, F32)],
    )
    early_total = early_total * norm_factor
    late_total = late_total * norm_factor
    d_out = early_total[:, :inner].T
    d_qkv = jnp.concatenate([late_total[:, : 2 * inner], early_total[:, inner:]], axis=1)
    gain_gradient_scaled = late_total[:, 2 * inner]
    d_bias = late_total[:, 2 * inner + 1]
    return (y_out, token_gradient, d_qkv, d_out, gain_gradient_scaled, d_bias)


def solution(mesh):
    in_specs = (P(None, "lat", "lon", None), P(), P(), P(), P(), P(None, "lat", "lon", None))
    out_specs = (
        P(None, "lat", "lon", None),
        P(None, "lat", "lon", None),
        P(("lat", "lon"), None),
        P(None, ("lat", "lon")),
        P(("lat", "lon")),
        P(("lat", "lon")),
    )
    return jax.shard_map(
        on_device, mesh=mesh, in_specs=in_specs, out_specs=out_specs, check_vma=False
    )
```

time: 278 us -> 103 us (0.37)
  local copies, waits for them, and re-layouts: 78 us -> 14.5 us
  waiting for transfers between devices: 85.4 us -> 23.1 us
  Pallas kernels: 0 us -> 33.5 us
  matrix products: 30.3 us -> 0 us
  blocking collectives: 24.5 us -> 0 us
  other arithmetic: 21.7 us -> 2.25 us
  between operations: 15.5 us -> 0.76 us
  starting transfers between devices: 21.3 us -> 28.5 us
    reduce_scatter x3 -> x0, waiting for transfers between devices: 74.4 us -> none  [the longest x1 65.3 us: on_device(): lax.psum_scatter(term_qkv, 'lat', scatter_dimension=0, tiled=True)]
    pallas_call x0 -> x10, Pallas kernels: none -> 33.5 us  [call(): pl.pallas_call(body, name=name, out_shape=[jax.ShapeDtypeStruct(s, d) for...]
    dot_general x11 -> x0, matrix products: 26.7 us -> none  [the longest x1 3.8 us: on_device(): jnp.einsum('td,tj->dj', flat_normed, grad_proj, preferred_element_type=jn...]
    unnamed x2 -> x0, blocking collectives: 24.5 us -> none
    slice x14 -> x2, local copies, waits for them, and re-layouts: 18.9 us -> 0.71 us  [the longest x1 0.7 us: on_device(): d_bias = late_total[:, 2 * inner + 1]]
    reshape x8 -> x0, local copies, waits for them, and re-layouts: 12.6 us -> none  [the longest x2 6.75 us: windows(): return grid_data.reshape(-1, levels * win_rows * WLON, channels)]
    ppermute x8 -> x22, waiting for transfers between devices: 10.9 us -> 23.1 us  [the longest x2 5.66 us: scatter_sum(): got_a = lax.ppermute(send_a, 'lat', xor_pairs(lat_count, 2))]
    concatenate x5 -> x0, local copies, waits for them, and re-layouts: 11.9 us -> none  [the longest x2 6.4 us: run_windows(): jnp.concatenate([grad_key.reshape(win_count, key_len, inner_width), grad_...]
  transfers between devices with their start and end apart: 12 -> 22, of which waited for: 5 -> 10; matrix products, arithmetic and copies ran while one was open for 24% -> 6% of each run, Pallas kernels for 0% -> 19%
where the time goes in v1:
time: 103 us
  Pallas kernels  33.5 us (33%)
  starting transfers between devices  28.5 us (28%)
  waiting for transfers between devices  23.1 us (22%)
  local copies, waits for them, and re-layouts  14.5 us (14%)
  other arithmetic  2.25 us (2%)
    pallas_call x10, Pallas kernels, call(): pl.pallas_call(body, name=name, out_shape=[jax.ShapeDtypeStruct(s, d) for...  33.5 us
    unnamed x44, local copies, waits for them, and re-layouts  12.5 us
    ppermute x6, starting transfers between devices, scatter_sum(): lax.ppermute(pieces[k], 'lon', [(i, (i + k) % lon_count) for i in range(l...  9.22 us
    ppermute x3, starting transfers between devices, on_device(): lax.ppermute(item, ('lat', 'lon'), moved(-a, -b))  7.52 us
    ppermute x2, waiting for transfers between devices, scatter_sum(): got_a = lax.ppermute(send_a, 'lat', xor_pairs(lat_count, 2))  5.66 us
    ppermute x3, waiting for transfers between devices, on_device(): lax.ppermute(item, ('lat', 'lon'), moved(a, b))  5.07 us
    ppermute x2, waiting for transfers between devices, scatter_sum(): got_a = lax.ppermute(send_a, 'lat', xor_pairs(lat_count, 4))  4.18 us
    ppermute x3, waiting for transfers between devices, on_device(): lax.ppermute(item, ('lat', 'lon'), moved(-a, -b))  3.64 us
  transfers between devices with their start and end apart: 22, of which 10 were waited for; matrix products, arithmetic and copies ran while one was open for 6% of the time, Pallas kernels for 19%

profile of v1, /device:TPU:0, one launch (start us, length us, event | category | flops | bytes accessed | tf_op | source)
XLA Modules:
  0.0 102.7 jit_solution(12301144589001578730)
XLA Ops:
  0.6 1.8 %copy.16.tok_ref = bf16[2,6,12,1024]{3,2,1,0:T(8,128)(2,1)} copy(bf16[2,6,12,1024]{3,0,2,1:T(2,128)(2,1)} %param.6) | data formatting | bytes 589824 | tf_op args[0]
  2.4 1.8 %copy.17.cot_ref = bf16[2,6,12,1024]{3,2,1,0:T(8,128)(2,1)} copy(bf16[2,6,12,1024]{3,0,2,1:T(2,128)(2,1)} %param.11) | data formatting | bytes 589824 | tf_op args[5]
  4.2 2.1 %pack.1 = (bf16[36,2048]{1,0:T(8,128)(2,1)}, bf16[36,2048]{1,0:T(8,128)(2,1)}, bf16[36,2048]{1,0:T(8,128)(2,1)}, bf16[36,2048]{1,0:T(8,128)(2,1)}) custom-call(bf16[2,6,12,1024]{3,2,1,0:T(8,128)(2,1)} %copy.16.tok_ref, bf16[2,6,12,1024]{3,2,1,0:T(8,128)(2,1)} %copy.17.cot_ref), custom_call_target="tpu_custom_call" | custom-call | tf_op jit(solution)/shard_map/pack/pallas_call | solution.py:28
  6.3 5.1 %collective-permute-start = (bf16[36,2048]{1,0:T(8,128)(2,1)}, bf16[36,2048]{1,0:T(8,128)(2,1)S(1)}, u32[]{:S(2)}, u32[]{:S(2)}) collective-permute-start(bf16[36,2048]{1,0:T(8,128)(2,1)} %get-tuple-element.44), channel_id=1, source_target_pairs={{0,3},{1,0},{2,1},{3,2},{4,7},{5,4},{6,5},{7,6},{8,11},{9,8},{10,9... | collective-permute-start | bytes 442376 | tf_op jit(solution)/shard_map/ppermute | solution.py:278
  11.4 1.6 %collective-permute-start.1 = (bf16[36,2048]{1,0:T(8,128)(2,1)}, bf16[36,2048]{1,0:T(8,128)(2,1)S(1)}, u32[]{:S(2)}, u32[]{:S(2)}) collective-permute-start(bf16[36,2048]{1,0:T(8,128)(2,1)} %get-tuple-element.45), channel_id=1, source_target_pairs={{0,28},{1,29},{2,30},{3,31},{4,0},{5,1},{6,2},{7,3},{8,4},{9,5},{1... | collective-permute-start | bytes 442376 | tf_op jit(solution)/shard_map/ppermute | solution.py:278
  13.0 0.8 collective-permute-start.2
  13.8 0.7 stack.140.order_ref
  14.5 0.6 add_convert_fusion.edge_ref
  15.1 1.0 collective-permute-done.q1
  16.1 2.6 %collective-permute-done.2.q3 = bf16[36,2048]{1,0:T(8,128)(2,1)S(1)} collective-permute-done((bf16[36,2048]{1,0:T(8,128)(2,1)}, bf16[36,2048]{1,0:T(8,128)(2,1)S(1)}, u32[]{:S(2)}, u32[]{:S(2)}) %collective-permute-start.2) | collective-permute-done | bytes 147488 | tf_op jit(solution)/shard_map/ppermute | solution.py:278
  18.7 0.7 copy-done.4
  19.4 10.2 %attention.1 = (bf16[512,1024]{1,0:T(8,128)(2,1)}, bf16[512,1024]{1,0:T(8,128)(2,1)}, bf16[4,36,1024]{2,1,0:T(8,128)(2,1)}, bf16[144,1536]{1,0:T(8,128)(2,1)}, bf16[1024,144]{1,0:T(8,128)(2,1)}) custom-call(s32[32]{0:T(128)} %stack.140.order_ref, s32[2]{0:T(128)} %add_convert_fusion.edge_ref, bf16[36,2048]{1,0:T(8,128)(2,1)} %get-tuple-element.43.q0, ...), custom_call_target="tpu_custom_call" | custom-call | tf_op jit(solution)/shard_map/attention/pallas_call | solution.py:28
  29.7 5.9 %gradient.1 = (bf16[512,1152]{1,0:T(8,128)(2,1)}, bf16[512,1152]{1,0:T(8,128)(2,1)}, bf16[36,2048]{1,0:T(8,128)(2,1)}, bf16[36,2048]{1,0:T(8,128)(2,1)}, bf16[36...) custom-call(s32[32]{0:T(128)} %stack.140.order_ref, bf16[36,2048]{1,0:T(8,128)(2,1)} %get-tuple-element.43.q0, ...), custom_call_target="tpu_custom_call" | custom-call | tf_op jit(solution)/shard_map/gradient/pallas_call | solution.py:28
  36.0 1.0 copy-done.1
  37.0 2.6 %sum_first.3 = (bf16[256,1024]{1,0:T(8,128)(2,1)}, bf16[128,1024]{1,0:T(8,128)(2,1)}, bf16[128,1024]{1,0:T(8,128)(2,1)}) custom-call(bf16[512,1024]{1,0:T(8,128)(2,1)} %get-tuple-element.68.keep, bf16[512,1024]{1,0:T(8,128)(2,1)} %copy-done.1), custom_call_target="tpu_custom_call" | custom-call | tf_op jit(solution)/shard_map/sum_first/pallas_call | solution.py:28
  39.6 1.7 %collective-permute-start.15 = (bf16[128,1024]{1,0:T(8,128)(2,1)}, bf16[128,1024]{1,0:T(8,128)(2,1)S(1)}, u32[]{:S(2)}, u32[]{:S(2)}) collective-permute-start(bf16[128,1024]{1,0:T(8,128)(2,1)} %get-tuple-element.71), channel_id=1, source_target_pairs={{0,8},{4,12},{8,0},{12,4},{16,24},{20,28},{24,16},{28,20},{1,9},{5... | collective-permute-start | bytes 786440 | tf_op jit(solution)/shard_map/ppermute | solution.py:234
  41.3 1.5 %collective-permute-start.16 = (bf16[128,1024]{1,0:T(8,128)(2,1)}, bf16[128,1024]{1,0:T(8,128)(2,1)S(1)}, u32[]{:S(2)}, u32[]{:S(2)}) collective-permute-start(bf16[128,1024]{1,0:T(8,128)(2,1)} %get-tuple-element.72), channel_id=1, source_target_pairs={{0,16},{4,20},{8,24},{12,28},{16,0},{20,4},{24,8},{28,12},{1,17},{... | collective-permute-start | bytes 786440 | tf_op jit(solution)/shard_map/ppermute | solution.py:235
  42.8 5.7 %collective-permute-done.15.got_a = bf16[128,1024]{1,0:T(8,128)(2,1)S(1)} collective-permute-done((bf16[128,1024]{1,0:T(8,128)(2,1)}, bf16[128,1024]{1,0:T(8,128)(2,1)S(1)}, u32[]{:S(2)}, u32[]{:S(2)}) %collective-permute-start.15) | collective-permute-done | bytes 262176 | tf_op jit(solution)/shard_map/ppermute | solution.py:234
  48.5 1.5 %collective-permute-done.16.got_b = bf16[128,1024]{1,0:T(8,128)(2,1)S(1)} collective-permute-done((bf16[128,1024]{1,0:T(8,128)(2,1)}, bf16[128,1024]{1,0:T(8,128)(2,1)S(1)}, u32[]{:S(2)}, u32[]{:S(2)}) %collective-permute-start.16) | collective-permute-done | bytes 262176 | tf_op jit(solution)/shard_map/ppermute | solution.py:235
  49.9 0.7 copy-done.8
  50.6 2.0 %sum_second.3 = (bf16[128,1024]{1,0:T(8,128)(2,1)}, bf16[64,1024]{1,0:T(8,128)(2,1)}, bf16[64,1024]{1,0:T(8,128)(2,1)}) custom-call(bf16[256,1024]{1,0:T(8,128)(2,1)} %get-tuple-element.70.keep, bf16[128,1024]{1,0:T(8,128)(2,1)} %copy-done.7, bf16[128,1024]{1,0:T(8,128)(2,1)} %copy-done.8), custom_call_target="tpu_custom_call" | custom-call | tf_op jit(solution)/shard_map/sum_second/pallas_call | solution.py:28
  52.6 1.5 %collective-permute-start.17 = (bf16[64,1024]{1,0:T(8,128)(2,1)}, bf16[64,1024]{1,0:T(8,128)(2,1)S(1)}, u32[]{:S(2)}, u32[]{:S(2)}) collective-permute-start(bf16[64,1024]{1,0:T(8,128)(2,1)} %get-tuple-element.74), channel_id=1, source_target_pairs={{0,16},{4,20},{8,24},{12,28},{16,0},{20,4},{24,8},{28,12},{1,17},{... | collective-permute-start | bytes 393224 | tf_op jit(solution)/shard_map/ppermute | solution.py:240
  54.5 1.0 %copy-done = bf16[512,1152]{1,0:T(8,128)(2,1)} copy-done((bf16[512,1152]{1,0:T(8,128)(2,1)}, bf16[512,1152]{1,0:T(8,128)(2,1)S(1)}, u32[]{:S(2)}) %copy-start) | copy-done | bytes 1179672
  55.6 2.8 %sum_first.2 = (bf16[256,1152]{1,0:T(8,128)(2,1)}, bf16[128,1152]{1,0:T(8,128)(2,1)}, bf16[128,1152]{1,0:T(8,128)(2,1)}) custom-call(bf16[512,1152]{1,0:T(8,128)(2,1)} %get-tuple-element.56.keep, bf16[512,1152]{1,0:T(8,128)(2,1)} %copy-done), custom_call_target="tpu_custom_call" | custom-call | tf_op jit(solution)/shard_map/sum_first/pallas_call | solution.py:28
  58.4 1.7 %collective-permute-start.7 = (bf16[128,1152]{1,0:T(8,128)(2,1)}, bf16[128,1152]{1,0:T(8,128)(2,1)S(1)}, u32[]{:S(2)}, u32[]{:S(2)}) collective-permute-start(bf16[128,1152]{1,0:T(8,128)(2,1)} %get-tuple-element.59), channel_id=1, source_target_pairs={{0,8},{4,12},{8,0},{12,4},{16,24},{20,28},{24,16},{28,20},{1,9},{5... | collective-permute-start | bytes 884744 | tf_op jit(solution)/shard_map/ppermute | solution.py:234
  61.0 1.8 %collective-permute-start.5 = (bf16[36,2048]{1,0:T(8,128)(2,1)S(1)}, bf16[36,2048]{1,0:T(8,128)(2,1)S(1)}, u32[]{:S(2)}, u32[]{:S(2)}) collective-permute-start(bf16[36,2048]{1,0:T(8,128)(2,1)S(1)} %copy-done.17), channel_id=1, source_target_pairs={{0,5},{1,6},{2,7},{3,4},{4,9},{5,10},{6,11},{7,8},{8,13},{9,14},{1... | collective-permute-start | bytes 442376 | tf_op jit(solution)/shard_map/ppermute | solution.py:347
  62.8 1.7 %sum_third.3 = (bf16[32,1024]{1,0:T(8,128)(2,1)}, bf16[32,1024]{1,0:T(8,128)(2,1)}, bf16[32,1024]{1,0:T(8,128)(2,1)}, bf16[32,1024]{1,0:T(8,128)(2,1)}) custom-call(bf16[128,1024]{1,0:T(8,128)(2,1)} %get-tuple-element.73.keep, bf16[64,1024]{1,0:T(8,128)(2,1)} %copy-done.14, bf16[64,1024]{1,0:T(8,128)(2,1)} %copy-done.15), custom_call_target="tpu_custom_call" | custom-call | tf_op jit(solution)/shard_map/sum_third/pallas_call | solution.py:28
  64.6 5.1 %collective-permute-done.3.q1 = bf16[36,2048]{1,0:T(8,128)(2,1)S(1)} collective-permute-done((bf16[36,2048]{1,0:T(8,128)(2,1)S(1)}, bf16[36,2048]{1,0:T(8,128)(2,1)S(1)}, u32[]{:S(2)}, u32[]{:S(2)}) %collective-permute-start.3) | collective-permute-done | bytes 147488 | tf_op jit(solution)/shard_map/ppermute | solution.py:347
  69.7 2.9 %collective-permute-start.20 = (bf16[32,1024]{1,0:T(8,128)(2,1)}, bf16[32,1024]{1,0:T(8,128)(2,1)S(1)}, u32[]{:S(2)}, u32[]{:S(2)}) collective-permute-start(bf16[32,1024]{1,0:T(8,128)(2,1)} %get-tuple-element.78), channel_id=1, source_target_pairs={{0,2},{1,3},{2,0},{3,1},{4,6},{5,7},{6,4},{7,5},{8,10},{9,11},{10,... | collective-permute-start | bytes 196616 | tf_op jit(solution)/shard_map/ppermute | solution.py:246
  72.5 1.5 %collective-permute-start.21 = (bf16[32,1024]{1,0:T(8,128)(2,1)}, bf16[32,1024]{1,0:T(8,128)(2,1)S(1)}, u32[]{:S(2)}, u32[]{:S(2)}) collective-permute-start(bf16[32,1024]{1,0:T(8,128)(2,1)} %get-tuple-element.79), channel_id=1, source_target_pairs={{0,3},{1,0},{2,1},{3,2},{4,7},{5,4},{6,5},{7,6},{8,11},{9,8},{10,9... | collective-permute-start | bytes 196616 | tf_op jit(solution)/shard_map/ppermute | solution.py:246
  74.0 2.3 %unpack.1 = (bf16[2,6,12,1024]{3,2,1,0:T(8,128)(2,1)}, bf16[2,6,12,1024]{3,2,1,0:T(8,128)(2,1)}) custom-call(bf16[36,2048]{1,0:T(8,128)(2,1)} %get-tuple-element.50.q0, bf16[36,2048]{1,0:T(8,128)(2,1)} %copy-done.9, bf16[36,2048]{1,0:T(8,128)(2,1)} %copy-done.10, bf16[36,2048]{1,0:T(8,128)(2,1)} %copy-done.11), custom_call_target="tpu_custom_call" | custom-call | tf_op jit(solution)/shard_map/unpack/pallas_call | solution.py:28
  76.3 2.0 %copy.18 = bf16[2,6,12,1024]{3,0,2,1:T(2,128)(2,1)} copy(bf16[2,6,12,1024]{3,2,1,0:T(8,128)(2,1)} %get-tuple-element.86) | data formatting | bytes 589824
  78.4 2.0 %copy.19 = bf16[2,6,12,1024]{3,0,2,1:T(2,128)(2,1)} copy(bf16[2,6,12,1024]{3,2,1,0:T(8,128)(2,1)} %get-tuple-element.87) | data formatting | bytes 589824
  80.4 0.7 copy-done.5
  81.2 2.1 %sum_second.2 = (bf16[128,1152]{1,0:T(8,128)(2,1)}, bf16[64,1152]{1,0:T(8,128)(2,1)}, bf16[64,1152]{1,0:T(8,128)(2,1)}) custom-call(bf16[256,1152]{1,0:T(8,128)(2,1)} %get-tuple-element.58.keep, bf16[128,1152]{1,0:T(8,128)(2,1)} %copy-done.5, bf16[128,1152]{1,0:T(8,128)(2,1)} %copy-done.6), custom_call_target="tpu_custom_call" | custom-call | tf_op jit(solution)/shard_map/sum_second/pallas_call | solution.py:28
  83.3 1.2 %collective-permute-start.9 = (bf16[64,1152]{1,0:T(8,128)(2,1)}, bf16[64,1152]{1,0:T(8,128)(2,1)S(1)}, u32[]{:S(2)}, u32[]{:S(2)}) collective-permute-start(bf16[64,1152]{1,0:T(8,128)(2,1)} %get-tuple-element.62), channel_id=1, source_target_pairs={{0,16},{4,20},{8,24},{12,28},{16,0},{20,4},{24,8},{28,12},{1,17},{... | collective-permute-start | bytes 442376 | tf_op jit(solution)/shard_map/ppermute | solution.py:240
  85.1 4.2 %collective-permute-done.9.got_a = bf16[64,1152]{1,0:T(8,128)(2,1)S(1)} collective-permute-done((bf16[64,1152]{1,0:T(8,128)(2,1)}, bf16[64,1152]{1,0:T(8,128)(2,1)S(1)}, u32[]{:S(2)}, u32[]{:S(2)}) %collective-permute-start.9) | collective-permute-done | bytes 147488 | tf_op jit(solution)/shard_map/ppermute | solution.py:240
  89.3 0.6 collective-permute-done.10.got_b
  90.5 1.8 %sum_third.2 = (bf16[32,1152]{1,0:T(8,128)(2,1)}, bf16[32,1152]{1,0:T(8,128)(2,1)}, bf16[32,1152]{1,0:T(8,128)(2,1)}, bf16[32,1152]{1,0:T(8,128)(2,1)}) custom-call(bf16[128,1152]{1,0:T(8,128)(2,1)} %get-tuple-element.61.keep, bf16[64,1152]{1,0:T(8,128)(2,1)} %copy-done.12, bf16[64,1152]{1,0:T(8,128)(2,1)} %copy-done.13), custom_call_target="tpu_custom_call" | custom-call | tf_op jit(solution)/shard_map/sum_third/pallas_call | solution.py:28
  92.3 1.2 %collective-permute-start.11 = (bf16[32,1152]{1,0:T(8,128)(2,1)}, bf16[32,1152]{1,0:T(8,128)(2,1)S(1)}, u32[]{:S(2)}, u32[]{:S(2)}) collective-permute-start(bf16[32,1152]{1,0:T(8,128)(2,1)} %get-tuple-element.65), channel_id=1, source_target_pairs={{0,1},{1,2},{2,3},{3,0},{4,5},{5,6},{6,7},{7,4},{8,9},{9,10},{10,1... | collective-permute-start | bytes 221192 | tf_op jit(solution)/shard_map/ppermute | solution.py:246
  93.5 0.8 collective-permute-start.12
  94.3 2.9 %collective-permute-start.13 = (bf16[32,1152]{1,0:T(8,128)(2,1)}, bf16[32,1152]{1,0:T(8,128)(2,1)S(1)}, u32[]{:S(2)}, u32[]{:S(2)}) collective-permute-start(bf16[32,1152]{1,0:T(8,128)(2,1)} %get-tuple-element.67), channel_id=1, source_target_pairs={{0,3},{1,0},{2,1},{3,2},{4,7},{5,4},{6,5},{7,6},{8,11},{9,8},{10,9... | collective-permute-start | bytes 221192 | tf_op jit(solution)/shard_map/ppermute | solution.py:246
  97.2 0.6 slice_bitcast_fusion
  97.9 1.0 collective-permute-done.11
  98.9 1.5 %collective-permute-done.12 = bf16[32,1152]{1,0:T(8,128)(2,1)S(1)} collective-permute-done((bf16[32,1152]{1,0:T(8,128)(2,1)}, bf16[32,1152]{1,0:T(8,128)(2,1)S(1)}, u32[]{:S(2)}, u32[]{:S(2)}) %collective-permute-start.12) | collective-permute-done | bytes 73760 | tf_op jit(solution)/shard_map/ppermute | solution.py:246
  100.4 0.9 add_multiply_fusion
  101.3 0.7 slice_reduce_fusion
  102.0 0.7 pad_maximum_fusion
  (58 shorter events, 3.3 us)
Async XLA Ops:
  6.3 9.7 %collective-permute-start = (bf16[36,2048]{1,0:T(8,128)(2,1)}, bf16[36,2048]{1,0:T(8,128)(2,1)S(1)}, u32[]{:S(2)}, u32[]{:S(2)}) collective-permute-start(bf16[36,2048]{1,0:T(8,128)(2,1)} %get-tuple-element.44), channel_id=1, source_target_pairs={{0,3},{1,0},{2,1},{3,2},{4,7},{5,4},{6,5},{7,6},{8,11},{9,8},{10,9... | collective-permute-start | bytes 442376 | tf_op jit(solution)/shard_map/ppermute | solution.py:278
  11.4 4.8 %collective-permute-start.1 = (bf16[36,2048]{1,0:T(8,128)(2,1)}, bf16[36,2048]{1,0:T(8,128)(2,1)S(1)}, u32[]{:S(2)}, u32[]{:S(2)}) collective-permute-start(bf16[36,2048]{1,0:T(8,128)(2,1)} %get-tuple-element.45), channel_id=1, source_target_pairs={{0,28},{1,29},{2,30},{3,31},{4,0},{5,1},{6,2},{7,3},{8,4},{9,5},{1... | collective-permute-start | bytes 442376 | tf_op jit(solution)/shard_map/ppermute | solution.py:278
  13.0 5.7 %collective-permute-start.2 = (bf16[36,2048]{1,0:T(8,128)(2,1)}, bf16[36,2048]{1,0:T(8,128)(2,1)S(1)}, u32[]{:S(2)}, u32[]{:S(2)}) collective-permute-start(bf16[36,2048]{1,0:T(8,128)(2,1)} %get-tuple-element.46), channel_id=1, source_target_pairs={{0,31},{1,28},{2,29},{3,30},{4,3},{5,0},{6,1},{7,2},{8,7},{9,4},{1... | collective-permute-start | bytes 442376 | tf_op jit(solution)/shard_map/ppermute | solution.py:278
  16.0 2.7 %copy-start.2 = (bf16[36,2048]{1,0:T(8,128)(2,1)}, bf16[36,2048]{1,0:T(8,128)(2,1)S(1)}, u32[]{:S(2)}) copy-start(bf16[36,2048]{1,0:T(8,128)(2,1)S(1)} %collective-permute-done.q1) | copy-start | bytes 442372
  16.1 2.6 %copy-start.3 = (bf16[36,2048]{1,0:T(8,128)(2,1)}, bf16[36,2048]{1,0:T(8,128)(2,1)S(1)}, u32[]{:S(2)}) copy-start(bf16[36,2048]{1,0:T(8,128)(2,1)S(1)} %collective-permute-done.1.q2) | copy-start | bytes 442372
  18.7 0.7 copy-start.4
  29.6 6.4 %collective-permute-start.14 = (bf16[512,1024]{1,0:T(8,128)(2,1)}, bf16[512,1024]{1,0:T(8,128)(2,1)S(1)}, u32[]{:S(2)}, u32[]{:S(2)}) collective-permute-start(bf16[512,1024]{1,0:T(8,128)(2,1)} %get-tuple-element.69), channel_id=1, source_target_pairs={{0,4},{4,0},{8,12},{12,8},{16,20},{20,16},{24,28},{28,24},{1,5},{5... | collective-permute-start | bytes 3145736 | tf_op jit(solution)/shard_map/ppermute | solution.py:228
  35.6 18.9 %collective-permute-start.6 = (bf16[512,1152]{1,0:T(8,128)(2,1)}, bf16[512,1152]{1,0:T(8,128)(2,1)S(1)}, u32[]{:S(2)}, u32[]{:S(2)}) collective-permute-start(bf16[512,1152]{1,0:T(8,128)(2,1)} %get-tuple-element.57), channel_id=1, source_target_pairs={{0,4},{4,0},{8,12},{12,8},{16,20},{20,16},{24,28},{28,24},{1,5},{5... | collective-permute-start | bytes 3538952 | tf_op jit(solution)/shard_map/ppermute | solution.py:228
  36.0 1.0 copy-start.1
  39.6 8.9 %collective-permute-start.15 = (bf16[128,1024]{1,0:T(8,128)(2,1)}, bf16[128,1024]{1,0:T(8,128)(2,1)S(1)}, u32[]{:S(2)}, u32[]{:S(2)}) collective-permute-start(bf16[128,1024]{1,0:T(8,128)(2,1)} %get-tuple-element.71), channel_id=1, source_target_pairs={{0,8},{4,12},{8,0},{12,4},{16,24},{20,28},{24,16},{28,20},{1,9},{5... | collective-permute-start | bytes 786440 | tf_op jit(solution)/shard_map/ppermute | solution.py:234
  41.3 8.6 %collective-permute-start.16 = (bf16[128,1024]{1,0:T(8,128)(2,1)}, bf16[128,1024]{1,0:T(8,128)(2,1)S(1)}, u32[]{:S(2)}, u32[]{:S(2)}) collective-permute-start(bf16[128,1024]{1,0:T(8,128)(2,1)} %get-tuple-element.72), channel_id=1, source_target_pairs={{0,16},{4,20},{8,24},{12,28},{16,0},{20,4},{24,8},{28,12},{1,17},{... | collective-permute-start | bytes 786440 | tf_op jit(solution)/shard_map/ppermute | solution.py:235
  48.5 1.5 %copy-start.7 = (bf16[128,1024]{1,0:T(8,128)(2,1)}, bf16[128,1024]{1,0:T(8,128)(2,1)S(1)}, u32[]{:S(2)}) copy-start(bf16[128,1024]{1,0:T(8,128)(2,1)S(1)} %collective-permute-done.15.got_a) | copy-start | bytes 786436
  49.9 0.7 copy-start.8
  52.6 8.2 %collective-permute-start.17 = (bf16[64,1024]{1,0:T(8,128)(2,1)}, bf16[64,1024]{1,0:T(8,128)(2,1)S(1)}, u32[]{:S(2)}, u32[]{:S(2)}) collective-permute-start(bf16[64,1024]{1,0:T(8,128)(2,1)} %get-tuple-element.74), channel_id=1, source_target_pairs={{0,16},{4,20},{8,24},{12,28},{16,0},{20,4},{24,8},{28,12},{1,17},{... | collective-permute-start | bytes 393224 | tf_op jit(solution)/shard_map/ppermute | solution.py:240
  54.2 6.8 %collective-permute-start.18 = (bf16[64,1024]{1,0:T(8,128)(2,1)}, bf16[64,1024]{1,0:T(8,128)(2,1)S(1)}, u32[]{:S(2)}, u32[]{:S(2)}) collective-permute-start(bf16[64,1024]{1,0:T(8,128)(2,1)} %get-tuple-element.75), channel_id=1, source_target_pairs={{0,8},{4,12},{8,0},{12,4},{16,24},{20,28},{24,16},{28,20},{1,9},{5... | collective-permute-start | bytes 393224 | tf_op jit(solution)/shard_map/ppermute | solution.py:241
  54.5 1.0 %copy-start = (bf16[512,1152]{1,0:T(8,128)(2,1)}, bf16[512,1152]{1,0:T(8,128)(2,1)S(1)}, u32[]{:S(2)}) copy-start(bf16[512,1152]{1,0:T(8,128)(2,1)S(1)} %collective-permute-done.6.got) | copy-start | bytes 3538948
  55.6 5.0 %copy-start.19 = (bf16[36,2048]{1,0:T(8,128)(2,1)S(1)}, bf16[36,2048]{1,0:T(8,128)(2,1)}, u32[]{:S(2)}) copy-start(bf16[36,2048]{1,0:T(8,128)(2,1)} %get-tuple-element.51) | copy-start | bytes 442372
  55.6 5.3 %copy-start.18 = (bf16[36,2048]{1,0:T(8,128)(2,1)S(1)}, bf16[36,2048]{1,0:T(8,128)(2,1)}, u32[]{:S(2)}) copy-start(bf16[36,2048]{1,0:T(8,128)(2,1)} %get-tuple-element.52) | copy-start | bytes 442372
  55.6 5.4 %copy-start.17 = (bf16[36,2048]{1,0:T(8,128)(2,1)S(1)}, bf16[36,2048]{1,0:T(8,128)(2,1)}, u32[]{:S(2)}) copy-start(bf16[36,2048]{1,0:T(8,128)(2,1)} %get-tuple-element.53) | copy-start | bytes 442372
  58.4 22.0 %collective-permute-start.7 = (bf16[128,1152]{1,0:T(8,128)(2,1)}, bf16[128,1152]{1,0:T(8,128)(2,1)S(1)}, u32[]{:S(2)}, u32[]{:S(2)}) collective-permute-start(bf16[128,1152]{1,0:T(8,128)(2,1)} %get-tuple-element.59), channel_id=1, source_target_pairs={{0,8},{4,12},{8,0},{12,4},{16,24},{20,28},{24,16},{28,20},{1,9},{5... | collective-permute-start | bytes 884744 | tf_op jit(solution)/shard_map/ppermute | solution.py:234
  60.0 20.3 %collective-permute-start.8 = (bf16[128,1152]{1,0:T(8,128)(2,1)}, bf16[128,1152]{1,0:T(8,128)(2,1)S(1)}, u32[]{:S(2)}, u32[]{:S(2)}) collective-permute-start(bf16[128,1152]{1,0:T(8,128)(2,1)} %get-tuple-element.60), channel_id=1, source_target_pairs={{0,16},{4,20},{8,24},{12,28},{16,0},{20,4},{24,8},{28,12},{1,17},{... | collective-permute-start | bytes 884744 | tf_op jit(solution)/shard_map/ppermute | solution.py:235
  60.5 9.1 %collective-permute-start.3 = (bf16[36,2048]{1,0:T(8,128)(2,1)S(1)}, bf16[36,2048]{1,0:T(8,128)(2,1)S(1)}, u32[]{:S(2)}, u32[]{:S(2)}) collective-permute-start(bf16[36,2048]{1,0:T(8,128)(2,1)S(1)} %copy-done.19), channel_id=1, source_target_pairs={{0,1},{1,2},{2,3},{3,0},{4,5},{5,6},{6,7},{7,4},{8,9},{9,10},{10,1... | collective-permute-start | bytes 442376 | tf_op jit(solution)/shard_map/ppermute | solution.py:347
  60.9 1.9 %copy-start.14 = (bf16[64,1024]{1,0:T(8,128)(2,1)}, bf16[64,1024]{1,0:T(8,128)(2,1)S(1)}, u32[]{:S(2)}) copy-start(bf16[64,1024]{1,0:T(8,128)(2,1)S(1)} %collective-permute-done.17.got_a) | copy-start | bytes 393220
  60.9 8.8 %collective-permute-start.4 = (bf16[36,2048]{1,0:T(8,128)(2,1)S(1)}, bf16[36,2048]{1,0:T(8,128)(2,1)S(1)}, u32[]{:S(2)}, u32[]{:S(2)}) collective-permute-start(bf16[36,2048]{1,0:T(8,128)(2,1)S(1)} %copy-done.18), channel_id=1, source_target_pairs={{0,4},{1,5},{2,6},{3,7},{4,8},{5,9},{6,10},{7,11},{8,12},{9,13},{1... | collective-permute-start | bytes 442376 | tf_op jit(solution)/shard_map/ppermute | solution.py:347
  61.0 1.9 %copy-start.15 = (bf16[64,1024]{1,0:T(8,128)(2,1)}, bf16[64,1024]{1,0:T(8,128)(2,1)S(1)}, u32[]{:S(2)}) copy-start(bf16[64,1024]{1,0:T(8,128)(2,1)S(1)} %collective-permute-done.18.got_b) | copy-start | bytes 393220
  61.0 11.6 %collective-permute-start.5 = (bf16[36,2048]{1,0:T(8,128)(2,1)S(1)}, bf16[36,2048]{1,0:T(8,128)(2,1)S(1)}, u32[]{:S(2)}, u32[]{:S(2)}) collective-permute-start(bf16[36,2048]{1,0:T(8,128)(2,1)S(1)} %copy-done.17), channel_id=1, source_target_pairs={{0,5},{1,6},{2,7},{3,4},{4,9},{5,10},{6,11},{7,8},{8,13},{9,14},{1... | collective-permute-start | bytes 442376 | tf_op jit(solution)/shard_map/ppermute | solution.py:347
  69.6 4.4 %copy-start.9 = (bf16[36,2048]{1,0:T(8,128)(2,1)}, bf16[36,2048]{1,0:T(8,128)(2,1)S(1)}, u32[]{:S(2)}) copy-start(bf16[36,2048]{1,0:T(8,128)(2,1)S(1)} %collective-permute-done.3.q1) | copy-start | bytes 442372
  69.6 15.4 %collective-permute-start.19 = (bf16[32,1024]{1,0:T(8,128)(2,1)}, bf16[32,1024]{1,0:T(8,128)(2,1)S(1)}, u32[]{:S(2)}, u32[]{:S(2)}) collective-permute-start(bf16[32,1024]{1,0:T(8,128)(2,1)} %get-tuple-element.77), channel_id=1, source_target_pairs={{0,1},{1,2},{2,3},{3,0},{4,5},{5,6},{6,7},{7,4},{8,9},{9,10},{10,1... | collective-permute-start | bytes 196616 | tf_op jit(solution)/shard_map/ppermute | solution.py:246
  69.7 4.4 %copy-start.10 = (bf16[36,2048]{1,0:T(8,128)(2,1)}, bf16[36,2048]{1,0:T(8,128)(2,1)S(1)}, u32[]{:S(2)}) copy-start(bf16[36,2048]{1,0:T(8,128)(2,1)S(1)} %collective-permute-done.4.q2) | copy-start | bytes 442372
  69.7 15.4 %collective-permute-start.20 = (bf16[32,1024]{1,0:T(8,128)(2,1)}, bf16[32,1024]{1,0:T(8,128)(2,1)S(1)}, u32[]{:S(2)}, u32[]{:S(2)}) collective-permute-start(bf16[32,1024]{1,0:T(8,128)(2,1)} %get-tuple-element.78), channel_id=1, source_target_pairs={{0,2},{1,3},{2,0},{3,1},{4,6},{5,7},{6,4},{7,5},{8,10},{9,11},{10,... | collective-permute-start | bytes 196616 | tf_op jit(solution)/shard_map/ppermute | solution.py:246
  72.5 1.5 %copy-start.11 = (bf16[36,2048]{1,0:T(8,128)(2,1)}, bf16[36,2048]{1,0:T(8,128)(2,1)S(1)}, u32[]{:S(2)}) copy-start(bf16[36,2048]{1,0:T(8,128)(2,1)S(1)} %collective-permute-done.5.q3) | copy-start | bytes 442372
  72.5 12.5 %collective-permute-start.21 = (bf16[32,1024]{1,0:T(8,128)(2,1)}, bf16[32,1024]{1,0:T(8,128)(2,1)S(1)}, u32[]{:S(2)}, u32[]{:S(2)}) collective-permute-start(bf16[32,1024]{1,0:T(8,128)(2,1)} %get-tuple-element.79), channel_id=1, source_target_pairs={{0,3},{1,0},{2,1},{3,2},{4,7},{5,4},{6,5},{7,6},{8,11},{9,8},{10,9... | collective-permute-start | bytes 196616 | tf_op jit(solution)/shard_map/ppermute | solution.py:246
  76.3 8.8 %copy-start.16 = (bf16[32,1024]{1,0:T(8,128)(2,1)S(1)}, bf16[32,1024]{1,0:T(8,128)(2,1)}, u32[]{:S(2)}) copy-start(bf16[32,1024]{1,0:T(8,128)(2,1)} %get-tuple-element.76) | copy-start | bytes 196612
  80.4 0.7 copy-start.5
  80.4 0.8 copy-start.6
  83.3 6.0 %collective-permute-start.9 = (bf16[64,1152]{1,0:T(8,128)(2,1)}, bf16[64,1152]{1,0:T(8,128)(2,1)S(1)}, u32[]{:S(2)}, u32[]{:S(2)}) collective-permute-start(bf16[64,1152]{1,0:T(8,128)(2,1)} %get-tuple-element.62), channel_id=1, source_target_pairs={{0,16},{4,20},{8,24},{12,28},{16,0},{20,4},{24,8},{28,12},{1,17},{... | collective-permute-start | bytes 442376 | tf_op jit(solution)/shard_map/ppermute | solution.py:240
  84.5 5.4 %collective-permute-start.10 = (bf16[64,1152]{1,0:T(8,128)(2,1)}, bf16[64,1152]{1,0:T(8,128)(2,1)S(1)}, u32[]{:S(2)}, u32[]{:S(2)}) collective-permute-start(bf16[64,1152]{1,0:T(8,128)(2,1)} %get-tuple-element.63), channel_id=1, source_target_pairs={{0,8},{4,12},{8,0},{12,4},{16,24},{20,28},{24,16},{28,20},{1,9},{5... | collective-permute-start | bytes 442376 | tf_op jit(solution)/shard_map/ppermute | solution.py:241
  89.3 0.7 copy-start.12
  89.9 0.7 copy-start.13
  92.3 6.5 %collective-permute-start.11 = (bf16[32,1152]{1,0:T(8,128)(2,1)}, bf16[32,1152]{1,0:T(8,128)(2,1)S(1)}, u32[]{:S(2)}, u32[]{:S(2)}) collective-permute-start(bf16[32,1152]{1,0:T(8,128)(2,1)} %get-tuple-element.65), channel_id=1, source_target_pairs={{0,1},{1,2},{2,3},{3,0},{4,5},{5,6},{6,7},{7,4},{8,9},{9,10},{10,1... | collective-permute-start | bytes 221192 | tf_op jit(solution)/shard_map/ppermute | solution.py:246
  93.5 6.9 %collective-permute-start.12 = (bf16[32,1152]{1,0:T(8,128)(2,1)}, bf16[32,1152]{1,0:T(8,128)(2,1)S(1)}, u32[]{:S(2)}, u32[]{:S(2)}) collective-permute-start(bf16[32,1152]{1,0:T(8,128)(2,1)} %get-tuple-element.66), channel_id=1, source_target_pairs={{0,2},{1,3},{2,0},{3,1},{4,6},{5,7},{6,4},{7,5},{8,10},{9,11},{10,... | collective-permute-start | bytes 221192 | tf_op jit(solution)/shard_map/ppermute | solution.py:246
  94.3 6.1 %collective-permute-start.13 = (bf16[32,1152]{1,0:T(8,128)(2,1)}, bf16[32,1152]{1,0:T(8,128)(2,1)S(1)}, u32[]{:S(2)}, u32[]{:S(2)}) collective-permute-start(bf16[32,1152]{1,0:T(8,128)(2,1)} %get-tuple-element.67), channel_id=1, source_target_pairs={{0,3},{1,0},{2,1},{3,2},{4,7},{5,4},{6,5},{7,6},{8,11},{9,8},{10,9... | collective-permute-start | bytes 221192 | tf_op jit(solution)/shard_map/ppermute | solution.py:246

commit v2 on v1

v2 whole, which is shorter than its diff:
```python
import functools
import math

import jax
import jax.numpy as jnp
from jax import lax
from jax.experimental import pallas as pl
from jax.experimental.pallas import tpu as pltpu
from jax.sharding import PartitionSpec as P

HDIM = 64
WLAT = 6
WLON = 12
F32 = jnp.float32
BF16 = jnp.bfloat16
LANES = 128

ANY_SPEC = pl.BlockSpec(memory_space=pl.ANY)
VMEM_SPEC = pl.BlockSpec(memory_space=pltpu.VMEM)
SMEM_SPEC = pl.BlockSpec(memory_space=pltpu.SMEM)


def dot(a, b, contract):
    return lax.dot_general(a, b, ((contract[0], contract[1]), ((), ())), preferred_element_type=F32)


def call(body, name, outs, args, scratch=(), smem=0, cost=None):
    specs = [SMEM_SPEC] * smem + [VMEM_SPEC] * (len(args) - smem)
    return pl.pallas_call(
        body,
        name=name,
        out_shape=[jax.ShapeDtypeStruct(s, d) for s, d in outs],
        in_specs=specs,
        out_specs=[VMEM_SPEC] * len(outs),
        scratch_shapes=list(scratch),
        cost_estimate=cost,
    )(*args)


def corners(rows, cols):
    return ((rows // 2, cols // 2), (rows // 2, 0), (0, cols // 2), (0, 0))


def run_copies(copies):
    for item in copies:
        item.start()
    for item in copies:
        item.wait()


def pack_body(tok_ref, cot_ref, *refs):
    outs, sem = refs[:-1], refs[-1]
    rows, cols = tok_ref.shape[:2]
    copies = []
    for out_ref, (row, col) in zip(outs, corners(rows, cols)[1:]):
        for part, ref in enumerate((tok_ref, cot_ref)):
            copies.append(
                pltpu.make_async_copy(
                    ref.at[pl.ds(row, rows // 2), pl.ds(col, cols // 2)],
                    out_ref.at[part],
                    sem.at[len(copies)],
                )
            )
    run_copies(copies)


def unpack_body(q0, q1, q2, q3, y_ref, grad_ref, sem):
    rows, cols = y_ref.shape[:2]
    copies = []
    for quad, (row, col) in zip((q0, q1, q2, q3), corners(rows, cols)):
        for part, ref in enumerate((y_ref, grad_ref)):
            copies.append(
                pltpu.make_async_copy(
                    quad.at[part],
                    ref.at[pl.ds(row, rows // 2), pl.ds(col, cols // 2)],
                    sem.at[len(copies)],
                )
            )
    run_copies(copies)


def move_cells(body, name, outs, args, count):
    return pl.pallas_call(
        body,
        name=name,
        out_shape=[jax.ShapeDtypeStruct(shape, BF16) for shape in outs],
        in_specs=[ANY_SPEC] * len(args),
        out_specs=[ANY_SPEC] * len(outs),
        scratch_shapes=[pltpu.SemaphoreType.DMA((count,))],
    )(*args)


def gather_window(own, received, part, wide):
    rows, cols, levels, width = own.shape
    count = levels * (rows // 2) * (cols // 2)
    pieces = [own[rows // 2 :, cols // 2 :]] + [item[part] for item in received]
    for place, piece in enumerate(pieces):
        wide[place * count : (place + 1) * count, :] = piece.reshape(count, width).astype(F32)
    return wide[...]


def normalize(tokens_wide):
    average = jnp.mean(tokens_wide, axis=-1, keepdims=True)
    centered = tokens_wide - average
    inverse = lax.rsqrt(jnp.mean(centered * centered, axis=-1, keepdims=True) + 1e-05)
    return centered * inverse, inverse


def reorder(order_ref, source, targets, group, base=0):
    half = source.shape[0] // 2
    for place in range(source.shape[0] // group):
        start = pl.multiple_of(order_ref[place] * group, group)
        at = place * group
        target = targets[at // half]
        at = base + at % half
        target[at : at + group, :] = source[pl.ds(start, group), :]


def attention_body(
    group, order_ref, edge_ref, tok_ref, cot_ref, r1, r2, r3, gain_ref, bias_ref, w_qkv_ref,
    w_out_ref, mine_ref, peer_ref, factor_ref, wide, side,
):
    received = (r1, r2, r3)
    inner, width = w_out_ref.shape
    heads = inner // HDIM
    scale = HDIM ** (-0.5)
    grad = gather_window(cot_ref, received, 1, wide).astype(BF16)
    total = grad.shape[0]
    side[...] = grad.T
    reorder(order_ref, side, (mine_ref, peer_ref), group, width // 2)
    standard, _ = normalize(gather_window(tok_ref, received, 0, wide))
    normed = (standard * gain_ref[...] + bias_ref[...]).astype(BF16)
    side[...] = normed.T
    reorder(order_ref, side, (mine_ref, peer_ref), group)
    projected = dot(normed, w_qkv_ref[...], ((1,), (0,))).astype(BF16)
    grad_att = dot(grad, w_out_ref[...], ((1,), (1,))).astype(BF16)
    count = total // 4
    row_id = lax.broadcasted_iota(jnp.int32, (total, total), 0) // count
    col_id = lax.broadcasted_iota(jnp.int32, (total, total), 1) // count
    apart = jnp.where((row_id >= 2) != (col_id >= 2), edge_ref[0], 0) + jnp.where(
        (row_id % 2) != (col_id % 2), edge_ref[1], 0
    )
    blocked = apart > 0
    for head in range(heads):
        at = head * HDIM
        query = projected[:, at : at + HDIM]
        key = projected[:, inner + at : inner + at + HDIM]
        value = projected[:, 2 * inner + at : 2 * inner + at + HDIM]
        grad_head = grad_att[:, at : at + HDIM]
        scores = dot(query, key, ((1,), (1,))) * scale
        scores = jnp.where(blocked, -1e30, scores)
        exps = jnp.exp(scores - jnp.max(scores, axis=-1, keepdims=True))
        probs = exps / jnp.sum(exps, axis=-1, keepdims=True)
        low = probs.astype(BF16)
        factor_ref[:, at : at + HDIM] = dot(low, value, ((1,), (0,))).astype(BF16)
        grad_prob = dot(grad_head, value, ((1,), (1,)))
        inner_sum = jnp.sum(probs * grad_prob, axis=-1, keepdims=True)
        grad_score = (probs * (grad_prob - inner_sum)).astype(BF16)
        factor_ref[:, inner + at : inner + at + HDIM] = dot(low, grad_head, ((0,), (0,))).astype(
            BF16
        )
        factor_ref[:, 2 * inner + at : 2 * inner + at + HDIM] = (
            dot(grad_score, key, ((1,), (0,))) * scale
        ).astype(BF16)
        factor_ref[:, 3 * inner + at : 3 * inner + at + HDIM] = (
            dot(grad_score, query, ((0,), (0,))) * scale
        ).astype(BF16)


def gradient_body(
    group, order_ref, tok_ref, cot_ref, r1, r2, r3, factor_ref, gain_ref, w_qkv_ref, w_out_ref,
    o0, o1, o2, o3, mine_ref, peer_ref, wide, flat,
):
    received = (r1, r2, r3)
    inner, width = w_out_ref.shape
    outs = (o0, o1, o2, o3)
    quad = o0.shape[1:]
    count = quad[0] * quad[1] * quad[2]
    tokens_wide = gather_window(tok_ref, received, 0, wide)
    standard, inverse = normalize(tokens_wide)
    grad_normed = dot(factor_ref[:, inner : 2 * inner], w_qkv_ref[:, 2 * inner :], ((1,), (1,)))
    grad_normed += dot(factor_ref[:, 2 * inner :], w_qkv_ref[:, : 2 * inner], ((1,), (1,)))
    sums = [
        jnp.sum(grad_normed * standard, axis=0, keepdims=True),
        jnp.sum(grad_normed, axis=0, keepdims=True),
    ]
    line = lax.broadcasted_iota(jnp.int32, (LANES, width), 0)
    flat[...] = jnp.where(line == 0, sums[0], jnp.where(line == 1, sums[1], 0.0)).T
    reorder(order_ref, flat, (mine_ref, peer_ref), group)
    wide[...] = tokens_wide + dot(factor_ref[:, :inner], w_out_ref[...], ((1,), (0,)))
    for place, out in enumerate(outs):
        out[0] = wide[place * count : (place + 1) * count, :].astype(BF16).reshape(quad)
    grad_hat = grad_normed * gain_ref[...]
    first = jnp.mean(grad_hat, axis=-1, keepdims=True)
    second = jnp.mean(grad_hat * standard, axis=-1, keepdims=True)
    change = (grad_hat - first - standard * second) * inverse
    wide[...] = gather_window(cot_ref, received, 1, wide) + change
    for place, out in enumerate(outs):
        out[1] = wide[place * count : (place + 1) * count, :].astype(BF16).reshape(quad)


def split_store(value, outs, cols):
    both, send_a, send_b = outs
    quarter = send_a.shape[0]
    for out, to, start in (
        (both, 0, 0), (send_a, 0, quarter), (both, quarter, 2 * quarter), (send_b, 0, 3 * quarter),
    ):
        out[to : to + quarter, cols] = value[start : start + quarter].astype(BF16)


def early_body(mine, got, factor, factor_got, *outs):
    half = mine.shape[0] // 2
    inner = factor.shape[1] // 4
    for part in range(2):
        rows = slice((1 - part) * half, (2 - part) * half)
        cols = slice(part * inner, (part + 1) * inner)
        value = dot(mine[rows, :], factor[:, cols], ((1,), (0,)))
        value += dot(got[rows, :], factor_got[:, cols], ((1,), (0,)))
        split_store(value, outs, cols)


def late_body(mine, got, factor, factor_got, sums, sums_got, *outs):
    half = mine.shape[0] // 2
    inner = factor.shape[1] // 4
    for part in range(2):
        cols = slice((2 + part) * inner, (3 + part) * inner)
        value = dot(mine[:half, :], factor[:, cols], ((1,), (0,)))
        value += dot(got[:half, :], factor_got[:, cols], ((1,), (0,)))
        split_store(value, outs, slice(part * inner, (part + 1) * inner))
    split_store(sums[...] + sums_got[...], outs, slice(2 * inner, 2 * inner + LANES))


def second_body(keep, got_a, got_b, both, send_a, send_b):
    part = send_a.shape[0]
    for side, (got, send) in enumerate(((got_a, send_a), (got_b, send_b))):
        base = 2 * part * side
        for out, to, start in ((both, part * side, 0), (send, 0, part)):
            out[to : to + part, :] = (
                keep[base + start : base + start + part, :].astype(F32)
                + got[start : start + part, :].astype(F32)
            ).astype(BF16)


def third_body(keep, got_a, got_b, *outs):
    part = got_a.shape[0]
    size = outs[0].shape[0]
    for place, out in enumerate(outs):
        start = place * size
        got = got_a if start < part else got_b
        within = start % part
        out[...] = (
            keep[start : start + size, :].astype(F32) + got[within : within + size, :].astype(F32)
        ).astype(BF16)


def xor_pairs(bit):
    return [(i, i ^ bit) for i in range(lax.axis_size("lat"))]


def swap(value, bit):
    return lax.ppermute(value, "lat", xor_pairs(bit))


def scatter_sum(both, send_a, send_b, lon_count):
    quarter, cols = send_a.shape
    shape = lambda n: ((n, cols), BF16)
    got_a, got_b = swap(send_a, 2), swap(send_b, 4)
    part = quarter // 2
    both, send_a, send_b = call(
        second_body, "sum_second", [shape(2 * part), shape(part), shape(part)], (both, got_a, got_b)
    )
    got_a, got_b = swap(send_a, 4), swap(send_b, 2)
    size = 2 * part // lon_count
    pieces = call(third_body, "sum_third", [shape(size)] * lon_count, (both, got_a, got_b))
    total = pieces[0].astype(F32)
    arrived = [
        lax.ppermute(pieces[k], "lon", [(i, (i + k) % lon_count) for i in range(lon_count)])
        for k in range(1, lon_count)
    ]
    for item in arrived:
        total = total + item.astype(F32)
    return total


def on_device(tokens, layer_norm_gain, layer_norm_bias, w_qkv, w_out, output_cotangent):
    levels, lat_rows, lon_cols, width = tokens.shape
    inner = w_out.shape[0]
    lat_count, lon_count = lax.axis_size("lat"), lax.axis_size("lon")
    lat_place, lon_place = lax.axis_index("lat"), lax.axis_index("lon")
    cells = levels * lat_rows * lon_cols
    norm_factor = 1.0 / math.sqrt(cells * lat_count * lon_count)

    def moved(lat_step, lon_step):
        pairs = []
        for i in range(lat_count):
            for j in range(lon_count):
                to = ((i + lat_step) % lat_count) * lon_count + (j + lon_step) % lon_count
                pairs.append((i * lon_count + j, to))
        return pairs

    steps = ((0, 1), (1, 0), (1, 1))
    grid = (lat_rows, lon_cols, levels, width)
    quad = (2, lat_rows // 2, lon_cols // 2, levels, width)
    tok = tokens.transpose(1, 2, 0, 3)
    cot = output_cotangent.transpose(1, 2, 0, 3)
    sends = move_cells(pack_body, "pack", [quad] * 3, (tok, cot), 6)
    received = [
        lax.ppermute(item, ("lat", "lon"), moved(-a, -b)) for item, (a, b) in zip(sends, steps)
    ]

    share = width // (lat_count * lon_count)
    hyper = lat_count == 8 and lon_count % 2 == 0 and share % 16 == 0
    if hyper:
        group = share
        order = []
        half_lon = lon_count // 2
        for core in range(2):
            for side in range(2):
                for outer in range(2):
                    for nested in range(2):
                        x_bit, y_bit = (outer, nested) if side == 0 else (nested, outer)
                        for k in range(half_lon):
                            order.append((core + 2 * x_bit + 4 * y_bit, side * half_lon + k))
        flips = jnp.array([item[0] for item in order], jnp.int32)
        turns = jnp.array([item[1] for item in order], jnp.int32)
        order = (lat_place ^ flips) * lon_count + (lon_place + turns) % lon_count
    else:
        group = 16
        order = jnp.arange(width // group, dtype=jnp.int32)
    ends = jnp.array([lat_count - 1, lon_count - 1], jnp.int32)
    edges = (jnp.array([1, 0]) * lat_place + jnp.array([0, 1]) * lon_place == ends).astype(jnp.int32)

    gain_row = layer_norm_gain.reshape(1, width)
    bias_row = layer_norm_bias.reshape(1, width)
    mine, peer, factor = call(
        functools.partial(attention_body, group),
        "attention",
        [((width, cells), BF16)] * 2 + [((cells, 4 * inner), BF16)],
        (order, edges, tok, cot, *received, gain_row, bias_row, w_qkv, w_out),
        scratch=[pltpu.VMEM((cells, width), F32), pltpu.VMEM((width, cells), BF16)],
        smem=2,
    )
    q0, q1, q2, q3, sums, sums_peer = call(
        functools.partial(gradient_body, group),
        "gradient",
        [(quad, BF16)] * 4 + [((width // 2, LANES), F32)] * 2,
        (order, tok, cot, *received, factor, gain_row, w_qkv, w_out),
        scratch=[pltpu.VMEM((cells, width), F32), pltpu.VMEM((width, LANES), F32)],
        smem=1,
    )
    if hyper:
        got, factor_got, sums_got = swap(peer, 1), swap(factor, 1), swap(sums_peer, 1)
        quarter = width // 8

        def shapes(cols):
            return [((rows, cols), BF16) for rows in (2 * quarter, quarter, quarter)]

        early = call(early_body, "early", shapes(2 * inner), (mine, got, factor, factor_got))
        late = call(
            late_body, "late", shapes(2 * inner + LANES),
            (mine, got, factor, factor_got, sums, sums_got),
        )
        early_total = scatter_sum(*early, lon_count)
        late_total = scatter_sum(*late, lon_count)
    else:
        half = width // 2
        normed_t = jnp.concatenate([mine[:half], peer[:half]], axis=0)
        cot_t = jnp.concatenate([mine[half:], peer[half:]], axis=0)
        whole = jnp.concatenate(
            [
                dot(cot_t, factor[:, :inner], ((1,), (0,))),
                dot(normed_t, factor[:, inner:], ((1,), (0,))),
                jnp.concatenate([sums, sums_peer], axis=0),
            ],
            axis=1,
        )
        whole = lax.psum_scatter(whole, "lat", scatter_dimension=0, tiled=True)
        whole = lax.psum_scatter(whole, "lon", scatter_dimension=0, tiled=True)
        early_total, late_total = whole[:, : 2 * inner], whole[:, 2 * inner :]
    back = [q0] + [
        lax.ppermute(item, ("lat", "lon"), moved(a, b)) for item, (a, b) in zip((q1, q2, q3), steps)
    ]
    y_out, token_gradient = move_cells(unpack_body, "unpack", [grid] * 2, back, 8)
    early_total = early_total * norm_factor
    late_total = late_total * norm_factor
    d_out = early_total[:, :inner].T
    d_qkv = jnp.concatenate([late_total[:, : 2 * inner], early_total[:, inner:]], axis=1)
    gain_gradient_scaled = late_total[:, 2 * inner]
    d_bias = late_total[:, 2 * inner + 1]
    return (
        y_out.transpose(2, 0, 1, 3),
        token_gradient.transpose(2, 0, 1, 3),
        d_qkv,
        d_out,
        gain_gradient_scaled,
        d_bias,
    )


def solution(mesh):
    in_specs = (P(None, "lat", "lon", None), P(), P(), P(), P(), P(None, "lat", "lon", None))
    out_specs = (
        P(None, "lat", "lon", None),
        P(None, "lat", "lon", None),
        P(("lat", "lon"), None),
        P(None, ("lat", "lon")),
        P(("lat", "lon")),
        P(("lat", "lon")),
    )
    return jax.shard_map(
        on_device, mesh=mesh, in_specs=in_specs, out_specs=out_specs, check_vma=False
    )
```

time: 103 us -> 112 us (1.087)
  Pallas kernels: 33.5 us -> 62.7 us
  waiting for transfers between devices: 23.1 us -> 8.83 us
  local copies, waits for them, and re-layouts: 14.5 us -> 5.63 us
  other arithmetic: 2.25 us -> 4.88 us
    pallas_call x0 -> x2, Pallas kernels: none -> 33.6 us  [move_cells(): pl.pallas_call(body, name=name, out_shape=[jax.ShapeDtypeStruct(shape, BF...]
    unnamed x44 -> x40, local copies, waits for them, and re-layouts: 12.5 us -> 4.28 us
    ppermute x10 -> x11, waiting for transfers between devices: 11.9 us -> 4.21 us  [swap(): return lax.ppermute(value, 'lat', xor_pairs(bit))]
    ppermute x3, waiting for transfers between devices: 5.07 us -> 0.01 us  [on_device(): lax.ppermute(item, ('lat', 'lon'), moved(a, b))]
    pallas_call x10 -> x8, Pallas kernels: 33.5 us -> 29.1 us  [call(): pl.pallas_call(body, name=name, out_shape=[jax.ShapeDtypeStruct(s, d) for...]
    ppermute x6, starting transfers between devices: 9.22 us -> 11.1 us  [scatter_sum(): lax.ppermute(pieces[k], 'lon', [(i, (i + k) % lon_count) for i in range(l...]
    ppermute x3, starting transfers between devices: 2.23 us -> 0.54 us  [on_device(): lax.ppermute(item, ('lat', 'lon'), moved(a, b))]
    ppermute x3, waiting for transfers between devices: 3.64 us -> 2.15 us  [on_device(): lax.ppermute(item, ('lat', 'lon'), moved(-a, -b))]
  transfers between devices with their start and end apart: 22 -> 23, of which waited for: 10 -> 6; matrix products, arithmetic and copies ran while one was open for 6% -> 3% of each run, Pallas kernels for 19% -> 34%
where the time goes in v2:
time: 112 us
  Pallas kernels  62.7 us (56%)
  starting transfers between devices  29 us (26%)
  waiting for transfers between devices  8.83 us (8%)
  local copies, waits for them, and re-layouts  5.63 us (5%)
  other arithmetic  4.88 us (4%)
    pallas_call x2, Pallas kernels, move_cells(): pl.pallas_call(body, name=name, out_shape=[jax.ShapeDtypeStruct(shape, BF...  33.6 us
    pallas_call x8, Pallas kernels, call(): pl.pallas_call(body, name=name, out_shape=[jax.ShapeDtypeStruct(s, d) for...  29.1 us
    ppermute x6, starting transfers between devices, scatter_sum(): lax.ppermute(pieces[k], 'lon', [(i, (i + k) % lon_count) for i in range(l...  11.1 us
    ppermute x11, starting transfers between devices, swap(): return lax.ppermute(value, 'lat', xor_pairs(bit))  9.81 us
    ppermute x3, starting transfers between devices, on_device(): lax.ppermute(item, ('lat', 'lon'), moved(-a, -b))  7.58 us
    unnamed x40, local copies, waits for them, and re-layouts  4.28 us
    ppermute x11, waiting for transfers between devices, swap(): return lax.ppermute(value, 'lat', xor_pairs(bit))  4.21 us
    ppermute x6, waiting for transfers between devices, scatter_sum(): lax.ppermute(pieces[k], 'lon', [(i, (i + k) % lon_count) for i in range(l...  2.46 us
  transfers between devices with their start and end apart: 23, of which 6 were waited for; matrix products, arithmetic and copies ran while one was open for 3% of the time, Pallas kernels for 34%

profile of v2, /device:TPU:0, one launch (start us, length us, event | category | flops | bytes accessed | tf_op | source)
XLA Modules:
  0.0 111.9 jit_solution(10279999767139273363)
XLA Ops:
  0.6 14.6 %pack.1 = (bf16[2,3,6,2,1024]{4,3,2,1,0:T(2,128)(2,1)}, bf16[2,3,6,2,1024]{4,3,2,1,0:T(2,128)(2,1)}, bf16[2,3,6,2,1024]{4,3,2,1,0:T(2,128)(2,1)}) custom-call(bf16[6,12,2,1024]{3,2,1,0:T(2,128)(2,1)} %bitcast.8, bf16[6,12,2,1024]{3,2,1,0:T(2,128)(2,1)} %bitcast.11), custom_call_target="tpu_custom_call" | custom-call | tf_op jit(solution)/shard_map/pack/pallas_call | solution.py:83
  15.2 5.1 %collective-permute-start = (bf16[2,3,6,2,1024]{4,3,2,1,0:T(2,128)(2,1)}, bf16[2,3,6,2,1024]{4,3,2,1,0:T(2,128)(2,1)S(1)}, u32[]{:S(2)}, u32[]{:S(2)}) collective-permute-start(bf16[2,3,6,2,1024]{4,3,2,1,0:T(2,128)(2,1)} %get-tuple-element.40), channel_id=1, source_target_pairs={{0,3},{1,0},{2,1},{3,2},{4,7},{5,4},{6,5},{7,6},{8,11},{9,8},{10,9... | collective-permute-start | bytes 442376 | tf_op jit(solution)/shard_map/ppermute | solution.py:308
  20.3 1.6 %collective-permute-start.1 = (bf16[2,3,6,2,1024]{4,3,2,1,0:T(2,128)(2,1)}, bf16[2,3,6,2,1024]{4,3,2,1,0:T(2,128)(2,1)S(1)}, u32[]{:S(2)}, u32[]{:S(2)}) collective-permute-start(bf16[2,3,6,2,1024]{4,3,2,1,0:T(2,128)(2,1)} %get-tuple-element.41), channel_id=1, source_target_pairs={{0,28},{1,29},{2,30},{3,31},{4,0},{5,1},{6,2},{7,3},{8,4},{9,5},{1... | collective-permute-start | bytes 442376 | tf_op jit(solution)/shard_map/ppermute | solution.py:308
  21.9 0.8 collective-permute-start.2
  22.8 1.2 %fusion.order_ref = s32[32]{0:T(128)} fusion(s32[32]{0:T(128)} %constant.39.clone, s32[32]{0:T(128)} %constant.38.clone, s32[]{:T(128)S(6)} %axis_index.25, s32[]{:T(128)S(6)} %axis_index.23), kind=kLoop, calls=%fused_computation.10 | loop fusion | flops 480 | bytes 392 | tf_op jit(solution)/shard_map/add | solution.py:326
  24.0 1.2 %compare_convert_fusion.edge_ref = s32[2]{0:T(128)} fusion(s32[2]{0:T(128)} %constant.40.clone, s32[2]{0:T(128)} %constant.41.clone, s32[]{:T(128)S(6)} %axis_index.25, s32[]{:T(128)S(6)} %axis_index.23), kind=kLoop, calls=%fused_computation.8 | loop fusion | flops 10 | bytes 32 | tf_op jit(solution)/shard_map/convert_element_type | solution.py:331
  25.2 2.1 %collective-permute-done.2.r3 = bf16[2,3,6,2,1024]{4,3,2,1,0:T(2,128)(2,1)S(1)} collective-permute-done((bf16[2,3,6,2,1024]{4,3,2,1,0:T(2,128)(2,1)}, bf16[2,3,6,2,1024]{4,3,2,1,0:T(2,128)(2,1)S(1)}, u32[]{:S(2)}, u32[]{:S(2)}) %collective-permute-start.2) | collective-permute-done | bytes 147488 | tf_op jit(solution)/shard_map/ppermute | solution.py:308
  27.3 0.7 copy-done.4
  28.0 9.7 %attention.1 = (bf16[1024,144]{1,0:T(8,128)(2,1)}, bf16[1024,144]{1,0:T(8,128)(2,1)}, bf16[144,2048]{1,0:T(8,128)(2,1)}) custom-call(s32[32]{0:T(128)} %fusion.order_ref, s32[2]{0:T(128)} %compare_convert_fusion.edge_ref, bf16[6,12,2,1024]{3,2,1,0:T(2,128)(2,1)} %bitcast.9, bf16[6,12,2,1024]{3,2,1,0:T(2,128)(2,1)} %bitcast.12, ...), custom_call_target="tpu_custom_call" | custom-call | tf_op jit(solution)/shard_map/attention/pallas_call | solution.py:29
  37.8 0.4 collective-permute-start.6
  38.2 5.3 %gradient.1 = (bf16[2,3,6,2,1024]{4,3,2,1,0:T(2,128)(2,1)}, bf16[2,3,6,2,1024]{4,3,2,1,0:T(2,128)(2,1)}, bf16[2,3,6,2,1024]{4,3,2,1,0:T(2,128)(2,1)}, bf16[2,3,6...) custom-call(s32[32]{0:T(128)} %fusion.order_ref, bf16[6,12,2,1024]{3,2,1,0:T(2,128)(2,1)} %bitcast.10, ...), custom_call_target="tpu_custom_call" | custom-call | tf_op jit(solution)/shard_map/gradient/pallas_call | solution.py:29
  43.5 0.2 collective-permute-start.8
  43.7 0.8 copy-done.1
  44.5 0.2 copy-done
  44.7 3.2 %early.1 = (bf16[256,1024]{1,0:T(8,128)(2,1)}, bf16[128,1024]{1,0:T(8,128)(2,1)}, bf16[128,1024]{1,0:T(8,128)(2,1)}) custom-call(bf16[1024,144]{1,0:T(8,128)(2,1)} %get-tuple-element.50.mine, bf16[1024,144]{1,0:T(8,128)(2,1)} %copy-done.1, bf16[144,2048]{1,0:T(8,128)(2,1)} %get-tuple-element.43.factor_ref.factor, bf16[144,2048]{1,0:T(8,128)(2,1)} %copy-done), custom_call_target="tpu_custom_call" | custom-call | tf_op jit(solution)/shard_map/early/pallas_call | solution.py:29
  47.8 2.1 %collective-permute-start.16 = (bf16[128,1024]{1,0:T(8,128)(2,1)}, bf16[128,1024]{1,0:T(8,128)(2,1)S(1)}, u32[]{:S(2)}, u32[]{:S(2)}) collective-permute-start(bf16[128,1024]{1,0:T(8,128)(2,1)} %get-tuple-element.65), channel_id=1, source_target_pairs={{0,8},{4,12},{8,0},{12,4},{16,24},{20,28},{24,16},{28,20},{1,9},{5... | collective-permute-start | bytes 786440 | tf_op jit(solution)/shard_map/ppermute | solution.py:261
  49.9 1.5 %collective-permute-start.17 = (bf16[128,1024]{1,0:T(8,128)(2,1)}, bf16[128,1024]{1,0:T(8,128)(2,1)S(1)}, u32[]{:S(2)}, u32[]{:S(2)}) collective-permute-start(bf16[128,1024]{1,0:T(8,128)(2,1)} %get-tuple-element.66), channel_id=1, source_target_pairs={{0,16},{4,20},{8,24},{12,28},{16,0},{20,4},{24,8},{28,12},{1,17},{... | collective-permute-start | bytes 786440 | tf_op jit(solution)/shard_map/ppermute | solution.py:261
  51.4 0.7 copy-done.9
  52.2 3.3 %late.1 = (bf16[256,1152]{1,0:T(8,128)(2,1)}, bf16[128,1152]{1,0:T(8,128)(2,1)}, bf16[128,1152]{1,0:T(8,128)(2,1)}) custom-call(bf16[1024,144]{1,0:T(8,128)(2,1)} %get-tuple-element.50.mine, bf16[1024,144]{1,0:T(8,128)(2,1)} %copy-done.1, bf16[144,2048]{1,0:T(8,128)(2,1)} %get-tuple-element.43.factor_ref.factor, bf16[144,2048]{1,0:T(8,128)(2,1)} %copy-done, ...), custom_call_target="tpu_custom_call" | custom-call | tf_op jit(solution)/shard_map/late/pallas_call | solution.py:29
  55.5 0.5 collective-permute-start.10
  56.0 0.7 collective-permute-done.16.got_a
  56.7 1.8 %collective-permute-done.17.got_b = bf16[128,1024]{1,0:T(8,128)(2,1)S(1)} collective-permute-done((bf16[128,1024]{1,0:T(8,128)(2,1)}, bf16[128,1024]{1,0:T(8,128)(2,1)S(1)}, u32[]{:S(2)}, u32[]{:S(2)}) %collective-permute-start.17) | collective-permute-done | bytes 262176 | tf_op jit(solution)/shard_map/ppermute | solution.py:261
  58.5 0.7 copy-done.8
  59.1 2.0 %sum_second.3 = (bf16[128,1024]{1,0:T(8,128)(2,1)}, bf16[64,1024]{1,0:T(8,128)(2,1)}, bf16[64,1024]{1,0:T(8,128)(2,1)}) custom-call(bf16[256,1024]{1,0:T(8,128)(2,1)} %get-tuple-element.64.keep, bf16[128,1024]{1,0:T(8,128)(2,1)} %copy-done.7, bf16[128,1024]{1,0:T(8,128)(2,1)} %copy-done.8), custom_call_target="tpu_custom_call" | custom-call | tf_op jit(solution)/shard_map/sum_second/pallas_call | solution.py:29
  61.2 2.4 %collective-permute-start.18 = (bf16[64,1024]{1,0:T(8,128)(2,1)}, bf16[64,1024]{1,0:T(8,128)(2,1)S(1)}, u32[]{:S(2)}, u32[]{:S(2)}) collective-permute-start(bf16[64,1024]{1,0:T(8,128)(2,1)} %get-tuple-element.68), channel_id=1, source_target_pairs={{0,16},{4,20},{8,24},{12,28},{16,0},{20,4},{24,8},{28,12},{1,17},{... | collective-permute-start | bytes 393224 | tf_op jit(solution)/shard_map/ppermute | solution.py:261
  63.5 0.3 collective-permute-start.3
  63.8 1.7 %collective-permute-done.10.got_b = bf16[128,1152]{1,0:T(8,128)(2,1)S(1)} collective-permute-done((bf16[128,1152]{1,0:T(8,128)(2,1)}, bf16[128,1152]{1,0:T(8,128)(2,1)S(1)}, u32[]{:S(2)}, u32[]{:S(2)}) %collective-permute-start.10) | collective-permute-done | bytes 294944 | tf_op jit(solution)/shard_map/ppermute | solution.py:261
  65.6 0.3 collective-permute-start.5
  65.9 0.4 copy-done.5
  66.4 2.1 %sum_second.2 = (bf16[128,1152]{1,0:T(8,128)(2,1)}, bf16[64,1152]{1,0:T(8,128)(2,1)}, bf16[64,1152]{1,0:T(8,128)(2,1)}) custom-call(bf16[256,1152]{1,0:T(8,128)(2,1)} %get-tuple-element.54.keep, bf16[128,1152]{1,0:T(8,128)(2,1)} %copy-done.6, bf16[128,1152]{1,0:T(8,128)(2,1)} %copy-done.5), custom_call_target="tpu_custom_call" | custom-call | tf_op jit(solution)/shard_map/sum_second/pallas_call | solution.py:29
  68.5 1.6 %collective-permute-start.11 = (bf16[64,1152]{1,0:T(8,128)(2,1)}, bf16[64,1152]{1,0:T(8,128)(2,1)S(1)}, u32[]{:S(2)}, u32[]{:S(2)}) collective-permute-start(bf16[64,1152]{1,0:T(8,128)(2,1)} %get-tuple-element.58), channel_id=1, source_target_pairs={{0,16},{4,20},{8,24},{12,28},{16,0},{20,4},{24,8},{28,12},{1,17},{... | collective-permute-start | bytes 442376 | tf_op jit(solution)/shard_map/ppermute | solution.py:261
  70.1 1.0 collective-permute-start.12
  71.1 1.8 %sum_third.3 = (bf16[32,1024]{1,0:T(8,128)(2,1)}, bf16[32,1024]{1,0:T(8,128)(2,1)}, bf16[32,1024]{1,0:T(8,128)(2,1)}, bf16[32,1024]{1,0:T(8,128)(2,1)}) custom-call(bf16[128,1024]{1,0:T(8,128)(2,1)} %get-tuple-element.67.keep, bf16[64,1024]{1,0:T(8,128)(2,1)} %copy-done.15, bf16[64,1024]{1,0:T(8,128)(2,1)} %copy-done.16), custom_call_target="tpu_custom_call" | custom-call | tf_op jit(solution)/shard_map/sum_third/pallas_call | solution.py:29
  72.9 3.4 %collective-permute-start.20 = (bf16[32,1024]{1,0:T(8,128)(2,1)}, bf16[32,1024]{1,0:T(8,128)(2,1)S(1)}, u32[]{:S(2)}, u32[]{:S(2)}) collective-permute-start(bf16[32,1024]{1,0:T(8,128)(2,1)} %get-tuple-element.71), channel_id=1, source_target_pairs={{0,1},{1,2},{2,3},{3,0},{4,5},{5,6},{6,7},{7,4},{8,9},{9,10},{10,1... | collective-permute-start | bytes 196616 | tf_op jit(solution)/shard_map/ppermute | solution.py:277
  76.3 1.0 collective-permute-start.21
  77.3 2.8 %collective-permute-start.22 = (bf16[32,1024]{1,0:T(8,128)(2,1)}, bf16[32,1024]{1,0:T(8,128)(2,1)S(1)}, u32[]{:S(2)}, u32[]{:S(2)}) collective-permute-start(bf16[32,1024]{1,0:T(8,128)(2,1)} %get-tuple-element.73), channel_id=1, source_target_pairs={{0,3},{1,0},{2,1},{3,2},{4,7},{5,4},{6,5},{7,6},{8,11},{9,8},{10,9... | collective-permute-start | bytes 196616 | tf_op jit(solution)/shard_map/ppermute | solution.py:277
  80.2 19.0 %unpack.1 = (bf16[6,12,2,1024]{3,2,1,0:T(2,128)(2,1)}, bf16[6,12,2,1024]{3,2,1,0:T(2,128)(2,1)}) custom-call(bf16[2,3,6,2,1024]{4,3,2,1,0:T(2,128)(2,1)} %get-tuple-element.44.q0, bf16[2,3,6,2,1024]{4,3,2,1,0:T(2,128)(2,1)} %copy-done.10, bf16[2,3,6,2,1024]{4,3,2,1,0:T(2,128)(2,1)} %copy-done.11, bf16[2,3,6,2,1024]{4,3,2,1,0:T(2,128)(2,1)} %copy-done.12), custom_call_target="tpu_custom_call" | custom-call | tf_op jit(solution)/shard_map/unpack/pallas_call | solution.py:83
  99.3 0.6 copy-done.13
  99.9 1.8 %sum_third.2 = (bf16[32,1152]{1,0:T(8,128)(2,1)}, bf16[32,1152]{1,0:T(8,128)(2,1)}, bf16[32,1152]{1,0:T(8,128)(2,1)}, bf16[32,1152]{1,0:T(8,128)(2,1)}) custom-call(bf16[128,1152]{1,0:T(8,128)(2,1)} %get-tuple-element.57.keep, bf16[64,1152]{1,0:T(8,128)(2,1)} %copy-done.13, bf16[64,1152]{1,0:T(8,128)(2,1)} %copy-done.14), custom_call_target="tpu_custom_call" | custom-call | tf_op jit(solution)/shard_map/sum_third/pallas_call | solution.py:29
  101.7 1.2 %collective-permute-start.14 = (bf16[32,1152]{1,0:T(8,128)(2,1)}, bf16[32,1152]{1,0:T(8,128)(2,1)S(1)}, u32[]{:S(2)}, u32[]{:S(2)}) collective-permute-start(bf16[32,1152]{1,0:T(8,128)(2,1)} %get-tuple-element.62), channel_id=1, source_target_pairs={{0,2},{1,3},{2,0},{3,1},{4,6},{5,7},{6,4},{7,5},{8,10},{9,11},{10,... | collective-permute-start | bytes 221192 | tf_op jit(solution)/shard_map/ppermute | solution.py:277
  102.9 2.6 %collective-permute-start.15 = (bf16[32,1152]{1,0:T(8,128)(2,1)}, bf16[32,1152]{1,0:T(8,128)(2,1)S(1)}, u32[]{:S(2)}, u32[]{:S(2)}) collective-permute-start(bf16[32,1152]{1,0:T(8,128)(2,1)} %get-tuple-element.63), channel_id=1, source_target_pairs={{0,3},{1,0},{2,1},{3,2},{4,7},{5,4},{6,5},{7,6},{8,11},{9,8},{10,9... | collective-permute-start | bytes 221192 | tf_op jit(solution)/shard_map/ppermute | solution.py:277
  105.6 0.9 add_multiply_fusion.1
  106.5 0.6 slice_bitcast_fusion
  107.1 1.1 %collective-permute-done.13 = bf16[32,1152]{1,0:T(8,128)(2,1)S(1)} collective-permute-done((bf16[32,1152]{1,0:T(8,128)(2,1)}, bf16[32,1152]{1,0:T(8,128)(2,1)S(1)}, u32[]{:S(2)}, u32[]{:S(2)}) %collective-permute-start.13) | collective-permute-done | bytes 73760 | tf_op jit(solution)/shard_map/ppermute | solution.py:277
  108.2 1.3 %collective-permute-done.14 = bf16[32,1152]{1,0:T(8,128)(2,1)S(1)} collective-permute-done((bf16[32,1152]{1,0:T(8,128)(2,1)}, bf16[32,1152]{1,0:T(8,128)(2,1)S(1)}, u32[]{:S(2)}, u32[]{:S(2)}) %collective-permute-start.14) | collective-permute-done | bytes 73760 | tf_op jit(solution)/shard_map/ppermute | solution.py:277
  109.6 0.9 add_multiply_fusion
  110.5 0.7 slice_reduce_fusion
  111.2 0.7 pad_maximum_fusion
  (56 shorter events, 0.4 us)
Async XLA Ops:
  15.2 10.0 %collective-permute-start = (bf16[2,3,6,2,1024]{4,3,2,1,0:T(2,128)(2,1)}, bf16[2,3,6,2,1024]{4,3,2,1,0:T(2,128)(2,1)S(1)}, u32[]{:S(2)}, u32[]{:S(2)}) collective-permute-start(bf16[2,3,6,2,1024]{4,3,2,1,0:T(2,128)(2,1)} %get-tuple-element.40), channel_id=1, source_target_pairs={{0,3},{1,0},{2,1},{3,2},{4,7},{5,4},{6,5},{7,6},{8,11},{9,8},{10,9... | collective-permute-start | bytes 442376 | tf_op jit(solution)/shard_map/ppermute | solution.py:308
  20.3 4.8 %collective-permute-start.1 = (bf16[2,3,6,2,1024]{4,3,2,1,0:T(2,128)(2,1)}, bf16[2,3,6,2,1024]{4,3,2,1,0:T(2,128)(2,1)S(1)}, u32[]{:S(2)}, u32[]{:S(2)}) collective-permute-start(bf16[2,3,6,2,1024]{4,3,2,1,0:T(2,128)(2,1)} %get-tuple-element.41), channel_id=1, source_target_pairs={{0,28},{1,29},{2,30},{3,31},{4,0},{5,1},{6,2},{7,3},{8,4},{9,5},{1... | collective-permute-start | bytes 442376 | tf_op jit(solution)/shard_map/ppermute | solution.py:308
  21.9 5.4 %collective-permute-start.2 = (bf16[2,3,6,2,1024]{4,3,2,1,0:T(2,128)(2,1)}, bf16[2,3,6,2,1024]{4,3,2,1,0:T(2,128)(2,1)S(1)}, u32[]{:S(2)}, u32[]{:S(2)}) collective-permute-start(bf16[2,3,6,2,1024]{4,3,2,1,0:T(2,128)(2,1)} %get-tuple-element.42), channel_id=1, source_target_pairs={{0,31},{1,28},{2,29},{3,30},{4,3},{5,0},{6,1},{7,2},{8,7},{9,4},{1... | collective-permute-start | bytes 442376 | tf_op jit(solution)/shard_map/ppermute | solution.py:308
  25.2 2.2 %copy-start.2 = (bf16[2,3,6,2,1024]{4,3,2,1,0:T(2,128)(2,1)}, bf16[2,3,6,2,1024]{4,3,2,1,0:T(2,128)(2,1)S(1)}, u32[]{:S(2)}) copy-start(bf16[2,3,6,2,1024]{4,3,2,1,0:T(2,128)(2,1)S(1)} %collective-permute-done.r1) | copy-start | bytes 442372
  25.2 2.2 %copy-start.3 = (bf16[2,3,6,2,1024]{4,3,2,1,0:T(2,128)(2,1)}, bf16[2,3,6,2,1024]{4,3,2,1,0:T(2,128)(2,1)S(1)}, u32[]{:S(2)}) copy-start(bf16[2,3,6,2,1024]{4,3,2,1,0:T(2,128)(2,1)S(1)} %collective-permute-done.1.r2) | copy-start | bytes 442372
  27.3 0.7 copy-start.4
  37.6 6.0 %collective-permute-start.7 = (bf16[144,2048]{1,0:T(8,128)(2,1)}, bf16[144,2048]{1,0:T(8,128)(2,1)S(1)}, u32[]{:S(2)}, u32[]{:S(2)}) collective-permute-start(bf16[144,2048]{1,0:T(8,128)(2,1)} %get-tuple-element.43.factor_ref.factor), channel_id=1, source_target_pairs={{0,4},{4,0},{8,12},{12,8},{16,20},{20,16},{24,28},{28,24},{1,5},{5... | collective-permute-start | bytes 1769480 | tf_op jit(solution)/shard_map/ppermute | solution.py:261
  37.8 5.9 %collective-permute-start.6 = (bf16[1024,144]{1,0:T(8,128)(2,1)}, bf16[1024,144]{1,0:T(8,128)(2,1)S(1)}, u32[]{:S(2)}, u32[]{:S(2)}) collective-permute-start(bf16[1024,144]{1,0:T(8,128)(2,1)} %get-tuple-element.51), channel_id=1, source_target_pairs={{0,4},{4,0},{8,12},{12,8},{16,20},{20,16},{24,28},{28,24},{1,5},{5... | collective-permute-start | bytes 884744 | tf_op jit(solution)/shard_map/ppermute | solution.py:261
  43.4 20.1 %copy-start.19 = (bf16[2,3,6,2,1024]{4,3,2,1,0:T(2,128)(2,1)S(1)}, bf16[2,3,6,2,1024]{4,3,2,1,0:T(2,128)(2,1)}, u32[]{:S(2)}) copy-start(bf16[2,3,6,2,1024]{4,3,2,1,0:T(2,128)(2,1)} %get-tuple-element.45) | copy-start | bytes 442372
  43.4 22.1 %copy-start.18 = (bf16[2,3,6,2,1024]{4,3,2,1,0:T(2,128)(2,1)S(1)}, bf16[2,3,6,2,1024]{4,3,2,1,0:T(2,128)(2,1)}, u32[]{:S(2)}) copy-start(bf16[2,3,6,2,1024]{4,3,2,1,0:T(2,128)(2,1)} %get-tuple-element.46) | copy-start | bytes 442372
  43.4 22.2 %copy-start.17 = (bf16[2,3,6,2,1024]{4,3,2,1,0:T(2,128)(2,1)S(1)}, bf16[2,3,6,2,1024]{4,3,2,1,0:T(2,128)(2,1)}, u32[]{:S(2)}) copy-start(bf16[2,3,6,2,1024]{4,3,2,1,0:T(2,128)(2,1)} %get-tuple-element.47) | copy-start | bytes 442372
  43.5 8.0 %collective-permute-start.8 = (f32[512,128]{1,0:T(8,128)}, f32[512,128]{1,0:T(8,128)S(1)}, u32[]{:S(2)}, u32[]{:S(2)}) collective-permute-start(f32[512,128]{1,0:T(8,128)} %get-tuple-element.53), channel_id=1, source_target_pairs={{0,4},{4,0},{8,12},{12,8},{16,20},{20,16},{24,28},{28,24},{1,5},{5... | collective-permute-start | bytes 786440 | tf_op jit(solution)/shard_map/ppermute | solution.py:261
  43.7 0.8 copy-start.1
  43.7 1.0 copy-start
  47.8 8.8 %collective-permute-start.16 = (bf16[128,1024]{1,0:T(8,128)(2,1)}, bf16[128,1024]{1,0:T(8,128)(2,1)S(1)}, u32[]{:S(2)}, u32[]{:S(2)}) collective-permute-start(bf16[128,1024]{1,0:T(8,128)(2,1)} %get-tuple-element.65), channel_id=1, source_target_pairs={{0,8},{4,12},{8,0},{12,4},{16,24},{20,28},{24,16},{28,20},{1,9},{5... | collective-permute-start | bytes 786440 | tf_op jit(solution)/shard_map/ppermute | solution.py:261
  49.9 8.5 %collective-permute-start.17 = (bf16[128,1024]{1,0:T(8,128)(2,1)}, bf16[128,1024]{1,0:T(8,128)(2,1)S(1)}, u32[]{:S(2)}, u32[]{:S(2)}) collective-permute-start(bf16[128,1024]{1,0:T(8,128)(2,1)} %get-tuple-element.66), channel_id=1, source_target_pairs={{0,16},{4,20},{8,24},{12,28},{16,0},{20,4},{24,8},{28,12},{1,17},{... | collective-permute-start | bytes 786440 | tf_op jit(solution)/shard_map/ppermute | solution.py:261
  51.4 0.7 copy-start.9
  55.5 10.1 %collective-permute-start.10 = (bf16[128,1152]{1,0:T(8,128)(2,1)}, bf16[128,1152]{1,0:T(8,128)(2,1)S(1)}, u32[]{:S(2)}, u32[]{:S(2)}) collective-permute-start(bf16[128,1152]{1,0:T(8,128)(2,1)} %get-tuple-element.56), channel_id=1, source_target_pairs={{0,16},{4,20},{8,24},{12,28},{16,0},{20,4},{24,8},{28,12},{1,17},{... | collective-permute-start | bytes 884744 | tf_op jit(solution)/shard_map/ppermute | solution.py:261
  56.0 9.6 %collective-permute-start.9 = (bf16[128,1152]{1,0:T(8,128)(2,1)}, bf16[128,1152]{1,0:T(8,128)(2,1)S(1)}, u32[]{:S(2)}, u32[]{:S(2)}) collective-permute-start(bf16[128,1152]{1,0:T(8,128)(2,1)} %get-tuple-element.55), channel_id=1, source_target_pairs={{0,8},{4,12},{8,0},{12,4},{16,24},{20,28},{24,16},{28,20},{1,9},{5... | collective-permute-start | bytes 884744 | tf_op jit(solution)/shard_map/ppermute | solution.py:261
  56.7 1.8 %copy-start.7 = (bf16[128,1024]{1,0:T(8,128)(2,1)}, bf16[128,1024]{1,0:T(8,128)(2,1)S(1)}, u32[]{:S(2)}) copy-start(bf16[128,1024]{1,0:T(8,128)(2,1)S(1)} %collective-permute-done.16.got_a) | copy-start | bytes 786436
  58.4 0.7 copy-start.8
  61.2 7.3 %collective-permute-start.18 = (bf16[64,1024]{1,0:T(8,128)(2,1)}, bf16[64,1024]{1,0:T(8,128)(2,1)S(1)}, u32[]{:S(2)}, u32[]{:S(2)}) collective-permute-start(bf16[64,1024]{1,0:T(8,128)(2,1)} %get-tuple-element.68), channel_id=1, source_target_pairs={{0,16},{4,20},{8,24},{12,28},{16,0},{20,4},{24,8},{28,12},{1,17},{... | collective-permute-start | bytes 393224 | tf_op jit(solution)/shard_map/ppermute | solution.py:261
  63.5 6.6 %collective-permute-start.19 = (bf16[64,1024]{1,0:T(8,128)(2,1)}, bf16[64,1024]{1,0:T(8,128)(2,1)S(1)}, u32[]{:S(2)}, u32[]{:S(2)}) collective-permute-start(bf16[64,1024]{1,0:T(8,128)(2,1)} %get-tuple-element.69), channel_id=1, source_target_pairs={{0,8},{4,12},{8,0},{12,4},{16,24},{20,28},{24,16},{28,20},{1,9},{5... | collective-permute-start | bytes 393224 | tf_op jit(solution)/shard_map/ppermute | solution.py:261
  63.5 9.3 %collective-permute-start.3 = (bf16[2,3,6,2,1024]{4,3,2,1,0:T(2,128)(2,1)S(1)}, bf16[2,3,6,2,1024]{4,3,2,1,0:T(2,128)(2,1)S(1)}, u32[]{:S(2)}, u32[]{:S(2)}) collective-permute-start(bf16[2,3,6,2,1024]{4,3,2,1,0:T(2,128)(2,1)S(1)} %copy-done.19), channel_id=1, source_target_pairs={{0,1},{1,2},{2,3},{3,0},{4,5},{5,6},{6,7},{7,4},{8,9},{9,10},{10,1... | collective-permute-start | bytes 442376 | tf_op jit(solution)/shard_map/ppermute | solution.py:381
  65.6 0.7 copy-start.5
  65.6 10.7 %collective-permute-start.4 = (bf16[2,3,6,2,1024]{4,3,2,1,0:T(2,128)(2,1)S(1)}, bf16[2,3,6,2,1024]{4,3,2,1,0:T(2,128)(2,1)S(1)}, u32[]{:S(2)}, u32[]{:S(2)}) collective-permute-start(bf16[2,3,6,2,1024]{4,3,2,1,0:T(2,128)(2,1)S(1)} %copy-done.18), channel_id=1, source_target_pairs={{0,4},{1,5},{2,6},{3,7},{4,8},{5,9},{6,10},{7,11},{8,12},{9,13},{1... | collective-permute-start | bytes 442376 | tf_op jit(solution)/shard_map/ppermute | solution.py:381
  65.6 0.8 copy-start.6
  65.6 11.7 %collective-permute-start.5 = (bf16[2,3,6,2,1024]{4,3,2,1,0:T(2,128)(2,1)S(1)}, bf16[2,3,6,2,1024]{4,3,2,1,0:T(2,128)(2,1)S(1)}, u32[]{:S(2)}, u32[]{:S(2)}) collective-permute-start(bf16[2,3,6,2,1024]{4,3,2,1,0:T(2,128)(2,1)S(1)} %copy-done.17), channel_id=1, source_target_pairs={{0,5},{1,6},{2,7},{3,4},{4,9},{5,10},{6,11},{7,8},{8,13},{9,14},{1... | collective-permute-start | bytes 442376 | tf_op jit(solution)/shard_map/ppermute | solution.py:381
  68.5 2.6 %copy-start.15 = (bf16[64,1024]{1,0:T(8,128)(2,1)}, bf16[64,1024]{1,0:T(8,128)(2,1)S(1)}, u32[]{:S(2)}) copy-start(bf16[64,1024]{1,0:T(8,128)(2,1)S(1)} %collective-permute-done.18.got_a) | copy-start | bytes 393220
  68.5 30.7 %collective-permute-start.11 = (bf16[64,1152]{1,0:T(8,128)(2,1)}, bf16[64,1152]{1,0:T(8,128)(2,1)S(1)}, u32[]{:S(2)}, u32[]{:S(2)}) collective-permute-start(bf16[64,1152]{1,0:T(8,128)(2,1)} %get-tuple-element.58), channel_id=1, source_target_pairs={{0,16},{4,20},{8,24},{12,28},{16,0},{20,4},{24,8},{28,12},{1,17},{... | collective-permute-start | bytes 442376 | tf_op jit(solution)/shard_map/ppermute | solution.py:261
  70.1 1.0 copy-start.16
  70.1 29.1 %collective-permute-start.12 = (bf16[64,1152]{1,0:T(8,128)(2,1)}, bf16[64,1152]{1,0:T(8,128)(2,1)S(1)}, u32[]{:S(2)}, u32[]{:S(2)}) collective-permute-start(bf16[64,1152]{1,0:T(8,128)(2,1)} %get-tuple-element.59), channel_id=1, source_target_pairs={{0,8},{4,12},{8,0},{12,4},{16,24},{20,28},{24,16},{28,20},{1,9},{5... | collective-permute-start | bytes 442376 | tf_op jit(solution)/shard_map/ppermute | solution.py:261
  72.9 7.3 %copy-start.10 = (bf16[2,3,6,2,1024]{4,3,2,1,0:T(2,128)(2,1)}, bf16[2,3,6,2,1024]{4,3,2,1,0:T(2,128)(2,1)S(1)}, u32[]{:S(2)}) copy-start(bf16[2,3,6,2,1024]{4,3,2,1,0:T(2,128)(2,1)S(1)} %collective-permute-done.3.q1) | copy-start | bytes 442372
  72.9 30.1 %collective-permute-start.20 = (bf16[32,1024]{1,0:T(8,128)(2,1)}, bf16[32,1024]{1,0:T(8,128)(2,1)S(1)}, u32[]{:S(2)}, u32[]{:S(2)}) collective-permute-start(bf16[32,1024]{1,0:T(8,128)(2,1)} %get-tuple-element.71), channel_id=1, source_target_pairs={{0,1},{1,2},{2,3},{3,0},{4,5},{5,6},{6,7},{7,4},{8,9},{9,10},{10,1... | collective-permute-start | bytes 196616 | tf_op jit(solution)/shard_map/ppermute | solution.py:277
  76.3 3.9 %copy-start.11 = (bf16[2,3,6,2,1024]{4,3,2,1,0:T(2,128)(2,1)}, bf16[2,3,6,2,1024]{4,3,2,1,0:T(2,128)(2,1)S(1)}, u32[]{:S(2)}) copy-start(bf16[2,3,6,2,1024]{4,3,2,1,0:T(2,128)(2,1)S(1)} %collective-permute-done.4.q2) | copy-start | bytes 442372
  76.3 29.3 %collective-permute-start.21 = (bf16[32,1024]{1,0:T(8,128)(2,1)}, bf16[32,1024]{1,0:T(8,128)(2,1)S(1)}, u32[]{:S(2)}, u32[]{:S(2)}) collective-permute-start(bf16[32,1024]{1,0:T(8,128)(2,1)} %get-tuple-element.72), channel_id=1, source_target_pairs={{0,2},{1,3},{2,0},{3,1},{4,6},{5,7},{6,4},{7,5},{8,10},{9,11},{10,... | collective-permute-start | bytes 196616 | tf_op jit(solution)/shard_map/ppermute | solution.py:277
  77.3 2.8 %copy-start.12 = (bf16[2,3,6,2,1024]{4,3,2,1,0:T(2,128)(2,1)}, bf16[2,3,6,2,1024]{4,3,2,1,0:T(2,128)(2,1)S(1)}, u32[]{:S(2)}) copy-start(bf16[2,3,6,2,1024]{4,3,2,1,0:T(2,128)(2,1)S(1)} %collective-permute-done.5.q3) | copy-start | bytes 442372
  77.3 28.3 %collective-permute-start.22 = (bf16[32,1024]{1,0:T(8,128)(2,1)}, bf16[32,1024]{1,0:T(8,128)(2,1)S(1)}, u32[]{:S(2)}, u32[]{:S(2)}) collective-permute-start(bf16[32,1024]{1,0:T(8,128)(2,1)} %get-tuple-element.73), channel_id=1, source_target_pairs={{0,3},{1,0},{2,1},{3,2},{4,7},{5,4},{6,5},{7,6},{8,11},{9,8},{10,9... | collective-permute-start | bytes 196616 | tf_op jit(solution)/shard_map/ppermute | solution.py:277
  99.2 0.7 copy-start.13
  99.3 0.7 copy-start.14
  101.7 6.5 %collective-permute-start.13 = (bf16[32,1152]{1,0:T(8,128)(2,1)}, bf16[32,1152]{1,0:T(8,128)(2,1)S(1)}, u32[]{:S(2)}, u32[]{:S(2)}) collective-permute-start(bf16[32,1152]{1,0:T(8,128)(2,1)} %get-tuple-element.61), channel_id=1, source_target_pairs={{0,1},{1,2},{2,3},{3,0},{4,5},{5,6},{6,7},{7,4},{8,9},{9,10},{10,1... | collective-permute-start | bytes 221192 | tf_op jit(solution)/shard_map/ppermute | solution.py:277
  101.7 7.8 %collective-permute-start.14 = (bf16[32,1152]{1,0:T(8,128)(2,1)}, bf16[32,1152]{1,0:T(8,128)(2,1)S(1)}, u32[]{:S(2)}, u32[]{:S(2)}) collective-permute-start(bf16[32,1152]{1,0:T(8,128)(2,1)} %get-tuple-element.62), channel_id=1, source_target_pairs={{0,2},{1,3},{2,0},{3,1},{4,6},{5,7},{6,4},{7,5},{8,10},{9,11},{10,... | collective-permute-start | bytes 221192 | tf_op jit(solution)/shard_map/ppermute | solution.py:277
  102.9 6.6 %collective-permute-start.15 = (bf16[32,1152]{1,0:T(8,128)(2,1)}, bf16[32,1152]{1,0:T(8,128)(2,1)S(1)}, u32[]{:S(2)}, u32[]{:S(2)}) collective-permute-start(bf16[32,1152]{1,0:T(8,128)(2,1)} %get-tuple-element.63), channel_id=1, source_target_pairs={{0,3},{1,0},{2,1},{3,2},{4,7},{5,4},{6,5},{7,6},{8,11},{9,8},{10,9... | collective-permute-start | bytes 221192 | tf_op jit(solution)/shard_map/ppermute | solution.py:277

commit v3 on v2

--- a/solution.py
+++ b/solution.py
@@ -15,7 +15,6 @@
 BF16 = jnp.bfloat16
 LANES = 128
 
-ANY_SPEC = pl.BlockSpec(memory_space=pl.ANY)
 VMEM_SPEC = pl.BlockSpec(memory_space=pltpu.VMEM)
 SMEM_SPEC = pl.BlockSpec(memory_space=pltpu.SMEM)
 
@@ -24,16 +23,34 @@
     return lax.dot_general(a, b, ((contract[0], contract[1]), ((), ())), preferred_element_type=F32)
 
 
-def call(body, name, outs, args, scratch=(), smem=0, cost=None):
-    specs = [SMEM_SPEC] * smem + [VMEM_SPEC] * (len(args) - smem)
+def size_of(shape, dtype):
+    rows = 16 if len(shape) > 1 and shape[-2] > 2 else shape[-2] if len(shape) > 1 else 1
+    padded = [*shape[:-2], -(-shape[-2] // rows) * rows] if len(shape) > 1 else []
+    return math.prod([*padded, -(-shape[-1] // LANES) * LANES]) * jnp.dtype(dtype).itemsize
+
+
+def call(body, name, outs, args, scratch=(), smem=0, near_in=None, near_out=None, room=4):
+    near_in = len(args) - smem if near_in is None else near_in
+    near_out = len(outs) if near_out is None else near_out
+    far = len(args) - near_in
+    held = sum(size_of(a.shape, a.dtype) for a in args[smem:far])
+    held += sum(size_of(s, d) for s, d in outs[near_out:])
+    held += sum(size_of(m.shape, m.dtype) for m in scratch)
+    args = [
+        a if i < far else pltpu.with_memory_space_constraint(a, pltpu.VMEM)
+        for i, a in enumerate(args)
+    ]
     return pl.pallas_call(
         body,
         name=name,
-        out_shape=[jax.ShapeDtypeStruct(s, d) for s, d in outs],
-        in_specs=specs,
+        out_shape=[
+            pltpu.VMEM(s, d) if i < near_out else jax.ShapeDtypeStruct(s, d)
+            for i, (s, d) in enumerate(outs)
+        ],
+        in_specs=[SMEM_SPEC] * smem + [VMEM_SPEC] * (len(args) - smem),
         out_specs=[VMEM_SPEC] * len(outs),
         scratch_shapes=list(scratch),
-        cost_estimate=cost,
+        compiler_params=pltpu.CompilerParams(vmem_limit_bytes=held + room * 2**20),
     )(*args)
 
 
@@ -41,53 +58,18 @@
     return ((rows // 2, cols // 2), (rows // 2, 0), (0, cols // 2), (0, 0))
 
 
-def run_copies(copies):
-    for item in copies:
-        item.start()
-    for item in copies:
-        item.wait()
-
-
-def pack_body(tok_ref, cot_ref, *refs):
-    outs, sem = refs[:-1], refs[-1]
+def pack_body(tok_ref, cot_ref, *outs):
     rows, cols = tok_ref.shape[:2]
-    copies = []
     for out_ref, (row, col) in zip(outs, corners(rows, cols)[1:]):
         for part, ref in enumerate((tok_ref, cot_ref)):
-            copies.append(
-                pltpu.make_async_copy(
-                    ref.at[pl.ds(row, rows // 2), pl.ds(col, cols // 2)],
-                    out_ref.at[part],
-                    sem.at[len(copies)],
-                )
-            )
-    run_copies(copies)
-
-
-def unpack_body(q0, q1, q2, q3, y_ref, grad_ref, sem):
+            out_ref[part] = ref[row : row + rows // 2, col : col + cols // 2]
+
+
+def unpack_body(q0, q1, q2, q3, y_ref, grad_ref):
     rows, cols = y_ref.shape[:2]
-    copies = []
     for quad, (row, col) in zip((q0, q1, q2, q3), corners(rows, cols)):
         for part, ref in enumerate((y_ref, grad_ref)):
-            copies.append(
-                pltpu.make_async_copy(
-                    quad.at[part],
-                    ref.at[pl.ds(row, rows // 2), pl.ds(col, cols // 2)],
-                    sem.at[len(copies)],
-                )
-            )
-    run_copies(copies)
-
-
-def move_cells(body, name, outs, args, count):
-    return pl.pallas_call(
-        body,
-        name=name,
-        out_shape=[jax.ShapeDtypeStruct(shape, BF16) for shape in outs],
-        in_specs=[ANY_SPEC] * len(args),
-        out_specs=[ANY_SPEC] * len(outs),
-        scratch_shapes=[pltpu.SemaphoreType.DMA((count,))],
-    )(*args)
+            ref[row : row + rows // 2, col : col + cols // 2] = quad[part]
 
 
 def gather_window(own, received, part, wide):
@@ -303,7 +285,7 @@
     quad = (2, lat_rows // 2, lon_cols // 2, levels, width)
     tok = tokens.transpose(1, 2, 0, 3)
     cot = output_cotangent.transpose(1, 2, 0, 3)
-    sends = move_cells(pack_body, "pack", [quad] * 3, (tok, cot), 6)
+    sends = call(pack_body, "pack", [(quad, BF16)] * 3, (tok, cot), near_in=0)
     received = [
         lax.ppermute(item, ("lat", "lon"), moved(-a, -b)) for item, (a, b) in zip(sends, steps)
     ]
@@ -380,7 +362,7 @@
     back = [q0] + [
         lax.ppermute(item, ("lat", "lon"), moved(a, b)) for item, (a, b) in zip((q1, q2, q3), steps)
     ]
-    y_out, token_gradient = move_cells(unpack_body, "unpack", [grid] * 2, back, 8)
+    y_out, token_gradient = call(unpack_body, "unpack", [(grid, BF16)] * 2, back, near_out=0)
     early_total = early_total * norm_factor
     late_total = late_total * norm_factor
     d_out = early_total[:, :inner].T

time: 112 us -> 71.3 us (0.64)
  Pallas kernels: 62.7 us -> 11.3 us
  waiting for transfers between devices: 8.83 us -> 20.1 us
  local copies, waits for them, and re-layouts: 5.63 us -> 9.68 us
  other arithmetic: 4.88 us -> 2.13 us
  starting transfers between devices: 29 us -> 27 us
    pallas_call x10, Pallas kernels: 62.7 us -> 11.3 us  [call(): pl.pallas_call(body, name=name, out_shape=[pltpu.VMEM(s, d) if i < near_o...]
    ppermute x11, waiting for transfers between devices: 4.21 us -> 11.7 us  [swap(): return lax.ppermute(value, 'lat', xor_pairs(bit))]
    unnamed x40 -> x18, local copies, waits for them, and re-layouts: 4.28 us -> 8.33 us
    ppermute x3, waiting for transfers between devices: 0.01 us -> 2.34 us  [on_device(): lax.ppermute(item, ('lat', 'lon'), moved(a, b))]
    ppermute x11, starting transfers between devices: 9.81 us -> 8.6 us  [swap(): return lax.ppermute(value, 'lat', xor_pairs(bit))]
  transfers between devices with their start and end apart: 23 -> 23, of which waited for: 6 -> 10; matrix products, arithmetic and copies ran while one was open for 3% -> 3% of each run, Pallas kernels for 34% -> 7%
where the time goes in v3:
time: 71.3 us; the launch traced here: 70.9 us
  starting transfers between devices  27 us (38%)
  waiting for transfers between devices  20.1 us (28%)
  Pallas kernels  11.3 us (16%)
  local copies, waits for them, and re-layouts  9.68 us (14%)
  other arithmetic  2.13 us (3%)
  between operations  0.74 us (1%)
    ppermute x11, waiting for transfers between devices, swap(): return lax.ppermute(value, 'lat', xor_pairs(bit))  11.7 us
    pallas_call x10, Pallas kernels, call(): pl.pallas_call(body, name=name, out_shape=[pltpu.VMEM(s, d) if i < near_o...  11.3 us
    ppermute x6, starting transfers between devices, scatter_sum(): lax.ppermute(pieces[k], 'lon', [(i, (i + k) % lon_count) for i in range(l...  10.2 us
    ppermute x11, starting transfers between devices, swap(): return lax.ppermute(value, 'lat', xor_pairs(bit))  8.6 us
    unnamed x18, local copies, waits for them, and re-layouts  8.33 us
    ppermute x3, starting transfers between devices, on_device(): lax.ppermute(item, ('lat', 'lon'), moved(-a, -b))  7.58 us
    ppermute x6, waiting for transfers between devices, scatter_sum(): lax.ppermute(pieces[k], 'lon', [(i, (i + k) % lon_count) for i in range(l...  3.08 us
    ppermute x3, waiting for transfers between devices, on_device(): lax.ppermute(item, ('lat', 'lon'), moved(-a, -b))  2.97 us
  transfers between devices with their start and end apart: 23, of which 10 were waited for; matrix products, arithmetic and copies ran while one was open for 3% of the time, Pallas kernels for 7%

profile of v3, /device:TPU:0, one launch (start us, length us, event | category | flops | bytes accessed | tf_op | source)
XLA Modules:
  0.0 70.9 jit_solution(3548472547807579057)
XLA Ops:
  0.6 1.0 %copy-done.3 = bf16[2,6,12,1024]{3,0,2,1:T(2,128)(2,1)S(1)} copy-done((bf16[2,6,12,1024]{3,0,2,1:T(2,128)(2,1)S(1)}, bf16[2,6,12,1024]{3,0,2,1:T(2,128)(2,1)}, u32[]{:S(2)}) %copy-start.3) | copy-done | bytes 294936
  1.6 1.0 %copy-done.5 = bf16[2,6,12,1024]{3,0,2,1:T(2,128)(2,1)S(1)} copy-done((bf16[2,6,12,1024]{3,0,2,1:T(2,128)(2,1)S(1)}, bf16[2,6,12,1024]{3,0,2,1:T(2,128)(2,1)}, u32[]{:S(2)}) %copy-start.5) | copy-done | bytes 294936
  2.6 5.1 %collective-permute-start = (bf16[2,3,6,2,1024]{4,3,2,1,0:T(2,128)(2,1)S(1)}, bf16[2,3,6,2,1024]{4,3,2,1,0:T(2,128)(2,1)S(1)}, u32[]{:S(2)}, u32[]{:S(2)}) collective-permute-start(bf16[2,3,6,2,1024]{4,3,2,1,0:T(2,128)(2,1)S(1)} %get-tuple-element.40), channel_id=1, source_target_pairs={{0,3},{1,0},{2,1},{3,2},{4,7},{5,4},{6,5},{7,6},{8,11},{9,8},{10,9... | collective-permute-start | bytes 442376 | tf_op jit(solution)/shard_map/ppermute | solution.py:290
  7.7 1.6 %collective-permute-start.1 = (bf16[2,3,6,2,1024]{4,3,2,1,0:T(2,128)(2,1)S(1)}, bf16[2,3,6,2,1024]{4,3,2,1,0:T(2,128)(2,1)S(1)}, u32[]{:S(2)}, u32[]{:S(2)}) collective-permute-start(bf16[2,3,6,2,1024]{4,3,2,1,0:T(2,128)(2,1)S(1)} %get-tuple-element.41), channel_id=1, source_target_pairs={{0,28},{1,29},{2,30},{3,31},{4,0},{5,1},{6,2},{7,3},{8,4},{9,5},{1... | collective-permute-start | bytes 442376 | tf_op jit(solution)/shard_map/ppermute | solution.py:290
  9.3 0.8 %collective-permute-start.2 = (bf16[2,3,6,2,1024]{4,3,2,1,0:T(2,128)(2,1)S(1)}, bf16[2,3,6,2,1024]{4,3,2,1,0:T(2,128)(2,1)S(1)}, u32[]{:S(2)}, u32[]{:S(2)}) collective-permute-start(bf16[2,3,6,2,1024]{4,3,2,1,0:T(2,128)(2,1)S(1)} %get-tuple-element.42), channel_id=1, source_target_pairs={{0,31},{1,28},{2,29},{3,30},{4,3},{5,0},{6,1},{7,2},{8,7},{9,4},{1... | collective-permute-start | bytes 442376 | tf_op jit(solution)/shard_map/ppermute | solution.py:290
  10.2 0.7 fusion.order_ref
  10.9 0.7 compare_convert_fusion.edge_ref
  11.5 0.5 collective-permute-done.1.r2
  12.0 2.5 %collective-permute-done.2.r3 = bf16[2,3,6,2,1024]{4,3,2,1,0:T(2,128)(2,1)S(1)} collective-permute-done((bf16[2,3,6,2,1024]{4,3,2,1,0:T(2,128)(2,1)S(1)}, bf16[2,3,6,2,1024]{4,3,2,1,0:T(2,128)(2,1)S(1)}, u32[]{:S(2)}, u32[]{:S(2)}) %collective-permute-start.2) | collective-permute-done | bytes 147488 | tf_op jit(solution)/shard_map/ppermute | solution.py:290
  14.5 1.9 %copy-done = bf16[1024,1536]{1,0:T(8,128)(2,1)S(1)} copy-done((bf16[1024,1536]{1,0:T(8,128)(2,1)S(1)}, bf16[1024,1536]{1,0:T(8,128)(2,1)}, u32[]{:S(2)}) %copy-start) | copy-done | bytes 3145752
  16.4 1.2 %copy-done.2 = bf16[512,1024]{1,0:T(8,128)(2,1)S(1)} copy-done((bf16[512,1024]{1,0:T(8,128)(2,1)S(1)}, bf16[512,1024]{1,0:T(8,128)(2,1)}, u32[]{:S(2)}) %copy-start.2) | copy-done | bytes 1048600
  17.6 1.0 %copy-done.4 = bf16[2,6,12,1024]{3,0,2,1:T(2,128)(2,1)S(1)} copy-done((bf16[2,6,12,1024]{3,0,2,1:T(2,128)(2,1)S(1)}, bf16[2,6,12,1024]{3,0,2,1:T(2,128)(2,1)}, u32[]{:S(2)}) %copy-start.4) | copy-done | bytes 294936
  18.6 1.0 %copy-done.6 = bf16[2,6,12,1024]{3,0,2,1:T(2,128)(2,1)S(1)} copy-done((bf16[2,6,12,1024]{3,0,2,1:T(2,128)(2,1)S(1)}, bf16[2,6,12,1024]{3,0,2,1:T(2,128)(2,1)}, u32[]{:S(2)}) %copy-start.6) | copy-done | bytes 294936
  19.5 0.7 copy-done.7
  20.2 0.7 copy-done.8
  20.9 6.4 %attention.1 = (bf16[1024,144]{1,0:T(8,128)(2,1)S(1)}, bf16[1024,144]{1,0:T(8,128)(2,1)S(1)}, bf16[144,2048]{1,0:T(8,128)(2,1)S(1)}) custom-call(s32[32]{0:T(128)S(1)} %fusion.order_ref, s32[2]{0:T(128)S(1)} %compare_convert_fusion.edge_ref, bf16[6,12,2,1024]{3,2,1,0:T(2,128)(2,1)S(1)} %bitcast.9, bf16[6,12,2,1024]{3,2,1,0:T(2,128)(2,1)S(1)} %bitcast.12, ...), custom_call_target="tpu_custom_call" | custom-call | tf_op jit(solution)/shard_map/attention/pallas_call | solution.py:43
  27.4 0.2 collective-permute-start.7
  27.5 0.4 collective-permute-start.6
  27.9 2.2 %gradient.1 = (bf16[2,3,6,2,1024]{4,3,2,1,0:T(2,128)(2,1)S(1)}, bf16[2,3,6,2,1024]{4,3,2,1,0:T(2,128)(2,1)S(1)}, bf16[2,3,6,2,1024]{4,3,2,1,0:T(2,128)(2,1)S(1)}...) custom-call(s32[32]{0:T(128)S(1)} %fusion.order_ref, ...), custom_call_target="tpu_custom_call" | custom-call | tf_op jit(solution)/shard_map/gradient/pallas_call | solution.py:43
  30.1 0.2 collective-permute-start.8
  30.3 0.7 early.1
  31.0 2.2 %collective-permute-start.16 = (bf16[128,1024]{1,0:T(8,128)(2,1)S(1)}, bf16[128,1024]{1,0:T(8,128)(2,1)S(1)}, u32[]{:S(2)}, u32[]{:S(2)}) collective-permute-start(bf16[128,1024]{1,0:T(8,128)(2,1)S(1)} %get-tuple-element.65), channel_id=1, source_target_pairs={{0,8},{4,12},{8,0},{12,4},{16,24},{20,28},{24,16},{28,20},{1,9},{5... | collective-permute-start | bytes 786440 | tf_op jit(solution)/shard_map/ppermute | solution.py:243
  33.2 1.5 %collective-permute-start.17 = (bf16[128,1024]{1,0:T(8,128)(2,1)S(1)}, bf16[128,1024]{1,0:T(8,128)(2,1)S(1)}, u32[]{:S(2)}, u32[]{:S(2)}) collective-permute-start(bf16[128,1024]{1,0:T(8,128)(2,1)S(1)} %get-tuple-element.66), channel_id=1, source_target_pairs={{0,16},{4,20},{8,24},{12,28},{16,0},{20,4},{24,8},{28,12},{1,17},{... | collective-permute-start | bytes 786440 | tf_op jit(solution)/shard_map/ppermute | solution.py:243
  34.7 0.7 late.1
  35.4 0.6 collective-permute-start.10
  36.1 4.3 %collective-permute-done.16.got_a = bf16[128,1024]{1,0:T(8,128)(2,1)S(1)} collective-permute-done((bf16[128,1024]{1,0:T(8,128)(2,1)S(1)}, bf16[128,1024]{1,0:T(8,128)(2,1)S(1)}, u32[]{:S(2)}, u32[]{:S(2)}) %collective-permute-start.16) | collective-permute-done | bytes 262176 | tf_op jit(solution)/shard_map/ppermute | solution.py:243
  40.3 2.0 %collective-permute-done.17.got_b = bf16[128,1024]{1,0:T(8,128)(2,1)S(1)} collective-permute-done((bf16[128,1024]{1,0:T(8,128)(2,1)S(1)}, bf16[128,1024]{1,0:T(8,128)(2,1)S(1)}, u32[]{:S(2)}, u32[]{:S(2)}) %collective-permute-start.17) | collective-permute-done | bytes 262176 | tf_op jit(solution)/shard_map/ppermute | solution.py:243
  42.5 1.6 %collective-permute-start.18 = (bf16[64,1024]{1,0:T(8,128)(2,1)S(1)}, bf16[64,1024]{1,0:T(8,128)(2,1)S(1)}, u32[]{:S(2)}, u32[]{:S(2)}) collective-permute-start(bf16[64,1024]{1,0:T(8,128)(2,1)S(1)} %get-tuple-element.68), channel_id=1, source_target_pairs={{0,16},{4,20},{8,24},{12,28},{16,0},{20,4},{24,8},{28,12},{1,17},{... | collective-permute-start | bytes 393224 | tf_op jit(solution)/shard_map/ppermute | solution.py:243
  44.1 0.4 collective-permute-start.3
  44.6 4.1 %collective-permute-done.10.got_b = bf16[128,1152]{1,0:T(8,128)(2,1)S(1)} collective-permute-done((bf16[128,1152]{1,0:T(8,128)(2,1)S(1)}, bf16[128,1152]{1,0:T(8,128)(2,1)S(1)}, u32[]{:S(2)}, u32[]{:S(2)}) %collective-permute-start.10) | collective-permute-done | bytes 294944 | tf_op jit(solution)/shard_map/ppermute | solution.py:243
  48.7 0.2 collective-permute-start.5
  49.1 1.3 %collective-permute-done.18.got_a = bf16[64,1024]{1,0:T(8,128)(2,1)S(1)} collective-permute-done((bf16[64,1024]{1,0:T(8,128)(2,1)S(1)}, bf16[64,1024]{1,0:T(8,128)(2,1)S(1)}, u32[]{:S(2)}, u32[]{:S(2)}) %collective-permute-start.18) | collective-permute-done | bytes 131104 | tf_op jit(solution)/shard_map/ppermute | solution.py:243
  50.3 1.5 %collective-permute-start.11 = (bf16[64,1152]{1,0:T(8,128)(2,1)S(1)}, bf16[64,1152]{1,0:T(8,128)(2,1)S(1)}, u32[]{:S(2)}, u32[]{:S(2)}) collective-permute-start(bf16[64,1152]{1,0:T(8,128)(2,1)S(1)} %get-tuple-element.58), channel_id=1, source_target_pairs={{0,16},{4,20},{8,24},{12,28},{16,0},{20,4},{24,8},{28,12},{1,17},{... | collective-permute-start | bytes 442376 | tf_op jit(solution)/shard_map/ppermute | solution.py:243
  51.8 0.4 collective-permute-start.12
  52.3 1.5 %collective-permute-start.20 = (bf16[32,1024]{1,0:T(8,128)(2,1)S(1)}, bf16[32,1024]{1,0:T(8,128)(2,1)S(1)}, u32[]{:S(2)}, u32[]{:S(2)}) collective-permute-start(bf16[32,1024]{1,0:T(8,128)(2,1)S(1)} %get-tuple-element.71), channel_id=1, source_target_pairs={{0,1},{1,2},{2,3},{3,0},{4,5},{5,6},{6,7},{7,4},{8,9},{9,10},{10,1... | collective-permute-start | bytes 196616 | tf_op jit(solution)/shard_map/ppermute | solution.py:259
  53.8 0.5 collective-permute-done.4.q2
  54.3 2.6 %collective-permute-start.21 = (bf16[32,1024]{1,0:T(8,128)(2,1)S(1)}, bf16[32,1024]{1,0:T(8,128)(2,1)S(1)}, u32[]{:S(2)}, u32[]{:S(2)}) collective-permute-start(bf16[32,1024]{1,0:T(8,128)(2,1)S(1)} %get-tuple-element.72), channel_id=1, source_target_pairs={{0,2},{1,3},{2,0},{3,1},{4,6},{5,7},{6,4},{7,5},{8,10},{9,11},{10,... | collective-permute-start | bytes 196616 | tf_op jit(solution)/shard_map/ppermute | solution.py:259
  56.9 1.9 %collective-permute-done.5.q3 = bf16[2,3,6,2,1024]{4,3,2,1,0:T(2,128)(2,1)S(1)} collective-permute-done((bf16[2,3,6,2,1024]{4,3,2,1,0:T(2,128)(2,1)S(1)}, bf16[2,3,6,2,1024]{4,3,2,1,0:T(2,128)(2,1)S(1)}, u32[]{:S(2)}, u32[]{:S(2)}) %collective-permute-start.5) | collective-permute-done | bytes 147488 | tf_op jit(solution)/shard_map/ppermute | solution.py:363
  58.7 1.0 %collective-permute-start.22 = (bf16[32,1024]{1,0:T(8,128)(2,1)S(1)}, bf16[32,1024]{1,0:T(8,128)(2,1)S(1)}, u32[]{:S(2)}, u32[]{:S(2)}) collective-permute-start(bf16[32,1024]{1,0:T(8,128)(2,1)S(1)} %get-tuple-element.73), channel_id=1, source_target_pairs={{0,3},{1,0},{2,1},{3,2},{4,7},{5,4},{6,5},{7,6},{8,11},{9,8},{10,9... | collective-permute-start | bytes 196616 | tf_op jit(solution)/shard_map/ppermute | solution.py:259
  59.8 0.8 %unpack.1 = (bf16[6,12,2,1024]{3,2,1,0:T(2,128)(2,1)}, bf16[6,12,2,1024]{3,2,1,0:T(2,128)(2,1)}) custom-call(bf16[2,3,6,2,1024]{4,3,2,1,0:T(2,128)(2,1)S(1)} %get-tuple-element.44.q0, bf16[2,3,6,2,1024]{4,3,2,1,0:T(2,128)(2,1)S(1)} %collective-permute-done.3.q1, bf16[2,3,6,2,1024]{4,3,2,1,0:T(2,128)(2,1)S(1)} %collective-permute-done.4.q2, ...), custom_call_target="tpu_custom_call" | custom-call | tf_op jit(solution)/shard_map/unpack/pallas_call | solution.py:43
  60.7 1.0 %collective-permute-start.13 = (bf16[32,1152]{1,0:T(8,128)(2,1)S(1)}, bf16[32,1152]{1,0:T(8,128)(2,1)S(1)}, u32[]{:S(2)}, u32[]{:S(2)}) collective-permute-start(bf16[32,1152]{1,0:T(8,128)(2,1)S(1)} %get-tuple-element.61), channel_id=1, source_target_pairs={{0,1},{1,2},{2,3},{3,0},{4,5},{5,6},{6,7},{7,4},{8,9},{9,10},{10,1... | collective-permute-start | bytes 221192 | tf_op jit(solution)/shard_map/ppermute | solution.py:259
  61.8 1.2 %collective-permute-start.14 = (bf16[32,1152]{1,0:T(8,128)(2,1)S(1)}, bf16[32,1152]{1,0:T(8,128)(2,1)S(1)}, u32[]{:S(2)}, u32[]{:S(2)}) collective-permute-start(bf16[32,1152]{1,0:T(8,128)(2,1)S(1)} %get-tuple-element.62), channel_id=1, source_target_pairs={{0,2},{1,3},{2,0},{3,1},{4,6},{5,7},{6,4},{7,5},{8,10},{9,11},{10,... | collective-permute-start | bytes 221192 | tf_op jit(solution)/shard_map/ppermute | solution.py:259
  63.0 2.8 %collective-permute-start.15 = (bf16[32,1152]{1,0:T(8,128)(2,1)S(1)}, bf16[32,1152]{1,0:T(8,128)(2,1)S(1)}, u32[]{:S(2)}, u32[]{:S(2)}) collective-permute-start(bf16[32,1152]{1,0:T(8,128)(2,1)S(1)} %get-tuple-element.63), channel_id=1, source_target_pairs={{0,3},{1,0},{2,1},{3,2},{4,7},{5,4},{6,5},{7,6},{8,11},{9,8},{10,9... | collective-permute-start | bytes 221192 | tf_op jit(solution)/shard_map/ppermute | solution.py:259
  65.8 0.6 slice_bitcast_fusion
  66.4 0.9 %collective-permute-done.13 = bf16[32,1152]{1,0:T(8,128)(2,1)S(1)} collective-permute-done((bf16[32,1152]{1,0:T(8,128)(2,1)S(1)}, bf16[32,1152]{1,0:T(8,128)(2,1)S(1)}, u32[]{:S(2)}, u32[]{:S(2)}) %collective-permute-start.13) | collective-permute-done | bytes 73760 | tf_op jit(solution)/shard_map/ppermute | solution.py:259
  67.3 2.2 %collective-permute-done.14 = bf16[32,1152]{1,0:T(8,128)(2,1)S(1)} collective-permute-done((bf16[32,1152]{1,0:T(8,128)(2,1)S(1)}, bf16[32,1152]{1,0:T(8,128)(2,1)S(1)}, u32[]{:S(2)}, u32[]{:S(2)}) %collective-permute-start.14) | collective-permute-done | bytes 73760 | tf_op jit(solution)/shard_map/ppermute | solution.py:259
  69.5 0.7 slice_reduce_fusion
  70.2 0.7 pad_maximum_fusion
  (34 shorter events, 0.7 us)
Async XLA Ops:
  0.6 1.0 %copy-start.3 = (bf16[2,6,12,1024]{3,0,2,1:T(2,128)(2,1)S(1)}, bf16[2,6,12,1024]{3,0,2,1:T(2,128)(2,1)}, u32[]{:S(2)}) copy-start(bf16[2,6,12,1024]{3,0,2,1:T(2,128)(2,1)} %param.11) | copy-start | bytes 884740
  1.6 1.0 %copy-start.5 = (bf16[2,6,12,1024]{3,0,2,1:T(2,128)(2,1)S(1)}, bf16[2,6,12,1024]{3,0,2,1:T(2,128)(2,1)}, u32[]{:S(2)}) copy-start(bf16[2,6,12,1024]{3,0,2,1:T(2,128)(2,1)} %param.16) | copy-start | bytes 884740
  2.6 8.9 %collective-permute-start = (bf16[2,3,6,2,1024]{4,3,2,1,0:T(2,128)(2,1)S(1)}, bf16[2,3,6,2,1024]{4,3,2,1,0:T(2,128)(2,1)S(1)}, u32[]{:S(2)}, u32[]{:S(2)}) collective-permute-start(bf16[2,3,6,2,1024]{4,3,2,1,0:T(2,128)(2,1)S(1)} %get-tuple-element.40), channel_id=1, source_target_pairs={{0,3},{1,0},{2,1},{3,2},{4,7},{5,4},{6,5},{7,6},{8,11},{9,8},{10,9... | collective-permute-start | bytes 442376 | tf_op jit(solution)/shard_map/ppermute | solution.py:290
  7.7 4.3 %collective-permute-start.1 = (bf16[2,3,6,2,1024]{4,3,2,1,0:T(2,128)(2,1)S(1)}, bf16[2,3,6,2,1024]{4,3,2,1,0:T(2,128)(2,1)S(1)}, u32[]{:S(2)}, u32[]{:S(2)}) collective-permute-start(bf16[2,3,6,2,1024]{4,3,2,1,0:T(2,128)(2,1)S(1)} %get-tuple-element.41), channel_id=1, source_target_pairs={{0,28},{1,29},{2,30},{3,31},{4,0},{5,1},{6,2},{7,3},{8,4},{9,5},{1... | collective-permute-start | bytes 442376 | tf_op jit(solution)/shard_map/ppermute | solution.py:290
  9.3 5.2 %collective-permute-start.2 = (bf16[2,3,6,2,1024]{4,3,2,1,0:T(2,128)(2,1)S(1)}, bf16[2,3,6,2,1024]{4,3,2,1,0:T(2,128)(2,1)S(1)}, u32[]{:S(2)}, u32[]{:S(2)}) collective-permute-start(bf16[2,3,6,2,1024]{4,3,2,1,0:T(2,128)(2,1)S(1)} %get-tuple-element.42), channel_id=1, source_target_pairs={{0,31},{1,28},{2,29},{3,30},{4,3},{5,0},{6,1},{7,2},{8,7},{9,4},{1... | collective-permute-start | bytes 442376 | tf_op jit(solution)/shard_map/ppermute | solution.py:290
  14.5 1.9 %copy-start = (bf16[1024,1536]{1,0:T(8,128)(2,1)S(1)}, bf16[1024,1536]{1,0:T(8,128)(2,1)}, u32[]{:S(2)}) copy-start(bf16[1024,1536]{1,0:T(8,128)(2,1)} %w_qkv_ref.3) | copy-start | bytes 9437188
  16.4 1.2 %copy-start.2 = (bf16[512,1024]{1,0:T(8,128)(2,1)S(1)}, bf16[512,1024]{1,0:T(8,128)(2,1)}, u32[]{:S(2)}) copy-start(bf16[512,1024]{1,0:T(8,128)(2,1)} %w_out_ref.3) | copy-start | bytes 3145732
  17.6 1.0 %copy-start.4 = (bf16[2,6,12,1024]{3,0,2,1:T(2,128)(2,1)S(1)}, bf16[2,6,12,1024]{3,0,2,1:T(2,128)(2,1)}, u32[]{:S(2)}) copy-start(bf16[2,6,12,1024]{3,0,2,1:T(2,128)(2,1)} %param.11) | copy-start | bytes 884740
  18.6 1.0 %copy-start.6 = (bf16[2,6,12,1024]{3,0,2,1:T(2,128)(2,1)S(1)}, bf16[2,6,12,1024]{3,0,2,1:T(2,128)(2,1)}, u32[]{:S(2)}) copy-start(bf16[2,6,12,1024]{3,0,2,1:T(2,128)(2,1)} %param.16) | copy-start | bytes 884740
  19.5 0.7 copy-start.7
  20.2 0.7 copy-start.8
  20.9 7.0 %copy-start.1 = (bf16[1024,1536]{1,0:T(8,128)(2,1)S(1)}, bf16[1024,1536]{1,0:T(8,128)(2,1)}, u32[]{:S(2)}) copy-start(bf16[1024,1536]{1,0:T(8,128)(2,1)} %w_qkv_ref.3) | copy-start | bytes 9437188
  27.4 3.0 %collective-permute-start.7 = (bf16[144,2048]{1,0:T(8,128)(2,1)S(1)}, bf16[144,2048]{1,0:T(8,128)(2,1)S(1)}, u32[]{:S(2)}, u32[]{:S(2)}) collective-permute-start(bf16[144,2048]{1,0:T(8,128)(2,1)S(1)} %get-tuple-element.43.factor_ref.factor), channel_id=1, source_target_pairs={{0,4},{4,0},{8,12},{12,8},{16,20},{20,16},{24,28},{28,24},{1,5},{5... | collective-permute-start | bytes 1769480 | tf_op jit(solution)/shard_map/ppermute | solution.py:243
  27.5 2.8 %collective-permute-start.6 = (bf16[1024,144]{1,0:T(8,128)(2,1)S(1)}, bf16[1024,144]{1,0:T(8,128)(2,1)S(1)}, u32[]{:S(2)}, u32[]{:S(2)}) collective-permute-start(bf16[1024,144]{1,0:T(8,128)(2,1)S(1)} %get-tuple-element.51), channel_id=1, source_target_pairs={{0,4},{4,0},{8,12},{12,8},{16,20},{20,16},{24,28},{28,24},{1,5},{5... | collective-permute-start | bytes 884744 | tf_op jit(solution)/shard_map/ppermute | solution.py:243
  30.1 4.6 %collective-permute-start.8 = (f32[512,128]{1,0:T(8,128)S(1)}, f32[512,128]{1,0:T(8,128)S(1)}, u32[]{:S(2)}, u32[]{:S(2)}) collective-permute-start(f32[512,128]{1,0:T(8,128)S(1)} %get-tuple-element.53), channel_id=1, source_target_pairs={{0,4},{4,0},{8,12},{12,8},{16,20},{20,16},{24,28},{28,24},{1,5},{5... | collective-permute-start | bytes 786440 | tf_op jit(solution)/shard_map/ppermute | solution.py:243
  31.0 9.3 %collective-permute-start.16 = (bf16[128,1024]{1,0:T(8,128)(2,1)S(1)}, bf16[128,1024]{1,0:T(8,128)(2,1)S(1)}, u32[]{:S(2)}, u32[]{:S(2)}) collective-permute-start(bf16[128,1024]{1,0:T(8,128)(2,1)S(1)} %get-tuple-element.65), channel_id=1, source_target_pairs={{0,8},{4,12},{8,0},{12,4},{16,24},{20,28},{24,16},{28,20},{1,9},{5... | collective-permute-start | bytes 786440 | tf_op jit(solution)/shard_map/ppermute | solution.py:243
  33.2 9.2 %collective-permute-start.17 = (bf16[128,1024]{1,0:T(8,128)(2,1)S(1)}, bf16[128,1024]{1,0:T(8,128)(2,1)S(1)}, u32[]{:S(2)}, u32[]{:S(2)}) collective-permute-start(bf16[128,1024]{1,0:T(8,128)(2,1)S(1)} %get-tuple-element.66), channel_id=1, source_target_pairs={{0,16},{4,20},{8,24},{12,28},{16,0},{20,4},{24,8},{28,12},{1,17},{... | collective-permute-start | bytes 786440 | tf_op jit(solution)/shard_map/ppermute | solution.py:243
  35.4 13.3 %collective-permute-start.10 = (bf16[128,1152]{1,0:T(8,128)(2,1)S(1)}, bf16[128,1152]{1,0:T(8,128)(2,1)S(1)}, u32[]{:S(2)}, u32[]{:S(2)}) collective-permute-start(bf16[128,1152]{1,0:T(8,128)(2,1)S(1)} %get-tuple-element.56), channel_id=1, source_target_pairs={{0,16},{4,20},{8,24},{12,28},{16,0},{20,4},{24,8},{28,12},{1,17},{... | collective-permute-start | bytes 884744 | tf_op jit(solution)/shard_map/ppermute | solution.py:243
  36.0 12.7 %collective-permute-start.9 = (bf16[128,1152]{1,0:T(8,128)(2,1)S(1)}, bf16[128,1152]{1,0:T(8,128)(2,1)S(1)}, u32[]{:S(2)}, u32[]{:S(2)}) collective-permute-start(bf16[128,1152]{1,0:T(8,128)(2,1)S(1)} %get-tuple-element.55), channel_id=1, source_target_pairs={{0,8},{4,12},{8,0},{12,4},{16,24},{20,28},{24,16},{28,20},{1,9},{5... | collective-permute-start | bytes 884744 | tf_op jit(solution)/shard_map/ppermute | solution.py:243
  42.5 7.8 %collective-permute-start.18 = (bf16[64,1024]{1,0:T(8,128)(2,1)S(1)}, bf16[64,1024]{1,0:T(8,128)(2,1)S(1)}, u32[]{:S(2)}, u32[]{:S(2)}) collective-permute-start(bf16[64,1024]{1,0:T(8,128)(2,1)S(1)} %get-tuple-element.68), channel_id=1, source_target_pairs={{0,16},{4,20},{8,24},{12,28},{16,0},{20,4},{24,8},{28,12},{1,17},{... | collective-permute-start | bytes 393224 | tf_op jit(solution)/shard_map/ppermute | solution.py:243
  44.1 7.8 %collective-permute-start.19 = (bf16[64,1024]{1,0:T(8,128)(2,1)S(1)}, bf16[64,1024]{1,0:T(8,128)(2,1)S(1)}, u32[]{:S(2)}, u32[]{:S(2)}) collective-permute-start(bf16[64,1024]{1,0:T(8,128)(2,1)S(1)} %get-tuple-element.69), channel_id=1, source_target_pairs={{0,8},{4,12},{8,0},{12,4},{16,24},{20,28},{24,16},{28,20},{1,9},{5... | collective-permute-start | bytes 393224 | tf_op jit(solution)/shard_map/ppermute | solution.py:243
  44.1 8.1 %collective-permute-start.3 = (bf16[2,3,6,2,1024]{4,3,2,1,0:T(2,128)(2,1)S(1)}, bf16[2,3,6,2,1024]{4,3,2,1,0:T(2,128)(2,1)S(1)}, u32[]{:S(2)}, u32[]{:S(2)}) collective-permute-start(bf16[2,3,6,2,1024]{4,3,2,1,0:T(2,128)(2,1)S(1)} %get-tuple-element.45), channel_id=1, source_target_pairs={{0,1},{1,2},{2,3},{3,0},{4,5},{5,6},{6,7},{7,4},{8,9},{9,10},{10,1... | collective-permute-start | bytes 442376 | tf_op jit(solution)/shard_map/ppermute | solution.py:363
  48.7 5.6 %collective-permute-start.4 = (bf16[2,3,6,2,1024]{4,3,2,1,0:T(2,128)(2,1)S(1)}, bf16[2,3,6,2,1024]{4,3,2,1,0:T(2,128)(2,1)S(1)}, u32[]{:S(2)}, u32[]{:S(2)}) collective-permute-start(bf16[2,3,6,2,1024]{4,3,2,1,0:T(2,128)(2,1)S(1)} %get-tuple-element.46), channel_id=1, source_target_pairs={{0,4},{1,5},{2,6},{3,7},{4,8},{5,9},{6,10},{7,11},{8,12},{9,13},{1... | collective-permute-start | bytes 442376 | tf_op jit(solution)/shard_map/ppermute | solution.py:363
  48.7 10.1 %collective-permute-start.5 = (bf16[2,3,6,2,1024]{4,3,2,1,0:T(2,128)(2,1)S(1)}, bf16[2,3,6,2,1024]{4,3,2,1,0:T(2,128)(2,1)S(1)}, u32[]{:S(2)}, u32[]{:S(2)}) collective-permute-start(bf16[2,3,6,2,1024]{4,3,2,1,0:T(2,128)(2,1)S(1)} %get-tuple-element.47), channel_id=1, source_target_pairs={{0,5},{1,6},{2,7},{3,4},{4,9},{5,10},{6,11},{7,8},{8,13},{9,14},{1... | collective-permute-start | bytes 442376 | tf_op jit(solution)/shard_map/ppermute | solution.py:363
  50.3 10.3 %collective-permute-start.11 = (bf16[64,1152]{1,0:T(8,128)(2,1)S(1)}, bf16[64,1152]{1,0:T(8,128)(2,1)S(1)}, u32[]{:S(2)}, u32[]{:S(2)}) collective-permute-start(bf16[64,1152]{1,0:T(8,128)(2,1)S(1)} %get-tuple-element.58), channel_id=1, source_target_pairs={{0,16},{4,20},{8,24},{12,28},{16,0},{20,4},{24,8},{28,12},{1,17},{... | collective-permute-start | bytes 442376 | tf_op jit(solution)/shard_map/ppermute | solution.py:243
  51.8 8.8 %collective-permute-start.12 = (bf16[64,1152]{1,0:T(8,128)(2,1)S(1)}, bf16[64,1152]{1,0:T(8,128)(2,1)S(1)}, u32[]{:S(2)}, u32[]{:S(2)}) collective-permute-start(bf16[64,1152]{1,0:T(8,128)(2,1)S(1)} %get-tuple-element.59), channel_id=1, source_target_pairs={{0,8},{4,12},{8,0},{12,4},{16,24},{20,28},{24,16},{28,20},{1,9},{5... | collective-permute-start | bytes 442376 | tf_op jit(solution)/shard_map/ppermute | solution.py:243
  52.3 10.7 %collective-permute-start.20 = (bf16[32,1024]{1,0:T(8,128)(2,1)S(1)}, bf16[32,1024]{1,0:T(8,128)(2,1)S(1)}, u32[]{:S(2)}, u32[]{:S(2)}) collective-permute-start(bf16[32,1024]{1,0:T(8,128)(2,1)S(1)} %get-tuple-element.71), channel_id=1, source_target_pairs={{0,1},{1,2},{2,3},{3,0},{4,5},{5,6},{6,7},{7,4},{8,9},{9,10},{10,1... | collective-permute-start | bytes 196616 | tf_op jit(solution)/shard_map/ppermute | solution.py:259
  54.3 11.5 %collective-permute-start.21 = (bf16[32,1024]{1,0:T(8,128)(2,1)S(1)}, bf16[32,1024]{1,0:T(8,128)(2,1)S(1)}, u32[]{:S(2)}, u32[]{:S(2)}) collective-permute-start(bf16[32,1024]{1,0:T(8,128)(2,1)S(1)} %get-tuple-element.72), channel_id=1, source_target_pairs={{0,2},{1,3},{2,0},{3,1},{4,6},{5,7},{6,4},{7,5},{8,10},{9,11},{10,... | collective-permute-start | bytes 196616 | tf_op jit(solution)/shard_map/ppermute | solution.py:259
  58.7 7.0 %collective-permute-start.22 = (bf16[32,1024]{1,0:T(8,128)(2,1)S(1)}, bf16[32,1024]{1,0:T(8,128)(2,1)S(1)}, u32[]{:S(2)}, u32[]{:S(2)}) collective-permute-start(bf16[32,1024]{1,0:T(8,128)(2,1)S(1)} %get-tuple-element.73), channel_id=1, source_target_pairs={{0,3},{1,0},{2,1},{3,2},{4,7},{5,4},{6,5},{7,6},{8,11},{9,8},{10,9... | collective-permute-start | bytes 196616 | tf_op jit(solution)/shard_map/ppermute | solution.py:259
  60.7 6.6 %collective-permute-start.13 = (bf16[32,1152]{1,0:T(8,128)(2,1)S(1)}, bf16[32,1152]{1,0:T(8,128)(2,1)S(1)}, u32[]{:S(2)}, u32[]{:S(2)}) collective-permute-start(bf16[32,1152]{1,0:T(8,128)(2,1)S(1)} %get-tuple-element.61), channel_id=1, source_target_pairs={{0,1},{1,2},{2,3},{3,0},{4,5},{5,6},{6,7},{7,4},{8,9},{9,10},{10,1... | collective-permute-start | bytes 221192 | tf_op jit(solution)/shard_map/ppermute | solution.py:259
  61.8 7.7 %collective-permute-start.14 = (bf16[32,1152]{1,0:T(8,128)(2,1)S(1)}, bf16[32,1152]{1,0:T(8,128)(2,1)S(1)}, u32[]{:S(2)}, u32[]{:S(2)}) collective-permute-start(bf16[32,1152]{1,0:T(8,128)(2,1)S(1)} %get-tuple-element.62), channel_id=1, source_target_pairs={{0,2},{1,3},{2,0},{3,1},{4,6},{5,7},{6,4},{7,5},{8,10},{9,11},{10,... | collective-permute-start | bytes 221192 | tf_op jit(solution)/shard_map/ppermute | solution.py:259
  63.0 6.5 %collective-permute-start.15 = (bf16[32,1152]{1,0:T(8,128)(2,1)S(1)}, bf16[32,1152]{1,0:T(8,128)(2,1)S(1)}, u32[]{:S(2)}, u32[]{:S(2)}) collective-permute-start(bf16[32,1152]{1,0:T(8,128)(2,1)S(1)} %get-tuple-element.63), channel_id=1, source_target_pairs={{0,3},{1,0},{2,1},{3,2},{4,7},{5,4},{6,5},{7,6},{8,11},{9,8},{10,9... | collective-permute-start | bytes 221192 | tf_op jit(solution)/shard_map/ppermute | solution.py:259

commit v4 on v3

v4 whole, which is shorter than its diff:
```python
import functools
import itertools
import math

import jax
import jax.numpy as jnp
from jax import lax
from jax.experimental import pallas as pl
from jax.experimental.pallas import tpu as pltpu
from jax.sharding import PartitionSpec as P


HDIM = 64
F32 = jnp.float32
BF16 = jnp.bfloat16
LANES = 128

HBM_SPEC = pl.BlockSpec(memory_space=pltpu.HBM)

VMEM_SPEC = pl.BlockSpec(memory_space=pltpu.VMEM)
SMEM_SPEC = pl.BlockSpec(memory_space=pltpu.SMEM)


def dot(a, b, contract):
    return lax.dot_general(a, b, ((contract[0], contract[1]), ((), ())), preferred_element_type=F32)


def size_of(shape, dtype):
    rows = 16 if len(shape) > 1 and shape[-2] > 2 else shape[-2] if len(shape) > 1 else 1
    padded = [*shape[:-2], -(-shape[-2] // rows) * rows] if len(shape) > 1 else []
    return math.prod([*padded, -(-shape[-1] // LANES) * LANES]) * jnp.dtype(dtype).itemsize


def call(body, outs, args, scratch=(), smem=0, far=0, near_out=None, room=4):
    near_out = len(outs) if near_out is None else near_out
    near_at = smem + far
    held = sum(size_of(s, d) for s, d in outs[near_out:])
    held += sum(size_of(m.shape, m.dtype) for m in scratch if m.dtype in (F32, BF16))
    spaces = [None] * smem + [pltpu.HBM] * far + [pltpu.VMEM] * (len(args) - near_at)
    args = [
        a if space is None else pltpu.with_memory_space_constraint(a, space)
        for a, space in zip(args, spaces)
    ]
    return pl.pallas_call(
        body,
        out_shape=[
            pltpu.VMEM(s, d) if i < near_out else jax.ShapeDtypeStruct(s, d)
            for i, (s, d) in enumerate(outs)
        ],
        in_specs=[SMEM_SPEC] * smem + [HBM_SPEC] * far + [VMEM_SPEC] * (len(args) - near_at),
        out_specs=[VMEM_SPEC] * len(outs),
        scratch_shapes=list(scratch),
        compiler_params=pltpu.CompilerParams(vmem_limit_bytes=held + room * 2**20),
    )(*args)


def corners(rows, cols):
    return ((rows // 2, cols // 2), (rows // 2, 0), (0, cols // 2), (0, 0))


def run_copies(pairs, sem):
    copies = [
        pltpu.make_async_copy(source, target, sem.at[place])
        for place, (source, target) in enumerate(pairs)
    ]
    for item in copies:
        item.start()
    for item in copies:
        item.wait()


def pack_body(tok_ref, cot_ref, *refs):
    outs, sem = refs[:-1], refs[-1]
    rows, cols = tok_ref.shape[:2]
    pairs = []
    for out_ref, (row, col) in zip(outs, corners(rows, cols)):
        for part, ref in enumerate((tok_ref, cot_ref)):
            source = ref.at[pl.ds(row, rows // 2), pl.ds(col, cols // 2)]
            pairs.append((source, out_ref.at[part]))
    run_copies(pairs, sem)


def fetch_body(*refs):
    count = len(refs) // 2
    run_copies(list(zip(refs[:count], refs[count:-1])), refs[-1])


def unpack_body(q0, q1, q2, q3, y_ref, grad_ref):
    rows, cols = y_ref.shape[:2]
    for quad, (row, col) in zip((q0, q1, q2, q3), corners(rows, cols)):
        for part, ref in enumerate((y_ref, grad_ref)):
            ref[row : row + rows // 2, col : col + cols // 2] = quad[part]


def gather_window(quads, part, wide):
    levels, width = quads[0].shape[-2:]
    count = levels * quads[0].shape[1] * quads[0].shape[2]
    for place, item in enumerate(quads):
        wide[place * count : (place + 1) * count, :] = (
            item[part].reshape(count, width).astype(F32)
        )
    return wide[...]


def normalize(tokens_wide):
    average = jnp.mean(tokens_wide, axis=-1, keepdims=True)
    centered = tokens_wide - average
    inverse = lax.rsqrt(jnp.mean(centered * centered, axis=-1, keepdims=True) + 1e-05)
    return centered * inverse, inverse


def reorder(plan, places_ref, source, targets, base=0):
    group, counts, steps = plan
    half = source.shape[0] // 2
    for place in range(source.shape[0] // group):
        start = place * group
        if steps:
            block = places_ref[0] ^ steps[place][0]
            turned = lax.rem(places_ref[1] + steps[place][1], counts[1])
            start = pl.multiple_of((block * counts[1] + turned) * group, group)
        at = place * group
        target = targets[at // half]
        at = base + at % half
        target[at : at + group, :] = source[pl.ds(start, group), :]


def attention_body(
    plan, places_ref, r0, r1, r2, r3, w_qkv_ref, w_out_ref, gain_ref, bias_ref,
    mine_ref, peer_ref, factor_ref, wide, side,
):
    quads = (r0, r1, r2, r3)
    inner, width = w_out_ref.shape
    heads = inner // HDIM
    scale = HDIM ** (-0.5)
    grad = gather_window(quads, 1, wide).astype(BF16)
    total = grad.shape[0]
    side[...] = grad.T
    reorder(plan, places_ref, side, (mine_ref, peer_ref), width // 2)
    standard, _ = normalize(gather_window(quads, 0, wide))
    normed = (standard * gain_ref[...] + bias_ref[...]).astype(BF16)
    side[...] = normed.T
    reorder(plan, places_ref, side, (mine_ref, peer_ref))
    projected = dot(normed, w_qkv_ref[...], ((1,), (0,))).astype(BF16)
    grad_att = dot(grad, w_out_ref[...], ((1,), (1,))).astype(BF16)
    count = total // 4
    row_id = lax.broadcasted_iota(jnp.int32, (total, total), 0) // count
    col_id = lax.broadcasted_iota(jnp.int32, (total, total), 1) // count
    last_lat, last_lon = ((places_ref[i] == n - 1).astype(jnp.int32) for i, n in enumerate(plan[1]))
    apart = jnp.where((row_id >= 2) != (col_id >= 2), last_lat, 0) + jnp.where(
        (row_id % 2) != (col_id % 2), last_lon, 0
    )
    blocked = apart > 0
    for head in range(heads):
        at = head * HDIM
        query = projected[:, at : at + HDIM]
        key = projected[:, inner + at : inner + at + HDIM]
        value = projected[:, 2 * inner + at : 2 * inner + at + HDIM]
        grad_head = grad_att[:, at : at + HDIM]
        scores = dot(query, key, ((1,), (1,))) * scale
        scores = jnp.where(blocked, -1e30, scores)
        exps = jnp.exp(scores - jnp.max(scores, axis=-1, keepdims=True))
        probs = exps / jnp.sum(exps, axis=-1, keepdims=True)
        low = probs.astype(BF16)
        factor_ref[:, at : at + HDIM] = dot(low, value, ((1,), (0,))).astype(BF16)
        grad_prob = dot(grad_head, value, ((1,), (1,)))
        inner_sum = jnp.sum(probs * grad_prob, axis=-1, keepdims=True)
        grad_score = (probs * (grad_prob - inner_sum)).astype(BF16)
        factor_ref[:, inner + at : inner + at + HDIM] = dot(low, grad_head, ((0,), (0,))).astype(
            BF16
        )
        factor_ref[:, 2 * inner + at : 2 * inner + at + HDIM] = (
            dot(grad_score, key, ((1,), (0,))) * scale
        ).astype(BF16)
        factor_ref[:, 3 * inner + at : 3 * inner + at + HDIM] = (
            dot(grad_score, query, ((0,), (0,))) * scale
        ).astype(BF16)


def gradient_body(
    plan, places_ref, r0, r1, r2, r3, factor_ref, w_qkv_ref, w_out_ref, gain_ref,
    o0, o1, o2, o3, mine_ref, peer_ref, wide, flat,
):
    quads = (r0, r1, r2, r3)
    inner, width = w_out_ref.shape
    outs = (o0, o1, o2, o3)
    quad = o0.shape[1:]
    count = quad[0] * quad[1] * quad[2]
    tokens_wide = gather_window(quads, 0, wide)
    standard, inverse = normalize(tokens_wide)
    grad_normed = dot(factor_ref[:, inner : 2 * inner], w_qkv_ref[:, 2 * inner :], ((1,), (1,)))
    grad_normed += dot(factor_ref[:, 2 * inner :], w_qkv_ref[:, : 2 * inner], ((1,), (1,)))
    sums = [
        jnp.sum(grad_normed * standard, axis=0, keepdims=True),
        jnp.sum(grad_normed, axis=0, keepdims=True),
    ]
    line = lax.broadcasted_iota(jnp.int32, (LANES, width), 0)
    flat[...] = jnp.where(line == 0, sums[0], jnp.where(line == 1, sums[1], 0.0)).T
    reorder(plan, places_ref, flat, (mine_ref, peer_ref))
    wide[...] = tokens_wide + dot(factor_ref[:, :inner], w_out_ref[...], ((1,), (0,)))
    for place, out in enumerate(outs):
        out[0] = wide[place * count : (place + 1) * count, :].astype(BF16).reshape(quad)
    grad_hat = grad_normed * gain_ref[...]
    first = jnp.mean(grad_hat, axis=-1, keepdims=True)
    second = jnp.mean(grad_hat * standard, axis=-1, keepdims=True)
    change = (grad_hat - first - standard * second) * inverse
    wide[...] = gather_window(quads, 1, wide) + change
    for place, out in enumerate(outs):
        out[1] = wide[place * count : (place + 1) * count, :].astype(BF16).reshape(quad)


def split_store(value, outs, cols):
    both, send_a, send_b = outs
    quarter = send_a.shape[0]
    for out, to, start in (
        (both, 0, 0), (send_a, 0, quarter), (both, quarter, 2 * quarter), (send_b, 0, 3 * quarter),
    ):
        out[to : to + quarter, cols] = value[start : start + quarter].astype(BF16)


def early_body(mine, got, factor, factor_got, *outs):
    half = mine.shape[0] // 2
    inner = factor.shape[1] // 4
    for part in range(2):
        rows = slice((1 - part) * half, (2 - part) * half)
        cols = slice(part * inner, (part + 1) * inner)
        value = dot(mine[rows, :], factor[:, cols], ((1,), (0,)))
        value += dot(got[rows, :], factor_got[:, cols], ((1,), (0,)))
        split_store(value, outs, cols)


def late_body(mine, got, factor, factor_got, sums, sums_got, *outs):
    half = mine.shape[0] // 2
    inner = factor.shape[1] // 4
    for part in range(2):
        cols = slice((2 + part) * inner, (3 + part) * inner)
        value = dot(mine[:half, :], factor[:, cols], ((1,), (0,)))
        value += dot(got[:half, :], factor_got[:, cols], ((1,), (0,)))
        split_store(value, outs, slice(part * inner, (part + 1) * inner))
    split_store(sums[...] + sums_got[...], outs, slice(2 * inner, 2 * inner + LANES))


def added(*refs):
    total = refs[0].astype(F32)
    for ref in refs[1:]:
        total += ref.astype(F32)
    return total


def second_body(keep, got_a, got_b, both, send_a, send_b):
    part = send_a.shape[0]
    for side, (got, send) in enumerate(((got_a, send_a), (got_b, send_b))):
        at = 2 * part * side
        both[part * side : part * (side + 1), :] = added(
            keep[at : at + part, :], got[:part, :]
        ).astype(BF16)
        send[...] = added(keep[at + part : at + 2 * part, :], got[part:, :]).astype(BF16)


def third_body(keep, got_a, got_b, *outs):
    part = got_a.shape[0]
    size = outs[0].shape[0]
    for place, out in enumerate(outs):
        start = place * size
        got = got_a if start < part else got_b
        within = start % part
        out[...] = added(keep[start : start + size, :], got[within : within + size, :]).astype(BF16)


def turn_body(keep, got_a, got_b, *outs):
    part = got_a.shape[0]
    size = outs[0].shape[0] // 2
    per_side = len(outs) // 2
    for place, out in enumerate(outs):
        got, base = (got_a, 0) if place < per_side else (got_b, part)
        for nested in range(2):
            at = nested * (part // 2) + (place % per_side) * size
            out[nested * size : (nested + 1) * size, :] = added(
                keep[base + at : base + at + size, :], got[at : at + size, :]
            ).astype(BF16)


def meet_body(*refs):
    pieces, (base, send_a, send_b) = refs[:-3], refs[-3:]
    size = base.shape[0]
    per_side = len(pieces) // 2
    base[...] = added(*(item[:size, :] for item in pieces))
    send_a[...] = added(*(item[size:, :] for item in pieces[:per_side])).astype(BF16)
    send_b[...] = added(*(item[size:, :] for item in pieces[per_side:])).astype(BF16)


def early_end_body(factor, base, got_a, got_b, value_ref, out_ref):
    total = added(base[...], got_a[...], got_b[...]) * factor
    inner = out_ref.shape[1]
    out_ref[...] = total[:, :inner]
    value_ref[...] = total[:, inner:]


def late_end_body(factor, value_ref, *refs):
    pieces, (qkv_ref, gain_ref, bias_ref) = refs[:-3], refs[-3:]
    total = added(*(item[...] for item in pieces)) * factor
    cols = total.shape[1] - LANES
    qkv_ref[:, :cols] = total[:, :cols]
    qkv_ref[:, cols:] = value_ref[...]
    rows = total.shape[0]
    flat = jnp.concatenate([total[:, cols:], jnp.zeros((LANES - rows, LANES), F32)], axis=0).T
    gain_ref[...] = flat[0:1, :rows]
    bias_ref[...] = flat[1:2, :rows]


def xor_pairs(bit):
    return [(i, i ^ bit) for i in range(lax.axis_size("lat"))]


def swap(value, bit):
    return lax.ppermute(value, "lat", xor_pairs(bit))


def turn(pieces):
    count = len(pieces)
    return [pieces[0]] + [
        lax.ppermute(pieces[k], "lon", [(i, (i + k) % count) for i in range(count)])
        for k in range(1, count)
    ]


def sum_early(both, send_a, send_b, lon_count, factor):
    quarter, cols = send_a.shape
    size = quarter // lon_count
    got_a, got_b = swap(send_a, 2), swap(send_b, 4)
    pieces = call(turn_body, [((2 * size, cols), BF16)] * lon_count, (both, got_a, got_b))
    pieces = turn(pieces)
    base, send_a, send_b = call(
        meet_body, [((size, cols), F32)] + [((size, cols), BF16)] * 2, pieces
    )
    got_a, got_b = swap(send_a, 4), swap(send_b, 2)
    shape = ((size, cols // 2), F32)
    return call(
        functools.partial(early_end_body, factor), [shape] * 2,
        (base, got_a, got_b), near_out=1,
    )


def sum_late(both, send_a, send_b, value, lon_count, factor):
    quarter, cols = send_a.shape
    part = quarter // 2
    size = 2 * part // lon_count
    got_a, got_b = swap(send_a, 2), swap(send_b, 4)
    both, send_a, send_b = call(
        second_body, [((n * part, cols), BF16) for n in (2, 1, 1)], (both, got_a, got_b)
    )
    got_a, got_b = swap(send_a, 4), swap(send_b, 2)
    pieces = call(third_body, [((size, cols), BF16)] * lon_count, (both, got_a, got_b))
    pieces = turn(pieces)
    return call(
        functools.partial(late_end_body, factor),
        [((size, cols - LANES + value.shape[1]), F32)] + [((1, size), F32)] * 2,
        (value, *pieces), near_out=0,
    )


def device_step(tokens, layer_norm_gain, layer_norm_bias, w_qkv, w_out, output_cotangent):
    levels, lat_rows, lon_cols, width = tokens.shape
    inner = w_out.shape[0]
    lat_count, lon_count = lax.axis_size("lat"), lax.axis_size("lon")
    lat_place, lon_place = lax.axis_index("lat"), lax.axis_index("lon")
    cells = levels * lat_rows * lon_cols
    norm_factor = 1.0 / math.sqrt(cells * lat_count * lon_count)

    def moved(lat_step, lon_step):
        pairs = []
        for i in range(lat_count):
            for j in range(lon_count):
                to = ((i + lat_step) % lat_count) * lon_count + (j + lon_step) % lon_count
                pairs.append((i * lon_count + j, to))
        return pairs

    steps = ((0, 1), (1, 0), (1, 1))
    grid = (lat_rows, lon_cols, levels, width)
    quad = (2, lat_rows // 2, lon_cols // 2, levels, width)
    tok = tokens.transpose(1, 2, 0, 3)
    cot = output_cotangent.transpose(1, 2, 0, 3)
    own, *sends = call(
        pack_body, [(quad, BF16)] * 4, (tok, cot), far=2,
        scratch=[pltpu.SemaphoreType.DMA((8,))],
    )
    quads = [own] + [
        lax.ppermute(item, ("lat", "lon"), moved(-a, -b)) for item, (a, b) in zip(sends, steps)
    ]
    params = (w_qkv, w_out, layer_norm_gain.reshape(1, width), layer_norm_bias.reshape(1, width))
    params = call(
        fetch_body, [(item.shape, item.dtype) for item in params], params, far=4,
        scratch=[pltpu.SemaphoreType.DMA((4,))],
    )

    share = width // (lat_count * lon_count)
    hyper = lat_count == 8 and lon_count % 2 == 0 and share % 16 == 0
    order = []
    if hyper:
        half_lon = lon_count // 2
        for core, side, outer, nested, k in itertools.product(
            range(2), range(2), range(2), range(2), range(half_lon)
        ):
            x_bit, y_bit = (outer, nested) if side == 0 else (nested, outer)
            order.append((core + 2 * x_bit + 4 * y_bit, side * half_lon + k))
    plan = (share if hyper else 16, (lat_count, lon_count), tuple(order))
    places = jnp.where(jnp.arange(2) == 0, lat_place, lon_place).astype(jnp.int32)
    mine, peer, factor = call(
        functools.partial(attention_body, plan),
        [((width, cells), BF16)] * 2 + [((cells, 4 * inner), BF16)],
        (places, *quads, *params),
        scratch=[pltpu.VMEM((cells, width), F32), pltpu.VMEM((width, cells), BF16)],
        smem=1,
    )
    q0, q1, q2, q3, sums, sums_peer = call(
        functools.partial(gradient_body, plan),
        [(quad, BF16)] * 4 + [((width // 2, LANES), F32)] * 2,
        (places, *quads, factor, *params[:3]),
        scratch=[pltpu.VMEM((cells, width), F32), pltpu.VMEM((width, LANES), F32)],
        smem=1,
    )
    if hyper:
        factor_got = swap(factor, 1)
        got = swap(peer, 1)
        sums_got = swap(sums_peer, 1)
        quarter = width // 8

        def shapes(cols):
            return [((rows, cols), BF16) for rows in (2 * quarter, quarter, quarter)]

        early = call(early_body, shapes(2 * inner), (mine, got, factor, factor_got))
        late = call(
            late_body, shapes(2 * inner + LANES),
            (mine, got, factor, factor_got, sums, sums_got),
        )
        value, d_out = sum_early(*early, lon_count, norm_factor)
        d_qkv, gain, bias = sum_late(*late, value, lon_count, norm_factor)
    else:
        half = width // 2
        normed_t = jnp.concatenate([mine[:half], peer[:half]], axis=0)
        cot_t = jnp.concatenate([mine[half:], peer[half:]], axis=0)
        whole = jnp.concatenate(
            [
                dot(cot_t, factor[:, :inner], ((1,), (0,))),
                dot(normed_t, factor[:, inner:], ((1,), (0,))),
                jnp.concatenate([sums, sums_peer], axis=0),
            ],
            axis=1,
        )
        whole = lax.psum_scatter(whole, "lat", scatter_dimension=0, tiled=True)
        whole = lax.psum_scatter(whole, "lon", scatter_dimension=0, tiled=True)
        whole = whole * norm_factor
        d_out = whole[:, :inner]
        d_qkv = jnp.concatenate([whole[:, 2 * inner : 4 * inner], whole[:, inner : 2 * inner]], axis=1)
        gain, bias = whole[:, 4 * inner], whole[:, 4 * inner + 1]
    back = [q0] + [
        lax.ppermute(item, ("lat", "lon"), moved(a, b))
        for item, (a, b) in zip((q1, q2, q3), steps)
    ]
    y_out, token_gradient = call(unpack_body, [(grid, BF16)] * 2, back, near_out=0)
    return (
        y_out.transpose(2, 0, 1, 3),
        token_gradient.transpose(2, 0, 1, 3),
        d_qkv,
        d_out.T,
        gain.reshape(share),
        bias.reshape(share),
    )


def solution(mesh):
    in_specs = (P(None, "lat", "lon", None), P(), P(), P(), P(), P(None, "lat", "lon", None))
    out_specs = (
        P(None, "lat", "lon", None),
        P(None, "lat", "lon", None),
        P(("lat", "lon"), None),
        P(None, ("lat", "lon")),
        P(("lat", "lon")),
        P(("lat", "lon")),
    )
    return jax.shard_map(
        device_step, mesh=mesh, in_specs=in_specs, out_specs=out_specs, check_vma=False
    )
```

time: 71.3 us -> 70.1 us (0.983); the launches traced: 70.9 us -> 69 us
  local copies, waits for them, and re-layouts: 9.68 us -> 0 us
  waiting for transfers between devices: 20.1 us -> 25.6 us
  Pallas kernels: 11.3 us -> 16.1 us
  other arithmetic: 2.13 us -> 0.01 us
    unnamed x18 -> x0, local copies, waits for them, and re-layouts: 8.33 us -> none
    pallas_call x10 -> x13, Pallas kernels: 11.3 us -> 16.1 us  [call(): pl.pallas_call(body, out_shape=[pltpu.VMEM(s, d) if i < near_out else jax...]
    ppermute x11, waiting for transfers between devices: 11.7 us -> 15.9 us  [swap(): return lax.ppermute(value, 'lat', xor_pairs(bit))]
    ppermute x12, waiting for transfers between devices: 8.39 us -> 9.62 us  [the longest x6 7.52 us: turn(): lax.ppermute(pieces[k], 'lon', [(i, (i + k) % count) for i in range(count)])]
  transfers between devices with their start and end apart: 23 -> 23, of which waited for: 10 -> 12; matrix products, arithmetic and copies ran while one was open for 3% -> 0% of each run, Pallas kernels for 7% -> 10%
where the time goes in v4:
time: 70.1 us; the launch traced here: 69 us
  starting transfers between devices  26.6 us (38%)
  waiting for transfers between devices  25.6 us (37%)
  Pallas kernels  16.1 us (23%)
  between operations  0.75 us (1%)
    pallas_call x13, Pallas kernels, call(): pl.pallas_call(body, out_shape=[pltpu.VMEM(s, d) if i < near_out else jax...  16.1 us
    ppermute x11, waiting for transfers between devices, swap(): return lax.ppermute(value, 'lat', xor_pairs(bit))  15.9 us
    ppermute x6, starting transfers between devices, turn(): lax.ppermute(pieces[k], 'lon', [(i, (i + k) % count) for i in range(count)])  10.2 us
    ppermute x11, starting transfers between devices, swap(): return lax.ppermute(value, 'lat', xor_pairs(bit))  8.29 us
    ppermute x3, starting transfers between devices, device_step(): lax.ppermute(item, ('lat', 'lon'), moved(-a, -b))  7.58 us
    ppermute x6, waiting for transfers between devices, turn(): lax.ppermute(pieces[k], 'lon', [(i, (i + k) % count) for i in range(count)])  7.52 us
    ppermute x3, waiting for transfers between devices, device_step(): lax.ppermute(item, ('lat', 'lon'), moved(-a, -b))  2.09 us
  transfers between devices with their start and end apart: 23, of which 12 were waited for; matrix products, arithmetic and copies ran while one was open for 0% of the time, Pallas kernels for 10%

profile of v4, /device:TPU:0, one launch (start us, length us, event | category | flops | bytes accessed | tf_op | source)
XLA Modules:
  0.0 69.0 jit_solution(3750896143339847607)
XLA Ops:
  0.6 1.2 %shard_map.109 = (bf16[2,3,6,2,1024]{4,3,2,1,0:T(2,128)(2,1)S(1)}, bf16[2,3,6,2,1024]{4,3,2,1,0:T(2,128)(2,1)S(1)}, bf16[2,3,6,2,1024]{4,3,2,1,0:T(2,128)(2,1)S(1)}, bf16[2,3,6,2,1024]{4,3,2,1,0:T(2,128)(2,1)S(1)}) custom-call(bf16[6,12,2,1024]{3,2,1,0:T(2,128)(2,1)} %bitcast.9, bf16[6,12,2,1024]{3,2,1,0:T(2,128)(2,1)} %bitcast.10), custom_call_target="tpu_custom_call" | custom-call | tf_op jit(solution)/shard_map/pallas_call | solution.py:44
  1.8 5.1 %collective-permute-start = (bf16[2,3,6,2,1024]{4,3,2,1,0:T(2,128)(2,1)S(1)}, bf16[2,3,6,2,1024]{4,3,2,1,0:T(2,128)(2,1)S(1)}, u32[]{:S(2)}, u32[]{:S(2)}) collective-permute-start(bf16[2,3,6,2,1024]{4,3,2,1,0:T(2,128)(2,1)S(1)} %get-tuple-element.51), channel_id=1, source_target_pairs={{0,3},{1,0},{2,1},{3,2},{4,7},{5,4},{6,5},{7,6},{8,11},{9,8},{10,9... | collective-permute-start | bytes 442376 | tf_op jit(solution)/shard_map/ppermute | solution.py:387
  7.0 1.6 %collective-permute-start.1 = (bf16[2,3,6,2,1024]{4,3,2,1,0:T(2,128)(2,1)S(1)}, bf16[2,3,6,2,1024]{4,3,2,1,0:T(2,128)(2,1)S(1)}, u32[]{:S(2)}, u32[]{:S(2)}) collective-permute-start(bf16[2,3,6,2,1024]{4,3,2,1,0:T(2,128)(2,1)S(1)} %get-tuple-element.52), channel_id=1, source_target_pairs={{0,28},{1,29},{2,30},{3,31},{4,0},{5,1},{6,2},{7,3},{8,4},{9,5},{1... | collective-permute-start | bytes 442376 | tf_op jit(solution)/shard_map/ppermute | solution.py:387
  8.6 0.8 %collective-permute-start.2 = (bf16[2,3,6,2,1024]{4,3,2,1,0:T(2,128)(2,1)S(1)}, bf16[2,3,6,2,1024]{4,3,2,1,0:T(2,128)(2,1)S(1)}, u32[]{:S(2)}, u32[]{:S(2)}) collective-permute-start(bf16[2,3,6,2,1024]{4,3,2,1,0:T(2,128)(2,1)S(1)} %get-tuple-element.53), channel_id=1, source_target_pairs={{0,31},{1,28},{2,29},{3,30},{4,3},{5,0},{6,1},{7,2},{8,7},{9,4},{1... | collective-permute-start | bytes 442376 | tf_op jit(solution)/shard_map/ppermute | solution.py:387
  9.4 2.2 %shard_map.110 = (bf16[1024,1536]{1,0:T(8,128)(2,1)S(1)}, bf16[512,1024]{1,0:T(8,128)(2,1)S(1)}, f32[1,1024]{1,0:T(1,128)S(1)}, f32[1,1024]{1,0:T(1,128)S(1)}) custom-call(bf16[1024,1536]{1,0:T(8,128)(2,1)} %refs_0_.1, bf16[512,1024]{1,0:T(8,128)(2,1)} %refs_1_.1, f32[1,1024]{1,0:T(1,128)} %bitcast.11, f32[1,1024]{1,0:T(1,128)} %bitcast.12), custom_call_target="tpu_custom_call" | custom-call | tf_op jit(solution)/shard_map/pallas_call | solution.py:44
  11.7 0.0 collective-permute-done.1.r2
  11.7 2.1 %collective-permute-done.2.r3 = bf16[2,3,6,2,1024]{4,3,2,1,0:T(2,128)(2,1)S(1)} collective-permute-done((bf16[2,3,6,2,1024]{4,3,2,1,0:T(2,128)(2,1)S(1)}, bf16[2,3,6,2,1024]{4,3,2,1,0:T(2,128)(2,1)S(1)}, u32[]{:S(2)}, u32[]{:S(2)}) %collective-permute-start.2) | collective-permute-done | bytes 147488 | tf_op jit(solution)/shard_map/ppermute | solution.py:387
  13.8 6.4 %shard_map.111 = (bf16[1024,144]{1,0:T(8,128)(2,1)S(1)}, bf16[1024,144]{1,0:T(8,128)(2,1)S(1)}, bf16[144,2048]{1,0:T(8,128)(2,1)S(1)}) custom-call(s32[2]{0:T(128)S(1)} %compare_select_fusion.places_ref, bf16[2,3,6,2,1024]{4,3,2,1,0:T(2,128)(2,1)S(1)} %get-tuple-element.50.r0, bf16[2,3,6,2,1024]{4,3,2,1,0:T(2,128)(2,1)S(1)} %collective-permute-done.r1, ...), custom_call_target="tpu_custom_call" | custom-call | tf_op jit(solution)/shard_map/pallas_call | solution.py:44
  20.2 0.2 collective-permute-start.7
  20.4 0.4 collective-permute-start.6
  20.8 2.2 %shard_map.112 = (bf16[2,3,6,2,1024]{4,3,2,1,0:T(2,128)(2,1)S(1)}, bf16[2,3,6,2,1024]{4,3,2,1,0:T(2,128)(2,1)S(1)}, bf16[2,3,6,2,1024]{4,3,2,1,0:T(2,128)(2,1)S(...) custom-call(s32[2]{0:T(128)S(1)} %compare_select_fusion.places_ref, ...), custom_call_target="tpu_custom_call" | custom-call | tf_op jit(solution)/shard_map/pallas_call | solution.py:44
  23.0 0.2 collective-permute-start.15
  23.2 1.4 %collective-permute-done.15.sums_got = f32[512,128]{1,0:T(8,128)S(1)} collective-permute-done((f32[512,128]{1,0:T(8,128)S(1)}, f32[512,128]{1,0:T(8,128)S(1)}, u32[]{:S(2)}, u32[]{:S(2)}) %collective-permute-start.15) | collective-permute-done | bytes 262176 | tf_op jit(solution)/shard_map/ppermute | solution.py:315
  24.6 0.7 %shard_map.118 = (bf16[256,1152]{1,0:T(8,128)(2,1)S(1)}, bf16[128,1152]{1,0:T(8,128)(2,1)S(1)}, bf16[128,1152]{1,0:T(8,128)(2,1)S(1)}) custom-call(bf16[1024,144]{1,0:T(8,128)(2,1)S(1)} %get-tuple-element.65.mine, bf16[1024,144]{1,0:T(8,128)(2,1)S(1)} %collective-permute-done.6.got, bf16[144,2048]{1,0:T(8,128)(2,1)S(1)} %get-tuple-element.58.factor_ref.factor, ...), custom_call_target="tpu_custom_call" | custom-call | tf_op jit(solution)/shard_map/pallas_call | solution.py:44
  25.3 1.9 %collective-permute-start.16 = (bf16[128,1152]{1,0:T(8,128)(2,1)S(1)}, bf16[128,1152]{1,0:T(8,128)(2,1)S(1)}, u32[]{:S(2)}, u32[]{:S(2)}) collective-permute-start(bf16[128,1152]{1,0:T(8,128)(2,1)S(1)} %get-tuple-element.81), channel_id=1, source_target_pairs={{0,8},{4,12},{8,0},{12,4},{16,24},{20,28},{24,16},{28,20},{1,9},{5... | collective-permute-start | bytes 884744 | tf_op jit(solution)/shard_map/ppermute | solution.py:315
  27.2 1.5 %collective-permute-start.17 = (bf16[128,1152]{1,0:T(8,128)(2,1)S(1)}, bf16[128,1152]{1,0:T(8,128)(2,1)S(1)}, u32[]{:S(2)}, u32[]{:S(2)}) collective-permute-start(bf16[128,1152]{1,0:T(8,128)(2,1)S(1)} %get-tuple-element.82), channel_id=1, source_target_pairs={{0,16},{4,20},{8,24},{12,28},{16,0},{20,4},{24,8},{28,12},{1,17},{... | collective-permute-start | bytes 884744 | tf_op jit(solution)/shard_map/ppermute | solution.py:315
  28.7 0.7 %shard_map.114 = (bf16[256,1024]{1,0:T(8,128)(2,1)S(1)}, bf16[128,1024]{1,0:T(8,128)(2,1)S(1)}, bf16[128,1024]{1,0:T(8,128)(2,1)S(1)}) custom-call(bf16[1024,144]{1,0:T(8,128)(2,1)S(1)} %get-tuple-element.65.mine, bf16[1024,144]{1,0:T(8,128)(2,1)S(1)} %collective-permute-done.6.got, bf16[144,2048]{1,0:T(8,128)(2,1)S(1)} %get-tuple-element.58.factor_ref.factor, ...), custom_call_target="tpu_custom_call" | custom-call | tf_op jit(solution)/shard_map/pallas_call | solution.py:44
  29.4 0.1 collective-permute-start.8
  29.6 0.6 collective-permute-start.9
  30.2 0.5 collective-permute-start.3
  30.7 4.5 %collective-permute-done.16.got_a = bf16[128,1152]{1,0:T(8,128)(2,1)S(1)} collective-permute-done((bf16[128,1152]{1,0:T(8,128)(2,1)S(1)}, bf16[128,1152]{1,0:T(8,128)(2,1)S(1)}, u32[]{:S(2)}, u32[]{:S(2)}) %collective-permute-start.16) | collective-permute-done | bytes 294944 | tf_op jit(solution)/shard_map/ppermute | solution.py:315
  35.3 1.8 %collective-permute-done.17.got_b = bf16[128,1152]{1,0:T(8,128)(2,1)S(1)} collective-permute-done((bf16[128,1152]{1,0:T(8,128)(2,1)S(1)}, bf16[128,1152]{1,0:T(8,128)(2,1)S(1)}, u32[]{:S(2)}, u32[]{:S(2)}) %collective-permute-start.17) | collective-permute-done | bytes 294944 | tf_op jit(solution)/shard_map/ppermute | solution.py:315
  37.1 0.1 shard_map.119
  37.2 1.6 %collective-permute-start.18 = (bf16[64,1152]{1,0:T(8,128)(2,1)S(1)}, bf16[64,1152]{1,0:T(8,128)(2,1)S(1)}, u32[]{:S(2)}, u32[]{:S(2)}) collective-permute-start(bf16[64,1152]{1,0:T(8,128)(2,1)S(1)} %get-tuple-element.84), channel_id=1, source_target_pairs={{0,16},{4,20},{8,24},{12,28},{16,0},{20,4},{24,8},{28,12},{1,17},{... | collective-permute-start | bytes 442376 | tf_op jit(solution)/shard_map/ppermute | solution.py:315
  38.8 0.1 collective-permute-start.19
  38.9 2.0 %collective-permute-done.8.got_a = bf16[128,1024]{1,0:T(8,128)(2,1)S(1)} collective-permute-done((bf16[128,1024]{1,0:T(8,128)(2,1)S(1)}, bf16[128,1024]{1,0:T(8,128)(2,1)S(1)}, u32[]{:S(2)}, u32[]{:S(2)}) %collective-permute-start.8) | collective-permute-done | bytes 262176 | tf_op jit(solution)/shard_map/ppermute | solution.py:315
  40.9 1.8 %collective-permute-done.9.got_b = bf16[128,1024]{1,0:T(8,128)(2,1)S(1)} collective-permute-done((bf16[128,1024]{1,0:T(8,128)(2,1)S(1)}, bf16[128,1024]{1,0:T(8,128)(2,1)S(1)}, u32[]{:S(2)}, u32[]{:S(2)}) %collective-permute-start.9) | collective-permute-done | bytes 262176 | tf_op jit(solution)/shard_map/ppermute | solution.py:315
  42.7 0.1 shard_map.115
  42.8 1.3 %collective-permute-start.10 = (bf16[64,1024]{1,0:T(8,128)(2,1)S(1)}, bf16[64,1024]{1,0:T(8,128)(2,1)S(1)}, u32[]{:S(2)}, u32[]{:S(2)}) collective-permute-start(bf16[64,1024]{1,0:T(8,128)(2,1)S(1)} %get-tuple-element.71), channel_id=1, source_target_pairs={{0,1},{1,2},{2,3},{3,0},{4,5},{5,6},{6,7},{7,4},{8,9},{9,10},{10,1... | collective-permute-start | bytes 393224 | tf_op jit(solution)/shard_map/ppermute | solution.py:321
  44.2 2.4 %collective-permute-done.18.got_a = bf16[64,1152]{1,0:T(8,128)(2,1)S(1)} collective-permute-done((bf16[64,1152]{1,0:T(8,128)(2,1)S(1)}, bf16[64,1152]{1,0:T(8,128)(2,1)S(1)}, u32[]{:S(2)}, u32[]{:S(2)}) %collective-permute-start.18) | collective-permute-done | bytes 147488 | tf_op jit(solution)/shard_map/ppermute | solution.py:315
  46.6 0.7 %collective-permute-start.11 = (bf16[64,1024]{1,0:T(8,128)(2,1)S(1)}, bf16[64,1024]{1,0:T(8,128)(2,1)S(1)}, u32[]{:S(2)}, u32[]{:S(2)}) collective-permute-start(bf16[64,1024]{1,0:T(8,128)(2,1)S(1)} %get-tuple-element.72), channel_id=1, source_target_pairs={{0,2},{1,3},{2,0},{3,1},{4,6},{5,7},{6,4},{7,5},{8,10},{9,11},{10,... | collective-permute-start | bytes 393224 | tf_op jit(solution)/shard_map/ppermute | solution.py:321
  47.3 0.0 collective-permute-done.19.got_b
  47.3 2.6 %collective-permute-start.12 = (bf16[64,1024]{1,0:T(8,128)(2,1)S(1)}, bf16[64,1024]{1,0:T(8,128)(2,1)S(1)}, u32[]{:S(2)}, u32[]{:S(2)}) collective-permute-start(bf16[64,1024]{1,0:T(8,128)(2,1)S(1)} %get-tuple-element.73), channel_id=1, source_target_pairs={{0,3},{1,0},{2,1},{3,2},{4,7},{5,4},{6,5},{7,6},{8,11},{9,8},{10,9... | collective-permute-start | bytes 393224 | tf_op jit(solution)/shard_map/ppermute | solution.py:321
  49.9 0.1 shard_map.120
  50.0 4.2 %collective-permute-done.10.refs_1_ = bf16[64,1024]{1,0:T(8,128)(2,1)S(1)} collective-permute-done((bf16[64,1024]{1,0:T(8,128)(2,1)S(1)}, bf16[64,1024]{1,0:T(8,128)(2,1)S(1)}, u32[]{:S(2)}, u32[]{:S(2)}) %collective-permute-start.10) | collective-permute-done | bytes 131104 | tf_op jit(solution)/shard_map/ppermute | solution.py:321
  54.2 2.6 %collective-permute-start.20 = (bf16[32,1152]{1,0:T(8,128)(2,1)S(1)}, bf16[32,1152]{1,0:T(8,128)(2,1)S(1)}, u32[]{:S(2)}, u32[]{:S(2)}) collective-permute-start(bf16[32,1152]{1,0:T(8,128)(2,1)S(1)} %get-tuple-element.87), channel_id=1, source_target_pairs={{0,1},{1,2},{2,3},{3,0},{4,5},{5,6},{6,7},{7,4},{8,9},{9,10},{10,1... | collective-permute-start | bytes 221192 | tf_op jit(solution)/shard_map/ppermute | solution.py:321
  56.8 3.0 %collective-permute-done.11.refs_2_ = bf16[64,1024]{1,0:T(8,128)(2,1)S(1)} collective-permute-done((bf16[64,1024]{1,0:T(8,128)(2,1)S(1)}, bf16[64,1024]{1,0:T(8,128)(2,1)S(1)}, u32[]{:S(2)}, u32[]{:S(2)}) %collective-permute-start.11) | collective-permute-done | bytes 131104 | tf_op jit(solution)/shard_map/ppermute | solution.py:321
  59.8 0.0 collective-permute-start.21
  59.8 2.9 %collective-permute-start.22 = (bf16[32,1152]{1,0:T(8,128)(2,1)S(1)}, bf16[32,1152]{1,0:T(8,128)(2,1)S(1)}, u32[]{:S(2)}, u32[]{:S(2)}) collective-permute-start(bf16[32,1152]{1,0:T(8,128)(2,1)S(1)} %get-tuple-element.89), channel_id=1, source_target_pairs={{0,3},{1,0},{2,1},{3,2},{4,7},{5,4},{6,5},{7,6},{8,11},{9,8},{10,9... | collective-permute-start | bytes 221192 | tf_op jit(solution)/shard_map/ppermute | solution.py:321
  62.7 0.1 shard_map.116
  62.8 0.2 collective-permute-start.13
  63.0 1.4 %collective-permute-start.14 = (bf16[32,1024]{1,0:T(8,128)(2,1)S(1)}, bf16[32,1024]{1,0:T(8,128)(2,1)S(1)}, u32[]{:S(2)}, u32[]{:S(2)}) collective-permute-start(bf16[32,1024]{1,0:T(8,128)(2,1)S(1)} %get-tuple-element.76), channel_id=1, source_target_pairs={{0,8},{4,12},{8,0},{12,4},{16,24},{20,28},{24,16},{28,20},{1,9},{5... | collective-permute-start | bytes 196616 | tf_op jit(solution)/shard_map/ppermute | solution.py:315
  64.5 0.8 %shard_map.113 = (bf16[6,12,2,1024]{3,2,1,0:T(2,128)(2,1)}, bf16[6,12,2,1024]{3,2,1,0:T(2,128)(2,1)}) custom-call(bf16[2,3,6,2,1024]{4,3,2,1,0:T(2,128)(2,1)S(1)} %get-tuple-element.59.q0, bf16[2,3,6,2,1024]{4,3,2,1,0:T(2,128)(2,1)S(1)} %collective-permute-done.3.q1, bf16[2,3,6,2,1024]{4,3,2,1,0:T(2,128)(2,1)S(1)} %collective-permute-done.4.q2, ...), custom_call_target="tpu_custom_call" | custom-call | tf_op jit(solution)/shard_map/pallas_call | solution.py:44
  65.3 1.8 %collective-permute-done.13.got_a = bf16[32,1024]{1,0:T(8,128)(2,1)S(1)} collective-permute-done((bf16[32,1024]{1,0:T(8,128)(2,1)S(1)}, bf16[32,1024]{1,0:T(8,128)(2,1)S(1)}, u32[]{:S(2)}, u32[]{:S(2)}) %collective-permute-start.13) | collective-permute-done | bytes 65568 | tf_op jit(solution)/shard_map/ppermute | solution.py:315
  67.1 0.2 collective-permute-done.14.got_b
  67.3 0.6 shard_map.117
  67.9 0.3 collective-permute-done.22.refs_3_
  68.2 0.7 %shard_map.121 = (f32[32,1536]{1,0:T(8,128)}, f32[1,32]{1,0:T(1,128)}, f32[1,32]{1,0:T(1,128)}) custom-call(f32[32,512]{1,0:T(8,128)S(1)} %get-tuple-element.77.value_ref, bf16[32,1152]{1,0:T(8,128)(2,1)S(1)} %get-tuple-element.86.refs_0_, bf16[32,1152]{1,0:T(8,128)(2,1)S(1)} %collective-permute-done.20.refs_1_, ...), custom_call_target="tpu_custom_call" | custom-call | tf_op jit(solution)/shard_map/pallas_call | solution.py:44
  (12 shorter events, 0.0 us)
Async XLA Ops:
  1.8 9.8 %collective-permute-start = (bf16[2,3,6,2,1024]{4,3,2,1,0:T(2,128)(2,1)S(1)}, bf16[2,3,6,2,1024]{4,3,2,1,0:T(2,128)(2,1)S(1)}, u32[]{:S(2)}, u32[]{:S(2)}) collective-permute-start(bf16[2,3,6,2,1024]{4,3,2,1,0:T(2,128)(2,1)S(1)} %get-tuple-element.51), channel_id=1, source_target_pairs={{0,3},{1,0},{2,1},{3,2},{4,7},{5,4},{6,5},{7,6},{8,11},{9,8},{10,9... | collective-permute-start | bytes 442376 | tf_op jit(solution)/shard_map/ppermute | solution.py:387
  7.0 4.7 %collective-permute-start.1 = (bf16[2,3,6,2,1024]{4,3,2,1,0:T(2,128)(2,1)S(1)}, bf16[2,3,6,2,1024]{4,3,2,1,0:T(2,128)(2,1)S(1)}, u32[]{:S(2)}, u32[]{:S(2)}) collective-permute-start(bf16[2,3,6,2,1024]{4,3,2,1,0:T(2,128)(2,1)S(1)} %get-tuple-element.52), channel_id=1, source_target_pairs={{0,28},{1,29},{2,30},{3,31},{4,0},{5,1},{6,2},{7,3},{8,4},{9,5},{1... | collective-permute-start | bytes 442376 | tf_op jit(solution)/shard_map/ppermute | solution.py:387
  8.6 5.2 %collective-permute-start.2 = (bf16[2,3,6,2,1024]{4,3,2,1,0:T(2,128)(2,1)S(1)}, bf16[2,3,6,2,1024]{4,3,2,1,0:T(2,128)(2,1)S(1)}, u32[]{:S(2)}, u32[]{:S(2)}) collective-permute-start(bf16[2,3,6,2,1024]{4,3,2,1,0:T(2,128)(2,1)S(1)} %get-tuple-element.53), channel_id=1, source_target_pairs={{0,31},{1,28},{2,29},{3,30},{4,3},{5,0},{6,1},{7,2},{8,7},{9,4},{1... | collective-permute-start | bytes 442376 | tf_op jit(solution)/shard_map/ppermute | solution.py:387
  20.2 4.4 %collective-permute-start.7 = (bf16[144,2048]{1,0:T(8,128)(2,1)S(1)}, bf16[144,2048]{1,0:T(8,128)(2,1)S(1)}, u32[]{:S(2)}, u32[]{:S(2)}) collective-permute-start(bf16[144,2048]{1,0:T(8,128)(2,1)S(1)} %get-tuple-element.58.factor_ref.factor), channel_id=1, source_target_pairs={{0,4},{4,0},{8,12},{12,8},{16,20},{20,16},{24,28},{28,24},{1,5},{5... | collective-permute-start | bytes 1769480 | tf_op jit(solution)/shard_map/ppermute | solution.py:315
  20.4 4.2 %collective-permute-start.6 = (bf16[1024,144]{1,0:T(8,128)(2,1)S(1)}, bf16[1024,144]{1,0:T(8,128)(2,1)S(1)}, u32[]{:S(2)}, u32[]{:S(2)}) collective-permute-start(bf16[1024,144]{1,0:T(8,128)(2,1)S(1)} %get-tuple-element.66), channel_id=1, source_target_pairs={{0,4},{4,0},{8,12},{12,8},{16,20},{20,16},{24,28},{28,24},{1,5},{5... | collective-permute-start | bytes 884744 | tf_op jit(solution)/shard_map/ppermute | solution.py:315
  23.0 1.6 %collective-permute-start.15 = (f32[512,128]{1,0:T(8,128)S(1)}, f32[512,128]{1,0:T(8,128)S(1)}, u32[]{:S(2)}, u32[]{:S(2)}) collective-permute-start(f32[512,128]{1,0:T(8,128)S(1)} %get-tuple-element.79), channel_id=1, source_target_pairs={{0,4},{4,0},{8,12},{12,8},{16,20},{20,16},{24,28},{28,24},{1,5},{5... | collective-permute-start | bytes 786440 | tf_op jit(solution)/shard_map/ppermute | solution.py:315
  25.3 9.9 %collective-permute-start.16 = (bf16[128,1152]{1,0:T(8,128)(2,1)S(1)}, bf16[128,1152]{1,0:T(8,128)(2,1)S(1)}, u32[]{:S(2)}, u32[]{:S(2)}) collective-permute-start(bf16[128,1152]{1,0:T(8,128)(2,1)S(1)} %get-tuple-element.81), channel_id=1, source_target_pairs={{0,8},{4,12},{8,0},{12,4},{16,24},{20,28},{24,16},{28,20},{1,9},{5... | collective-permute-start | bytes 884744 | tf_op jit(solution)/shard_map/ppermute | solution.py:315
  27.2 9.9 %collective-permute-start.17 = (bf16[128,1152]{1,0:T(8,128)(2,1)S(1)}, bf16[128,1152]{1,0:T(8,128)(2,1)S(1)}, u32[]{:S(2)}, u32[]{:S(2)}) collective-permute-start(bf16[128,1152]{1,0:T(8,128)(2,1)S(1)} %get-tuple-element.82), channel_id=1, source_target_pairs={{0,16},{4,20},{8,24},{12,28},{16,0},{20,4},{24,8},{28,12},{1,17},{... | collective-permute-start | bytes 884744 | tf_op jit(solution)/shard_map/ppermute | solution.py:315
  29.4 11.5 %collective-permute-start.8 = (bf16[128,1024]{1,0:T(8,128)(2,1)S(1)}, bf16[128,1024]{1,0:T(8,128)(2,1)S(1)}, u32[]{:S(2)}, u32[]{:S(2)}) collective-permute-start(bf16[128,1024]{1,0:T(8,128)(2,1)S(1)} %get-tuple-element.68), channel_id=1, source_target_pairs={{0,8},{4,12},{8,0},{12,4},{16,24},{20,28},{24,16},{28,20},{1,9},{5... | collective-permute-start | bytes 786440 | tf_op jit(solution)/shard_map/ppermute | solution.py:315
  29.6 13.1 %collective-permute-start.9 = (bf16[128,1024]{1,0:T(8,128)(2,1)S(1)}, bf16[128,1024]{1,0:T(8,128)(2,1)S(1)}, u32[]{:S(2)}, u32[]{:S(2)}) collective-permute-start(bf16[128,1024]{1,0:T(8,128)(2,1)S(1)} %get-tuple-element.69), channel_id=1, source_target_pairs={{0,16},{4,20},{8,24},{12,28},{16,0},{20,4},{24,8},{28,12},{1,17},{... | collective-permute-start | bytes 786440 | tf_op jit(solution)/shard_map/ppermute | solution.py:315
  30.2 12.6 %collective-permute-start.3 = (bf16[2,3,6,2,1024]{4,3,2,1,0:T(2,128)(2,1)S(1)}, bf16[2,3,6,2,1024]{4,3,2,1,0:T(2,128)(2,1)S(1)}, u32[]{:S(2)}, u32[]{:S(2)}) collective-permute-start(bf16[2,3,6,2,1024]{4,3,2,1,0:T(2,128)(2,1)S(1)} %get-tuple-element.60), channel_id=1, source_target_pairs={{0,1},{1,2},{2,3},{3,0},{4,5},{5,6},{6,7},{7,4},{8,9},{9,10},{10,1... | collective-permute-start | bytes 442376 | tf_op jit(solution)/shard_map/ppermute | solution.py:456
  37.2 9.3 %collective-permute-start.18 = (bf16[64,1152]{1,0:T(8,128)(2,1)S(1)}, bf16[64,1152]{1,0:T(8,128)(2,1)S(1)}, u32[]{:S(2)}, u32[]{:S(2)}) collective-permute-start(bf16[64,1152]{1,0:T(8,128)(2,1)S(1)} %get-tuple-element.84), channel_id=1, source_target_pairs={{0,16},{4,20},{8,24},{12,28},{16,0},{20,4},{24,8},{28,12},{1,17},{... | collective-permute-start | bytes 442376 | tf_op jit(solution)/shard_map/ppermute | solution.py:315
  38.8 8.5 %collective-permute-start.19 = (bf16[64,1152]{1,0:T(8,128)(2,1)S(1)}, bf16[64,1152]{1,0:T(8,128)(2,1)S(1)}, u32[]{:S(2)}, u32[]{:S(2)}) collective-permute-start(bf16[64,1152]{1,0:T(8,128)(2,1)S(1)} %get-tuple-element.85), channel_id=1, source_target_pairs={{0,8},{4,12},{8,0},{12,4},{16,24},{20,28},{24,16},{28,20},{1,9},{5... | collective-permute-start | bytes 442376 | tf_op jit(solution)/shard_map/ppermute | solution.py:315
  40.9 21.9 %collective-permute-start.4 = (bf16[2,3,6,2,1024]{4,3,2,1,0:T(2,128)(2,1)S(1)}, bf16[2,3,6,2,1024]{4,3,2,1,0:T(2,128)(2,1)S(1)}, u32[]{:S(2)}, u32[]{:S(2)}) collective-permute-start(bf16[2,3,6,2,1024]{4,3,2,1,0:T(2,128)(2,1)S(1)} %get-tuple-element.61), channel_id=1, source_target_pairs={{0,4},{1,5},{2,6},{3,7},{4,8},{5,9},{6,10},{7,11},{8,12},{9,13},{1... | collective-permute-start | bytes 442376 | tf_op jit(solution)/shard_map/ppermute | solution.py:456
  42.7 20.3 %collective-permute-start.5 = (bf16[2,3,6,2,1024]{4,3,2,1,0:T(2,128)(2,1)S(1)}, bf16[2,3,6,2,1024]{4,3,2,1,0:T(2,128)(2,1)S(1)}, u32[]{:S(2)}, u32[]{:S(2)}) collective-permute-start(bf16[2,3,6,2,1024]{4,3,2,1,0:T(2,128)(2,1)S(1)} %get-tuple-element.62), channel_id=1, source_target_pairs={{0,5},{1,6},{2,7},{3,4},{4,9},{5,10},{6,11},{7,8},{8,13},{9,14},{1... | collective-permute-start | bytes 442376 | tf_op jit(solution)/shard_map/ppermute | solution.py:456
  42.8 11.3 %collective-permute-start.10 = (bf16[64,1024]{1,0:T(8,128)(2,1)S(1)}, bf16[64,1024]{1,0:T(8,128)(2,1)S(1)}, u32[]{:S(2)}, u32[]{:S(2)}) collective-permute-start(bf16[64,1024]{1,0:T(8,128)(2,1)S(1)} %get-tuple-element.71), channel_id=1, source_target_pairs={{0,1},{1,2},{2,3},{3,0},{4,5},{5,6},{6,7},{7,4},{8,9},{9,10},{10,1... | collective-permute-start | bytes 393224 | tf_op jit(solution)/shard_map/ppermute | solution.py:321
  46.6 13.2 %collective-permute-start.11 = (bf16[64,1024]{1,0:T(8,128)(2,1)S(1)}, bf16[64,1024]{1,0:T(8,128)(2,1)S(1)}, u32[]{:S(2)}, u32[]{:S(2)}) collective-permute-start(bf16[64,1024]{1,0:T(8,128)(2,1)S(1)} %get-tuple-element.72), channel_id=1, source_target_pairs={{0,2},{1,3},{2,0},{3,1},{4,6},{5,7},{6,4},{7,5},{8,10},{9,11},{10,... | collective-permute-start | bytes 393224 | tf_op jit(solution)/shard_map/ppermute | solution.py:321
  47.3 12.5 %collective-permute-start.12 = (bf16[64,1024]{1,0:T(8,128)(2,1)S(1)}, bf16[64,1024]{1,0:T(8,128)(2,1)S(1)}, u32[]{:S(2)}, u32[]{:S(2)}) collective-permute-start(bf16[64,1024]{1,0:T(8,128)(2,1)S(1)} %get-tuple-element.73), channel_id=1, source_target_pairs={{0,3},{1,0},{2,1},{3,2},{4,7},{5,4},{6,5},{7,6},{8,11},{9,8},{10,9... | collective-permute-start | bytes 393224 | tf_op jit(solution)/shard_map/ppermute | solution.py:321
  54.2 13.8 %collective-permute-start.20 = (bf16[32,1152]{1,0:T(8,128)(2,1)S(1)}, bf16[32,1152]{1,0:T(8,128)(2,1)S(1)}, u32[]{:S(2)}, u32[]{:S(2)}) collective-permute-start(bf16[32,1152]{1,0:T(8,128)(2,1)S(1)} %get-tuple-element.87), channel_id=1, source_target_pairs={{0,1},{1,2},{2,3},{3,0},{4,5},{5,6},{6,7},{7,4},{8,9},{9,10},{10,1... | collective-permute-start | bytes 221192 | tf_op jit(solution)/shard_map/ppermute | solution.py:321
  59.8 8.1 %collective-permute-start.21 = (bf16[32,1152]{1,0:T(8,128)(2,1)S(1)}, bf16[32,1152]{1,0:T(8,128)(2,1)S(1)}, u32[]{:S(2)}, u32[]{:S(2)}) collective-permute-start(bf16[32,1152]{1,0:T(8,128)(2,1)S(1)} %get-tuple-element.88), channel_id=1, source_target_pairs={{0,2},{1,3},{2,0},{3,1},{4,6},{5,7},{6,4},{7,5},{8,10},{9,11},{10,... | collective-permute-start | bytes 221192 | tf_op jit(solution)/shard_map/ppermute | solution.py:321
  59.8 8.5 %collective-permute-start.22 = (bf16[32,1152]{1,0:T(8,128)(2,1)S(1)}, bf16[32,1152]{1,0:T(8,128)(2,1)S(1)}, u32[]{:S(2)}, u32[]{:S(2)}) collective-permute-start(bf16[32,1152]{1,0:T(8,128)(2,1)S(1)} %get-tuple-element.89), channel_id=1, source_target_pairs={{0,3},{1,0},{2,1},{3,2},{4,7},{5,4},{6,5},{7,6},{8,11},{9,8},{10,9... | collective-permute-start | bytes 221192 | tf_op jit(solution)/shard_map/ppermute | solution.py:321
  62.8 4.3 %collective-permute-start.13 = (bf16[32,1024]{1,0:T(8,128)(2,1)S(1)}, bf16[32,1024]{1,0:T(8,128)(2,1)S(1)}, u32[]{:S(2)}, u32[]{:S(2)}) collective-permute-start(bf16[32,1024]{1,0:T(8,128)(2,1)S(1)} %get-tuple-element.75), channel_id=1, source_target_pairs={{0,16},{4,20},{8,24},{12,28},{16,0},{20,4},{24,8},{28,12},{1,17},{... | collective-permute-start | bytes 196616 | tf_op jit(solution)/shard_map/ppermute | solution.py:315
  63.0 4.3 %collective-permute-start.14 = (bf16[32,1024]{1,0:T(8,128)(2,1)S(1)}, bf16[32,1024]{1,0:T(8,128)(2,1)S(1)}, u32[]{:S(2)}, u32[]{:S(2)}) collective-permute-start(bf16[32,1024]{1,0:T(8,128)(2,1)S(1)} %get-tuple-element.76), channel_id=1, source_target_pairs={{0,8},{4,12},{8,0},{12,4},{16,24},{20,28},{24,16},{28,20},{1,9},{5... | collective-permute-start | bytes 196616 | tf_op jit(solution)/shard_map/ppermute | solution.py:315

commit v5 on v4

--- a/solution.py
+++ b/solution.py
@@ -124,24 +124,27 @@
         target[at : at + group, :] = source[pl.ds(start, group), :]
 
 
-def attention_body(
+def pair_tools(total):
+    lane = lax.broadcasted_iota(jnp.int32, (total, LANES), 1)
+    first = lane < HDIM
+
+    def alone(value, head):
+        return jnp.where(first if head == 0 else ~first, value, jnp.zeros_like(value))
+
+    def pick(results):
+        return jnp.where(first, results[0], results[1])
+
+    return alone, pick
+
+
+def forward_body(
     plan, places_ref, r0, r1, r2, r3, w_qkv_ref, w_out_ref, gain_ref, bias_ref,
-    mine_ref, peer_ref, factor_ref, wide, side,
+    mine_ref, peer_ref, factor_ref, query_ref, pair_ref, probs_ref, wide, side, bias_of,
 ):
     quads = (r0, r1, r2, r3)
     inner, width = w_out_ref.shape
-    heads = inner // HDIM
-    scale = HDIM ** (-0.5)
     grad = gather_window(quads, 1, wide).astype(BF16)
     total = grad.shape[0]
-    side[...] = grad.T
-    reorder(plan, places_ref, side, (mine_ref, peer_ref), width // 2)
-    standard, _ = normalize(gather_window(quads, 0, wide))
-    normed = (standard * gain_ref[...] + bias_ref[...]).astype(BF16)
-    side[...] = normed.T
-    reorder(plan, places_ref, side, (mine_ref, peer_ref))
-    projected = dot(normed, w_qkv_ref[...], ((1,), (0,))).astype(BF16)
-    grad_att = dot(grad, w_out_ref[...], ((1,), (1,))).astype(BF16)
     count = total // 4
     row_id = lax.broadcasted_iota(jnp.int32, (total, total), 0) // count
     col_id = lax.broadcasted_iota(jnp.int32, (total, total), 1) // count
@@ -149,35 +152,63 @@
     apart = jnp.where((row_id >= 2) != (col_id >= 2), last_lat, 0) + jnp.where(
         (row_id % 2) != (col_id % 2), last_lon, 0
     )
-    blocked = apart > 0
-    for head in range(heads):
-        at = head * HDIM
-        query = projected[:, at : at + HDIM]
-        key = projected[:, inner + at : inner + at + HDIM]
-        value = projected[:, 2 * inner + at : 2 * inner + at + HDIM]
-        grad_head = grad_att[:, at : at + HDIM]
-        scores = dot(query, key, ((1,), (1,))) * scale
-        scores = jnp.where(blocked, -1e30, scores)
-        exps = jnp.exp(scores - jnp.max(scores, axis=-1, keepdims=True))
-        probs = exps / jnp.sum(exps, axis=-1, keepdims=True)
-        low = probs.astype(BF16)
-        factor_ref[:, at : at + HDIM] = dot(low, value, ((1,), (0,))).astype(BF16)
-        grad_prob = dot(grad_head, value, ((1,), (1,)))
-        inner_sum = jnp.sum(probs * grad_prob, axis=-1, keepdims=True)
-        grad_score = (probs * (grad_prob - inner_sum)).astype(BF16)
-        factor_ref[:, inner + at : inner + at + HDIM] = dot(low, grad_head, ((0,), (0,))).astype(
-            BF16
-        )
-        factor_ref[:, 2 * inner + at : 2 * inner + at + HDIM] = (
-            dot(grad_score, key, ((1,), (0,))) * scale
+    bias_of[...] = jnp.where(apart > 0, -1e30, 0.0)
+    side[...] = grad.T
+    reorder(plan, places_ref, side, (mine_ref, peer_ref), width // 2)
+    pair_ref[:, 2 * inner :] = dot(grad, w_out_ref[...], ((1,), (1,))).astype(BF16)
+    standard, _ = normalize(gather_window(quads, 0, wide))
+    normed = (standard * gain_ref[...] + bias_ref[...]).astype(BF16)
+    side[...] = normed.T
+    reorder(plan, places_ref, side, (mine_ref, peer_ref))
+    scale = jnp.asarray(HDIM ** (-0.5), BF16)
+    query_ref[...] = dot(normed, w_qkv_ref[:, :inner], ((1,), (0,))).astype(BF16) * scale
+    pair_ref[:, : 2 * inner] = dot(normed, w_qkv_ref[:, inner:], ((1,), (0,))).astype(BF16)
+    alone, pick = pair_tools(total)
+    for pair in range(inner // LANES):
+        cols = slice(pair * LANES, (pair + 1) * LANES)
+        query = query_ref[:, cols]
+        key = pair_ref[:, cols]
+        value = pair_ref[:, inner + pair * LANES : inner + (pair + 1) * LANES]
+        grad_pair = pair_ref[:, 2 * inner + pair * LANES : 2 * inner + (pair + 1) * LANES]
+        lows = []
+        for head in range(2):
+            scores = dot(alone(query, head), key, ((1,), (1,))) + bias_of[...]
+            exps = jnp.exp(scores - jnp.max(scores, axis=-1, keepdims=True))
+            probs = exps / jnp.sum(exps, axis=-1, keepdims=True)
+            probs_ref[2 * pair + head] = probs
+            lows.append(probs.astype(BF16))
+        factor_ref[:, cols] = pick([dot(low, value, ((1,), (0,))) for low in lows]).astype(BF16)
+        factor_ref[:, inner + pair * LANES : inner + (pair + 1) * LANES] = pick(
+            [dot(low, grad_pair, ((0,), (0,))) for low in lows]
         ).astype(BF16)
-        factor_ref[:, 3 * inner + at : 3 * inner + at + HDIM] = (
-            dot(grad_score, query, ((0,), (0,))) * scale
+
+
+def backward_body(query_ref, pair_ref, probs_ref, factor_ref):
+    inner = query_ref.shape[1]
+    scale = HDIM ** (-0.5)
+    alone, pick = pair_tools(query_ref.shape[0])
+    for pair in range(inner // LANES):
+        cols = slice(pair * LANES, (pair + 1) * LANES)
+        query = query_ref[:, cols]
+        key = pair_ref[:, cols]
+        value = pair_ref[:, inner + pair * LANES : inner + (pair + 1) * LANES]
+        grad_pair = pair_ref[:, 2 * inner + pair * LANES : 2 * inner + (pair + 1) * LANES]
+        lows = []
+        for head in range(2):
+            probs = probs_ref[2 * pair + head]
+            grad_prob = dot(alone(grad_pair, head), value, ((1,), (1,)))
+            inner_sum = jnp.sum(probs * grad_prob, axis=-1, keepdims=True)
+            lows.append((probs * (grad_prob - inner_sum)).astype(BF16))
+        factor_ref[:, cols] = (
+            pick([dot(low, key, ((1,), (0,))) for low in lows]) * scale
         ).astype(BF16)
+        factor_ref[:, inner + pair * LANES : inner + (pair + 1) * LANES] = pick(
+            [dot(low, query, ((0,), (0,))) for low in lows]
+        ).astype(BF16)
 
 
 def gradient_body(
-    plan, places_ref, r0, r1, r2, r3, factor_ref, w_qkv_ref, w_out_ref, gain_ref,
+    plan, places_ref, r0, r1, r2, r3, factor_ref, late_ref, w_qkv_ref, w_out_ref, gain_ref,
     o0, o1, o2, o3, mine_ref, peer_ref, wide, flat,
 ):
     quads = (r0, r1, r2, r3)
@@ -187,8 +218,8 @@
     count = quad[0] * quad[1] * quad[2]
     tokens_wide = gather_window(quads, 0, wide)
     standard, inverse = normalize(tokens_wide)
-    grad_normed = dot(factor_ref[:, inner : 2 * inner], w_qkv_ref[:, 2 * inner :], ((1,), (1,)))
-    grad_normed += dot(factor_ref[:, 2 * inner :], w_qkv_ref[:, : 2 * inner], ((1,), (1,)))
+    grad_normed = dot(factor_ref[:, inner:], w_qkv_ref[:, 2 * inner :], ((1,), (1,)))
+    grad_normed += dot(late_ref[...], w_qkv_ref[:, : 2 * inner], ((1,), (1,)))
     sums = [
         jnp.sum(grad_normed * standard, axis=0, keepdims=True),
         jnp.sum(grad_normed, axis=0, keepdims=True),
@@ -219,7 +250,7 @@
 
 def early_body(mine, got, factor, factor_got, *outs):
     half = mine.shape[0] // 2
-    inner = factor.shape[1] // 4
+    inner = factor.shape[1] // 2
     for part in range(2):
         rows = slice((1 - part) * half, (2 - part) * half)
         cols = slice(part * inner, (part + 1) * inner)
@@ -230,12 +261,12 @@
 
 def late_body(mine, got, factor, factor_got, sums, sums_got, *outs):
     half = mine.shape[0] // 2
-    inner = factor.shape[1] // 4
+    inner = factor.shape[1] // 2
     for part in range(2):
-        cols = slice((2 + part) * inner, (3 + part) * inner)
+        cols = slice(part * inner, (part + 1) * inner)
         value = dot(mine[:half, :], factor[:, cols], ((1,), (0,)))
         value += dot(got[:half, :], factor_got[:, cols], ((1,), (0,)))
-        split_store(value, outs, slice(part * inner, (part + 1) * inner))
+        split_store(value, outs, cols)
     split_store(sums[...] + sums_got[...], outs, slice(2 * inner, 2 * inner + LANES))
 
 
@@ -375,6 +406,15 @@
         return pairs
 
     steps = ((0, 1), (1, 0), (1, 1))
+    by_turn = (0, 2, 1)
+
+    def moved_all(items, sign):
+        moves = {}
+        for place in by_turn:
+            a, b = steps[place]
+            moves[place] = lax.ppermute(items[place], ("lat", "lon"), moved(sign * a, sign * b))
+        return [moves[place] for place in range(3)]
+
     grid = (lat_rows, lon_cols, levels, width)
     quad = (2, lat_rows // 2, lon_cols // 2, levels, width)
     tok = tokens.transpose(1, 2, 0, 3)
@@ -383,9 +423,7 @@
         pack_body, [(quad, BF16)] * 4, (tok, cot), far=2,
         scratch=[pltpu.SemaphoreType.DMA((8,))],
     )
-    quads = [own] + [
-        lax.ppermute(item, ("lat", "lon"), moved(-a, -b)) for item, (a, b) in zip(sends, steps)
-    ]
+    quads = [own, *moved_all(sends, -1)]
     params = (w_qkv, w_out, layer_norm_gain.reshape(1, width), layer_norm_bias.reshape(1, width))
     params = call(
         fetch_body, [(item.shape, item.dtype) for item in params], params, far=4,
@@ -404,22 +442,31 @@
             order.append((core + 2 * x_bit + 4 * y_bit, side * half_lon + k))
     plan = (share if hyper else 16, (lat_count, lon_count), tuple(order))
     places = jnp.where(jnp.arange(2) == 0, lat_place, lon_place).astype(jnp.int32)
-    mine, peer, factor = call(
-        functools.partial(attention_body, plan),
-        [((width, cells), BF16)] * 2 + [((cells, 4 * inner), BF16)],
+    heads = inner // HDIM
+    mine, peer, factor, query, pairs, probs = call(
+        functools.partial(forward_body, plan),
+        [((width, cells), BF16)] * 2
+        + [((cells, n * inner), BF16) for n in (2, 1, 3)]
+        + [((heads, cells, cells), F32)],
         (places, *quads, *params),
-        scratch=[pltpu.VMEM((cells, width), F32), pltpu.VMEM((width, cells), BF16)],
+        scratch=[
+            pltpu.VMEM((cells, width), F32),
+            pltpu.VMEM((width, cells), BF16),
+            pltpu.VMEM((cells, cells), F32),
+        ],
         smem=1,
     )
+    (factor_late,) = call(backward_body, [((cells, 2 * inner), BF16)], (query, pairs, probs))
     q0, q1, q2, q3, sums, sums_peer = call(
         functools.partial(gradient_body, plan),
         [(quad, BF16)] * 4 + [((width // 2, LANES), F32)] * 2,
-        (places, *quads, factor, *params[:3]),
+        (places, *quads, factor, factor_late, *params[:3]),
         scratch=[pltpu.VMEM((cells, width), F32), pltpu.VMEM((width, LANES), F32)],
         smem=1,
     )
     if hyper:
         factor_got = swap(factor, 1)
+        late_got = swap(factor_late, 1)
         got = swap(peer, 1)
         sums_got = swap(sums_peer, 1)
         quarter = width // 8
@@ -430,7 +477,7 @@
         early = call(early_body, shapes(2 * inner), (mine, got, factor, factor_got))
         late = call(
             late_body, shapes(2 * inner + LANES),
-            (mine, got, factor, factor_got, sums, sums_got),
+            (mine, got, factor_late, late_got, sums, sums_got),
         )
         value, d_out = sum_early(*early, lon_count, norm_factor)
         d_qkv, gain, bias = sum_late(*late, value, lon_count, norm_factor)
@@ -442,6 +489,7 @@
             [
                 dot(cot_t, factor[:, :inner], ((1,), (0,))),
                 dot(normed_t, factor[:, inner:], ((1,), (0,))),
+                dot(normed_t, factor_late, ((1,), (0,))),
                 jnp.concatenate([sums, sums_peer], axis=0),
             ],
             axis=1,
@@ -452,10 +500,7 @@
         d_out = whole[:, :inner]
         d_qkv = jnp.concatenate([whole[:, 2 * inner : 4 * inner], whole[:, inner : 2 * inner]], axis=1)
         gain, bias = whole[:, 4 * inner], whole[:, 4 * inner + 1]
-    back = [q0] + [
-        lax.ppermute(item, ("lat", "lon"), moved(a, b))
-        for item, (a, b) in zip((q1, q2, q3), steps)
-    ]
+    back = [q0, *moved_all((q1, q2, q3), 1)]
     y_out, token_gradient = call(unpack_body, [(grid, BF16)] * 2, back, near_out=0)
     return (
         y_out.transpose(2, 0, 1, 3),

time: 70.1 us -> 69 us (0.984)
  Pallas kernels: 16.1 us -> 15 us
    pallas_call x13 -> x14, Pallas kernels: 16.1 us -> 15 us  [call(): pl.pallas_call(body, out_shape=[pltpu.VMEM(s, d) if i < near_out else jax...]
    ppermute x11 -> x12, starting transfers between devices: 8.29 us -> 8.69 us  [swap(): return lax.ppermute(value, 'lat', xor_pairs(bit))]
    ppermute x11 -> x12, waiting for transfers between devices: 15.9 us -> 15.6 us  [swap(): return lax.ppermute(value, 'lat', xor_pairs(bit))]
  transfers between devices with their start and end apart: 23 -> 24, of which waited for: 12 -> 12; matrix products, arithmetic and copies ran while one was open for 0% -> 0% of each run, Pallas kernels for 10% -> 11%
where the time goes in v5:
time: 69 us; the launch traced here: 67.8 us
  starting transfers between devices  26.9 us (39%)
  waiting for transfers between devices  25.2 us (37%)
  Pallas kernels  15 us (22%)
  between operations  0.75 us (1%)
    ppermute x12, waiting for transfers between devices, swap(): return lax.ppermute(value, 'lat', xor_pairs(bit))  15.6 us
    pallas_call x14, Pallas kernels, call(): pl.pallas_call(body, out_shape=[pltpu.VMEM(s, d) if i < near_out else jax...  15 us
    ppermute x6, starting transfers between devices, turn(): lax.ppermute(pieces[k], 'lon', [(i, (i + k) % count) for i in range(count)])  10.1 us
    ppermute x12, starting transfers between devices, swap(): return lax.ppermute(value, 'lat', xor_pairs(bit))  8.69 us
    ppermute x6, starting transfers between devices, moved_all(): lax.ppermute(items[place], ('lat', 'lon'), moved(sign * a, sign * b))  8.11 us
    ppermute x6, waiting for transfers between devices, turn(): lax.ppermute(pieces[k], 'lon', [(i, (i + k) % count) for i in range(count)])  7.57 us
    ppermute x6, waiting for transfers between devices, moved_all(): lax.ppermute(items[place], ('lat', 'lon'), moved(sign * a, sign * b))  2.1 us
  transfers between devices with their start and end apart: 24, of which 12 were waited for; matrix products, arithmetic and copies ran while one was open for 0% of the time, Pallas kernels for 11%

profile of v5, /device:TPU:0, one launch (start us, length us, event | category | flops | bytes accessed | tf_op | source)
XLA Modules:
  0.0 67.8 jit_solution(10203376756398265413)
XLA Ops:
  0.6 1.2 %shard_map.109 = (bf16[2,3,6,2,1024]{4,3,2,1,0:T(2,128)(2,1)S(1)}, bf16[2,3,6,2,1024]{4,3,2,1,0:T(2,128)(2,1)S(1)}, bf16[2,3,6,2,1024]{4,3,2,1,0:T(2,128)(2,1)S(1)}, bf16[2,3,6,2,1024]{4,3,2,1,0:T(2,128)(2,1)S(1)}) custom-call(bf16[6,12,2,1024]{3,2,1,0:T(2,128)(2,1)} %bitcast.9, bf16[6,12,2,1024]{3,2,1,0:T(2,128)(2,1)} %bitcast.10), custom_call_target="tpu_custom_call" | custom-call | tf_op jit(solution)/shard_map/pallas_call | solution.py:44
  1.8 5.1 %collective-permute-start = (bf16[2,3,6,2,1024]{4,3,2,1,0:T(2,128)(2,1)S(1)}, bf16[2,3,6,2,1024]{4,3,2,1,0:T(2,128)(2,1)S(1)}, u32[]{:S(2)}, u32[]{:S(2)}) collective-permute-start(bf16[2,3,6,2,1024]{4,3,2,1,0:T(2,128)(2,1)S(1)} %get-tuple-element.54), channel_id=1, source_target_pairs={{0,3},{1,0},{2,1},{3,2},{4,7},{5,4},{6,5},{7,6},{8,11},{9,8},{10,9... | collective-permute-start | bytes 442376 | tf_op jit(solution)/shard_map/ppermute | solution.py:415
  7.0 1.6 %collective-permute-start.1 = (bf16[2,3,6,2,1024]{4,3,2,1,0:T(2,128)(2,1)S(1)}, bf16[2,3,6,2,1024]{4,3,2,1,0:T(2,128)(2,1)S(1)}, u32[]{:S(2)}, u32[]{:S(2)}) collective-permute-start(bf16[2,3,6,2,1024]{4,3,2,1,0:T(2,128)(2,1)S(1)} %get-tuple-element.55), channel_id=1, source_target_pairs={{0,28},{1,29},{2,30},{3,31},{4,0},{5,1},{6,2},{7,3},{8,4},{9,5},{1... | collective-permute-start | bytes 442376 | tf_op jit(solution)/shard_map/ppermute | solution.py:415
  8.6 0.8 %collective-permute-start.2 = (bf16[2,3,6,2,1024]{4,3,2,1,0:T(2,128)(2,1)S(1)}, bf16[2,3,6,2,1024]{4,3,2,1,0:T(2,128)(2,1)S(1)}, u32[]{:S(2)}, u32[]{:S(2)}) collective-permute-start(bf16[2,3,6,2,1024]{4,3,2,1,0:T(2,128)(2,1)S(1)} %get-tuple-element.56), channel_id=1, source_target_pairs={{0,31},{1,28},{2,29},{3,30},{4,3},{5,0},{6,1},{7,2},{8,7},{9,4},{1... | collective-permute-start | bytes 442376 | tf_op jit(solution)/shard_map/ppermute | solution.py:415
  9.4 2.2 %shard_map.110 = (bf16[1024,1536]{1,0:T(8,128)(2,1)S(1)}, bf16[512,1024]{1,0:T(8,128)(2,1)S(1)}, f32[1,1024]{1,0:T(1,128)S(1)}, f32[1,1024]{1,0:T(1,128)S(1)}) custom-call(bf16[1024,1536]{1,0:T(8,128)(2,1)} %refs_0_.1, bf16[512,1024]{1,0:T(8,128)(2,1)} %refs_1_.1, f32[1,1024]{1,0:T(1,128)} %bitcast.11, f32[1,1024]{1,0:T(1,128)} %bitcast.12), custom_call_target="tpu_custom_call" | custom-call | tf_op jit(solution)/shard_map/pallas_call | solution.py:44
  11.7 0.0 collective-permute-done.1.r2
  11.7 2.1 %collective-permute-done.2.r3 = bf16[2,3,6,2,1024]{4,3,2,1,0:T(2,128)(2,1)S(1)} collective-permute-done((bf16[2,3,6,2,1024]{4,3,2,1,0:T(2,128)(2,1)S(1)}, bf16[2,3,6,2,1024]{4,3,2,1,0:T(2,128)(2,1)S(1)}, u32[]{:S(2)}, u32[]{:S(2)}) %collective-permute-start.2) | collective-permute-done | bytes 147488 | tf_op jit(solution)/shard_map/ppermute | solution.py:415
  13.8 3.6 %shard_map.111 = (bf16[1024,144]{1,0:T(8,128)(2,1)S(1)}, bf16[1024,144]{1,0:T(8,128)(2,1)S(1)}, bf16[144,1024]{1,0:T(8,128)(2,1)S(1)}, bf16[144,512]{1,0:T(8,128...) custom-call(s32[2]{0:T(128)S(1)} %compare_select_fusion.places_ref, ...), custom_call_target="tpu_custom_call" | custom-call | tf_op jit(solution)/shard_map/pallas_call | solution.py:44
  17.4 1.7 %shard_map.112.late_ref.factor = bf16[144,1024]{1,0:T(8,128)(2,1)S(1)} custom-call(bf16[144,512]{1,0:T(8,128)(2,1)S(1)} %get-tuple-element.62.query_ref, bf16[144,1536]{1,0:T(8,128)(2,1)S(1)} %get-tuple-element.63.pair_ref, f32[8,144,144]{2,1,0:T(8,128)S(1)} %get-tuple-element.64.probs_ref), custom_call_target="tpu_custom_call" | custom-call | tf_op jit(solution)/shard_map/pallas_call | solution.py:44
  19.1 0.2 collective-permute-start.15
  19.3 0.4 collective-permute-start.6
  19.6 2.2 %shard_map.113 = (bf16[2,3,6,2,1024]{4,3,2,1,0:T(2,128)(2,1)S(1)}, bf16[2,3,6,2,1024]{4,3,2,1,0:T(2,128)(2,1)S(1)}, bf16[2,3,6,2,1024]{4,3,2,1,0:T(2,128)(2,1)S(...) custom-call(s32[2]{0:T(128)S(1)} %compare_select_fusion.places_ref, ...), custom_call_target="tpu_custom_call" | custom-call | tf_op jit(solution)/shard_map/pallas_call | solution.py:44
  21.9 0.2 collective-permute-start.16
  22.1 0.4 collective-permute-start.7
  22.5 1.0 %collective-permute-done.16.sums_got = f32[512,128]{1,0:T(8,128)S(1)} collective-permute-done((f32[512,128]{1,0:T(8,128)S(1)}, f32[512,128]{1,0:T(8,128)S(1)}, u32[]{:S(2)}, u32[]{:S(2)}) %collective-permute-start.16) | collective-permute-done | bytes 262176 | tf_op jit(solution)/shard_map/ppermute | solution.py:346
  23.5 0.7 %shard_map.119 = (bf16[256,1152]{1,0:T(8,128)(2,1)S(1)}, bf16[128,1152]{1,0:T(8,128)(2,1)S(1)}, bf16[128,1152]{1,0:T(8,128)(2,1)S(1)}) custom-call(bf16[1024,144]{1,0:T(8,128)(2,1)S(1)} %get-tuple-element.71.mine, bf16[1024,144]{1,0:T(8,128)(2,1)S(1)} %collective-permute-done.6.got, bf16[144,1024]{1,0:T(8,128)(2,1)S(1)} %shard_map.112.late_ref.factor, ...), custom_call_target="tpu_custom_call" | custom-call | tf_op jit(solution)/shard_map/pallas_call | solution.py:44
  24.2 1.9 %collective-permute-start.17 = (bf16[128,1152]{1,0:T(8,128)(2,1)S(1)}, bf16[128,1152]{1,0:T(8,128)(2,1)S(1)}, u32[]{:S(2)}, u32[]{:S(2)}) collective-permute-start(bf16[128,1152]{1,0:T(8,128)(2,1)S(1)} %get-tuple-element.87), channel_id=1, source_target_pairs={{0,8},{4,12},{8,0},{12,4},{16,24},{20,28},{24,16},{28,20},{1,9},{5... | collective-permute-start | bytes 884744 | tf_op jit(solution)/shard_map/ppermute | solution.py:346
  26.1 1.5 %collective-permute-start.18 = (bf16[128,1152]{1,0:T(8,128)(2,1)S(1)}, bf16[128,1152]{1,0:T(8,128)(2,1)S(1)}, u32[]{:S(2)}, u32[]{:S(2)}) collective-permute-start(bf16[128,1152]{1,0:T(8,128)(2,1)S(1)} %get-tuple-element.88), channel_id=1, source_target_pairs={{0,16},{4,20},{8,24},{12,28},{16,0},{20,4},{24,8},{28,12},{1,17},{... | collective-permute-start | bytes 884744 | tf_op jit(solution)/shard_map/ppermute | solution.py:346
  27.6 0.7 %shard_map.115 = (bf16[256,1024]{1,0:T(8,128)(2,1)S(1)}, bf16[128,1024]{1,0:T(8,128)(2,1)S(1)}, bf16[128,1024]{1,0:T(8,128)(2,1)S(1)}) custom-call(bf16[1024,144]{1,0:T(8,128)(2,1)S(1)} %get-tuple-element.71.mine, bf16[1024,144]{1,0:T(8,128)(2,1)S(1)} %collective-permute-done.6.got, bf16[144,1024]{1,0:T(8,128)(2,1)S(1)} %get-tuple-element.61.factor_ref.factor, ...), custom_call_target="tpu_custom_call" | custom-call | tf_op jit(solution)/shard_map/pallas_call | solution.py:44
  28.3 0.1 collective-permute-start.8
  28.4 0.6 collective-permute-start.9
  29.1 0.5 collective-permute-start.3
  29.6 4.5 %collective-permute-done.17.got_a = bf16[128,1152]{1,0:T(8,128)(2,1)S(1)} collective-permute-done((bf16[128,1152]{1,0:T(8,128)(2,1)S(1)}, bf16[128,1152]{1,0:T(8,128)(2,1)S(1)}, u32[]{:S(2)}, u32[]{:S(2)}) %collective-permute-start.17) | collective-permute-done | bytes 294944 | tf_op jit(solution)/shard_map/ppermute | solution.py:346
  34.1 1.8 %collective-permute-done.18.got_b = bf16[128,1152]{1,0:T(8,128)(2,1)S(1)} collective-permute-done((bf16[128,1152]{1,0:T(8,128)(2,1)S(1)}, bf16[128,1152]{1,0:T(8,128)(2,1)S(1)}, u32[]{:S(2)}, u32[]{:S(2)}) %collective-permute-start.18) | collective-permute-done | bytes 294944 | tf_op jit(solution)/shard_map/ppermute | solution.py:346
  36.0 0.1 shard_map.120
  36.1 1.6 %collective-permute-start.19 = (bf16[64,1152]{1,0:T(8,128)(2,1)S(1)}, bf16[64,1152]{1,0:T(8,128)(2,1)S(1)}, u32[]{:S(2)}, u32[]{:S(2)}) collective-permute-start(bf16[64,1152]{1,0:T(8,128)(2,1)S(1)} %get-tuple-element.90), channel_id=1, source_target_pairs={{0,16},{4,20},{8,24},{12,28},{16,0},{20,4},{24,8},{28,12},{1,17},{... | collective-permute-start | bytes 442376 | tf_op jit(solution)/shard_map/ppermute | solution.py:346
  37.7 0.1 collective-permute-start.20
  37.8 2.0 %collective-permute-done.8.got_a = bf16[128,1024]{1,0:T(8,128)(2,1)S(1)} collective-permute-done((bf16[128,1024]{1,0:T(8,128)(2,1)S(1)}, bf16[128,1024]{1,0:T(8,128)(2,1)S(1)}, u32[]{:S(2)}, u32[]{:S(2)}) %collective-permute-start.8) | collective-permute-done | bytes 262176 | tf_op jit(solution)/shard_map/ppermute | solution.py:346
  39.8 1.8 %collective-permute-done.9.got_b = bf16[128,1024]{1,0:T(8,128)(2,1)S(1)} collective-permute-done((bf16[128,1024]{1,0:T(8,128)(2,1)S(1)}, bf16[128,1024]{1,0:T(8,128)(2,1)S(1)}, u32[]{:S(2)}, u32[]{:S(2)}) %collective-permute-start.9) | collective-permute-done | bytes 262176 | tf_op jit(solution)/shard_map/ppermute | solution.py:346
  41.6 0.1 shard_map.116
  41.7 1.3 %collective-permute-start.10 = (bf16[64,1024]{1,0:T(8,128)(2,1)S(1)}, bf16[64,1024]{1,0:T(8,128)(2,1)S(1)}, u32[]{:S(2)}, u32[]{:S(2)}) collective-permute-start(bf16[64,1024]{1,0:T(8,128)(2,1)S(1)} %get-tuple-element.77), channel_id=1, source_target_pairs={{0,1},{1,2},{2,3},{3,0},{4,5},{5,6},{6,7},{7,4},{8,9},{9,10},{10,1... | collective-permute-start | bytes 393224 | tf_op jit(solution)/shard_map/ppermute | solution.py:352
  43.1 2.4 %collective-permute-done.19.got_a = bf16[64,1152]{1,0:T(8,128)(2,1)S(1)} collective-permute-done((bf16[64,1152]{1,0:T(8,128)(2,1)S(1)}, bf16[64,1152]{1,0:T(8,128)(2,1)S(1)}, u32[]{:S(2)}, u32[]{:S(2)}) %collective-permute-start.19) | collective-permute-done | bytes 147488 | tf_op jit(solution)/shard_map/ppermute | solution.py:346
  45.5 0.7 %collective-permute-start.11 = (bf16[64,1024]{1,0:T(8,128)(2,1)S(1)}, bf16[64,1024]{1,0:T(8,128)(2,1)S(1)}, u32[]{:S(2)}, u32[]{:S(2)}) collective-permute-start(bf16[64,1024]{1,0:T(8,128)(2,1)S(1)} %get-tuple-element.78), channel_id=1, source_target_pairs={{0,2},{1,3},{2,0},{3,1},{4,6},{5,7},{6,4},{7,5},{8,10},{9,11},{10,... | collective-permute-start | bytes 393224 | tf_op jit(solution)/shard_map/ppermute | solution.py:352
  46.2 2.6 %collective-permute-start.12 = (bf16[64,1024]{1,0:T(8,128)(2,1)S(1)}, bf16[64,1024]{1,0:T(8,128)(2,1)S(1)}, u32[]{:S(2)}, u32[]{:S(2)}) collective-permute-start(bf16[64,1024]{1,0:T(8,128)(2,1)S(1)} %get-tuple-element.79), channel_id=1, source_target_pairs={{0,3},{1,0},{2,1},{3,2},{4,7},{5,4},{6,5},{7,6},{8,11},{9,8},{10,9... | collective-permute-start | bytes 393224 | tf_op jit(solution)/shard_map/ppermute | solution.py:352
  48.8 0.1 shard_map.121
  48.9 4.2 %collective-permute-done.10.refs_1_ = bf16[64,1024]{1,0:T(8,128)(2,1)S(1)} collective-permute-done((bf16[64,1024]{1,0:T(8,128)(2,1)S(1)}, bf16[64,1024]{1,0:T(8,128)(2,1)S(1)}, u32[]{:S(2)}, u32[]{:S(2)}) %collective-permute-start.10) | collective-permute-done | bytes 131104 | tf_op jit(solution)/shard_map/ppermute | solution.py:352
  53.0 2.6 %collective-permute-start.21 = (bf16[32,1152]{1,0:T(8,128)(2,1)S(1)}, bf16[32,1152]{1,0:T(8,128)(2,1)S(1)}, u32[]{:S(2)}, u32[]{:S(2)}) collective-permute-start(bf16[32,1152]{1,0:T(8,128)(2,1)S(1)} %get-tuple-element.93), channel_id=1, source_target_pairs={{0,1},{1,2},{2,3},{3,0},{4,5},{5,6},{6,7},{7,4},{8,9},{9,10},{10,1... | collective-permute-start | bytes 221192 | tf_op jit(solution)/shard_map/ppermute | solution.py:352
  55.6 3.1 %collective-permute-done.11.refs_2_ = bf16[64,1024]{1,0:T(8,128)(2,1)S(1)} collective-permute-done((bf16[64,1024]{1,0:T(8,128)(2,1)S(1)}, bf16[64,1024]{1,0:T(8,128)(2,1)S(1)}, u32[]{:S(2)}, u32[]{:S(2)}) %collective-permute-start.11) | collective-permute-done | bytes 131104 | tf_op jit(solution)/shard_map/ppermute | solution.py:352
  58.7 2.9 %collective-permute-start.23 = (bf16[32,1152]{1,0:T(8,128)(2,1)S(1)}, bf16[32,1152]{1,0:T(8,128)(2,1)S(1)}, u32[]{:S(2)}, u32[]{:S(2)}) collective-permute-start(bf16[32,1152]{1,0:T(8,128)(2,1)S(1)} %get-tuple-element.95), channel_id=1, source_target_pairs={{0,3},{1,0},{2,1},{3,2},{4,7},{5,4},{6,5},{7,6},{8,11},{9,8},{10,9... | collective-permute-start | bytes 221192 | tf_op jit(solution)/shard_map/ppermute | solution.py:352
  61.6 0.1 shard_map.117
  61.6 0.2 collective-permute-start.13
  61.9 1.5 %collective-permute-start.14 = (bf16[32,1024]{1,0:T(8,128)(2,1)S(1)}, bf16[32,1024]{1,0:T(8,128)(2,1)S(1)}, u32[]{:S(2)}, u32[]{:S(2)}) collective-permute-start(bf16[32,1024]{1,0:T(8,128)(2,1)S(1)} %get-tuple-element.82), channel_id=1, source_target_pairs={{0,8},{4,12},{8,0},{12,4},{16,24},{20,28},{24,16},{28,20},{1,9},{5... | collective-permute-start | bytes 196616 | tf_op jit(solution)/shard_map/ppermute | solution.py:346
  63.4 0.8 %shard_map.114 = (bf16[6,12,2,1024]{3,2,1,0:T(2,128)(2,1)}, bf16[6,12,2,1024]{3,2,1,0:T(2,128)(2,1)}) custom-call(bf16[2,3,6,2,1024]{4,3,2,1,0:T(2,128)(2,1)S(1)} %get-tuple-element.65.q0, bf16[2,3,6,2,1024]{4,3,2,1,0:T(2,128)(2,1)S(1)} %collective-permute-done.3.q1, bf16[2,3,6,2,1024]{4,3,2,1,0:T(2,128)(2,1)S(1)} %collective-permute-done.4.q2, ...), custom_call_target="tpu_custom_call" | custom-call | tf_op jit(solution)/shard_map/pallas_call | solution.py:44
  64.2 1.8 %collective-permute-done.13.got_a = bf16[32,1024]{1,0:T(8,128)(2,1)S(1)} collective-permute-done((bf16[32,1024]{1,0:T(8,128)(2,1)S(1)}, bf16[32,1024]{1,0:T(8,128)(2,1)S(1)}, u32[]{:S(2)}, u32[]{:S(2)}) %collective-permute-start.13) | collective-permute-done | bytes 65568 | tf_op jit(solution)/shard_map/ppermute | solution.py:346
  66.0 0.2 collective-permute-done.14.got_b
  66.1 0.6 shard_map.118
  66.8 0.3 collective-permute-done.23.refs_3_
  67.1 0.7 %shard_map.122 = (f32[32,1536]{1,0:T(8,128)}, f32[1,32]{1,0:T(1,128)}, f32[1,32]{1,0:T(1,128)}) custom-call(f32[32,512]{1,0:T(8,128)S(1)} %get-tuple-element.83.value_ref, bf16[32,1152]{1,0:T(8,128)(2,1)S(1)} %get-tuple-element.92.refs_0_, bf16[32,1152]{1,0:T(8,128)(2,1)S(1)} %collective-permute-done.21.refs_1_, ...), custom_call_target="tpu_custom_call" | custom-call | tf_op jit(solution)/shard_map/pallas_call | solution.py:44
  (15 shorter events, 0.0 us)
Async XLA Ops:
  1.8 9.8 %collective-permute-start = (bf16[2,3,6,2,1024]{4,3,2,1,0:T(2,128)(2,1)S(1)}, bf16[2,3,6,2,1024]{4,3,2,1,0:T(2,128)(2,1)S(1)}, u32[]{:S(2)}, u32[]{:S(2)}) collective-permute-start(bf16[2,3,6,2,1024]{4,3,2,1,0:T(2,128)(2,1)S(1)} %get-tuple-element.54), channel_id=1, source_target_pairs={{0,3},{1,0},{2,1},{3,2},{4,7},{5,4},{6,5},{7,6},{8,11},{9,8},{10,9... | collective-permute-start | bytes 442376 | tf_op jit(solution)/shard_map/ppermute | solution.py:415
  7.0 4.7 %collective-permute-start.1 = (bf16[2,3,6,2,1024]{4,3,2,1,0:T(2,128)(2,1)S(1)}, bf16[2,3,6,2,1024]{4,3,2,1,0:T(2,128)(2,1)S(1)}, u32[]{:S(2)}, u32[]{:S(2)}) collective-permute-start(bf16[2,3,6,2,1024]{4,3,2,1,0:T(2,128)(2,1)S(1)} %get-tuple-element.55), channel_id=1, source_target_pairs={{0,28},{1,29},{2,30},{3,31},{4,0},{5,1},{6,2},{7,3},{8,4},{9,5},{1... | collective-permute-start | bytes 442376 | tf_op jit(solution)/shard_map/ppermute | solution.py:415
  8.6 5.2 %collective-permute-start.2 = (bf16[2,3,6,2,1024]{4,3,2,1,0:T(2,128)(2,1)S(1)}, bf16[2,3,6,2,1024]{4,3,2,1,0:T(2,128)(2,1)S(1)}, u32[]{:S(2)}, u32[]{:S(2)}) collective-permute-start(bf16[2,3,6,2,1024]{4,3,2,1,0:T(2,128)(2,1)S(1)} %get-tuple-element.56), channel_id=1, source_target_pairs={{0,31},{1,28},{2,29},{3,30},{4,3},{5,0},{6,1},{7,2},{8,7},{9,4},{1... | collective-permute-start | bytes 442376 | tf_op jit(solution)/shard_map/ppermute | solution.py:415
  19.1 4.4 %collective-permute-start.15 = (bf16[144,1024]{1,0:T(8,128)(2,1)S(1)}, bf16[144,1024]{1,0:T(8,128)(2,1)S(1)}, u32[]{:S(2)}, u32[]{:S(2)}) collective-permute-start(bf16[144,1024]{1,0:T(8,128)(2,1)S(1)} %shard_map.112.late_ref.factor), channel_id=1, source_target_pairs={{0,4},{4,0},{8,12},{12,8},{16,20},{20,16},{24,28},{28,24},{1,5},{5... | collective-permute-start | bytes 884744 | tf_op jit(solution)/shard_map/ppermute | solution.py:346
  19.3 4.2 %collective-permute-start.6 = (bf16[1024,144]{1,0:T(8,128)(2,1)S(1)}, bf16[1024,144]{1,0:T(8,128)(2,1)S(1)}, u32[]{:S(2)}, u32[]{:S(2)}) collective-permute-start(bf16[1024,144]{1,0:T(8,128)(2,1)S(1)} %get-tuple-element.72), channel_id=1, source_target_pairs={{0,4},{4,0},{8,12},{12,8},{16,20},{20,16},{24,28},{28,24},{1,5},{5... | collective-permute-start | bytes 884744 | tf_op jit(solution)/shard_map/ppermute | solution.py:346
  21.9 1.6 %collective-permute-start.16 = (f32[512,128]{1,0:T(8,128)S(1)}, f32[512,128]{1,0:T(8,128)S(1)}, u32[]{:S(2)}, u32[]{:S(2)}) collective-permute-start(f32[512,128]{1,0:T(8,128)S(1)} %get-tuple-element.85), channel_id=1, source_target_pairs={{0,4},{4,0},{8,12},{12,8},{16,20},{20,16},{24,28},{28,24},{1,5},{5... | collective-permute-start | bytes 786440 | tf_op jit(solution)/shard_map/ppermute | solution.py:346
  22.1 5.5 %collective-permute-start.7 = (bf16[144,1024]{1,0:T(8,128)(2,1)S(1)}, bf16[144,1024]{1,0:T(8,128)(2,1)S(1)}, u32[]{:S(2)}, u32[]{:S(2)}) collective-permute-start(bf16[144,1024]{1,0:T(8,128)(2,1)S(1)} %get-tuple-element.61.factor_ref.factor), channel_id=1, source_target_pairs={{0,4},{4,0},{8,12},{12,8},{16,20},{20,16},{24,28},{28,24},{1,5},{5... | collective-permute-start | bytes 884744 | tf_op jit(solution)/shard_map/ppermute | solution.py:346
  24.2 9.9 %collective-permute-start.17 = (bf16[128,1152]{1,0:T(8,128)(2,1)S(1)}, bf16[128,1152]{1,0:T(8,128)(2,1)S(1)}, u32[]{:S(2)}, u32[]{:S(2)}) collective-permute-start(bf16[128,1152]{1,0:T(8,128)(2,1)S(1)} %get-tuple-element.87), channel_id=1, source_target_pairs={{0,8},{4,12},{8,0},{12,4},{16,24},{20,28},{24,16},{28,20},{1,9},{5... | collective-permute-start | bytes 884744 | tf_op jit(solution)/shard_map/ppermute | solution.py:346
  26.1 9.9 %collective-permute-start.18 = (bf16[128,1152]{1,0:T(8,128)(2,1)S(1)}, bf16[128,1152]{1,0:T(8,128)(2,1)S(1)}, u32[]{:S(2)}, u32[]{:S(2)}) collective-permute-start(bf16[128,1152]{1,0:T(8,128)(2,1)S(1)} %get-tuple-element.88), channel_id=1, source_target_pairs={{0,16},{4,20},{8,24},{12,28},{16,0},{20,4},{24,8},{28,12},{1,17},{... | collective-permute-start | bytes 884744 | tf_op jit(solution)/shard_map/ppermute | solution.py:346
  28.3 11.5 %collective-permute-start.8 = (bf16[128,1024]{1,0:T(8,128)(2,1)S(1)}, bf16[128,1024]{1,0:T(8,128)(2,1)S(1)}, u32[]{:S(2)}, u32[]{:S(2)}) collective-permute-start(bf16[128,1024]{1,0:T(8,128)(2,1)S(1)} %get-tuple-element.74), channel_id=1, source_target_pairs={{0,8},{4,12},{8,0},{12,4},{16,24},{20,28},{24,16},{28,20},{1,9},{5... | collective-permute-start | bytes 786440 | tf_op jit(solution)/shard_map/ppermute | solution.py:346
  28.4 13.1 %collective-permute-start.9 = (bf16[128,1024]{1,0:T(8,128)(2,1)S(1)}, bf16[128,1024]{1,0:T(8,128)(2,1)S(1)}, u32[]{:S(2)}, u32[]{:S(2)}) collective-permute-start(bf16[128,1024]{1,0:T(8,128)(2,1)S(1)} %get-tuple-element.75), channel_id=1, source_target_pairs={{0,16},{4,20},{8,24},{12,28},{16,0},{20,4},{24,8},{28,12},{1,17},{... | collective-permute-start | bytes 786440 | tf_op jit(solution)/shard_map/ppermute | solution.py:346
  29.1 12.6 %collective-permute-start.3 = (bf16[2,3,6,2,1024]{4,3,2,1,0:T(2,128)(2,1)S(1)}, bf16[2,3,6,2,1024]{4,3,2,1,0:T(2,128)(2,1)S(1)}, u32[]{:S(2)}, u32[]{:S(2)}) collective-permute-start(bf16[2,3,6,2,1024]{4,3,2,1,0:T(2,128)(2,1)S(1)} %get-tuple-element.66), channel_id=1, source_target_pairs={{0,1},{1,2},{2,3},{3,0},{4,5},{5,6},{6,7},{7,4},{8,9},{9,10},{10,1... | collective-permute-start | bytes 442376 | tf_op jit(solution)/shard_map/ppermute | solution.py:415
  36.1 9.3 %collective-permute-start.19 = (bf16[64,1152]{1,0:T(8,128)(2,1)S(1)}, bf16[64,1152]{1,0:T(8,128)(2,1)S(1)}, u32[]{:S(2)}, u32[]{:S(2)}) collective-permute-start(bf16[64,1152]{1,0:T(8,128)(2,1)S(1)} %get-tuple-element.90), channel_id=1, source_target_pairs={{0,16},{4,20},{8,24},{12,28},{16,0},{20,4},{24,8},{28,12},{1,17},{... | collective-permute-start | bytes 442376 | tf_op jit(solution)/shard_map/ppermute | solution.py:346
  37.7 8.5 %collective-permute-start.20 = (bf16[64,1152]{1,0:T(8,128)(2,1)S(1)}, bf16[64,1152]{1,0:T(8,128)(2,1)S(1)}, u32[]{:S(2)}, u32[]{:S(2)}) collective-permute-start(bf16[64,1152]{1,0:T(8,128)(2,1)S(1)} %get-tuple-element.91), channel_id=1, source_target_pairs={{0,8},{4,12},{8,0},{12,4},{16,24},{20,28},{24,16},{28,20},{1,9},{5... | collective-permute-start | bytes 442376 | tf_op jit(solution)/shard_map/ppermute | solution.py:346
  39.8 21.9 %collective-permute-start.4 = (bf16[2,3,6,2,1024]{4,3,2,1,0:T(2,128)(2,1)S(1)}, bf16[2,3,6,2,1024]{4,3,2,1,0:T(2,128)(2,1)S(1)}, u32[]{:S(2)}, u32[]{:S(2)}) collective-permute-start(bf16[2,3,6,2,1024]{4,3,2,1,0:T(2,128)(2,1)S(1)} %get-tuple-element.67), channel_id=1, source_target_pairs={{0,4},{1,5},{2,6},{3,7},{4,8},{5,9},{6,10},{7,11},{8,12},{9,13},{1... | collective-permute-start | bytes 442376 | tf_op jit(solution)/shard_map/ppermute | solution.py:415
  41.6 20.3 %collective-permute-start.5 = (bf16[2,3,6,2,1024]{4,3,2,1,0:T(2,128)(2,1)S(1)}, bf16[2,3,6,2,1024]{4,3,2,1,0:T(2,128)(2,1)S(1)}, u32[]{:S(2)}, u32[]{:S(2)}) collective-permute-start(bf16[2,3,6,2,1024]{4,3,2,1,0:T(2,128)(2,1)S(1)} %get-tuple-element.68), channel_id=1, source_target_pairs={{0,5},{1,6},{2,7},{3,4},{4,9},{5,10},{6,11},{7,8},{8,13},{9,14},{1... | collective-permute-start | bytes 442376 | tf_op jit(solution)/shard_map/ppermute | solution.py:415
  41.7 11.3 %collective-permute-start.10 = (bf16[64,1024]{1,0:T(8,128)(2,1)S(1)}, bf16[64,1024]{1,0:T(8,128)(2,1)S(1)}, u32[]{:S(2)}, u32[]{:S(2)}) collective-permute-start(bf16[64,1024]{1,0:T(8,128)(2,1)S(1)} %get-tuple-element.77), channel_id=1, source_target_pairs={{0,1},{1,2},{2,3},{3,0},{4,5},{5,6},{6,7},{7,4},{8,9},{9,10},{10,1... | collective-permute-start | bytes 393224 | tf_op jit(solution)/shard_map/ppermute | solution.py:352
  45.5 13.2 %collective-permute-start.11 = (bf16[64,1024]{1,0:T(8,128)(2,1)S(1)}, bf16[64,1024]{1,0:T(8,128)(2,1)S(1)}, u32[]{:S(2)}, u32[]{:S(2)}) collective-permute-start(bf16[64,1024]{1,0:T(8,128)(2,1)S(1)} %get-tuple-element.78), channel_id=1, source_target_pairs={{0,2},{1,3},{2,0},{3,1},{4,6},{5,7},{6,4},{7,5},{8,10},{9,11},{10,... | collective-permute-start | bytes 393224 | tf_op jit(solution)/shard_map/ppermute | solution.py:352
  46.2 12.5 %collective-permute-start.12 = (bf16[64,1024]{1,0:T(8,128)(2,1)S(1)}, bf16[64,1024]{1,0:T(8,128)(2,1)S(1)}, u32[]{:S(2)}, u32[]{:S(2)}) collective-permute-start(bf16[64,1024]{1,0:T(8,128)(2,1)S(1)} %get-tuple-element.79), channel_id=1, source_target_pairs={{0,3},{1,0},{2,1},{3,2},{4,7},{5,4},{6,5},{7,6},{8,11},{9,8},{10,9... | collective-permute-start | bytes 393224 | tf_op jit(solution)/shard_map/ppermute | solution.py:352
  53.0 13.7 %collective-permute-start.21 = (bf16[32,1152]{1,0:T(8,128)(2,1)S(1)}, bf16[32,1152]{1,0:T(8,128)(2,1)S(1)}, u32[]{:S(2)}, u32[]{:S(2)}) collective-permute-start(bf16[32,1152]{1,0:T(8,128)(2,1)S(1)} %get-tuple-element.93), channel_id=1, source_target_pairs={{0,1},{1,2},{2,3},{3,0},{4,5},{5,6},{6,7},{7,4},{8,9},{9,10},{10,1... | collective-permute-start | bytes 221192 | tf_op jit(solution)/shard_map/ppermute | solution.py:352
  58.7 8.1 %collective-permute-start.22 = (bf16[32,1152]{1,0:T(8,128)(2,1)S(1)}, bf16[32,1152]{1,0:T(8,128)(2,1)S(1)}, u32[]{:S(2)}, u32[]{:S(2)}) collective-permute-start(bf16[32,1152]{1,0:T(8,128)(2,1)S(1)} %get-tuple-element.94), channel_id=1, source_target_pairs={{0,2},{1,3},{2,0},{3,1},{4,6},{5,7},{6,4},{7,5},{8,10},{9,11},{10,... | collective-permute-start | bytes 221192 | tf_op jit(solution)/shard_map/ppermute | solution.py:352
  58.7 8.5 %collective-permute-start.23 = (bf16[32,1152]{1,0:T(8,128)(2,1)S(1)}, bf16[32,1152]{1,0:T(8,128)(2,1)S(1)}, u32[]{:S(2)}, u32[]{:S(2)}) collective-permute-start(bf16[32,1152]{1,0:T(8,128)(2,1)S(1)} %get-tuple-element.95), channel_id=1, source_target_pairs={{0,3},{1,0},{2,1},{3,2},{4,7},{5,4},{6,5},{7,6},{8,11},{9,8},{10,9... | collective-permute-start | bytes 221192 | tf_op jit(solution)/shard_map/ppermute | solution.py:352
  61.6 4.3 %collective-permute-start.13 = (bf16[32,1024]{1,0:T(8,128)(2,1)S(1)}, bf16[32,1024]{1,0:T(8,128)(2,1)S(1)}, u32[]{:S(2)}, u32[]{:S(2)}) collective-permute-start(bf16[32,1024]{1,0:T(8,128)(2,1)S(1)} %get-tuple-element.81), channel_id=1, source_target_pairs={{0,16},{4,20},{8,24},{12,28},{16,0},{20,4},{24,8},{28,12},{1,17},{... | collective-permute-start | bytes 196616 | tf_op jit(solution)/shard_map/ppermute | solution.py:346
  61.9 4.3 %collective-permute-start.14 = (bf16[32,1024]{1,0:T(8,128)(2,1)S(1)}, bf16[32,1024]{1,0:T(8,128)(2,1)S(1)}, u32[]{:S(2)}, u32[]{:S(2)}) collective-permute-start(bf16[32,1024]{1,0:T(8,128)(2,1)S(1)} %get-tuple-element.82), channel_id=1, source_target_pairs={{0,8},{4,12},{8,0},{12,4},{16,24},{20,28},{24,16},{28,20},{1,9},{5... | collective-permute-start | bytes 196616 | tf_op jit(solution)/shard_map/ppermute | solution.py:346

commit v6 on v5

--- a/solution.py
+++ b/solution.py
@@ -12,6 +12,8 @@
 
 HDIM = 64
 F32 = jnp.float32
+EARLY = (0, 1)
+LATE = (2, 3)
 BF16 = jnp.bfloat16
 LANES = 128
 
@@ -85,11 +87,17 @@
     run_copies(list(zip(refs[:count], refs[count:-1])), refs[-1])
 
 
-def unpack_body(q0, q1, q2, q3, y_ref, grad_ref):
-    rows, cols = y_ref.shape[:2]
+def unpack_body(q0, q1, q2, q3, tok_ref, w_out_ref, y_ref, grad_ref, att):
+    rows, cols, levels, width = y_ref.shape
+    inner = att.shape[-1]
     for quad, (row, col) in zip((q0, q1, q2, q3), corners(rows, cols)):
-        for part, ref in enumerate((y_ref, grad_ref)):
-            ref[row : row + rows // 2, col : col + cols // 2] = quad[part]
+        at = (slice(row, row + rows // 2), slice(col, col + cols // 2))
+        att[at] = quad[:, :, :, :inner]
+        grad_ref[at] = quad[:, :, :, inner:]
+    flat = att[...].reshape(rows * cols * levels, inner)
+    mixed = dot(flat, w_out_ref[...], ((1,), (0,)))
+    total = tok_ref[...].reshape(rows * cols * levels, width).astype(F32) + mixed
+    y_ref[...] = total.astype(BF16).reshape(y_ref.shape)
 
 
 def gather_window(quads, part, wide):
@@ -116,7 +124,7 @@
         start = place * group
         if steps:
             block = places_ref[0] ^ steps[place][0]
-            turned = lax.rem(places_ref[1] + steps[place][1], counts[1])
+            turned = places_ref[1] ^ steps[place][1]
             start = pl.multiple_of((block * counts[1] + turned) * group, group)
         at = place * group
         target = targets[at // half]
@@ -208,13 +216,13 @@
 
 
 def gradient_body(
-    plan, places_ref, r0, r1, r2, r3, factor_ref, late_ref, w_qkv_ref, w_out_ref, gain_ref,
+    plan, places_ref, r0, r1, r2, r3, factor_ref, late_ref, w_qkv_ref, gain_ref,
     o0, o1, o2, o3, mine_ref, peer_ref, wide, flat,
 ):
     quads = (r0, r1, r2, r3)
-    inner, width = w_out_ref.shape
+    inner, width = late_ref.shape[1] // 2, wide.shape[1]
     outs = (o0, o1, o2, o3)
-    quad = o0.shape[1:]
+    quad = o0.shape[:3]
     count = quad[0] * quad[1] * quad[2]
     tokens_wide = gather_window(quads, 0, wide)
     standard, inverse = normalize(tokens_wide)
@@ -227,16 +235,18 @@
     line = lax.broadcasted_iota(jnp.int32, (LANES, width), 0)
     flat[...] = jnp.where(line == 0, sums[0], jnp.where(line == 1, sums[1], 0.0)).T
     reorder(plan, places_ref, flat, (mine_ref, peer_ref))
-    wide[...] = tokens_wide + dot(factor_ref[:, :inner], w_out_ref[...], ((1,), (0,)))
+    wide[:, :inner] = factor_ref[:, :inner].astype(F32)
     for place, out in enumerate(outs):
-        out[0] = wide[place * count : (place + 1) * count, :].astype(BF16).reshape(quad)
+        rows = wide[place * count : (place + 1) * count, :inner]
+        out[:, :, :, :inner] = rows.astype(BF16).reshape(*quad, inner)
     grad_hat = grad_normed * gain_ref[...]
     first = jnp.mean(grad_hat, axis=-1, keepdims=True)
     second = jnp.mean(grad_hat * standard, axis=-1, keepdims=True)
     change = (grad_hat - first - standard * second) * inverse
     wide[...] = gather_window(quads, 1, wide) + change
     for place, out in enumerate(outs):
-        out[1] = wide[place * count : (place + 1) * count, :].astype(BF16).reshape(quad)
+        rows = wide[place * count : (place + 1) * count, :]
+        out[:, :, :, inner:] = rows.astype(BF16).reshape(*quad, width)
 
 
 def split_store(value, outs, cols):
@@ -248,26 +258,27 @@
         out[to : to + quarter, cols] = value[start : start + quarter].astype(BF16)
 
 
-def early_body(mine, got, factor, factor_got, *outs):
+def multiply(mine, got, factors, blocks, outs):
     half = mine.shape[0] // 2
-    inner = factor.shape[1] // 2
-    for part in range(2):
-        rows = slice((1 - part) * half, (2 - part) * half)
-        cols = slice(part * inner, (part + 1) * inner)
-        value = dot(mine[rows, :], factor[:, cols], ((1,), (0,)))
-        value += dot(got[rows, :], factor_got[:, cols], ((1,), (0,)))
-        split_store(value, outs, cols)
-
-
-def late_body(mine, got, factor, factor_got, sums, sums_got, *outs):
-    half = mine.shape[0] // 2
-    inner = factor.shape[1] // 2
-    for part in range(2):
-        cols = slice(part * inner, (part + 1) * inner)
-        value = dot(mine[:half, :], factor[:, cols], ((1,), (0,)))
-        value += dot(got[:half, :], factor_got[:, cols], ((1,), (0,)))
-        split_store(value, outs, cols)
-    split_store(sums[...] + sums_got[...], outs, slice(2 * inner, 2 * inner + LANES))
+    inner = factors[0].shape[1] // 2
+    for place, block in enumerate(blocks):
+        rows = slice(half, 2 * half) if block == 0 else slice(0, half)
+        pair = 2 * (block // 2)
+        at = block % 2 * inner
+        value = dot(mine[rows, :], factors[pair][:, at : at + inner], ((1,), (0,)))
+        value += dot(got[rows, :], factors[pair + 1][:, at : at + inner], ((1,), (0,)))
+        split_store(value, outs, slice(place * inner, (place + 1) * inner))
+    return len(blocks) * inner
+
+
+def early_body(mine, got, *refs):
+    multiply(mine, got, refs[:-3], EARLY, refs[-3:])
+
+
+def late_body(mine, got, *refs):
+    factors, (sums, sums_got), outs = refs[:-5], refs[-5:-3], refs[-3:]
+    at = multiply(mine, got, factors, LATE, outs)
+    split_store(sums[...] + sums_got[...], outs, slice(at, at + LANES))
 
 
 def added(*refs):
@@ -330,8 +341,11 @@
     pieces, (qkv_ref, gain_ref, bias_ref) = refs[:-3], refs[-3:]
     total = added(*(item[...] for item in pieces)) * factor
     cols = total.shape[1] - LANES
-    qkv_ref[:, :cols] = total[:, :cols]
-    qkv_ref[:, cols:] = value_ref[...]
+    inner = cols // len(LATE)
+    sources = {block: value_ref[:, i * inner : (i + 1) * inner] for i, block in enumerate(EARLY[1:])}
+    sources |= {block: total[:, i * inner : (i + 1) * inner] for i, block in enumerate(LATE)}
+    for place, block in enumerate((2, 3, 1)):
+        qkv_ref[:, place * inner : (place + 1) * inner] = sources[block]
     rows = total.shape[0]
     flat = jnp.concatenate([total[:, cols:], jnp.zeros((LANES - rows, LANES), F32)], axis=0).T
     gain_ref[...] = flat[0:1, :rows]
@@ -349,7 +363,7 @@
 def turn(pieces):
     count = len(pieces)
     return [pieces[0]] + [
-        lax.ppermute(pieces[k], "lon", [(i, (i + k) % count) for i in range(count)])
+        lax.ppermute(pieces[k], "lon", [(i, i ^ k) for i in range(count)])
         for k in range(1, count)
     ]
 
@@ -364,9 +378,9 @@
         meet_body, [((size, cols), F32)] + [((size, cols), BF16)] * 2, pieces
     )
     got_a, got_b = swap(send_a, 4), swap(send_b, 2)
-    shape = ((size, cols // 2), F32)
     return call(
-        functools.partial(early_end_body, factor), [shape] * 2,
+        functools.partial(early_end_body, factor),
+        [((size, cols - cols // len(EARLY)), F32), ((size, cols // len(EARLY)), F32)],
         (base, got_a, got_b), near_out=1,
     )
 
@@ -425,13 +439,14 @@
     )
     quads = [own, *moved_all(sends, -1)]
     params = (w_qkv, w_out, layer_norm_gain.reshape(1, width), layer_norm_bias.reshape(1, width))
-    params = call(
-        fetch_body, [(item.shape, item.dtype) for item in params], params, far=4,
-        scratch=[pltpu.SemaphoreType.DMA((4,))],
+    params = (*params, tok)
+    *params, tok = call(
+        fetch_body, [(item.shape, item.dtype) for item in params], params, far=5,
+        scratch=[pltpu.SemaphoreType.DMA((5,))],
     )
 
     share = width // (lat_count * lon_count)
-    hyper = lat_count == 8 and lon_count % 2 == 0 and share % 16 == 0
+    hyper = lat_count == 8 and lon_count in (2, 4, 8) and share % 16 == 0
     order = []
     if hyper:
         half_lon = lon_count // 2
@@ -459,8 +474,8 @@
     (factor_late,) = call(backward_body, [((cells, 2 * inner), BF16)], (query, pairs, probs))
     q0, q1, q2, q3, sums, sums_peer = call(
         functools.partial(gradient_body, plan),
-        [(quad, BF16)] * 4 + [((width // 2, LANES), F32)] * 2,
-        (places, *quads, factor, factor_late, *params[:3]),
+        [((*quad[1:-1], inner + width), BF16)] * 4 + [((width // 2, LANES), F32)] * 2,
+        (places, *quads, factor, factor_late, params[0], params[2]),
         scratch=[pltpu.VMEM((cells, width), F32), pltpu.VMEM((width, LANES), F32)],
         smem=1,
     )
@@ -474,10 +489,14 @@
         def shapes(cols):
             return [((rows, cols), BF16) for rows in (2 * quarter, quarter, quarter)]
 
-        early = call(early_body, shapes(2 * inner), (mine, got, factor, factor_got))
+        factors = (factor, factor_got, factor_late, late_got)
+        early = call(
+            early_body, shapes(len(EARLY) * inner),
+            (mine, got, *factors[: 2 * (EARLY[-1] // 2 + 1)]),
+        )
         late = call(
-            late_body, shapes(2 * inner + LANES),
-            (mine, got, factor_late, late_got, sums, sums_got),
+            late_body, shapes(len(LATE) * inner + LANES),
+            (mine, got, *factors, sums, sums_got),
         )
         value, d_out = sum_early(*early, lon_count, norm_factor)
         d_qkv, gain, bias = sum_late(*late, value, lon_count, norm_factor)
@@ -501,7 +520,10 @@
         d_qkv = jnp.concatenate([whole[:, 2 * inner : 4 * inner], whole[:, inner : 2 * inner]], axis=1)
         gain, bias = whole[:, 4 * inner], whole[:, 4 * inner + 1]
     back = [q0, *moved_all((q1, q2, q3), 1)]
-    y_out, token_gradient = call(unpack_body, [(grid, BF16)] * 2, back, near_out=0)
+    y_out, token_gradient = call(
+        unpack_body, [(grid, BF16)] * 2, (*back, tok, params[1]), near_out=0,
+        scratch=[pltpu.VMEM((*grid[:-1], inner), BF16)],
+    )
     return (
         y_out.transpose(2, 0, 1, 3),
         token_gradient.transpose(2, 0, 1, 3),

time: 69 us -> 67.8 us (0.983)
  the two profiles are of different devices: /device:TPU:0 before, /device:TPU:16 now
where the time goes in v6:
time: 67.8 us; the launch traced here: 67.6 us
  starting transfers between devices  33.8 us (50%)
  waiting for transfers between devices  17.8 us (26%)
  Pallas kernels  15.3 us (23%)
  between operations  0.75 us (1%)
    pallas_call x14, Pallas kernels, call(): pl.pallas_call(body, out_shape=[pltpu.VMEM(s, d) if i < near_out else jax...  15.3 us
    ppermute x6, starting transfers between devices, turn(): lax.ppermute(pieces[k], 'lon', [(i, i ^ k) for i in range(count)])  12.6 us
    ppermute x12, starting transfers between devices, swap(): return lax.ppermute(value, 'lat', xor_pairs(bit))  11 us
    ppermute x6, starting transfers between devices, moved_all(): lax.ppermute(items[place], ('lat', 'lon'), moved(sign * a, sign * b))  10.3 us
    ppermute x12, waiting for transfers between devices, swap(): return lax.ppermute(value, 'lat', xor_pairs(bit))  9.69 us
    ppermute x6, waiting for transfers between devices, turn(): lax.ppermute(pieces[k], 'lon', [(i, i ^ k) for i in range(count)])  4.63 us
    ppermute x6, waiting for transfers between devices, moved_all(): lax.ppermute(items[place], ('lat', 'lon'), moved(sign * a, sign * b))  3.46 us
  transfers between devices with their start and end apart: 24, of which 10 were waited for; matrix products, arithmetic and copies ran while one was open for 0% of the time, Pallas kernels for 11%

profile of v6, /device:TPU:16, one launch (start us, length us, event | category | flops | bytes accessed | tf_op | source)
XLA Modules:
  0.0 67.6 jit_solution(16575003521611635173)
XLA Ops:
  0.6 1.2 %shard_map.109 = (bf16[2,3,6,2,1024]{4,3,2,1,0:T(2,128)(2,1)S(1)}, bf16[2,3,6,2,1024]{4,3,2,1,0:T(2,128)(2,1)S(1)}, bf16[2,3,6,2,1024]{4,3,2,1,0:T(2,128)(2,1)S(1)}, bf16[2,3,6,2,1024]{4,3,2,1,0:T(2,128)(2,1)S(1)}) custom-call(bf16[6,12,2,1024]{3,2,1,0:T(2,128)(2,1)} %bitcast.9, bf16[6,12,2,1024]{3,2,1,0:T(2,128)(2,1)} %bitcast.11), custom_call_target="tpu_custom_call" | custom-call | tf_op jit(solution)/shard_map/pallas_call | solution.py:46
  1.8 0.5 collective-permute-start
  2.4 1.6 %collective-permute-start.1 = (bf16[2,3,6,2,1024]{4,3,2,1,0:T(2,128)(2,1)S(1)}, bf16[2,3,6,2,1024]{4,3,2,1,0:T(2,128)(2,1)S(1)}, u32[]{:S(2)}, u32[]{:S(2)}) collective-permute-start(bf16[2,3,6,2,1024]{4,3,2,1,0:T(2,128)(2,1)S(1)} %get-tuple-element.56), channel_id=1, source_target_pairs={{0,28},{1,29},{2,30},{3,31},{4,0},{5,1},{6,2},{7,3},{8,4},{9,5},{1... | collective-permute-start | bytes 442376 | tf_op jit(solution)/shard_map/ppermute | solution.py:429
  4.0 0.8 %collective-permute-start.2 = (bf16[2,3,6,2,1024]{4,3,2,1,0:T(2,128)(2,1)S(1)}, bf16[2,3,6,2,1024]{4,3,2,1,0:T(2,128)(2,1)S(1)}, u32[]{:S(2)}, u32[]{:S(2)}) collective-permute-start(bf16[2,3,6,2,1024]{4,3,2,1,0:T(2,128)(2,1)S(1)} %get-tuple-element.57), channel_id=1, source_target_pairs={{0,31},{1,28},{2,29},{3,30},{4,3},{5,0},{6,1},{7,2},{8,7},{9,4},{1... | collective-permute-start | bytes 442376 | tf_op jit(solution)/shard_map/ppermute | solution.py:429
  4.8 2.3 %shard_map.110 = (bf16[1024,1536]{1,0:T(8,128)(2,1)S(1)}, bf16[512,1024]{1,0:T(8,128)(2,1)S(1)}, f32[1,1024]{1,0:T(1,128)S(1)}, f32[1,1024]{1,0:T(1,128)S(1)}, bf16[6,12,2,1024]{3,2,1,0:T(2,128)(2,1)S(1)}) custom-call(bf16[1024,1536]{1,0:T(8,128)(2,1)} %refs_0_.1, bf16[512,1024]{1,0:T(8,128)(2,1)} %refs_1_.1, f32[1,1024]{1,0:T(1,128)} %bitcast.12, ...), custom_call_target="tpu_custom_call" | custom-call | tf_op jit(solution)/shard_map/pallas_call | solution.py:46
  7.1 0.9 %collective-permute-done.r1 = bf16[2,3,6,2,1024]{4,3,2,1,0:T(2,128)(2,1)S(1)} collective-permute-done((bf16[2,3,6,2,1024]{4,3,2,1,0:T(2,128)(2,1)S(1)}, bf16[2,3,6,2,1024]{4,3,2,1,0:T(2,128)(2,1)S(1)}, u32[]{:S(2)}, u32[]{:S(2)}) %collective-permute-start) | collective-permute-done | bytes 147488 | tf_op jit(solution)/shard_map/ppermute | solution.py:429
  8.0 0.0 collective-permute-done.1.r2
  8.0 2.1 %collective-permute-done.2.r3 = bf16[2,3,6,2,1024]{4,3,2,1,0:T(2,128)(2,1)S(1)} collective-permute-done((bf16[2,3,6,2,1024]{4,3,2,1,0:T(2,128)(2,1)S(1)}, bf16[2,3,6,2,1024]{4,3,2,1,0:T(2,128)(2,1)S(1)}, u32[]{:S(2)}, u32[]{:S(2)}) %collective-permute-start.2) | collective-permute-done | bytes 147488 | tf_op jit(solution)/shard_map/ppermute | solution.py:429
  10.1 3.6 %shard_map.111 = (bf16[1024,144]{1,0:T(8,128)(2,1)S(1)}, bf16[1024,144]{1,0:T(8,128)(2,1)S(1)}, bf16[144,1024]{1,0:T(8,128)(2,1)S(1)}, bf16[144,512]{1,0:T(8,128...) custom-call(s32[2]{0:T(128)S(1)} %compare_select_fusion.places_ref, ...), custom_call_target="tpu_custom_call" | custom-call | tf_op jit(solution)/shard_map/pallas_call | solution.py:46
  13.7 1.7 %shard_map.112.late_ref.refs_2_ = bf16[144,1024]{1,0:T(8,128)(2,1)S(1)} custom-call(bf16[144,512]{1,0:T(8,128)(2,1)S(1)} %get-tuple-element.63.query_ref, bf16[144,1536]{1,0:T(8,128)(2,1)S(1)} %get-tuple-element.64.pair_ref, f32[8,144,144]{2,1,0:T(8,128)S(1)} %get-tuple-element.65.probs_ref), custom_call_target="tpu_custom_call" | custom-call | tf_op jit(solution)/shard_map/pallas_call | solution.py:46
  15.4 1.4 %collective-permute-start.15 = (bf16[144,1024]{1,0:T(8,128)(2,1)S(1)}, bf16[144,1024]{1,0:T(8,128)(2,1)S(1)}, u32[]{:S(2)}, u32[]{:S(2)}) collective-permute-start(bf16[144,1024]{1,0:T(8,128)(2,1)S(1)} %shard_map.112.late_ref.refs_2_), channel_id=1, source_target_pairs={{0,4},{4,0},{8,12},{12,8},{16,20},{20,16},{24,28},{28,24},{1,5},{5... | collective-permute-start | bytes 884744 | tf_op jit(solution)/shard_map/ppermute | solution.py:360
  16.8 0.1 collective-permute-start.7
  16.9 0.4 collective-permute-start.6
  17.3 2.1 %shard_map.113 = (bf16[3,6,2,1536]{3,2,1,0:T(2,128)(2,1)S(1)}, bf16[3,6,2,1536]{3,2,1,0:T(2,128)(2,1)S(1)}, bf16[3,6,2,1536]{3,2,1,0:T(2,128)(2,1)S(1)}, bf16[3,...) custom-call(s32[2]{0:T(128)S(1)} %compare_select_fusion.places_ref, ...), custom_call_target="tpu_custom_call" | custom-call | tf_op jit(solution)/shard_map/pallas_call | solution.py:46
  19.4 0.1 collective-permute-start.16
  19.5 1.5 %collective-permute-done.16.refs_5_ = f32[512,128]{1,0:T(8,128)S(1)} collective-permute-done((f32[512,128]{1,0:T(8,128)S(1)}, f32[512,128]{1,0:T(8,128)S(1)}, u32[]{:S(2)}, u32[]{:S(2)}) %collective-permute-start.16) | collective-permute-done | bytes 262176 | tf_op jit(solution)/shard_map/ppermute | solution.py:360
  21.0 0.7 %shard_map.119 = (bf16[256,1152]{1,0:T(8,128)(2,1)S(1)}, bf16[128,1152]{1,0:T(8,128)(2,1)S(1)}, bf16[128,1152]{1,0:T(8,128)(2,1)S(1)}) custom-call(bf16[1024,144]{1,0:T(8,128)(2,1)S(1)} %get-tuple-element.73.mine, bf16[1024,144]{1,0:T(8,128)(2,1)S(1)} %collective-permute-done.6.got, bf16[144,1024]{1,0:T(8,128)(2,1)S(1)} %get-tuple-element.62.factor_ref.refs_0_, ...), custom_call_target="tpu_custom_call" | custom-call | tf_op jit(solution)/shard_map/pallas_call | solution.py:46
  21.7 1.6 %collective-permute-start.17 = (bf16[128,1152]{1,0:T(8,128)(2,1)S(1)}, bf16[128,1152]{1,0:T(8,128)(2,1)S(1)}, u32[]{:S(2)}, u32[]{:S(2)}) collective-permute-start(bf16[128,1152]{1,0:T(8,128)(2,1)S(1)} %get-tuple-element.89), channel_id=1, source_target_pairs={{0,8},{4,12},{8,0},{12,4},{16,24},{20,28},{24,16},{28,20},{1,9},{5... | collective-permute-start | bytes 884744 | tf_op jit(solution)/shard_map/ppermute | solution.py:360
  23.2 0.5 collective-permute-start.18
  23.8 0.7 %shard_map.115 = (bf16[256,1024]{1,0:T(8,128)(2,1)S(1)}, bf16[128,1024]{1,0:T(8,128)(2,1)S(1)}, bf16[128,1024]{1,0:T(8,128)(2,1)S(1)}) custom-call(bf16[1024,144]{1,0:T(8,128)(2,1)S(1)} %get-tuple-element.73.mine, bf16[1024,144]{1,0:T(8,128)(2,1)S(1)} %collective-permute-done.6.got, bf16[144,1024]{1,0:T(8,128)(2,1)S(1)} %get-tuple-element.62.factor_ref.refs_0_, ...), custom_call_target="tpu_custom_call" | custom-call | tf_op jit(solution)/shard_map/pallas_call | solution.py:46
  24.5 1.6 %collective-permute-start.8 = (bf16[128,1024]{1,0:T(8,128)(2,1)S(1)}, bf16[128,1024]{1,0:T(8,128)(2,1)S(1)}, u32[]{:S(2)}, u32[]{:S(2)}) collective-permute-start(bf16[128,1024]{1,0:T(8,128)(2,1)S(1)} %get-tuple-element.76), channel_id=1, source_target_pairs={{0,8},{4,12},{8,0},{12,4},{16,24},{20,28},{24,16},{28,20},{1,9},{5... | collective-permute-start | bytes 786440 | tf_op jit(solution)/shard_map/ppermute | solution.py:360
  26.1 0.5 collective-permute-start.9
  26.6 5.1 %collective-permute-done.17.got_a = bf16[128,1152]{1,0:T(8,128)(2,1)S(1)} collective-permute-done((bf16[128,1152]{1,0:T(8,128)(2,1)S(1)}, bf16[128,1152]{1,0:T(8,128)(2,1)S(1)}, u32[]{:S(2)}, u32[]{:S(2)}) %collective-permute-start.17) | collective-permute-done | bytes 294944 | tf_op jit(solution)/shard_map/ppermute | solution.py:360
  31.6 1.5 %collective-permute-done.18.got_b = bf16[128,1152]{1,0:T(8,128)(2,1)S(1)} collective-permute-done((bf16[128,1152]{1,0:T(8,128)(2,1)S(1)}, bf16[128,1152]{1,0:T(8,128)(2,1)S(1)}, u32[]{:S(2)}, u32[]{:S(2)}) %collective-permute-start.18) | collective-permute-done | bytes 294944 | tf_op jit(solution)/shard_map/ppermute | solution.py:360
  33.1 0.1 shard_map.120
  33.3 0.6 collective-permute-start.19
  33.8 1.5 %collective-permute-start.20 = (bf16[64,1152]{1,0:T(8,128)(2,1)S(1)}, bf16[64,1152]{1,0:T(8,128)(2,1)S(1)}, u32[]{:S(2)}, u32[]{:S(2)}) collective-permute-start(bf16[64,1152]{1,0:T(8,128)(2,1)S(1)} %get-tuple-element.93), channel_id=1, source_target_pairs={{0,8},{4,12},{8,0},{12,4},{16,24},{20,28},{24,16},{28,20},{1,9},{5... | collective-permute-start | bytes 442376 | tf_op jit(solution)/shard_map/ppermute | solution.py:360
  35.4 3.4 %collective-permute-start.3 = (bf16[3,6,2,1536]{3,2,1,0:T(2,128)(2,1)S(1)}, bf16[3,6,2,1536]{3,2,1,0:T(2,128)(2,1)S(1)}, u32[]{:S(2)}, u32[]{:S(2)}) collective-permute-start(bf16[3,6,2,1536]{3,2,1,0:T(2,128)(2,1)S(1)} %get-tuple-element.67), channel_id=1, source_target_pairs={{0,1},{1,2},{2,3},{3,0},{4,5},{5,6},{6,7},{7,4},{8,9},{9,10},{10,1... | collective-permute-start | bytes 331784 | tf_op jit(solution)/shard_map/ppermute | solution.py:429
  38.8 0.1 shard_map.116
  38.9 3.4 %collective-permute-start.10 = (bf16[64,1024]{1,0:T(8,128)(2,1)S(1)}, bf16[64,1024]{1,0:T(8,128)(2,1)S(1)}, u32[]{:S(2)}, u32[]{:S(2)}) collective-permute-start(bf16[64,1024]{1,0:T(8,128)(2,1)S(1)} %get-tuple-element.79), channel_id=1, source_target_pairs={{0,1},{1,0},{2,3},{3,2},{4,5},{5,4},{6,7},{7,6},{8,9},{9,8},{10,11... | collective-permute-start | bytes 393224 | tf_op jit(solution)/shard_map/ppermute | solution.py:366
  42.3 0.5 collective-permute-done.3.q1
  42.8 1.1 %collective-permute-start.12 = (bf16[64,1024]{1,0:T(8,128)(2,1)S(1)}, bf16[64,1024]{1,0:T(8,128)(2,1)S(1)}, u32[]{:S(2)}, u32[]{:S(2)}) collective-permute-start(bf16[64,1024]{1,0:T(8,128)(2,1)S(1)} %get-tuple-element.81), channel_id=1, source_target_pairs={{0,3},{1,2},{2,1},{3,0},{4,7},{5,6},{6,5},{7,4},{8,11},{9,10},{10,... | collective-permute-start | bytes 393224 | tf_op jit(solution)/shard_map/ppermute | solution.py:366
  43.9 3.9 %collective-permute-start.5 = (bf16[3,6,2,1536]{3,2,1,0:T(2,128)(2,1)S(1)}, bf16[3,6,2,1536]{3,2,1,0:T(2,128)(2,1)S(1)}, u32[]{:S(2)}, u32[]{:S(2)}) collective-permute-start(bf16[3,6,2,1536]{3,2,1,0:T(2,128)(2,1)S(1)} %get-tuple-element.69), channel_id=1, source_target_pairs={{0,5},{1,6},{2,7},{3,4},{4,9},{5,10},{6,11},{7,8},{8,13},{9,14},{1... | collective-permute-start | bytes 331784 | tf_op jit(solution)/shard_map/ppermute | solution.py:429
  47.8 0.1 shard_map.121
  47.9 1.8 %collective-permute-start.21 = (bf16[32,1152]{1,0:T(8,128)(2,1)S(1)}, bf16[32,1152]{1,0:T(8,128)(2,1)S(1)}, u32[]{:S(2)}, u32[]{:S(2)}) collective-permute-start(bf16[32,1152]{1,0:T(8,128)(2,1)S(1)} %get-tuple-element.95), channel_id=1, source_target_pairs={{0,1},{1,0},{2,3},{3,2},{4,5},{5,4},{6,7},{7,6},{8,9},{9,8},{10,11... | collective-permute-start | bytes 221192 | tf_op jit(solution)/shard_map/ppermute | solution.py:366
  49.7 3.4 %collective-permute-done.11.refs_2_ = bf16[64,1024]{1,0:T(8,128)(2,1)S(1)} collective-permute-done((bf16[64,1024]{1,0:T(8,128)(2,1)S(1)}, bf16[64,1024]{1,0:T(8,128)(2,1)S(1)}, u32[]{:S(2)}, u32[]{:S(2)}) %collective-permute-start.11) | collective-permute-done | bytes 131104 | tf_op jit(solution)/shard_map/ppermute | solution.py:366
  53.1 3.8 %collective-permute-start.22 = (bf16[32,1152]{1,0:T(8,128)(2,1)S(1)}, bf16[32,1152]{1,0:T(8,128)(2,1)S(1)}, u32[]{:S(2)}, u32[]{:S(2)}) collective-permute-start(bf16[32,1152]{1,0:T(8,128)(2,1)S(1)} %get-tuple-element.96), channel_id=1, source_target_pairs={{0,2},{1,3},{2,0},{3,1},{4,6},{5,7},{6,4},{7,5},{8,10},{9,11},{10,... | collective-permute-start | bytes 221192 | tf_op jit(solution)/shard_map/ppermute | solution.py:366
  56.9 1.2 %collective-permute-done.12.refs_3_ = bf16[64,1024]{1,0:T(8,128)(2,1)S(1)} collective-permute-done((bf16[64,1024]{1,0:T(8,128)(2,1)S(1)}, bf16[64,1024]{1,0:T(8,128)(2,1)S(1)}, u32[]{:S(2)}, u32[]{:S(2)}) %collective-permute-start.12) | collective-permute-done | bytes 131104 | tf_op jit(solution)/shard_map/ppermute | solution.py:366
  58.2 2.5 %collective-permute-start.23 = (bf16[32,1152]{1,0:T(8,128)(2,1)S(1)}, bf16[32,1152]{1,0:T(8,128)(2,1)S(1)}, u32[]{:S(2)}, u32[]{:S(2)}) collective-permute-start(bf16[32,1152]{1,0:T(8,128)(2,1)S(1)} %get-tuple-element.97), channel_id=1, source_target_pairs={{0,3},{1,2},{2,1},{3,0},{4,7},{5,6},{6,5},{7,4},{8,11},{9,10},{10,... | collective-permute-start | bytes 221192 | tf_op jit(solution)/shard_map/ppermute | solution.py:366
  60.6 0.1 shard_map.117
  60.7 0.0 collective-permute-done.4.q2
  60.7 1.2 %collective-permute-start.13 = (bf16[32,1024]{1,0:T(8,128)(2,1)S(1)}, bf16[32,1024]{1,0:T(8,128)(2,1)S(1)}, u32[]{:S(2)}, u32[]{:S(2)}) collective-permute-start(bf16[32,1024]{1,0:T(8,128)(2,1)S(1)} %get-tuple-element.83), channel_id=1, source_target_pairs={{0,16},{4,20},{8,24},{12,28},{16,0},{20,4},{24,8},{28,12},{1,17},{... | collective-permute-start | bytes 196616 | tf_op jit(solution)/shard_map/ppermute | solution.py:360
  62.0 1.4 %collective-permute-start.14 = (bf16[32,1024]{1,0:T(8,128)(2,1)S(1)}, bf16[32,1024]{1,0:T(8,128)(2,1)S(1)}, u32[]{:S(2)}, u32[]{:S(2)}) collective-permute-start(bf16[32,1024]{1,0:T(8,128)(2,1)S(1)} %get-tuple-element.84), channel_id=1, source_target_pairs={{0,8},{4,12},{8,0},{12,4},{16,24},{20,28},{24,16},{28,20},{1,9},{5... | collective-permute-start | bytes 196616 | tf_op jit(solution)/shard_map/ppermute | solution.py:360
  63.4 1.2 %shard_map.114 = (bf16[6,12,2,1024]{3,2,1,0:T(2,128)(2,1)}, bf16[6,12,2,1024]{3,2,1,0:T(2,128)(2,1)}) custom-call(bf16[3,6,2,1536]{3,2,1,0:T(2,128)(2,1)S(1)} %get-tuple-element.66.q0, bf16[3,6,2,1536]{3,2,1,0:T(2,128)(2,1)S(1)} %collective-permute-done.3.q1, bf16[3,6,2,1536]{3,2,1,0:T(2,128)(2,1)S(1)} %collective-permute-done.4.q2, ...), custom_call_target="tpu_custom_call" | custom-call | tf_op jit(solution)/shard_map/pallas_call | solution.py:46
  64.6 0.5 collective-permute-done.13.got_a
  65.1 1.2 %collective-permute-done.14.got_b = bf16[32,1024]{1,0:T(8,128)(2,1)S(1)} collective-permute-done((bf16[32,1024]{1,0:T(8,128)(2,1)S(1)}, bf16[32,1024]{1,0:T(8,128)(2,1)S(1)}, u32[]{:S(2)}, u32[]{:S(2)}) %collective-permute-start.14) | collective-permute-done | bytes 65568 | tf_op jit(solution)/shard_map/ppermute | solution.py:360
  66.2 0.6 shard_map.118
  66.9 0.7 %shard_map.122 = (f32[32,1536]{1,0:T(8,128)}, f32[1,32]{1,0:T(1,128)}, f32[1,32]{1,0:T(1,128)}) custom-call(f32[32,512]{1,0:T(8,128)S(1)} %get-tuple-element.85.value_ref, bf16[32,1152]{1,0:T(8,128)(2,1)S(1)} %get-tuple-element.94.refs_0_, bf16[32,1152]{1,0:T(8,128)(2,1)S(1)} %collective-permute-done.21.refs_1_, ...), custom_call_target="tpu_custom_call" | custom-call | tf_op jit(solution)/shard_map/pallas_call | solution.py:46
  (15 shorter events, 0.0 us)
Async XLA Ops:
  1.8 6.2 %collective-permute-start = (bf16[2,3,6,2,1024]{4,3,2,1,0:T(2,128)(2,1)S(1)}, bf16[2,3,6,2,1024]{4,3,2,1,0:T(2,128)(2,1)S(1)}, u32[]{:S(2)}, u32[]{:S(2)}) collective-permute-start(bf16[2,3,6,2,1024]{4,3,2,1,0:T(2,128)(2,1)S(1)} %get-tuple-element.55), channel_id=1, source_target_pairs={{0,3},{1,0},{2,1},{3,2},{4,7},{5,4},{6,5},{7,6},{8,11},{9,8},{10,9... | collective-permute-start | bytes 442376 | tf_op jit(solution)/shard_map/ppermute | solution.py:429
  2.4 5.7 %collective-permute-start.1 = (bf16[2,3,6,2,1024]{4,3,2,1,0:T(2,128)(2,1)S(1)}, bf16[2,3,6,2,1024]{4,3,2,1,0:T(2,128)(2,1)S(1)}, u32[]{:S(2)}, u32[]{:S(2)}) collective-permute-start(bf16[2,3,6,2,1024]{4,3,2,1,0:T(2,128)(2,1)S(1)} %get-tuple-element.56), channel_id=1, source_target_pairs={{0,28},{1,29},{2,30},{3,31},{4,0},{5,1},{6,2},{7,3},{8,4},{9,5},{1... | collective-permute-start | bytes 442376 | tf_op jit(solution)/shard_map/ppermute | solution.py:429
  4.0 6.1 %collective-permute-start.2 = (bf16[2,3,6,2,1024]{4,3,2,1,0:T(2,128)(2,1)S(1)}, bf16[2,3,6,2,1024]{4,3,2,1,0:T(2,128)(2,1)S(1)}, u32[]{:S(2)}, u32[]{:S(2)}) collective-permute-start(bf16[2,3,6,2,1024]{4,3,2,1,0:T(2,128)(2,1)S(1)} %get-tuple-element.57), channel_id=1, source_target_pairs={{0,31},{1,28},{2,29},{3,30},{4,3},{5,0},{6,1},{7,2},{8,7},{9,4},{1... | collective-permute-start | bytes 442376 | tf_op jit(solution)/shard_map/ppermute | solution.py:429
  15.4 5.6 %collective-permute-start.15 = (bf16[144,1024]{1,0:T(8,128)(2,1)S(1)}, bf16[144,1024]{1,0:T(8,128)(2,1)S(1)}, u32[]{:S(2)}, u32[]{:S(2)}) collective-permute-start(bf16[144,1024]{1,0:T(8,128)(2,1)S(1)} %shard_map.112.late_ref.refs_2_), channel_id=1, source_target_pairs={{0,4},{4,0},{8,12},{12,8},{16,20},{20,16},{24,28},{28,24},{1,5},{5... | collective-permute-start | bytes 884744 | tf_op jit(solution)/shard_map/ppermute | solution.py:360
  16.8 4.2 %collective-permute-start.7 = (bf16[144,1024]{1,0:T(8,128)(2,1)S(1)}, bf16[144,1024]{1,0:T(8,128)(2,1)S(1)}, u32[]{:S(2)}, u32[]{:S(2)}) collective-permute-start(bf16[144,1024]{1,0:T(8,128)(2,1)S(1)} %get-tuple-element.62.factor_ref.refs_0_), channel_id=1, source_target_pairs={{0,4},{4,0},{8,12},{12,8},{16,20},{20,16},{24,28},{28,24},{1,5},{5... | collective-permute-start | bytes 884744 | tf_op jit(solution)/shard_map/ppermute | solution.py:360
  16.9 4.1 %collective-permute-start.6 = (bf16[1024,144]{1,0:T(8,128)(2,1)S(1)}, bf16[1024,144]{1,0:T(8,128)(2,1)S(1)}, u32[]{:S(2)}, u32[]{:S(2)}) collective-permute-start(bf16[1024,144]{1,0:T(8,128)(2,1)S(1)} %get-tuple-element.74), channel_id=1, source_target_pairs={{0,4},{4,0},{8,12},{12,8},{16,20},{20,16},{24,28},{28,24},{1,5},{5... | collective-permute-start | bytes 884744 | tf_op jit(solution)/shard_map/ppermute | solution.py:360
  19.4 1.6 %collective-permute-start.16 = (f32[512,128]{1,0:T(8,128)S(1)}, f32[512,128]{1,0:T(8,128)S(1)}, u32[]{:S(2)}, u32[]{:S(2)}) collective-permute-start(f32[512,128]{1,0:T(8,128)S(1)} %get-tuple-element.87), channel_id=1, source_target_pairs={{0,4},{4,0},{8,12},{12,8},{16,20},{20,16},{24,28},{28,24},{1,5},{5... | collective-permute-start | bytes 786440 | tf_op jit(solution)/shard_map/ppermute | solution.py:360
  21.7 9.9 %collective-permute-start.17 = (bf16[128,1152]{1,0:T(8,128)(2,1)S(1)}, bf16[128,1152]{1,0:T(8,128)(2,1)S(1)}, u32[]{:S(2)}, u32[]{:S(2)}) collective-permute-start(bf16[128,1152]{1,0:T(8,128)(2,1)S(1)} %get-tuple-element.89), channel_id=1, source_target_pairs={{0,8},{4,12},{8,0},{12,4},{16,24},{20,28},{24,16},{28,20},{1,9},{5... | collective-permute-start | bytes 884744 | tf_op jit(solution)/shard_map/ppermute | solution.py:360
  23.2 9.9 %collective-permute-start.18 = (bf16[128,1152]{1,0:T(8,128)(2,1)S(1)}, bf16[128,1152]{1,0:T(8,128)(2,1)S(1)}, u32[]{:S(2)}, u32[]{:S(2)}) collective-permute-start(bf16[128,1152]{1,0:T(8,128)(2,1)S(1)} %get-tuple-element.90), channel_id=1, source_target_pairs={{0,16},{4,20},{8,24},{12,28},{16,0},{20,4},{24,8},{28,12},{1,17},{... | collective-permute-start | bytes 884744 | tf_op jit(solution)/shard_map/ppermute | solution.py:360
  24.5 14.3 %collective-permute-start.8 = (bf16[128,1024]{1,0:T(8,128)(2,1)S(1)}, bf16[128,1024]{1,0:T(8,128)(2,1)S(1)}, u32[]{:S(2)}, u32[]{:S(2)}) collective-permute-start(bf16[128,1024]{1,0:T(8,128)(2,1)S(1)} %get-tuple-element.76), channel_id=1, source_target_pairs={{0,8},{4,12},{8,0},{12,4},{16,24},{20,28},{24,16},{28,20},{1,9},{5... | collective-permute-start | bytes 786440 | tf_op jit(solution)/shard_map/ppermute | solution.py:360
  26.1 12.7 %collective-permute-start.9 = (bf16[128,1024]{1,0:T(8,128)(2,1)S(1)}, bf16[128,1024]{1,0:T(8,128)(2,1)S(1)}, u32[]{:S(2)}, u32[]{:S(2)}) collective-permute-start(bf16[128,1024]{1,0:T(8,128)(2,1)S(1)} %get-tuple-element.77), channel_id=1, source_target_pairs={{0,16},{4,20},{8,24},{12,28},{16,0},{20,4},{24,8},{28,12},{1,17},{... | collective-permute-start | bytes 786440 | tf_op jit(solution)/shard_map/ppermute | solution.py:360
  33.3 10.6 %collective-permute-start.19 = (bf16[64,1152]{1,0:T(8,128)(2,1)S(1)}, bf16[64,1152]{1,0:T(8,128)(2,1)S(1)}, u32[]{:S(2)}, u32[]{:S(2)}) collective-permute-start(bf16[64,1152]{1,0:T(8,128)(2,1)S(1)} %get-tuple-element.92), channel_id=1, source_target_pairs={{0,16},{4,20},{8,24},{12,28},{16,0},{20,4},{24,8},{28,12},{1,17},{... | collective-permute-start | bytes 442376 | tf_op jit(solution)/shard_map/ppermute | solution.py:360
  33.8 10.0 %collective-permute-start.20 = (bf16[64,1152]{1,0:T(8,128)(2,1)S(1)}, bf16[64,1152]{1,0:T(8,128)(2,1)S(1)}, u32[]{:S(2)}, u32[]{:S(2)}) collective-permute-start(bf16[64,1152]{1,0:T(8,128)(2,1)S(1)} %get-tuple-element.93), channel_id=1, source_target_pairs={{0,8},{4,12},{8,0},{12,4},{16,24},{20,28},{24,16},{28,20},{1,9},{5... | collective-permute-start | bytes 442376 | tf_op jit(solution)/shard_map/ppermute | solution.py:360
  35.4 7.4 %collective-permute-start.3 = (bf16[3,6,2,1536]{3,2,1,0:T(2,128)(2,1)S(1)}, bf16[3,6,2,1536]{3,2,1,0:T(2,128)(2,1)S(1)}, u32[]{:S(2)}, u32[]{:S(2)}) collective-permute-start(bf16[3,6,2,1536]{3,2,1,0:T(2,128)(2,1)S(1)} %get-tuple-element.67), channel_id=1, source_target_pairs={{0,1},{1,2},{2,3},{3,0},{4,5},{5,6},{6,7},{7,4},{8,9},{9,10},{10,1... | collective-permute-start | bytes 331784 | tf_op jit(solution)/shard_map/ppermute | solution.py:429
  38.9 9.0 %collective-permute-start.10 = (bf16[64,1024]{1,0:T(8,128)(2,1)S(1)}, bf16[64,1024]{1,0:T(8,128)(2,1)S(1)}, u32[]{:S(2)}, u32[]{:S(2)}) collective-permute-start(bf16[64,1024]{1,0:T(8,128)(2,1)S(1)} %get-tuple-element.79), channel_id=1, source_target_pairs={{0,1},{1,0},{2,3},{3,2},{4,5},{5,4},{6,7},{7,6},{8,9},{9,8},{10,11... | collective-permute-start | bytes 393224 | tf_op jit(solution)/shard_map/ppermute | solution.py:366
  42.3 10.8 %collective-permute-start.11 = (bf16[64,1024]{1,0:T(8,128)(2,1)S(1)}, bf16[64,1024]{1,0:T(8,128)(2,1)S(1)}, u32[]{:S(2)}, u32[]{:S(2)}) collective-permute-start(bf16[64,1024]{1,0:T(8,128)(2,1)S(1)} %get-tuple-element.80), channel_id=1, source_target_pairs={{0,2},{1,3},{2,0},{3,1},{4,6},{5,7},{6,4},{7,5},{8,10},{9,11},{10,... | collective-permute-start | bytes 393224 | tf_op jit(solution)/shard_map/ppermute | solution.py:366
  42.8 15.4 %collective-permute-start.12 = (bf16[64,1024]{1,0:T(8,128)(2,1)S(1)}, bf16[64,1024]{1,0:T(8,128)(2,1)S(1)}, u32[]{:S(2)}, u32[]{:S(2)}) collective-permute-start(bf16[64,1024]{1,0:T(8,128)(2,1)S(1)} %get-tuple-element.81), channel_id=1, source_target_pairs={{0,3},{1,2},{2,1},{3,0},{4,7},{5,6},{6,5},{7,4},{8,11},{9,10},{10,... | collective-permute-start | bytes 393224 | tf_op jit(solution)/shard_map/ppermute | solution.py:366
  43.9 16.8 %collective-permute-start.4 = (bf16[3,6,2,1536]{3,2,1,0:T(2,128)(2,1)S(1)}, bf16[3,6,2,1536]{3,2,1,0:T(2,128)(2,1)S(1)}, u32[]{:S(2)}, u32[]{:S(2)}) collective-permute-start(bf16[3,6,2,1536]{3,2,1,0:T(2,128)(2,1)S(1)} %get-tuple-element.68), channel_id=1, source_target_pairs={{0,4},{1,5},{2,6},{3,7},{4,8},{5,9},{6,10},{7,11},{8,12},{9,13},{1... | collective-permute-start | bytes 331784 | tf_op jit(solution)/shard_map/ppermute | solution.py:429
  43.9 18.1 %collective-permute-start.5 = (bf16[3,6,2,1536]{3,2,1,0:T(2,128)(2,1)S(1)}, bf16[3,6,2,1536]{3,2,1,0:T(2,128)(2,1)S(1)}, u32[]{:S(2)}, u32[]{:S(2)}) collective-permute-start(bf16[3,6,2,1536]{3,2,1,0:T(2,128)(2,1)S(1)} %get-tuple-element.69), channel_id=1, source_target_pairs={{0,5},{1,6},{2,7},{3,4},{4,9},{5,10},{6,11},{7,8},{8,13},{9,14},{1... | collective-permute-start | bytes 331784 | tf_op jit(solution)/shard_map/ppermute | solution.py:429
  47.9 19.0 %collective-permute-start.21 = (bf16[32,1152]{1,0:T(8,128)(2,1)S(1)}, bf16[32,1152]{1,0:T(8,128)(2,1)S(1)}, u32[]{:S(2)}, u32[]{:S(2)}) collective-permute-start(bf16[32,1152]{1,0:T(8,128)(2,1)S(1)} %get-tuple-element.95), channel_id=1, source_target_pairs={{0,1},{1,0},{2,3},{3,2},{4,5},{5,4},{6,7},{7,6},{8,9},{9,8},{10,11... | collective-permute-start | bytes 221192 | tf_op jit(solution)/shard_map/ppermute | solution.py:366
  53.1 13.8 %collective-permute-start.22 = (bf16[32,1152]{1,0:T(8,128)(2,1)S(1)}, bf16[32,1152]{1,0:T(8,128)(2,1)S(1)}, u32[]{:S(2)}, u32[]{:S(2)}) collective-permute-start(bf16[32,1152]{1,0:T(8,128)(2,1)S(1)} %get-tuple-element.96), channel_id=1, source_target_pairs={{0,2},{1,3},{2,0},{3,1},{4,6},{5,7},{6,4},{7,5},{8,10},{9,11},{10,... | collective-permute-start | bytes 221192 | tf_op jit(solution)/shard_map/ppermute | solution.py:366
  58.2 8.7 %collective-permute-start.23 = (bf16[32,1152]{1,0:T(8,128)(2,1)S(1)}, bf16[32,1152]{1,0:T(8,128)(2,1)S(1)}, u32[]{:S(2)}, u32[]{:S(2)}) collective-permute-start(bf16[32,1152]{1,0:T(8,128)(2,1)S(1)} %get-tuple-element.97), channel_id=1, source_target_pairs={{0,3},{1,2},{2,1},{3,0},{4,7},{5,6},{6,5},{7,4},{8,11},{9,10},{10,... | collective-permute-start | bytes 221192 | tf_op jit(solution)/shard_map/ppermute | solution.py:366
  60.7 4.3 %collective-permute-start.13 = (bf16[32,1024]{1,0:T(8,128)(2,1)S(1)}, bf16[32,1024]{1,0:T(8,128)(2,1)S(1)}, u32[]{:S(2)}, u32[]{:S(2)}) collective-permute-start(bf16[32,1024]{1,0:T(8,128)(2,1)S(1)} %get-tuple-element.83), channel_id=1, source_target_pairs={{0,16},{4,20},{8,24},{12,28},{16,0},{20,4},{24,8},{28,12},{1,17},{... | collective-permute-start | bytes 196616 | tf_op jit(solution)/shard_map/ppermute | solution.py:360
  62.0 4.3 %collective-permute-start.14 = (bf16[32,1024]{1,0:T(8,128)(2,1)S(1)}, bf16[32,1024]{1,0:T(8,128)(2,1)S(1)}, u32[]{:S(2)}, u32[]{:S(2)}) collective-permute-start(bf16[32,1024]{1,0:T(8,128)(2,1)S(1)} %get-tuple-element.84), channel_id=1, source_target_pairs={{0,8},{4,12},{8,0},{12,4},{16,24},{20,28},{24,16},{28,20},{1,9},{5... | collective-permute-start | bytes 196616 | tf_op jit(solution)/shard_map/ppermute | solution.py:360

commit v7 on v6

--- a/solution.py
+++ b/solution.py
@@ -330,19 +330,14 @@
     send_b[...] = added(*(item[size:, :] for item in pieces[per_side:])).astype(BF16)
 
 
-def early_end_body(factor, base, got_a, got_b, value_ref, out_ref):
-    total = added(base[...], got_a[...], got_b[...]) * factor
-    inner = out_ref.shape[1]
-    out_ref[...] = total[:, :inner]
-    value_ref[...] = total[:, inner:]
-
-
-def late_end_body(factor, value_ref, *refs):
-    pieces, (qkv_ref, gain_ref, bias_ref) = refs[:-3], refs[-3:]
+def end_body(factor, base, got_a, got_b, *refs):
+    pieces, (qkv_ref, out_ref, gain_ref, bias_ref) = refs[:-4], refs[-4:]
+    early = added(base[...], got_a[...], got_b[...]) * factor
     total = added(*(item[...] for item in pieces)) * factor
     cols = total.shape[1] - LANES
     inner = cols // len(LATE)
-    sources = {block: value_ref[:, i * inner : (i + 1) * inner] for i, block in enumerate(EARLY[1:])}
+    sources = {block: early[:, i * inner : (i + 1) * inner] for i, block in enumerate(EARLY)}
+    out_ref[...] = sources[0]
     sources |= {block: total[:, i * inner : (i + 1) * inner] for i, block in enumerate(LATE)}
     for place, block in enumerate((2, 3, 1)):
         qkv_ref[:, place * inner : (place + 1) * inner] = sources[block]
@@ -368,7 +363,7 @@
     ]
 
 
-def sum_early(both, send_a, send_b, lon_count, factor):
+def sum_early(both, send_a, send_b, lon_count):
     quarter, cols = send_a.shape
     size = quarter // lon_count
     got_a, got_b = swap(send_a, 2), swap(send_b, 4)
@@ -378,14 +373,10 @@
         meet_body, [((size, cols), F32)] + [((size, cols), BF16)] * 2, pieces
     )
     got_a, got_b = swap(send_a, 4), swap(send_b, 2)
-    return call(
-        functools.partial(early_end_body, factor),
-        [((size, cols - cols // len(EARLY)), F32), ((size, cols // len(EARLY)), F32)],
-        (base, got_a, got_b), near_out=1,
-    )
-
-
-def sum_late(both, send_a, send_b, value, lon_count, factor):
+    return base, got_a, got_b
+
+
+def sum_late(both, send_a, send_b, lon_count):
     quarter, cols = send_a.shape
     part = quarter // 2
     size = 2 * part // lon_count
@@ -396,11 +387,7 @@
     got_a, got_b = swap(send_a, 4), swap(send_b, 2)
     pieces = call(third_body, [((size, cols), BF16)] * lon_count, (both, got_a, got_b))
     pieces = turn(pieces)
-    return call(
-        functools.partial(late_end_body, factor),
-        [((size, cols - LANES + value.shape[1]), F32)] + [((1, size), F32)] * 2,
-        (value, *pieces), near_out=0,
-    )
+    return pieces
 
 
 def device_step(tokens, layer_norm_gain, layer_norm_bias, w_qkv, w_out, output_cotangent):
@@ -426,7 +413,9 @@
         moves = {}
         for place in by_turn:
             a, b = steps[place]
-            moves[place] = lax.ppermute(items[place], ("lat", "lon"), moved(sign * a, sign * b))
+            moves[place] = lax.ppermute(
+                items[place], ("lat", "lon"), moved(sign * a, sign * b)
+            )
         return [moves[place] for place in range(3)]
 
     grid = (lat_rows, lon_cols, levels, width)
@@ -498,8 +487,12 @@
             late_body, shapes(len(LATE) * inner + LANES),
             (mine, got, *factors, sums, sums_got),
         )
-        value, d_out = sum_early(*early, lon_count, norm_factor)
-        d_qkv, gain, bias = sum_late(*late, value, lon_count, norm_factor)
+        parts = (*sum_early(*early, lon_count), *sum_late(*late, lon_count))
+        d_qkv, d_out, gain, bias = call(
+            functools.partial(end_body, norm_factor),
+            [((share, n * inner), F32) for n in (3, 1)] + [((1, share), F32)] * 2,
+            parts, near_out=0,
+        )
     else:
         half = width // 2
         normed_t = jnp.concatenate([mine[:half], peer[:half]], axis=0)

time: 67.8 us -> 67.2 us (level)
  Pallas kernels: 15.3 us -> 14.6 us
    pallas_call x14 -> x13, Pallas kernels: 15.3 us -> 14.6 us  [call(): pl.pallas_call(body, out_shape=[pltpu.VMEM(s, d) if i < near_out else jax...]
  transfers between devices with their start and end apart: 24 -> 24, of which waited for: 10 -> 10; matrix products, arithmetic and copies ran while one was open for 0% -> 0% of each run, Pallas kernels for 11% -> 10%
where the time goes in v7:
time: 67.2 us; the launch traced here: 67 us
  starting transfers between devices  33.8 us (50%)
  waiting for transfers between devices  17.8 us (26%)
  Pallas kernels  14.6 us (22%)
  between operations  0.75 us (1%)
    pallas_call x13, Pallas kernels, call(): pl.pallas_call(body, out_shape=[pltpu.VMEM(s, d) if i < near_out else jax...  14.6 us
    ppermute x6, starting transfers between devices, turn(): lax.ppermute(pieces[k], 'lon', [(i, i ^ k) for i in range(count)])  12.6 us
    ppermute x12, starting transfers between devices, swap(): return lax.ppermute(value, 'lat', xor_pairs(bit))  11 us
    ppermute x6, starting transfers between devices, moved_all(): lax.ppermute(items[place], ('lat', 'lon'), moved(sign * a, sign * b))  10.3 us
    ppermute x12, waiting for transfers between devices, swap(): return lax.ppermute(value, 'lat', xor_pairs(bit))  9.69 us
    ppermute x6, waiting for transfers between devices, turn(): lax.ppermute(pieces[k], 'lon', [(i, i ^ k) for i in range(count)])  4.63 us
    ppermute x6, waiting for transfers between devices, moved_all(): lax.ppermute(items[place], ('lat', 'lon'), moved(sign * a, sign * b))  3.46 us
  transfers between devices with their start and end apart: 24, of which 10 were waited for; matrix products, arithmetic and copies ran while one was open for 0% of the time, Pallas kernels for 10%

profile of v7, /device:TPU:16, one launch (start us, length us, event | category | flops | bytes accessed | tf_op | source)
XLA Modules:
  0.0 67.0 jit_solution(2614272259633921331)
XLA Ops:
  0.6 1.2 %shard_map.109 = (bf16[2,3,6,2,1024]{4,3,2,1,0:T(2,128)(2,1)S(1)}, bf16[2,3,6,2,1024]{4,3,2,1,0:T(2,128)(2,1)S(1)}, bf16[2,3,6,2,1024]{4,3,2,1,0:T(2,128)(2,1)S(1)}, bf16[2,3,6,2,1024]{4,3,2,1,0:T(2,128)(2,1)S(1)}) custom-call(bf16[6,12,2,1024]{3,2,1,0:T(2,128)(2,1)} %bitcast.9, bf16[6,12,2,1024]{3,2,1,0:T(2,128)(2,1)} %bitcast.11), custom_call_target="tpu_custom_call" | custom-call | tf_op jit(solution)/shard_map/pallas_call | solution.py:46
  1.8 0.5 collective-permute-start
  2.4 1.6 %collective-permute-start.1 = (bf16[2,3,6,2,1024]{4,3,2,1,0:T(2,128)(2,1)S(1)}, bf16[2,3,6,2,1024]{4,3,2,1,0:T(2,128)(2,1)S(1)}, u32[]{:S(2)}, u32[]{:S(2)}) collective-permute-start(bf16[2,3,6,2,1024]{4,3,2,1,0:T(2,128)(2,1)S(1)} %get-tuple-element.55), channel_id=1, source_target_pairs={{0,28},{1,29},{2,30},{3,31},{4,0},{5,1},{6,2},{7,3},{8,4},{9,5},{1... | collective-permute-start | bytes 442376 | tf_op jit(solution)/shard_map/ppermute | solution.py:416
  4.0 0.8 %collective-permute-start.2 = (bf16[2,3,6,2,1024]{4,3,2,1,0:T(2,128)(2,1)S(1)}, bf16[2,3,6,2,1024]{4,3,2,1,0:T(2,128)(2,1)S(1)}, u32[]{:S(2)}, u32[]{:S(2)}) collective-permute-start(bf16[2,3,6,2,1024]{4,3,2,1,0:T(2,128)(2,1)S(1)} %get-tuple-element.56), channel_id=1, source_target_pairs={{0,31},{1,28},{2,29},{3,30},{4,3},{5,0},{6,1},{7,2},{8,7},{9,4},{1... | collective-permute-start | bytes 442376 | tf_op jit(solution)/shard_map/ppermute | solution.py:416
  4.8 2.3 %shard_map.110 = (bf16[1024,1536]{1,0:T(8,128)(2,1)S(1)}, bf16[512,1024]{1,0:T(8,128)(2,1)S(1)}, f32[1,1024]{1,0:T(1,128)S(1)}, f32[1,1024]{1,0:T(1,128)S(1)}, bf16[6,12,2,1024]{3,2,1,0:T(2,128)(2,1)S(1)}) custom-call(bf16[1024,1536]{1,0:T(8,128)(2,1)} %refs_0_.1, bf16[512,1024]{1,0:T(8,128)(2,1)} %refs_1_.1, f32[1,1024]{1,0:T(1,128)} %bitcast.12, ...), custom_call_target="tpu_custom_call" | custom-call | tf_op jit(solution)/shard_map/pallas_call | solution.py:46
  7.1 0.9 %collective-permute-done.r1 = bf16[2,3,6,2,1024]{4,3,2,1,0:T(2,128)(2,1)S(1)} collective-permute-done((bf16[2,3,6,2,1024]{4,3,2,1,0:T(2,128)(2,1)S(1)}, bf16[2,3,6,2,1024]{4,3,2,1,0:T(2,128)(2,1)S(1)}, u32[]{:S(2)}, u32[]{:S(2)}) %collective-permute-start) | collective-permute-done | bytes 147488 | tf_op jit(solution)/shard_map/ppermute | solution.py:416
  8.0 0.0 collective-permute-done.1.r2
  8.0 2.1 %collective-permute-done.2.r3 = bf16[2,3,6,2,1024]{4,3,2,1,0:T(2,128)(2,1)S(1)} collective-permute-done((bf16[2,3,6,2,1024]{4,3,2,1,0:T(2,128)(2,1)S(1)}, bf16[2,3,6,2,1024]{4,3,2,1,0:T(2,128)(2,1)S(1)}, u32[]{:S(2)}, u32[]{:S(2)}) %collective-permute-start.2) | collective-permute-done | bytes 147488 | tf_op jit(solution)/shard_map/ppermute | solution.py:416
  10.1 3.6 %shard_map.111 = (bf16[1024,144]{1,0:T(8,128)(2,1)S(1)}, bf16[1024,144]{1,0:T(8,128)(2,1)S(1)}, bf16[144,1024]{1,0:T(8,128)(2,1)S(1)}, bf16[144,512]{1,0:T(8,128...) custom-call(s32[2]{0:T(128)S(1)} %compare_select_fusion.places_ref, ...), custom_call_target="tpu_custom_call" | custom-call | tf_op jit(solution)/shard_map/pallas_call | solution.py:46
  13.7 1.7 %shard_map.112.late_ref.refs_2_ = bf16[144,1024]{1,0:T(8,128)(2,1)S(1)} custom-call(bf16[144,512]{1,0:T(8,128)(2,1)S(1)} %get-tuple-element.62.query_ref, bf16[144,1536]{1,0:T(8,128)(2,1)S(1)} %get-tuple-element.63.pair_ref, f32[8,144,144]{2,1,0:T(8,128)S(1)} %get-tuple-element.64.probs_ref), custom_call_target="tpu_custom_call" | custom-call | tf_op jit(solution)/shard_map/pallas_call | solution.py:46
  15.4 1.4 %collective-permute-start.15 = (bf16[144,1024]{1,0:T(8,128)(2,1)S(1)}, bf16[144,1024]{1,0:T(8,128)(2,1)S(1)}, u32[]{:S(2)}, u32[]{:S(2)}) collective-permute-start(bf16[144,1024]{1,0:T(8,128)(2,1)S(1)} %shard_map.112.late_ref.refs_2_), channel_id=1, source_target_pairs={{0,4},{4,0},{8,12},{12,8},{16,20},{20,16},{24,28},{28,24},{1,5},{5... | collective-permute-start | bytes 884744 | tf_op jit(solution)/shard_map/ppermute | solution.py:355
  16.8 0.1 collective-permute-start.7
  16.9 0.4 collective-permute-start.6
  17.3 2.1 %shard_map.113 = (bf16[3,6,2,1536]{3,2,1,0:T(2,128)(2,1)S(1)}, bf16[3,6,2,1536]{3,2,1,0:T(2,128)(2,1)S(1)}, bf16[3,6,2,1536]{3,2,1,0:T(2,128)(2,1)S(1)}, bf16[3,...) custom-call(s32[2]{0:T(128)S(1)} %compare_select_fusion.places_ref, ...), custom_call_target="tpu_custom_call" | custom-call | tf_op jit(solution)/shard_map/pallas_call | solution.py:46
  19.4 0.1 collective-permute-start.16
  19.5 1.5 %collective-permute-done.16.refs_5_ = f32[512,128]{1,0:T(8,128)S(1)} collective-permute-done((f32[512,128]{1,0:T(8,128)S(1)}, f32[512,128]{1,0:T(8,128)S(1)}, u32[]{:S(2)}, u32[]{:S(2)}) %collective-permute-start.16) | collective-permute-done | bytes 262176 | tf_op jit(solution)/shard_map/ppermute | solution.py:355
  21.0 0.0 collective-permute-done.15.refs_3_
  21.0 0.7 %shard_map.118 = (bf16[256,1152]{1,0:T(8,128)(2,1)S(1)}, bf16[128,1152]{1,0:T(8,128)(2,1)S(1)}, bf16[128,1152]{1,0:T(8,128)(2,1)S(1)}) custom-call(bf16[1024,144]{1,0:T(8,128)(2,1)S(1)} %get-tuple-element.72.mine, bf16[1024,144]{1,0:T(8,128)(2,1)S(1)} %collective-permute-done.6.got, bf16[144,1024]{1,0:T(8,128)(2,1)S(1)} %get-tuple-element.61.factor_ref.refs_0_, ...), custom_call_target="tpu_custom_call" | custom-call | tf_op jit(solution)/shard_map/pallas_call | solution.py:46
  21.7 1.6 %collective-permute-start.17 = (bf16[128,1152]{1,0:T(8,128)(2,1)S(1)}, bf16[128,1152]{1,0:T(8,128)(2,1)S(1)}, u32[]{:S(2)}, u32[]{:S(2)}) collective-permute-start(bf16[128,1152]{1,0:T(8,128)(2,1)S(1)} %get-tuple-element.87), channel_id=1, source_target_pairs={{0,8},{4,12},{8,0},{12,4},{16,24},{20,28},{24,16},{28,20},{1,9},{5... | collective-permute-start | bytes 884744 | tf_op jit(solution)/shard_map/ppermute | solution.py:355
  23.2 0.5 collective-permute-start.18
  23.8 0.7 %shard_map.115 = (bf16[256,1024]{1,0:T(8,128)(2,1)S(1)}, bf16[128,1024]{1,0:T(8,128)(2,1)S(1)}, bf16[128,1024]{1,0:T(8,128)(2,1)S(1)}) custom-call(bf16[1024,144]{1,0:T(8,128)(2,1)S(1)} %get-tuple-element.72.mine, bf16[1024,144]{1,0:T(8,128)(2,1)S(1)} %collective-permute-done.6.got, bf16[144,1024]{1,0:T(8,128)(2,1)S(1)} %get-tuple-element.61.factor_ref.refs_0_, ...), custom_call_target="tpu_custom_call" | custom-call | tf_op jit(solution)/shard_map/pallas_call | solution.py:46
  24.5 1.6 %collective-permute-start.8 = (bf16[128,1024]{1,0:T(8,128)(2,1)S(1)}, bf16[128,1024]{1,0:T(8,128)(2,1)S(1)}, u32[]{:S(2)}, u32[]{:S(2)}) collective-permute-start(bf16[128,1024]{1,0:T(8,128)(2,1)S(1)} %get-tuple-element.75), channel_id=1, source_target_pairs={{0,8},{4,12},{8,0},{12,4},{16,24},{20,28},{24,16},{28,20},{1,9},{5... | collective-permute-start | bytes 786440 | tf_op jit(solution)/shard_map/ppermute | solution.py:355
  26.1 0.5 collective-permute-start.9
  26.6 5.1 %collective-permute-done.17.got_a = bf16[128,1152]{1,0:T(8,128)(2,1)S(1)} collective-permute-done((bf16[128,1152]{1,0:T(8,128)(2,1)S(1)}, bf16[128,1152]{1,0:T(8,128)(2,1)S(1)}, u32[]{:S(2)}, u32[]{:S(2)}) %collective-permute-start.17) | collective-permute-done | bytes 294944 | tf_op jit(solution)/shard_map/ppermute | solution.py:355
  31.6 1.5 %collective-permute-done.18.got_b = bf16[128,1152]{1,0:T(8,128)(2,1)S(1)} collective-permute-done((bf16[128,1152]{1,0:T(8,128)(2,1)S(1)}, bf16[128,1152]{1,0:T(8,128)(2,1)S(1)}, u32[]{:S(2)}, u32[]{:S(2)}) %collective-permute-start.18) | collective-permute-done | bytes 294944 | tf_op jit(solution)/shard_map/ppermute | solution.py:355
  33.1 0.1 shard_map.119
  33.3 0.6 collective-permute-start.19
  33.8 1.5 %collective-permute-start.20 = (bf16[64,1152]{1,0:T(8,128)(2,1)S(1)}, bf16[64,1152]{1,0:T(8,128)(2,1)S(1)}, u32[]{:S(2)}, u32[]{:S(2)}) collective-permute-start(bf16[64,1152]{1,0:T(8,128)(2,1)S(1)} %get-tuple-element.91), channel_id=1, source_target_pairs={{0,8},{4,12},{8,0},{12,4},{16,24},{20,28},{24,16},{28,20},{1,9},{5... | collective-permute-start | bytes 442376 | tf_op jit(solution)/shard_map/ppermute | solution.py:355
  35.4 3.4 %collective-permute-start.3 = (bf16[3,6,2,1536]{3,2,1,0:T(2,128)(2,1)S(1)}, bf16[3,6,2,1536]{3,2,1,0:T(2,128)(2,1)S(1)}, u32[]{:S(2)}, u32[]{:S(2)}) collective-permute-start(bf16[3,6,2,1536]{3,2,1,0:T(2,128)(2,1)S(1)} %get-tuple-element.66), channel_id=1, source_target_pairs={{0,1},{1,2},{2,3},{3,0},{4,5},{5,6},{6,7},{7,4},{8,9},{9,10},{10,1... | collective-permute-start | bytes 331784 | tf_op jit(solution)/shard_map/ppermute | solution.py:416
  38.8 0.1 shard_map.116
  38.9 3.4 %collective-permute-start.10 = (bf16[64,1024]{1,0:T(8,128)(2,1)S(1)}, bf16[64,1024]{1,0:T(8,128)(2,1)S(1)}, u32[]{:S(2)}, u32[]{:S(2)}) collective-permute-start(bf16[64,1024]{1,0:T(8,128)(2,1)S(1)} %get-tuple-element.78), channel_id=1, source_target_pairs={{0,1},{1,0},{2,3},{3,2},{4,5},{5,4},{6,7},{7,6},{8,9},{9,8},{10,11... | collective-permute-start | bytes 393224 | tf_op jit(solution)/shard_map/ppermute | solution.py:361
  42.3 0.5 collective-permute-done.3.q1
  42.8 1.1 %collective-permute-start.12 = (bf16[64,1024]{1,0:T(8,128)(2,1)S(1)}, bf16[64,1024]{1,0:T(8,128)(2,1)S(1)}, u32[]{:S(2)}, u32[]{:S(2)}) collective-permute-start(bf16[64,1024]{1,0:T(8,128)(2,1)S(1)} %get-tuple-element.80), channel_id=1, source_target_pairs={{0,3},{1,2},{2,1},{3,0},{4,7},{5,6},{6,5},{7,4},{8,11},{9,10},{10,... | collective-permute-start | bytes 393224 | tf_op jit(solution)/shard_map/ppermute | solution.py:361
  43.9 3.9 %collective-permute-start.5 = (bf16[3,6,2,1536]{3,2,1,0:T(2,128)(2,1)S(1)}, bf16[3,6,2,1536]{3,2,1,0:T(2,128)(2,1)S(1)}, u32[]{:S(2)}, u32[]{:S(2)}) collective-permute-start(bf16[3,6,2,1536]{3,2,1,0:T(2,128)(2,1)S(1)} %get-tuple-element.68), channel_id=1, source_target_pairs={{0,5},{1,6},{2,7},{3,4},{4,9},{5,10},{6,11},{7,8},{8,13},{9,14},{1... | collective-permute-start | bytes 331784 | tf_op jit(solution)/shard_map/ppermute | solution.py:416
  47.8 0.1 shard_map.120
  47.9 1.8 %collective-permute-start.21 = (bf16[32,1152]{1,0:T(8,128)(2,1)S(1)}, bf16[32,1152]{1,0:T(8,128)(2,1)S(1)}, u32[]{:S(2)}, u32[]{:S(2)}) collective-permute-start(bf16[32,1152]{1,0:T(8,128)(2,1)S(1)} %get-tuple-element.93), channel_id=1, source_target_pairs={{0,1},{1,0},{2,3},{3,2},{4,5},{5,4},{6,7},{7,6},{8,9},{9,8},{10,11... | collective-permute-start | bytes 221192 | tf_op jit(solution)/shard_map/ppermute | solution.py:361
  49.7 3.4 %collective-permute-done.11.refs_2_ = bf16[64,1024]{1,0:T(8,128)(2,1)S(1)} collective-permute-done((bf16[64,1024]{1,0:T(8,128)(2,1)S(1)}, bf16[64,1024]{1,0:T(8,128)(2,1)S(1)}, u32[]{:S(2)}, u32[]{:S(2)}) %collective-permute-start.11) | collective-permute-done | bytes 131104 | tf_op jit(solution)/shard_map/ppermute | solution.py:361
  53.1 3.8 %collective-permute-start.22 = (bf16[32,1152]{1,0:T(8,128)(2,1)S(1)}, bf16[32,1152]{1,0:T(8,128)(2,1)S(1)}, u32[]{:S(2)}, u32[]{:S(2)}) collective-permute-start(bf16[32,1152]{1,0:T(8,128)(2,1)S(1)} %get-tuple-element.94), channel_id=1, source_target_pairs={{0,2},{1,3},{2,0},{3,1},{4,6},{5,7},{6,4},{7,5},{8,10},{9,11},{10,... | collective-permute-start | bytes 221192 | tf_op jit(solution)/shard_map/ppermute | solution.py:361
  56.9 1.2 %collective-permute-done.12.refs_3_ = bf16[64,1024]{1,0:T(8,128)(2,1)S(1)} collective-permute-done((bf16[64,1024]{1,0:T(8,128)(2,1)S(1)}, bf16[64,1024]{1,0:T(8,128)(2,1)S(1)}, u32[]{:S(2)}, u32[]{:S(2)}) %collective-permute-start.12) | collective-permute-done | bytes 131104 | tf_op jit(solution)/shard_map/ppermute | solution.py:361
  58.2 2.5 %collective-permute-start.23 = (bf16[32,1152]{1,0:T(8,128)(2,1)S(1)}, bf16[32,1152]{1,0:T(8,128)(2,1)S(1)}, u32[]{:S(2)}, u32[]{:S(2)}) collective-permute-start(bf16[32,1152]{1,0:T(8,128)(2,1)S(1)} %get-tuple-element.95), channel_id=1, source_target_pairs={{0,3},{1,2},{2,1},{3,0},{4,7},{5,6},{6,5},{7,4},{8,11},{9,10},{10,... | collective-permute-start | bytes 221192 | tf_op jit(solution)/shard_map/ppermute | solution.py:361
  60.6 0.1 shard_map.117
  60.7 0.0 collective-permute-done.4.q2
  60.7 1.2 %collective-permute-start.13 = (bf16[32,1024]{1,0:T(8,128)(2,1)S(1)}, bf16[32,1024]{1,0:T(8,128)(2,1)S(1)}, u32[]{:S(2)}, u32[]{:S(2)}) collective-permute-start(bf16[32,1024]{1,0:T(8,128)(2,1)S(1)} %get-tuple-element.82), channel_id=1, source_target_pairs={{0,16},{4,20},{8,24},{12,28},{16,0},{20,4},{24,8},{28,12},{1,17},{... | collective-permute-start | bytes 196616 | tf_op jit(solution)/shard_map/ppermute | solution.py:355
  62.0 1.4 %collective-permute-start.14 = (bf16[32,1024]{1,0:T(8,128)(2,1)S(1)}, bf16[32,1024]{1,0:T(8,128)(2,1)S(1)}, u32[]{:S(2)}, u32[]{:S(2)}) collective-permute-start(bf16[32,1024]{1,0:T(8,128)(2,1)S(1)} %get-tuple-element.83), channel_id=1, source_target_pairs={{0,8},{4,12},{8,0},{12,4},{16,24},{20,28},{24,16},{28,20},{1,9},{5... | collective-permute-start | bytes 196616 | tf_op jit(solution)/shard_map/ppermute | solution.py:355
  63.4 1.2 %shard_map.114 = (bf16[6,12,2,1024]{3,2,1,0:T(2,128)(2,1)}, bf16[6,12,2,1024]{3,2,1,0:T(2,128)(2,1)}) custom-call(bf16[3,6,2,1536]{3,2,1,0:T(2,128)(2,1)S(1)} %get-tuple-element.65.q0, bf16[3,6,2,1536]{3,2,1,0:T(2,128)(2,1)S(1)} %collective-permute-done.3.q1, bf16[3,6,2,1536]{3,2,1,0:T(2,128)(2,1)S(1)} %collective-permute-done.4.q2, ...), custom_call_target="tpu_custom_call" | custom-call | tf_op jit(solution)/shard_map/pallas_call | solution.py:46
  64.6 0.5 collective-permute-done.13.got_a
  65.1 1.2 %collective-permute-done.14.got_b = bf16[32,1024]{1,0:T(8,128)(2,1)S(1)} collective-permute-done((bf16[32,1024]{1,0:T(8,128)(2,1)S(1)}, bf16[32,1024]{1,0:T(8,128)(2,1)S(1)}, u32[]{:S(2)}, u32[]{:S(2)}) %collective-permute-start.14) | collective-permute-done | bytes 65568 | tf_op jit(solution)/shard_map/ppermute | solution.py:355
  66.2 0.8 %shard_map.121 = (f32[32,1536]{1,0:T(8,128)}, f32[32,512]{1,0:T(8,128)}, f32[1,32]{1,0:T(1,128)}, f32[1,32]{1,0:T(1,128)}) custom-call(f32[32,1024]{1,0:T(8,128)S(1)} %get-tuple-element.81.base, bf16[32,1024]{1,0:T(8,128)(2,1)S(1)} %collective-permute-done.13.got_a, bf16[32,1024]{1,0:T(8,128)(2,1)S(1)} %collective-permute-done.14.got_b, ...), custom_call_target="tpu_custom_call" | custom-call | tf_op jit(solution)/shard_map/pallas_call | solution.py:46
  (14 shorter events, 0.0 us)
Async XLA Ops:
  1.8 6.2 %collective-permute-start = (bf16[2,3,6,2,1024]{4,3,2,1,0:T(2,128)(2,1)S(1)}, bf16[2,3,6,2,1024]{4,3,2,1,0:T(2,128)(2,1)S(1)}, u32[]{:S(2)}, u32[]{:S(2)}) collective-permute-start(bf16[2,3,6,2,1024]{4,3,2,1,0:T(2,128)(2,1)S(1)} %get-tuple-element.54), channel_id=1, source_target_pairs={{0,3},{1,0},{2,1},{3,2},{4,7},{5,4},{6,5},{7,6},{8,11},{9,8},{10,9... | collective-permute-start | bytes 442376 | tf_op jit(solution)/shard_map/ppermute | solution.py:416
  2.4 5.7 %collective-permute-start.1 = (bf16[2,3,6,2,1024]{4,3,2,1,0:T(2,128)(2,1)S(1)}, bf16[2,3,6,2,1024]{4,3,2,1,0:T(2,128)(2,1)S(1)}, u32[]{:S(2)}, u32[]{:S(2)}) collective-permute-start(bf16[2,3,6,2,1024]{4,3,2,1,0:T(2,128)(2,1)S(1)} %get-tuple-element.55), channel_id=1, source_target_pairs={{0,28},{1,29},{2,30},{3,31},{4,0},{5,1},{6,2},{7,3},{8,4},{9,5},{1... | collective-permute-start | bytes 442376 | tf_op jit(solution)/shard_map/ppermute | solution.py:416
  4.0 6.1 %collective-permute-start.2 = (bf16[2,3,6,2,1024]{4,3,2,1,0:T(2,128)(2,1)S(1)}, bf16[2,3,6,2,1024]{4,3,2,1,0:T(2,128)(2,1)S(1)}, u32[]{:S(2)}, u32[]{:S(2)}) collective-permute-start(bf16[2,3,6,2,1024]{4,3,2,1,0:T(2,128)(2,1)S(1)} %get-tuple-element.56), channel_id=1, source_target_pairs={{0,31},{1,28},{2,29},{3,30},{4,3},{5,0},{6,1},{7,2},{8,7},{9,4},{1... | collective-permute-start | bytes 442376 | tf_op jit(solution)/shard_map/ppermute | solution.py:416
  15.4 5.6 %collective-permute-start.15 = (bf16[144,1024]{1,0:T(8,128)(2,1)S(1)}, bf16[144,1024]{1,0:T(8,128)(2,1)S(1)}, u32[]{:S(2)}, u32[]{:S(2)}) collective-permute-start(bf16[144,1024]{1,0:T(8,128)(2,1)S(1)} %shard_map.112.late_ref.refs_2_), channel_id=1, source_target_pairs={{0,4},{4,0},{8,12},{12,8},{16,20},{20,16},{24,28},{28,24},{1,5},{5... | collective-permute-start | bytes 884744 | tf_op jit(solution)/shard_map/ppermute | solution.py:355
  16.8 4.2 %collective-permute-start.7 = (bf16[144,1024]{1,0:T(8,128)(2,1)S(1)}, bf16[144,1024]{1,0:T(8,128)(2,1)S(1)}, u32[]{:S(2)}, u32[]{:S(2)}) collective-permute-start(bf16[144,1024]{1,0:T(8,128)(2,1)S(1)} %get-tuple-element.61.factor_ref.refs_0_), channel_id=1, source_target_pairs={{0,4},{4,0},{8,12},{12,8},{16,20},{20,16},{24,28},{28,24},{1,5},{5... | collective-permute-start | bytes 884744 | tf_op jit(solution)/shard_map/ppermute | solution.py:355
  16.9 4.1 %collective-permute-start.6 = (bf16[1024,144]{1,0:T(8,128)(2,1)S(1)}, bf16[1024,144]{1,0:T(8,128)(2,1)S(1)}, u32[]{:S(2)}, u32[]{:S(2)}) collective-permute-start(bf16[1024,144]{1,0:T(8,128)(2,1)S(1)} %get-tuple-element.73), channel_id=1, source_target_pairs={{0,4},{4,0},{8,12},{12,8},{16,20},{20,16},{24,28},{28,24},{1,5},{5... | collective-permute-start | bytes 884744 | tf_op jit(solution)/shard_map/ppermute | solution.py:355
  19.4 1.6 %collective-permute-start.16 = (f32[512,128]{1,0:T(8,128)S(1)}, f32[512,128]{1,0:T(8,128)S(1)}, u32[]{:S(2)}, u32[]{:S(2)}) collective-permute-start(f32[512,128]{1,0:T(8,128)S(1)} %get-tuple-element.85), channel_id=1, source_target_pairs={{0,4},{4,0},{8,12},{12,8},{16,20},{20,16},{24,28},{28,24},{1,5},{5... | collective-permute-start | bytes 786440 | tf_op jit(solution)/shard_map/ppermute | solution.py:355
  21.7 9.9 %collective-permute-start.17 = (bf16[128,1152]{1,0:T(8,128)(2,1)S(1)}, bf16[128,1152]{1,0:T(8,128)(2,1)S(1)}, u32[]{:S(2)}, u32[]{:S(2)}) collective-permute-start(bf16[128,1152]{1,0:T(8,128)(2,1)S(1)} %get-tuple-element.87), channel_id=1, source_target_pairs={{0,8},{4,12},{8,0},{12,4},{16,24},{20,28},{24,16},{28,20},{1,9},{5... | collective-permute-start | bytes 884744 | tf_op jit(solution)/shard_map/ppermute | solution.py:355
  23.2 9.9 %collective-permute-start.18 = (bf16[128,1152]{1,0:T(8,128)(2,1)S(1)}, bf16[128,1152]{1,0:T(8,128)(2,1)S(1)}, u32[]{:S(2)}, u32[]{:S(2)}) collective-permute-start(bf16[128,1152]{1,0:T(8,128)(2,1)S(1)} %get-tuple-element.88), channel_id=1, source_target_pairs={{0,16},{4,20},{8,24},{12,28},{16,0},{20,4},{24,8},{28,12},{1,17},{... | collective-permute-start | bytes 884744 | tf_op jit(solution)/shard_map/ppermute | solution.py:355
  24.5 14.3 %collective-permute-start.8 = (bf16[128,1024]{1,0:T(8,128)(2,1)S(1)}, bf16[128,1024]{1,0:T(8,128)(2,1)S(1)}, u32[]{:S(2)}, u32[]{:S(2)}) collective-permute-start(bf16[128,1024]{1,0:T(8,128)(2,1)S(1)} %get-tuple-element.75), channel_id=1, source_target_pairs={{0,8},{4,12},{8,0},{12,4},{16,24},{20,28},{24,16},{28,20},{1,9},{5... | collective-permute-start | bytes 786440 | tf_op jit(solution)/shard_map/ppermute | solution.py:355
  26.1 12.7 %collective-permute-start.9 = (bf16[128,1024]{1,0:T(8,128)(2,1)S(1)}, bf16[128,1024]{1,0:T(8,128)(2,1)S(1)}, u32[]{:S(2)}, u32[]{:S(2)}) collective-permute-start(bf16[128,1024]{1,0:T(8,128)(2,1)S(1)} %get-tuple-element.76), channel_id=1, source_target_pairs={{0,16},{4,20},{8,24},{12,28},{16,0},{20,4},{24,8},{28,12},{1,17},{... | collective-permute-start | bytes 786440 | tf_op jit(solution)/shard_map/ppermute | solution.py:355
  33.3 10.6 %collective-permute-start.19 = (bf16[64,1152]{1,0:T(8,128)(2,1)S(1)}, bf16[64,1152]{1,0:T(8,128)(2,1)S(1)}, u32[]{:S(2)}, u32[]{:S(2)}) collective-permute-start(bf16[64,1152]{1,0:T(8,128)(2,1)S(1)} %get-tuple-element.90), channel_id=1, source_target_pairs={{0,16},{4,20},{8,24},{12,28},{16,0},{20,4},{24,8},{28,12},{1,17},{... | collective-permute-start | bytes 442376 | tf_op jit(solution)/shard_map/ppermute | solution.py:355
  33.8 10.0 %collective-permute-start.20 = (bf16[64,1152]{1,0:T(8,128)(2,1)S(1)}, bf16[64,1152]{1,0:T(8,128)(2,1)S(1)}, u32[]{:S(2)}, u32[]{:S(2)}) collective-permute-start(bf16[64,1152]{1,0:T(8,128)(2,1)S(1)} %get-tuple-element.91), channel_id=1, source_target_pairs={{0,8},{4,12},{8,0},{12,4},{16,24},{20,28},{24,16},{28,20},{1,9},{5... | collective-permute-start | bytes 442376 | tf_op jit(solution)/shard_map/ppermute | solution.py:355
  35.4 7.4 %collective-permute-start.3 = (bf16[3,6,2,1536]{3,2,1,0:T(2,128)(2,1)S(1)}, bf16[3,6,2,1536]{3,2,1,0:T(2,128)(2,1)S(1)}, u32[]{:S(2)}, u32[]{:S(2)}) collective-permute-start(bf16[3,6,2,1536]{3,2,1,0:T(2,128)(2,1)S(1)} %get-tuple-element.66), channel_id=1, source_target_pairs={{0,1},{1,2},{2,3},{3,0},{4,5},{5,6},{6,7},{7,4},{8,9},{9,10},{10,1... | collective-permute-start | bytes 331784 | tf_op jit(solution)/shard_map/ppermute | solution.py:416
  38.9 9.0 %collective-permute-start.10 = (bf16[64,1024]{1,0:T(8,128)(2,1)S(1)}, bf16[64,1024]{1,0:T(8,128)(2,1)S(1)}, u32[]{:S(2)}, u32[]{:S(2)}) collective-permute-start(bf16[64,1024]{1,0:T(8,128)(2,1)S(1)} %get-tuple-element.78), channel_id=1, source_target_pairs={{0,1},{1,0},{2,3},{3,2},{4,5},{5,4},{6,7},{7,6},{8,9},{9,8},{10,11... | collective-permute-start | bytes 393224 | tf_op jit(solution)/shard_map/ppermute | solution.py:361
  42.3 10.8 %collective-permute-start.11 = (bf16[64,1024]{1,0:T(8,128)(2,1)S(1)}, bf16[64,1024]{1,0:T(8,128)(2,1)S(1)}, u32[]{:S(2)}, u32[]{:S(2)}) collective-permute-start(bf16[64,1024]{1,0:T(8,128)(2,1)S(1)} %get-tuple-element.79), channel_id=1, source_target_pairs={{0,2},{1,3},{2,0},{3,1},{4,6},{5,7},{6,4},{7,5},{8,10},{9,11},{10,... | collective-permute-start | bytes 393224 | tf_op jit(solution)/shard_map/ppermute | solution.py:361
  42.8 15.4 %collective-permute-start.12 = (bf16[64,1024]{1,0:T(8,128)(2,1)S(1)}, bf16[64,1024]{1,0:T(8,128)(2,1)S(1)}, u32[]{:S(2)}, u32[]{:S(2)}) collective-permute-start(bf16[64,1024]{1,0:T(8,128)(2,1)S(1)} %get-tuple-element.80), channel_id=1, source_target_pairs={{0,3},{1,2},{2,1},{3,0},{4,7},{5,6},{6,5},{7,4},{8,11},{9,10},{10,... | collective-permute-start | bytes 393224 | tf_op jit(solution)/shard_map/ppermute | solution.py:361
  43.9 16.8 %collective-permute-start.4 = (bf16[3,6,2,1536]{3,2,1,0:T(2,128)(2,1)S(1)}, bf16[3,6,2,1536]{3,2,1,0:T(2,128)(2,1)S(1)}, u32[]{:S(2)}, u32[]{:S(2)}) collective-permute-start(bf16[3,6,2,1536]{3,2,1,0:T(2,128)(2,1)S(1)} %get-tuple-element.67), channel_id=1, source_target_pairs={{0,4},{1,5},{2,6},{3,7},{4,8},{5,9},{6,10},{7,11},{8,12},{9,13},{1... | collective-permute-start | bytes 331784 | tf_op jit(solution)/shard_map/ppermute | solution.py:416
  43.9 18.1 %collective-permute-start.5 = (bf16[3,6,2,1536]{3,2,1,0:T(2,128)(2,1)S(1)}, bf16[3,6,2,1536]{3,2,1,0:T(2,128)(2,1)S(1)}, u32[]{:S(2)}, u32[]{:S(2)}) collective-permute-start(bf16[3,6,2,1536]{3,2,1,0:T(2,128)(2,1)S(1)} %get-tuple-element.68), channel_id=1, source_target_pairs={{0,5},{1,6},{2,7},{3,4},{4,9},{5,10},{6,11},{7,8},{8,13},{9,14},{1... | collective-permute-start | bytes 331784 | tf_op jit(solution)/shard_map/ppermute | solution.py:416
  47.9 18.3 %collective-permute-start.21 = (bf16[32,1152]{1,0:T(8,128)(2,1)S(1)}, bf16[32,1152]{1,0:T(8,128)(2,1)S(1)}, u32[]{:S(2)}, u32[]{:S(2)}) collective-permute-start(bf16[32,1152]{1,0:T(8,128)(2,1)S(1)} %get-tuple-element.93), channel_id=1, source_target_pairs={{0,1},{1,0},{2,3},{3,2},{4,5},{5,4},{6,7},{7,6},{8,9},{9,8},{10,11... | collective-permute-start | bytes 221192 | tf_op jit(solution)/shard_map/ppermute | solution.py:361
  53.1 13.1 %collective-permute-start.22 = (bf16[32,1152]{1,0:T(8,128)(2,1)S(1)}, bf16[32,1152]{1,0:T(8,128)(2,1)S(1)}, u32[]{:S(2)}, u32[]{:S(2)}) collective-permute-start(bf16[32,1152]{1,0:T(8,128)(2,1)S(1)} %get-tuple-element.94), channel_id=1, source_target_pairs={{0,2},{1,3},{2,0},{3,1},{4,6},{5,7},{6,4},{7,5},{8,10},{9,11},{10,... | collective-permute-start | bytes 221192 | tf_op jit(solution)/shard_map/ppermute | solution.py:361
  58.2 8.1 %collective-permute-start.23 = (bf16[32,1152]{1,0:T(8,128)(2,1)S(1)}, bf16[32,1152]{1,0:T(8,128)(2,1)S(1)}, u32[]{:S(2)}, u32[]{:S(2)}) collective-permute-start(bf16[32,1152]{1,0:T(8,128)(2,1)S(1)} %get-tuple-element.95), channel_id=1, source_target_pairs={{0,3},{1,2},{2,1},{3,0},{4,7},{5,6},{6,5},{7,4},{8,11},{9,10},{10,... | collective-permute-start | bytes 221192 | tf_op jit(solution)/shard_map/ppermute | solution.py:361
  60.7 4.3 %collective-permute-start.13 = (bf16[32,1024]{1,0:T(8,128)(2,1)S(1)}, bf16[32,1024]{1,0:T(8,128)(2,1)S(1)}, u32[]{:S(2)}, u32[]{:S(2)}) collective-permute-start(bf16[32,1024]{1,0:T(8,128)(2,1)S(1)} %get-tuple-element.82), channel_id=1, source_target_pairs={{0,16},{4,20},{8,24},{12,28},{16,0},{20,4},{24,8},{28,12},{1,17},{... | collective-permute-start | bytes 196616 | tf_op jit(solution)/shard_map/ppermute | solution.py:355
  62.0 4.3 %collective-permute-start.14 = (bf16[32,1024]{1,0:T(8,128)(2,1)S(1)}, bf16[32,1024]{1,0:T(8,128)(2,1)S(1)}, u32[]{:S(2)}, u32[]{:S(2)}) collective-permute-start(bf16[32,1024]{1,0:T(8,128)(2,1)S(1)} %get-tuple-element.83), channel_id=1, source_target_pairs={{0,8},{4,12},{8,0},{12,4},{16,24},{20,28},{24,16},{28,20},{1,9},{5... | collective-permute-start | bytes 196616 | tf_op jit(solution)/shard_map/ppermute | solution.py:355

commit v8 on v7

--- a/solution.py
+++ b/solution.py
@@ -87,10 +87,17 @@
     run_copies(list(zip(refs[:count], refs[count:-1])), refs[-1])
 
 
-def unpack_body(q0, q1, q2, q3, tok_ref, w_out_ref, y_ref, grad_ref, att):
+def join_body(north_ref, east_ref, both_ref):
+    both_ref[0] = north_ref[...]
+    both_ref[1] = east_ref[1]
+
+
+def unpack_body(stay_ref, east_ref, both_ref, tok_ref, w_out_ref, y_ref, grad_ref, att):
     rows, cols, levels, width = y_ref.shape
     inner = att.shape[-1]
-    for quad, (row, col) in zip((q0, q1, q2, q3), corners(rows, cols)):
+    for quad, (row, col) in zip(
+        (stay_ref, east_ref.at[0], both_ref.at[0], both_ref.at[1]), corners(rows, cols)
+    ):
         at = (slice(row, row + rows // 2), slice(col, col + cols // 2))
         att[at] = quad[:, :, :, :inner]
         grad_ref[at] = quad[:, :, :, inner:]
@@ -154,12 +161,15 @@
     grad = gather_window(quads, 1, wide).astype(BF16)
     total = grad.shape[0]
     count = total // 4
-    row_id = lax.broadcasted_iota(jnp.int32, (total, total), 0) // count
-    col_id = lax.broadcasted_iota(jnp.int32, (total, total), 1) // count
+    row_id = lax.broadcasted_iota(jnp.int32, (total, 1), 0)
+    col_id = lax.broadcasted_iota(jnp.int32, (1, total), 1)
+    row_side, col_side = ((i >= 2 * count).astype(jnp.int32) for i in (row_id, col_id))
+    row_turn, col_turn = (
+        ((i >= count) & (i < 2 * count) | (i >= 3 * count)).astype(jnp.int32)
+        for i in (row_id, col_id)
+    )
     last_lat, last_lon = ((places_ref[i] == n - 1).astype(jnp.int32) for i, n in enumerate(plan[1]))
-    apart = jnp.where((row_id >= 2) != (col_id >= 2), last_lat, 0) + jnp.where(
-        (row_id % 2) != (col_id % 2), last_lon, 0
-    )
+    apart = (row_side ^ col_side) * last_lat + (row_turn ^ col_turn) * last_lon
     bias_of[...] = jnp.where(apart > 0, -1e30, 0.0)
     side[...] = grad.T
     reorder(plan, places_ref, side, (mine_ref, peer_ref), width // 2)
@@ -217,12 +227,12 @@
 
 def gradient_body(
     plan, places_ref, r0, r1, r2, r3, factor_ref, late_ref, w_qkv_ref, gain_ref,
-    o0, o1, o2, o3, mine_ref, peer_ref, wide, flat,
+    stay_ref, east_ref, north_ref, mine_ref, peer_ref, wide, flat,
 ):
     quads = (r0, r1, r2, r3)
     inner, width = late_ref.shape[1] // 2, wide.shape[1]
-    outs = (o0, o1, o2, o3)
-    quad = o0.shape[:3]
+    outs = (stay_ref, east_ref.at[0], north_ref, east_ref.at[1])
+    quad = stay_ref.shape[:3]
     count = quad[0] * quad[1] * quad[2]
     tokens_wide = gather_window(quads, 0, wide)
     standard, inverse = normalize(tokens_wide)
@@ -356,11 +366,11 @@
 
 
 def turn(pieces):
-    count = len(pieces)
-    return [pieces[0]] + [
-        lax.ppermute(pieces[k], "lon", [(i, i ^ k) for i in range(count)])
-        for k in range(1, count)
-    ]
+    pairs = lambda k: [(i, i ^ k) for i in range(len(pieces))]
+    moved = pieces[:1]
+    for k in range(1, len(pieces)):
+        moved.append(lax.ppermute(pieces[k], "lon", pairs(k)))
+    return moved
 
 
 def sum_early(both, send_a, send_b, lon_count):
@@ -368,7 +378,7 @@
     size = quarter // lon_count
     got_a, got_b = swap(send_a, 2), swap(send_b, 4)
     pieces = call(turn_body, [((2 * size, cols), BF16)] * lon_count, (both, got_a, got_b))
-    pieces = turn(pieces)
+    pieces = turn(list(pieces))
     base, send_a, send_b = call(
         meet_body, [((size, cols), F32)] + [((size, cols), BF16)] * 2, pieces
     )
@@ -386,7 +396,7 @@
     )
     got_a, got_b = swap(send_a, 4), swap(send_b, 2)
     pieces = call(third_body, [((size, cols), BF16)] * lon_count, (both, got_a, got_b))
-    pieces = turn(pieces)
+    pieces = turn(list(pieces))
     return pieces
 
 
@@ -461,9 +471,10 @@
         smem=1,
     )
     (factor_late,) = call(backward_body, [((cells, 2 * inner), BF16)], (query, pairs, probs))
-    q0, q1, q2, q3, sums, sums_peer = call(
+    part = (*quad[1:-1], inner + width)
+    stay, east, north, sums, sums_peer = call(
         functools.partial(gradient_body, plan),
-        [((*quad[1:-1], inner + width), BF16)] * 4 + [((width // 2, LANES), F32)] * 2,
+        [(shape, BF16) for shape in (part, (2, *part), part)] + [((width // 2, LANES), F32)] * 2,
         (places, *quads, factor, factor_late, params[0], params[2]),
         scratch=[pltpu.VMEM((cells, width), F32), pltpu.VMEM((width, LANES), F32)],
         smem=1,
@@ -512,9 +523,11 @@
         d_out = whole[:, :inner]
         d_qkv = jnp.concatenate([whole[:, 2 * inner : 4 * inner], whole[:, inner : 2 * inner]], axis=1)
         gain, bias = whole[:, 4 * inner], whole[:, 4 * inner + 1]
-    back = [q0, *moved_all((q1, q2, q3), 1)]
+    east = lax.ppermute(east, ("lat", "lon"), moved(0, 1))
+    (both,) = call(join_body, [((2, *part), BF16)], (north, east))
+    both = lax.ppermute(both, ("lat", "lon"), moved(1, 0))
     y_out, token_gradient = call(
-        unpack_body, [(grid, BF16)] * 2, (*back, tok, params[1]), near_out=0,
+        unpack_body, [(grid, BF16)] * 2, (stay, east, both, tok, params[1]), near_out=0,
         scratch=[pltpu.VMEM((*grid[:-1], inner), BF16)],
     )
     return (

time: 67.2 us -> 65.1 us (0.969)
  the two profiles are of different devices: /device:TPU:16 before, /device:TPU:0 now
where the time goes in v8:
time: 65.1 us; the launch traced here: 65 us
  starting transfers between devices  30.5 us (47%)
  waiting for transfers between devices  19 us (29%)
  Pallas kernels  14.7 us (23%)
  between operations  0.77 us (1%)
    pallas_call x14, Pallas kernels, call(): pl.pallas_call(body, out_shape=[pltpu.VMEM(s, d) if i < near_out else jax...  14.7 us
    ppermute x12, waiting for transfers between devices, swap(): return lax.ppermute(value, 'lat', xor_pairs(bit))  12.6 us
    ppermute x12, starting transfers between devices, swap(): return lax.ppermute(value, 'lat', xor_pairs(bit))  12.5 us
    ppermute x6, starting transfers between devices, turn(): moved.append(lax.ppermute(pieces[k], 'lon', pairs(k)))  10.3 us
    ppermute x3, starting transfers between devices, moved_all(): lax.ppermute(items[place], ('lat', 'lon'), moved(sign * a, sign * b))  7.58 us
    ppermute x6, waiting for transfers between devices, turn(): moved.append(lax.ppermute(pieces[k], 'lon', pairs(k)))  4.39 us
    ppermute x3, waiting for transfers between devices, moved_all(): lax.ppermute(items[place], ('lat', 'lon'), moved(sign * a, sign * b))  2 us
  transfers between devices with their start and end apart: 23, of which 8 were waited for; matrix products, arithmetic and copies ran while one was open for 0% of the time, Pallas kernels for 10%

profile of v8, /device:TPU:0, one launch (start us, length us, event | category | flops | bytes accessed | tf_op | source)
XLA Modules:
  0.0 65.0 jit_solution(2861943034960631150)
XLA Ops:
  0.6 1.2 %shard_map.109 = (bf16[2,3,6,2,1024]{4,3,2,1,0:T(2,128)(2,1)S(1)}, bf16[2,3,6,2,1024]{4,3,2,1,0:T(2,128)(2,1)S(1)}, bf16[2,3,6,2,1024]{4,3,2,1,0:T(2,128)(2,1)S(1)}, bf16[2,3,6,2,1024]{4,3,2,1,0:T(2,128)(2,1)S(1)}) custom-call(bf16[6,12,2,1024]{3,2,1,0:T(2,128)(2,1)} %bitcast.9, bf16[6,12,2,1024]{3,2,1,0:T(2,128)(2,1)} %bitcast.11), custom_call_target="tpu_custom_call" | custom-call | tf_op jit(solution)/shard_map/pallas_call | solution.py:46
  1.8 5.1 %collective-permute-start = (bf16[2,3,6,2,1024]{4,3,2,1,0:T(2,128)(2,1)S(1)}, bf16[2,3,6,2,1024]{4,3,2,1,0:T(2,128)(2,1)S(1)}, u32[]{:S(2)}, u32[]{:S(2)}) collective-permute-start(bf16[2,3,6,2,1024]{4,3,2,1,0:T(2,128)(2,1)S(1)} %get-tuple-element.53), channel_id=1, source_target_pairs={{0,3},{1,0},{2,1},{3,2},{4,7},{5,4},{6,5},{7,6},{8,11},{9,8},{10,9... | collective-permute-start | bytes 442376 | tf_op jit(solution)/shard_map/ppermute | solution.py:426
  7.0 1.6 %collective-permute-start.1 = (bf16[2,3,6,2,1024]{4,3,2,1,0:T(2,128)(2,1)S(1)}, bf16[2,3,6,2,1024]{4,3,2,1,0:T(2,128)(2,1)S(1)}, u32[]{:S(2)}, u32[]{:S(2)}) collective-permute-start(bf16[2,3,6,2,1024]{4,3,2,1,0:T(2,128)(2,1)S(1)} %get-tuple-element.54), channel_id=1, source_target_pairs={{0,28},{1,29},{2,30},{3,31},{4,0},{5,1},{6,2},{7,3},{8,4},{9,5},{1... | collective-permute-start | bytes 442376 | tf_op jit(solution)/shard_map/ppermute | solution.py:426
  8.6 0.8 %collective-permute-start.2 = (bf16[2,3,6,2,1024]{4,3,2,1,0:T(2,128)(2,1)S(1)}, bf16[2,3,6,2,1024]{4,3,2,1,0:T(2,128)(2,1)S(1)}, u32[]{:S(2)}, u32[]{:S(2)}) collective-permute-start(bf16[2,3,6,2,1024]{4,3,2,1,0:T(2,128)(2,1)S(1)} %get-tuple-element.55), channel_id=1, source_target_pairs={{0,31},{1,28},{2,29},{3,30},{4,3},{5,0},{6,1},{7,2},{8,7},{9,4},{1... | collective-permute-start | bytes 442376 | tf_op jit(solution)/shard_map/ppermute | solution.py:426
  9.4 2.3 %shard_map.110 = (bf16[1024,1536]{1,0:T(8,128)(2,1)S(1)}, bf16[512,1024]{1,0:T(8,128)(2,1)S(1)}, f32[1,1024]{1,0:T(1,128)S(1)}, f32[1,1024]{1,0:T(1,128)S(1)}, bf16[6,12,2,1024]{3,2,1,0:T(2,128)(2,1)S(1)}) custom-call(bf16[1024,1536]{1,0:T(8,128)(2,1)} %refs_0_.1, bf16[512,1024]{1,0:T(8,128)(2,1)} %refs_1_.1, f32[1,1024]{1,0:T(1,128)} %bitcast.12, ...), custom_call_target="tpu_custom_call" | custom-call | tf_op jit(solution)/shard_map/pallas_call | solution.py:46
  11.7 0.0 collective-permute-done.r1
  11.8 0.0 collective-permute-done.1.r2
  11.8 2.0 %collective-permute-done.2.r3 = bf16[2,3,6,2,1024]{4,3,2,1,0:T(2,128)(2,1)S(1)} collective-permute-done((bf16[2,3,6,2,1024]{4,3,2,1,0:T(2,128)(2,1)S(1)}, bf16[2,3,6,2,1024]{4,3,2,1,0:T(2,128)(2,1)S(1)}, u32[]{:S(2)}, u32[]{:S(2)}) %collective-permute-start.2) | collective-permute-done | bytes 147488 | tf_op jit(solution)/shard_map/ppermute | solution.py:426
  13.8 3.6 %shard_map.111 = (bf16[1024,144]{1,0:T(8,128)(2,1)S(1)}, bf16[1024,144]{1,0:T(8,128)(2,1)S(1)}, bf16[144,1024]{1,0:T(8,128)(2,1)S(1)}, bf16[144,512]{1,0:T(8,128...) custom-call(s32[2]{0:T(128)S(1)} %compare_select_fusion.places_ref, ...), custom_call_target="tpu_custom_call" | custom-call | tf_op jit(solution)/shard_map/pallas_call | solution.py:46
  17.4 1.7 %shard_map.112.late_ref.refs_2_ = bf16[144,1024]{1,0:T(8,128)(2,1)S(1)} custom-call(bf16[144,512]{1,0:T(8,128)(2,1)S(1)} %get-tuple-element.61.query_ref, bf16[144,1536]{1,0:T(8,128)(2,1)S(1)} %get-tuple-element.62.pair_ref, f32[8,144,144]{2,1,0:T(8,128)S(1)} %get-tuple-element.63.probs_ref), custom_call_target="tpu_custom_call" | custom-call | tf_op jit(solution)/shard_map/pallas_call | solution.py:46
  19.1 0.2 collective-permute-start.14
  19.3 0.4 collective-permute-start.6
  19.7 0.1 collective-permute-start.5
  19.8 2.1 %shard_map.113 = (bf16[3,6,2,1536]{3,2,1,0:T(2,128)(2,1)S(1)}, bf16[2,3,6,2,1536]{4,3,2,1,0:T(2,128)(2,1)S(1)}, bf16[3,6,2,1536]{3,2,1,0:T(2,128)(2,1)S(1)}, f32[512,128]{1,0:T(8,128)S(1)}, f32[512,128]{1,0:T(8,128)S(1)}) custom-call(s32[2]{0:T(128)S(1)} %compare_select_fusion.places_ref, bf16[2,3,6,2,1024]{4,3,2,1,0:T(2,128)(2,1)S(1)} %get-tuple-element.52.r0, ...), custom_call_target="tpu_custom_call" | custom-call | tf_op jit(solution)/shard_map/pallas_call | solution.py:46
  21.9 0.5 collective-permute-start.15
  22.3 1.2 %collective-permute-done.15.refs_5_ = f32[512,128]{1,0:T(8,128)S(1)} collective-permute-done((f32[512,128]{1,0:T(8,128)S(1)}, f32[512,128]{1,0:T(8,128)S(1)}, u32[]{:S(2)}, u32[]{:S(2)}) %collective-permute-start.15) | collective-permute-done | bytes 262176 | tf_op jit(solution)/shard_map/ppermute | solution.py:365
  23.5 0.0 collective-permute-done.6.refs_1_
  23.5 0.0 collective-permute-done.5.got
  23.5 0.7 %shard_map.119 = (bf16[256,1152]{1,0:T(8,128)(2,1)S(1)}, bf16[128,1152]{1,0:T(8,128)(2,1)S(1)}, bf16[128,1152]{1,0:T(8,128)(2,1)S(1)}) custom-call(bf16[1024,144]{1,0:T(8,128)(2,1)S(1)} %get-tuple-element.70.mine, bf16[1024,144]{1,0:T(8,128)(2,1)S(1)} %collective-permute-done.5.got, bf16[144,1024]{1,0:T(8,128)(2,1)S(1)} %get-tuple-element.60.factor_ref.refs_0_, ...), custom_call_target="tpu_custom_call" | custom-call | tf_op jit(solution)/shard_map/pallas_call | solution.py:46
  24.2 2.1 %collective-permute-start.16 = (bf16[128,1152]{1,0:T(8,128)(2,1)S(1)}, bf16[128,1152]{1,0:T(8,128)(2,1)S(1)}, u32[]{:S(2)}, u32[]{:S(2)}) collective-permute-start(bf16[128,1152]{1,0:T(8,128)(2,1)S(1)} %get-tuple-element.85), channel_id=1, source_target_pairs={{0,8},{4,12},{8,0},{12,4},{16,24},{20,28},{24,16},{28,20},{1,9},{5... | collective-permute-start | bytes 884744 | tf_op jit(solution)/shard_map/ppermute | solution.py:365
  26.3 1.5 %collective-permute-start.17 = (bf16[128,1152]{1,0:T(8,128)(2,1)S(1)}, bf16[128,1152]{1,0:T(8,128)(2,1)S(1)}, u32[]{:S(2)}, u32[]{:S(2)}) collective-permute-start(bf16[128,1152]{1,0:T(8,128)(2,1)S(1)} %get-tuple-element.86), channel_id=1, source_target_pairs={{0,16},{4,20},{8,24},{12,28},{16,0},{20,4},{24,8},{28,12},{1,17},{... | collective-permute-start | bytes 884744 | tf_op jit(solution)/shard_map/ppermute | solution.py:365
  27.8 0.0 collective-permute-start.3
  27.9 0.7 %shard_map.116 = (bf16[256,1024]{1,0:T(8,128)(2,1)S(1)}, bf16[128,1024]{1,0:T(8,128)(2,1)S(1)}, bf16[128,1024]{1,0:T(8,128)(2,1)S(1)}) custom-call(bf16[1024,144]{1,0:T(8,128)(2,1)S(1)} %get-tuple-element.70.mine, bf16[1024,144]{1,0:T(8,128)(2,1)S(1)} %collective-permute-done.5.got, bf16[144,1024]{1,0:T(8,128)(2,1)S(1)} %get-tuple-element.60.factor_ref.refs_0_, ...), custom_call_target="tpu_custom_call" | custom-call | tf_op jit(solution)/shard_map/pallas_call | solution.py:46
  28.5 0.6 collective-permute-start.7
  29.1 0.5 collective-permute-start.8
  29.6 4.6 %collective-permute-done.16.got_a = bf16[128,1152]{1,0:T(8,128)(2,1)S(1)} collective-permute-done((bf16[128,1152]{1,0:T(8,128)(2,1)S(1)}, bf16[128,1152]{1,0:T(8,128)(2,1)S(1)}, u32[]{:S(2)}, u32[]{:S(2)}) %collective-permute-start.16) | collective-permute-done | bytes 294944 | tf_op jit(solution)/shard_map/ppermute | solution.py:365
  34.2 2.0 %collective-permute-done.17.got_b = bf16[128,1152]{1,0:T(8,128)(2,1)S(1)} collective-permute-done((bf16[128,1152]{1,0:T(8,128)(2,1)S(1)}, bf16[128,1152]{1,0:T(8,128)(2,1)S(1)}, u32[]{:S(2)}, u32[]{:S(2)}) %collective-permute-start.17) | collective-permute-done | bytes 294944 | tf_op jit(solution)/shard_map/ppermute | solution.py:365
  36.2 0.1 shard_map.120
  36.4 1.6 %collective-permute-start.18 = (bf16[64,1152]{1,0:T(8,128)(2,1)S(1)}, bf16[64,1152]{1,0:T(8,128)(2,1)S(1)}, u32[]{:S(2)}, u32[]{:S(2)}) collective-permute-start(bf16[64,1152]{1,0:T(8,128)(2,1)S(1)} %get-tuple-element.88), channel_id=1, source_target_pairs={{0,16},{4,20},{8,24},{12,28},{16,0},{20,4},{24,8},{28,12},{1,17},{... | collective-permute-start | bytes 442376 | tf_op jit(solution)/shard_map/ppermute | solution.py:365
  37.9 0.0 collective-permute-done.3.east_ref
  38.0 0.1 collective-permute-start.4
  38.0 0.1 collective-permute-start.19
  38.2 1.1 %collective-permute-done.7.got_a = bf16[128,1024]{1,0:T(8,128)(2,1)S(1)} collective-permute-done((bf16[128,1024]{1,0:T(8,128)(2,1)S(1)}, bf16[128,1024]{1,0:T(8,128)(2,1)S(1)}, u32[]{:S(2)}, u32[]{:S(2)}) %collective-permute-start.7) | collective-permute-done | bytes 262176 | tf_op jit(solution)/shard_map/ppermute | solution.py:365
  39.2 2.8 %collective-permute-done.8.got_b = bf16[128,1024]{1,0:T(8,128)(2,1)S(1)} collective-permute-done((bf16[128,1024]{1,0:T(8,128)(2,1)S(1)}, bf16[128,1024]{1,0:T(8,128)(2,1)S(1)}, u32[]{:S(2)}, u32[]{:S(2)}) %collective-permute-start.8) | collective-permute-done | bytes 262176 | tf_op jit(solution)/shard_map/ppermute | solution.py:365
  42.0 0.1 shard_map.117
  42.1 1.5 %collective-permute-start.9 = (bf16[64,1024]{1,0:T(8,128)(2,1)S(1)}, bf16[64,1024]{1,0:T(8,128)(2,1)S(1)}, u32[]{:S(2)}, u32[]{:S(2)}) collective-permute-start(bf16[64,1024]{1,0:T(8,128)(2,1)S(1)} %get-tuple-element.76), channel_id=1, source_target_pairs={{0,1},{1,0},{2,3},{3,2},{4,5},{5,4},{6,7},{7,6},{8,9},{9,8},{10,11... | collective-permute-start | bytes 393224 | tf_op jit(solution)/shard_map/ppermute | solution.py:372
  43.7 4.3 %collective-permute-start.10 = (bf16[64,1024]{1,0:T(8,128)(2,1)S(1)}, bf16[64,1024]{1,0:T(8,128)(2,1)S(1)}, u32[]{:S(2)}, u32[]{:S(2)}) collective-permute-start(bf16[64,1024]{1,0:T(8,128)(2,1)S(1)} %get-tuple-element.77), channel_id=1, source_target_pairs={{0,2},{1,3},{2,0},{3,1},{4,6},{5,7},{6,4},{7,5},{8,10},{9,11},{10,... | collective-permute-start | bytes 393224 | tf_op jit(solution)/shard_map/ppermute | solution.py:372
  48.0 2.0 %collective-permute-start.11 = (bf16[64,1024]{1,0:T(8,128)(2,1)S(1)}, bf16[64,1024]{1,0:T(8,128)(2,1)S(1)}, u32[]{:S(2)}, u32[]{:S(2)}) collective-permute-start(bf16[64,1024]{1,0:T(8,128)(2,1)S(1)} %get-tuple-element.78), channel_id=1, source_target_pairs={{0,3},{1,2},{2,1},{3,0},{4,7},{5,6},{6,5},{7,4},{8,11},{9,10},{10,... | collective-permute-start | bytes 393224 | tf_op jit(solution)/shard_map/ppermute | solution.py:372
  50.0 0.1 shard_map.121
  50.1 0.1 collective-permute-start.20
  50.2 2.3 %collective-permute-start.21 = (bf16[32,1152]{1,0:T(8,128)(2,1)S(1)}, bf16[32,1152]{1,0:T(8,128)(2,1)S(1)}, u32[]{:S(2)}, u32[]{:S(2)}) collective-permute-start(bf16[32,1152]{1,0:T(8,128)(2,1)S(1)} %get-tuple-element.92), channel_id=1, source_target_pairs={{0,2},{1,3},{2,0},{3,1},{4,6},{5,7},{6,4},{7,5},{8,10},{9,11},{10,... | collective-permute-start | bytes 221192 | tf_op jit(solution)/shard_map/ppermute | solution.py:372
  52.5 4.4 %collective-permute-done.10.refs_2_ = bf16[64,1024]{1,0:T(8,128)(2,1)S(1)} collective-permute-done((bf16[64,1024]{1,0:T(8,128)(2,1)S(1)}, bf16[64,1024]{1,0:T(8,128)(2,1)S(1)}, u32[]{:S(2)}, u32[]{:S(2)}) %collective-permute-start.10) | collective-permute-done | bytes 131104 | tf_op jit(solution)/shard_map/ppermute | solution.py:372
  56.9 0.1 shard_map.118
  57.0 2.8 %collective-permute-start.12 = (bf16[32,1024]{1,0:T(8,128)(2,1)S(1)}, bf16[32,1024]{1,0:T(8,128)(2,1)S(1)}, u32[]{:S(2)}, u32[]{:S(2)}) collective-permute-start(bf16[32,1024]{1,0:T(8,128)(2,1)S(1)} %get-tuple-element.80), channel_id=1, source_target_pairs={{0,16},{4,20},{8,24},{12,28},{16,0},{20,4},{24,8},{28,12},{1,17},{... | collective-permute-start | bytes 196616 | tf_op jit(solution)/shard_map/ppermute | solution.py:365
  59.8 2.1 %collective-permute-start.13 = (bf16[32,1024]{1,0:T(8,128)(2,1)S(1)}, bf16[32,1024]{1,0:T(8,128)(2,1)S(1)}, u32[]{:S(2)}, u32[]{:S(2)}) collective-permute-start(bf16[32,1024]{1,0:T(8,128)(2,1)S(1)} %get-tuple-element.81), channel_id=1, source_target_pairs={{0,8},{4,12},{8,0},{12,4},{16,24},{20,28},{24,16},{28,20},{1,9},{5... | collective-permute-start | bytes 196616 | tf_op jit(solution)/shard_map/ppermute | solution.py:365
  61.9 1.2 %shard_map.115 = (bf16[6,12,2,1024]{3,2,1,0:T(2,128)(2,1)}, bf16[6,12,2,1024]{3,2,1,0:T(2,128)(2,1)}) custom-call(bf16[3,6,2,1536]{3,2,1,0:T(2,128)(2,1)S(1)} %get-tuple-element.64.stay_ref, bf16[2,3,6,2,1536]{4,3,2,1,0:T(2,128)(2,1)S(1)} %collective-permute-done.3.east_ref, bf16[2,3,6,2,1536]{4,3,2,1,0:T(2,128)(2,1)S(1)} %collective-permute-done.4.both_ref, ...), custom_call_target="tpu_custom_call" | custom-call | tf_op jit(solution)/shard_map/pallas_call | solution.py:46
  63.1 1.0 %collective-permute-done.13.got_b = bf16[32,1024]{1,0:T(8,128)(2,1)S(1)} collective-permute-done((bf16[32,1024]{1,0:T(8,128)(2,1)S(1)}, bf16[32,1024]{1,0:T(8,128)(2,1)S(1)}, u32[]{:S(2)}, u32[]{:S(2)}) %collective-permute-start.13) | collective-permute-done | bytes 65568 | tf_op jit(solution)/shard_map/ppermute | solution.py:365
  64.2 0.8 %shard_map.122 = (f32[32,1536]{1,0:T(8,128)}, f32[32,512]{1,0:T(8,128)}, f32[1,32]{1,0:T(1,128)}, f32[1,32]{1,0:T(1,128)}) custom-call(f32[32,1024]{1,0:T(8,128)S(1)} %get-tuple-element.79.base, bf16[32,1024]{1,0:T(8,128)(2,1)S(1)} %collective-permute-done.12.got_a, bf16[32,1024]{1,0:T(8,128)(2,1)S(1)} %collective-permute-done.13.got_b, ...), custom_call_target="tpu_custom_call" | custom-call | tf_op jit(solution)/shard_map/pallas_call | solution.py:46
  (13 shorter events, 0.1 us)
Async XLA Ops:
  1.8 9.9 %collective-permute-start = (bf16[2,3,6,2,1024]{4,3,2,1,0:T(2,128)(2,1)S(1)}, bf16[2,3,6,2,1024]{4,3,2,1,0:T(2,128)(2,1)S(1)}, u32[]{:S(2)}, u32[]{:S(2)}) collective-permute-start(bf16[2,3,6,2,1024]{4,3,2,1,0:T(2,128)(2,1)S(1)} %get-tuple-element.53), channel_id=1, source_target_pairs={{0,3},{1,0},{2,1},{3,2},{4,7},{5,4},{6,5},{7,6},{8,11},{9,8},{10,9... | collective-permute-start | bytes 442376 | tf_op jit(solution)/shard_map/ppermute | solution.py:426
  7.0 4.8 %collective-permute-start.1 = (bf16[2,3,6,2,1024]{4,3,2,1,0:T(2,128)(2,1)S(1)}, bf16[2,3,6,2,1024]{4,3,2,1,0:T(2,128)(2,1)S(1)}, u32[]{:S(2)}, u32[]{:S(2)}) collective-permute-start(bf16[2,3,6,2,1024]{4,3,2,1,0:T(2,128)(2,1)S(1)} %get-tuple-element.54), channel_id=1, source_target_pairs={{0,28},{1,29},{2,30},{3,31},{4,0},{5,1},{6,2},{7,3},{8,4},{9,5},{1... | collective-permute-start | bytes 442376 | tf_op jit(solution)/shard_map/ppermute | solution.py:426
  8.6 5.2 %collective-permute-start.2 = (bf16[2,3,6,2,1024]{4,3,2,1,0:T(2,128)(2,1)S(1)}, bf16[2,3,6,2,1024]{4,3,2,1,0:T(2,128)(2,1)S(1)}, u32[]{:S(2)}, u32[]{:S(2)}) collective-permute-start(bf16[2,3,6,2,1024]{4,3,2,1,0:T(2,128)(2,1)S(1)} %get-tuple-element.55), channel_id=1, source_target_pairs={{0,31},{1,28},{2,29},{3,30},{4,3},{5,0},{6,1},{7,2},{8,7},{9,4},{1... | collective-permute-start | bytes 442376 | tf_op jit(solution)/shard_map/ppermute | solution.py:426
  19.1 4.4 %collective-permute-start.14 = (bf16[144,1024]{1,0:T(8,128)(2,1)S(1)}, bf16[144,1024]{1,0:T(8,128)(2,1)S(1)}, u32[]{:S(2)}, u32[]{:S(2)}) collective-permute-start(bf16[144,1024]{1,0:T(8,128)(2,1)S(1)} %shard_map.112.late_ref.refs_2_), channel_id=1, source_target_pairs={{0,4},{4,0},{8,12},{12,8},{16,20},{20,16},{24,28},{28,24},{1,5},{5... | collective-permute-start | bytes 884744 | tf_op jit(solution)/shard_map/ppermute | solution.py:365
  19.3 4.2 %collective-permute-start.6 = (bf16[144,1024]{1,0:T(8,128)(2,1)S(1)}, bf16[144,1024]{1,0:T(8,128)(2,1)S(1)}, u32[]{:S(2)}, u32[]{:S(2)}) collective-permute-start(bf16[144,1024]{1,0:T(8,128)(2,1)S(1)} %get-tuple-element.60.factor_ref.refs_0_), channel_id=1, source_target_pairs={{0,4},{4,0},{8,12},{12,8},{16,20},{20,16},{24,28},{28,24},{1,5},{5... | collective-permute-start | bytes 884744 | tf_op jit(solution)/shard_map/ppermute | solution.py:365
  19.7 3.8 %collective-permute-start.5 = (bf16[1024,144]{1,0:T(8,128)(2,1)S(1)}, bf16[1024,144]{1,0:T(8,128)(2,1)S(1)}, u32[]{:S(2)}, u32[]{:S(2)}) collective-permute-start(bf16[1024,144]{1,0:T(8,128)(2,1)S(1)} %get-tuple-element.71), channel_id=1, source_target_pairs={{0,4},{4,0},{8,12},{12,8},{16,20},{20,16},{24,28},{28,24},{1,5},{5... | collective-permute-start | bytes 884744 | tf_op jit(solution)/shard_map/ppermute | solution.py:365
  21.9 1.6 %collective-permute-start.15 = (f32[512,128]{1,0:T(8,128)S(1)}, f32[512,128]{1,0:T(8,128)S(1)}, u32[]{:S(2)}, u32[]{:S(2)}) collective-permute-start(f32[512,128]{1,0:T(8,128)S(1)} %get-tuple-element.83), channel_id=1, source_target_pairs={{0,4},{4,0},{8,12},{12,8},{16,20},{20,16},{24,28},{28,24},{1,5},{5... | collective-permute-start | bytes 786440 | tf_op jit(solution)/shard_map/ppermute | solution.py:365
  24.2 10.0 %collective-permute-start.16 = (bf16[128,1152]{1,0:T(8,128)(2,1)S(1)}, bf16[128,1152]{1,0:T(8,128)(2,1)S(1)}, u32[]{:S(2)}, u32[]{:S(2)}) collective-permute-start(bf16[128,1152]{1,0:T(8,128)(2,1)S(1)} %get-tuple-element.85), channel_id=1, source_target_pairs={{0,8},{4,12},{8,0},{12,4},{16,24},{20,28},{24,16},{28,20},{1,9},{5... | collective-permute-start | bytes 884744 | tf_op jit(solution)/shard_map/ppermute | solution.py:365
  26.3 9.9 %collective-permute-start.17 = (bf16[128,1152]{1,0:T(8,128)(2,1)S(1)}, bf16[128,1152]{1,0:T(8,128)(2,1)S(1)}, u32[]{:S(2)}, u32[]{:S(2)}) collective-permute-start(bf16[128,1152]{1,0:T(8,128)(2,1)S(1)} %get-tuple-element.86), channel_id=1, source_target_pairs={{0,16},{4,20},{8,24},{12,28},{16,0},{20,4},{24,8},{28,12},{1,17},{... | collective-permute-start | bytes 884744 | tf_op jit(solution)/shard_map/ppermute | solution.py:365
  27.8 10.1 %collective-permute-start.3 = (bf16[2,3,6,2,1536]{4,3,2,1,0:T(2,128)(2,1)S(1)}, bf16[2,3,6,2,1536]{4,3,2,1,0:T(2,128)(2,1)S(1)}, u32[]{:S(2)}, u32[]{:S(2)}) collective-permute-start(bf16[2,3,6,2,1536]{4,3,2,1,0:T(2,128)(2,1)S(1)} %get-tuple-element.65), channel_id=1, source_target_pairs={{0,1},{1,2},{2,3},{3,0},{4,5},{5,6},{6,7},{7,4},{8,9},{9,10},{10,1... | collective-permute-start | bytes 663560 | tf_op jit(solution)/shard_map/ppermute | solution.py:526
  28.5 10.7 %collective-permute-start.7 = (bf16[128,1024]{1,0:T(8,128)(2,1)S(1)}, bf16[128,1024]{1,0:T(8,128)(2,1)S(1)}, u32[]{:S(2)}, u32[]{:S(2)}) collective-permute-start(bf16[128,1024]{1,0:T(8,128)(2,1)S(1)} %get-tuple-element.73), channel_id=1, source_target_pairs={{0,8},{4,12},{8,0},{12,4},{16,24},{20,28},{24,16},{28,20},{1,9},{5... | collective-permute-start | bytes 786440 | tf_op jit(solution)/shard_map/ppermute | solution.py:365
  29.1 12.9 %collective-permute-start.8 = (bf16[128,1024]{1,0:T(8,128)(2,1)S(1)}, bf16[128,1024]{1,0:T(8,128)(2,1)S(1)}, u32[]{:S(2)}, u32[]{:S(2)}) collective-permute-start(bf16[128,1024]{1,0:T(8,128)(2,1)S(1)} %get-tuple-element.74), channel_id=1, source_target_pairs={{0,16},{4,20},{8,24},{12,28},{16,0},{20,4},{24,8},{28,12},{1,17},{... | collective-permute-start | bytes 786440 | tf_op jit(solution)/shard_map/ppermute | solution.py:365
  36.4 11.6 %collective-permute-start.18 = (bf16[64,1152]{1,0:T(8,128)(2,1)S(1)}, bf16[64,1152]{1,0:T(8,128)(2,1)S(1)}, u32[]{:S(2)}, u32[]{:S(2)}) collective-permute-start(bf16[64,1152]{1,0:T(8,128)(2,1)S(1)} %get-tuple-element.88), channel_id=1, source_target_pairs={{0,16},{4,20},{8,24},{12,28},{16,0},{20,4},{24,8},{28,12},{1,17},{... | collective-permute-start | bytes 442376 | tf_op jit(solution)/shard_map/ppermute | solution.py:365
  38.0 21.9 %collective-permute-start.4 = (bf16[2,3,6,2,1536]{4,3,2,1,0:T(2,128)(2,1)S(1)}, bf16[2,3,6,2,1536]{4,3,2,1,0:T(2,128)(2,1)S(1)}, u32[]{:S(2)}, u32[]{:S(2)}) collective-permute-start(bf16[2,3,6,2,1536]{4,3,2,1,0:T(2,128)(2,1)S(1)} %shard_map.114), channel_id=1, source_target_pairs={{0,4},{1,5},{2,6},{3,7},{4,8},{5,9},{6,10},{7,11},{8,12},{9,13},{1... | collective-permute-start | bytes 663560 | tf_op jit(solution)/shard_map/ppermute | solution.py:528
  38.0 12.0 %collective-permute-start.19 = (bf16[64,1152]{1,0:T(8,128)(2,1)S(1)}, bf16[64,1152]{1,0:T(8,128)(2,1)S(1)}, u32[]{:S(2)}, u32[]{:S(2)}) collective-permute-start(bf16[64,1152]{1,0:T(8,128)(2,1)S(1)} %get-tuple-element.89), channel_id=1, source_target_pairs={{0,8},{4,12},{8,0},{12,4},{16,24},{20,28},{24,16},{28,20},{1,9},{5... | collective-permute-start | bytes 442376 | tf_op jit(solution)/shard_map/ppermute | solution.py:365
  42.1 8.1 %collective-permute-start.9 = (bf16[64,1024]{1,0:T(8,128)(2,1)S(1)}, bf16[64,1024]{1,0:T(8,128)(2,1)S(1)}, u32[]{:S(2)}, u32[]{:S(2)}) collective-permute-start(bf16[64,1024]{1,0:T(8,128)(2,1)S(1)} %get-tuple-element.76), channel_id=1, source_target_pairs={{0,1},{1,0},{2,3},{3,2},{4,5},{5,4},{6,7},{7,6},{8,9},{9,8},{10,11... | collective-permute-start | bytes 393224 | tf_op jit(solution)/shard_map/ppermute | solution.py:372
  43.7 13.3 %collective-permute-start.10 = (bf16[64,1024]{1,0:T(8,128)(2,1)S(1)}, bf16[64,1024]{1,0:T(8,128)(2,1)S(1)}, u32[]{:S(2)}, u32[]{:S(2)}) collective-permute-start(bf16[64,1024]{1,0:T(8,128)(2,1)S(1)} %get-tuple-element.77), channel_id=1, source_target_pairs={{0,2},{1,3},{2,0},{3,1},{4,6},{5,7},{6,4},{7,5},{8,10},{9,11},{10,... | collective-permute-start | bytes 393224 | tf_op jit(solution)/shard_map/ppermute | solution.py:372
  48.0 8.9 %collective-permute-start.11 = (bf16[64,1024]{1,0:T(8,128)(2,1)S(1)}, bf16[64,1024]{1,0:T(8,128)(2,1)S(1)}, u32[]{:S(2)}, u32[]{:S(2)}) collective-permute-start(bf16[64,1024]{1,0:T(8,128)(2,1)S(1)} %get-tuple-element.78), channel_id=1, source_target_pairs={{0,3},{1,2},{2,1},{3,0},{4,7},{5,6},{6,5},{7,4},{8,11},{9,10},{10,... | collective-permute-start | bytes 393224 | tf_op jit(solution)/shard_map/ppermute | solution.py:372
  50.1 14.1 %collective-permute-start.20 = (bf16[32,1152]{1,0:T(8,128)(2,1)S(1)}, bf16[32,1152]{1,0:T(8,128)(2,1)S(1)}, u32[]{:S(2)}, u32[]{:S(2)}) collective-permute-start(bf16[32,1152]{1,0:T(8,128)(2,1)S(1)} %get-tuple-element.91), channel_id=1, source_target_pairs={{0,1},{1,0},{2,3},{3,2},{4,5},{5,4},{6,7},{7,6},{8,9},{9,8},{10,11... | collective-permute-start | bytes 221192 | tf_op jit(solution)/shard_map/ppermute | solution.py:372
  50.2 14.0 %collective-permute-start.21 = (bf16[32,1152]{1,0:T(8,128)(2,1)S(1)}, bf16[32,1152]{1,0:T(8,128)(2,1)S(1)}, u32[]{:S(2)}, u32[]{:S(2)}) collective-permute-start(bf16[32,1152]{1,0:T(8,128)(2,1)S(1)} %get-tuple-element.92), channel_id=1, source_target_pairs={{0,2},{1,3},{2,0},{3,1},{4,6},{5,7},{6,4},{7,5},{8,10},{9,11},{10,... | collective-permute-start | bytes 221192 | tf_op jit(solution)/shard_map/ppermute | solution.py:372
  56.9 7.3 %collective-permute-start.22 = (bf16[32,1152]{1,0:T(8,128)(2,1)S(1)}, bf16[32,1152]{1,0:T(8,128)(2,1)S(1)}, u32[]{:S(2)}, u32[]{:S(2)}) collective-permute-start(bf16[32,1152]{1,0:T(8,128)(2,1)S(1)} %get-tuple-element.93), channel_id=1, source_target_pairs={{0,3},{1,2},{2,1},{3,0},{4,7},{5,6},{6,5},{7,4},{8,11},{9,10},{10,... | collective-permute-start | bytes 221192 | tf_op jit(solution)/shard_map/ppermute | solution.py:372
  57.0 6.2 %collective-permute-start.12 = (bf16[32,1024]{1,0:T(8,128)(2,1)S(1)}, bf16[32,1024]{1,0:T(8,128)(2,1)S(1)}, u32[]{:S(2)}, u32[]{:S(2)}) collective-permute-start(bf16[32,1024]{1,0:T(8,128)(2,1)S(1)} %get-tuple-element.80), channel_id=1, source_target_pairs={{0,16},{4,20},{8,24},{12,28},{16,0},{20,4},{24,8},{28,12},{1,17},{... | collective-permute-start | bytes 196616 | tf_op jit(solution)/shard_map/ppermute | solution.py:365
  59.8 4.3 %collective-permute-start.13 = (bf16[32,1024]{1,0:T(8,128)(2,1)S(1)}, bf16[32,1024]{1,0:T(8,128)(2,1)S(1)}, u32[]{:S(2)}, u32[]{:S(2)}) collective-permute-start(bf16[32,1024]{1,0:T(8,128)(2,1)S(1)} %get-tuple-element.81), channel_id=1, source_target_pairs={{0,8},{4,12},{8,0},{12,4},{16,24},{20,28},{24,16},{28,20},{1,9},{5... | collective-permute-start | bytes 196616 | tf_op jit(solution)/shard_map/ppermute | solution.py:365

commit v9 on v8

--- a/solution.py
+++ b/solution.py
@@ -154,7 +154,8 @@
 
 def forward_body(
     plan, places_ref, r0, r1, r2, r3, w_qkv_ref, w_out_ref, gain_ref, bias_ref,
-    mine_ref, peer_ref, factor_ref, query_ref, pair_ref, probs_ref, wide, side, bias_of,
+    mine_ref, peer_ref, factor_ref, query_ref, pair_ref, probs_ref, standard_ref, inverse_ref,
+    wide, side, bias_of,
 ):
     quads = (r0, r1, r2, r3)
     inner, width = w_out_ref.shape
@@ -174,7 +175,9 @@
     side[...] = grad.T
     reorder(plan, places_ref, side, (mine_ref, peer_ref), width // 2)
     pair_ref[:, 2 * inner :] = dot(grad, w_out_ref[...], ((1,), (1,))).astype(BF16)
-    standard, _ = normalize(gather_window(quads, 0, wide))
+    standard, inverse = normalize(gather_window(quads, 0, wide))
+    standard_ref[...] = standard
+    inverse_ref[...] = jnp.broadcast_to(inverse, inverse_ref.shape)
     normed = (standard * gain_ref[...] + bias_ref[...]).astype(BF16)
     side[...] = normed.T
     reorder(plan, places_ref, side, (mine_ref, peer_ref))
@@ -226,7 +229,8 @@
 
 
 def gradient_body(
-    plan, places_ref, r0, r1, r2, r3, factor_ref, late_ref, w_qkv_ref, gain_ref,
+    plan, places_ref, r0, r1, r2, r3, standard_ref, inverse_ref, factor_ref, late_ref, w_qkv_ref,
+    gain_ref,
     stay_ref, east_ref, north_ref, mine_ref, peer_ref, wide, flat,
 ):
     quads = (r0, r1, r2, r3)
@@ -234,8 +238,7 @@
     outs = (stay_ref, east_ref.at[0], north_ref, east_ref.at[1])
     quad = stay_ref.shape[:3]
     count = quad[0] * quad[1] * quad[2]
-    tokens_wide = gather_window(quads, 0, wide)
-    standard, inverse = normalize(tokens_wide)
+    standard, inverse = standard_ref[...], inverse_ref[:, 0:1]
     grad_normed = dot(factor_ref[:, inner:], w_qkv_ref[:, 2 * inner :], ((1,), (1,)))
     grad_normed += dot(late_ref[...], w_qkv_ref[:, : 2 * inner], ((1,), (1,)))
     sums = [
@@ -457,11 +460,11 @@
     plan = (share if hyper else 16, (lat_count, lon_count), tuple(order))
     places = jnp.where(jnp.arange(2) == 0, lat_place, lon_place).astype(jnp.int32)
     heads = inner // HDIM
-    mine, peer, factor, query, pairs, probs = call(
+    mine, peer, factor, query, pairs, probs, standard, inverse = call(
         functools.partial(forward_body, plan),
         [((width, cells), BF16)] * 2
         + [((cells, n * inner), BF16) for n in (2, 1, 3)]
-        + [((heads, cells, cells), F32)],
+        + [(shape, F32) for shape in ((heads, cells, cells), (cells, width), (cells, LANES))],
         (places, *quads, *params),
         scratch=[
             pltpu.VMEM((cells, width), F32),
@@ -475,7 +478,7 @@
     stay, east, north, sums, sums_peer = call(
         functools.partial(gradient_body, plan),
         [(shape, BF16) for shape in (part, (2, *part), part)] + [((width // 2, LANES), F32)] * 2,
-        (places, *quads, factor, factor_late, params[0], params[2]),
+        (places, *quads, standard, inverse, factor, factor_late, params[0], params[2]),
         scratch=[pltpu.VMEM((cells, width), F32), pltpu.VMEM((width, LANES), F32)],
         smem=1,
     )

time: 65.1 us -> 65.1 us (level)
  no operation moved by 1% of the time
where the time goes in v9:
time: 65.1 us; the launch traced here: 64.9 us
  starting transfers between devices  30.5 us (47%)
  waiting for transfers between devices  19 us (29%)
  Pallas kernels  14.6 us (22%)
  between operations  0.77 us (1%)
    pallas_call x14, Pallas kernels, call(): pl.pallas_call(body, out_shape=[pltpu.VMEM(s, d) if i < near_out else jax...  14.6 us
    ppermute x12, waiting for transfers between devices, swap(): return lax.ppermute(value, 'lat', xor_pairs(bit))  12.6 us
    ppermute x12, starting transfers between devices, swap(): return lax.ppermute(value, 'lat', xor_pairs(bit))  12.5 us
    ppermute x6, starting transfers between devices, turn(): moved.append(lax.ppermute(pieces[k], 'lon', pairs(k)))  10.3 us
    ppermute x3, starting transfers between devices, moved_all(): lax.ppermute(items[place], ('lat', 'lon'), moved(sign * a, sign * b))  7.58 us
    ppermute x6, waiting for transfers between devices, turn(): moved.append(lax.ppermute(pieces[k], 'lon', pairs(k)))  4.39 us
    ppermute x3, waiting for transfers between devices, moved_all(): lax.ppermute(items[place], ('lat', 'lon'), moved(sign * a, sign * b))  2 us
  transfers between devices with their start and end apart: 23, of which 8 were waited for; matrix products, arithmetic and copies ran while one was open for 0% of the time, Pallas kernels for 10%

profile of v9, /device:TPU:0, one launch (start us, length us, event | category | flops | bytes accessed | tf_op | source)
XLA Modules:
  0.0 64.9 jit_solution(16752713742588722338)
XLA Ops:
  0.6 1.2 %shard_map.109 = (bf16[2,3,6,2,1024]{4,3,2,1,0:T(2,128)(2,1)S(1)}, bf16[2,3,6,2,1024]{4,3,2,1,0:T(2,128)(2,1)S(1)}, bf16[2,3,6,2,1024]{4,3,2,1,0:T(2,128)(2,1)S(1)}, bf16[2,3,6,2,1024]{4,3,2,1,0:T(2,128)(2,1)S(1)}) custom-call(bf16[6,12,2,1024]{3,2,1,0:T(2,128)(2,1)} %bitcast.9, bf16[6,12,2,1024]{3,2,1,0:T(2,128)(2,1)} %bitcast.11), custom_call_target="tpu_custom_call" | custom-call | tf_op jit(solution)/shard_map/pallas_call | solution.py:46
  1.8 5.1 %collective-permute-start = (bf16[2,3,6,2,1024]{4,3,2,1,0:T(2,128)(2,1)S(1)}, bf16[2,3,6,2,1024]{4,3,2,1,0:T(2,128)(2,1)S(1)}, u32[]{:S(2)}, u32[]{:S(2)}) collective-permute-start(bf16[2,3,6,2,1024]{4,3,2,1,0:T(2,128)(2,1)S(1)} %get-tuple-element.55), channel_id=1, source_target_pairs={{0,3},{1,0},{2,1},{3,2},{4,7},{5,4},{6,5},{7,6},{8,11},{9,8},{10,9... | collective-permute-start | bytes 442376 | tf_op jit(solution)/shard_map/ppermute | solution.py:429
  7.0 1.6 %collective-permute-start.1 = (bf16[2,3,6,2,1024]{4,3,2,1,0:T(2,128)(2,1)S(1)}, bf16[2,3,6,2,1024]{4,3,2,1,0:T(2,128)(2,1)S(1)}, u32[]{:S(2)}, u32[]{:S(2)}) collective-permute-start(bf16[2,3,6,2,1024]{4,3,2,1,0:T(2,128)(2,1)S(1)} %get-tuple-element.56), channel_id=1, source_target_pairs={{0,28},{1,29},{2,30},{3,31},{4,0},{5,1},{6,2},{7,3},{8,4},{9,5},{1... | collective-permute-start | bytes 442376 | tf_op jit(solution)/shard_map/ppermute | solution.py:429
  8.6 0.8 %collective-permute-start.2 = (bf16[2,3,6,2,1024]{4,3,2,1,0:T(2,128)(2,1)S(1)}, bf16[2,3,6,2,1024]{4,3,2,1,0:T(2,128)(2,1)S(1)}, u32[]{:S(2)}, u32[]{:S(2)}) collective-permute-start(bf16[2,3,6,2,1024]{4,3,2,1,0:T(2,128)(2,1)S(1)} %get-tuple-element.57), channel_id=1, source_target_pairs={{0,31},{1,28},{2,29},{3,30},{4,3},{5,0},{6,1},{7,2},{8,7},{9,4},{1... | collective-permute-start | bytes 442376 | tf_op jit(solution)/shard_map/ppermute | solution.py:429
  9.4 2.3 %shard_map.110 = (bf16[1024,1536]{1,0:T(8,128)(2,1)S(1)}, bf16[512,1024]{1,0:T(8,128)(2,1)S(1)}, f32[1,1024]{1,0:T(1,128)S(1)}, f32[1,1024]{1,0:T(1,128)S(1)}, bf16[6,12,2,1024]{3,2,1,0:T(2,128)(2,1)S(1)}) custom-call(bf16[1024,1536]{1,0:T(8,128)(2,1)} %refs_0_.1, bf16[512,1024]{1,0:T(8,128)(2,1)} %refs_1_.1, f32[1,1024]{1,0:T(1,128)} %bitcast.12, ...), custom_call_target="tpu_custom_call" | custom-call | tf_op jit(solution)/shard_map/pallas_call | solution.py:46
  11.7 0.0 collective-permute-done.r1
  11.8 0.0 collective-permute-done.1.r2
  11.8 2.0 %collective-permute-done.2.r3 = bf16[2,3,6,2,1024]{4,3,2,1,0:T(2,128)(2,1)S(1)} collective-permute-done((bf16[2,3,6,2,1024]{4,3,2,1,0:T(2,128)(2,1)S(1)}, bf16[2,3,6,2,1024]{4,3,2,1,0:T(2,128)(2,1)S(1)}, u32[]{:S(2)}, u32[]{:S(2)}) %collective-permute-start.2) | collective-permute-done | bytes 147488 | tf_op jit(solution)/shard_map/ppermute | solution.py:429
  13.8 3.7 %shard_map.111 = (bf16[1024,144]{1,0:T(8,128)(2,1)S(1)}, bf16[1024,144]{1,0:T(8,128)(2,1)S(1)}, bf16[144,1024]{1,0:T(8,128)(2,1)S(1)}, bf16[144,512]{1,0:T(8,128...) custom-call(s32[2]{0:T(128)S(1)} %compare_select_fusion.places_ref, ...), custom_call_target="tpu_custom_call" | custom-call | tf_op jit(solution)/shard_map/pallas_call | solution.py:46
  17.4 1.7 %shard_map.112.late_ref.refs_2_ = bf16[144,1024]{1,0:T(8,128)(2,1)S(1)} custom-call(bf16[144,512]{1,0:T(8,128)(2,1)S(1)} %get-tuple-element.65.query_ref, bf16[144,1536]{1,0:T(8,128)(2,1)S(1)} %get-tuple-element.66.pair_ref, f32[8,144,144]{2,1,0:T(8,128)S(1)} %get-tuple-element.67.probs_ref), custom_call_target="tpu_custom_call" | custom-call | tf_op jit(solution)/shard_map/pallas_call | solution.py:46
  19.1 0.2 collective-permute-start.14
  19.3 0.4 collective-permute-start.6
  19.7 0.1 collective-permute-start.5
  19.8 2.1 %shard_map.113 = (bf16[3,6,2,1536]{3,2,1,0:T(2,128)(2,1)S(1)}, bf16[2,3,6,2,1536]{4,3,2,1,0:T(2,128)(2,1)S(1)}, bf16[3,6,2,1536]{3,2,1,0:T(2,128)(2,1)S(1)}, f32[512,128]{1,0:T(8,128)S(1)}, f32[512,128]{1,0:T(8,128)S(1)}) custom-call(s32[2]{0:T(128)S(1)} %compare_select_fusion.places_ref, bf16[2,3,6,2,1024]{4,3,2,1,0:T(2,128)(2,1)S(1)} %get-tuple-element.54.r0, ...), custom_call_target="tpu_custom_call" | custom-call | tf_op jit(solution)/shard_map/pallas_call | solution.py:46
  21.8 0.5 collective-permute-start.15
  22.3 1.2 %collective-permute-done.15.refs_5_ = f32[512,128]{1,0:T(8,128)S(1)} collective-permute-done((f32[512,128]{1,0:T(8,128)S(1)}, f32[512,128]{1,0:T(8,128)S(1)}, u32[]{:S(2)}, u32[]{:S(2)}) %collective-permute-start.15) | collective-permute-done | bytes 262176 | tf_op jit(solution)/shard_map/ppermute | solution.py:368
  23.5 0.0 collective-permute-done.14.refs_3_
  23.5 0.0 collective-permute-done.6.refs_1_
  23.5 0.0 collective-permute-done.5.got
  23.5 0.7 %shard_map.119 = (bf16[256,1152]{1,0:T(8,128)(2,1)S(1)}, bf16[128,1152]{1,0:T(8,128)(2,1)S(1)}, bf16[128,1152]{1,0:T(8,128)(2,1)S(1)}) custom-call(bf16[1024,144]{1,0:T(8,128)(2,1)S(1)} %get-tuple-element.74.mine, bf16[1024,144]{1,0:T(8,128)(2,1)S(1)} %collective-permute-done.5.got, bf16[144,1024]{1,0:T(8,128)(2,1)S(1)} %get-tuple-element.64.factor_ref.refs_0_, ...), custom_call_target="tpu_custom_call" | custom-call | tf_op jit(solution)/shard_map/pallas_call | solution.py:46
  24.2 2.1 %collective-permute-start.16 = (bf16[128,1152]{1,0:T(8,128)(2,1)S(1)}, bf16[128,1152]{1,0:T(8,128)(2,1)S(1)}, u32[]{:S(2)}, u32[]{:S(2)}) collective-permute-start(bf16[128,1152]{1,0:T(8,128)(2,1)S(1)} %get-tuple-element.89), channel_id=1, source_target_pairs={{0,8},{4,12},{8,0},{12,4},{16,24},{20,28},{24,16},{28,20},{1,9},{5... | collective-permute-start | bytes 884744 | tf_op jit(solution)/shard_map/ppermute | solution.py:368
  26.3 1.5 %collective-permute-start.17 = (bf16[128,1152]{1,0:T(8,128)(2,1)S(1)}, bf16[128,1152]{1,0:T(8,128)(2,1)S(1)}, u32[]{:S(2)}, u32[]{:S(2)}) collective-permute-start(bf16[128,1152]{1,0:T(8,128)(2,1)S(1)} %get-tuple-element.90), channel_id=1, source_target_pairs={{0,16},{4,20},{8,24},{12,28},{16,0},{20,4},{24,8},{28,12},{1,17},{... | collective-permute-start | bytes 884744 | tf_op jit(solution)/shard_map/ppermute | solution.py:368
  27.8 0.0 collective-permute-start.3
  27.8 0.7 %shard_map.116 = (bf16[256,1024]{1,0:T(8,128)(2,1)S(1)}, bf16[128,1024]{1,0:T(8,128)(2,1)S(1)}, bf16[128,1024]{1,0:T(8,128)(2,1)S(1)}) custom-call(bf16[1024,144]{1,0:T(8,128)(2,1)S(1)} %get-tuple-element.74.mine, bf16[1024,144]{1,0:T(8,128)(2,1)S(1)} %collective-permute-done.5.got, bf16[144,1024]{1,0:T(8,128)(2,1)S(1)} %get-tuple-element.64.factor_ref.refs_0_, ...), custom_call_target="tpu_custom_call" | custom-call | tf_op jit(solution)/shard_map/pallas_call | solution.py:46
  28.5 0.6 collective-permute-start.7
  29.1 0.5 collective-permute-start.8
  29.6 4.6 %collective-permute-done.16.got_a = bf16[128,1152]{1,0:T(8,128)(2,1)S(1)} collective-permute-done((bf16[128,1152]{1,0:T(8,128)(2,1)S(1)}, bf16[128,1152]{1,0:T(8,128)(2,1)S(1)}, u32[]{:S(2)}, u32[]{:S(2)}) %collective-permute-start.16) | collective-permute-done | bytes 294944 | tf_op jit(solution)/shard_map/ppermute | solution.py:368
  34.2 2.0 %collective-permute-done.17.got_b = bf16[128,1152]{1,0:T(8,128)(2,1)S(1)} collective-permute-done((bf16[128,1152]{1,0:T(8,128)(2,1)S(1)}, bf16[128,1152]{1,0:T(8,128)(2,1)S(1)}, u32[]{:S(2)}, u32[]{:S(2)}) %collective-permute-start.17) | collective-permute-done | bytes 294944 | tf_op jit(solution)/shard_map/ppermute | solution.py:368
  36.2 0.1 shard_map.120
  36.3 1.6 %collective-permute-start.18 = (bf16[64,1152]{1,0:T(8,128)(2,1)S(1)}, bf16[64,1152]{1,0:T(8,128)(2,1)S(1)}, u32[]{:S(2)}, u32[]{:S(2)}) collective-permute-start(bf16[64,1152]{1,0:T(8,128)(2,1)S(1)} %get-tuple-element.92), channel_id=1, source_target_pairs={{0,16},{4,20},{8,24},{12,28},{16,0},{20,4},{24,8},{28,12},{1,17},{... | collective-permute-start | bytes 442376 | tf_op jit(solution)/shard_map/ppermute | solution.py:368
  37.9 0.1 collective-permute-start.4
  38.0 0.1 collective-permute-start.19
  38.2 1.1 %collective-permute-done.7.got_a = bf16[128,1024]{1,0:T(8,128)(2,1)S(1)} collective-permute-done((bf16[128,1024]{1,0:T(8,128)(2,1)S(1)}, bf16[128,1024]{1,0:T(8,128)(2,1)S(1)}, u32[]{:S(2)}, u32[]{:S(2)}) %collective-permute-start.7) | collective-permute-done | bytes 262176 | tf_op jit(solution)/shard_map/ppermute | solution.py:368
  39.2 2.8 %collective-permute-done.8.got_b = bf16[128,1024]{1,0:T(8,128)(2,1)S(1)} collective-permute-done((bf16[128,1024]{1,0:T(8,128)(2,1)S(1)}, bf16[128,1024]{1,0:T(8,128)(2,1)S(1)}, u32[]{:S(2)}, u32[]{:S(2)}) %collective-permute-start.8) | collective-permute-done | bytes 262176 | tf_op jit(solution)/shard_map/ppermute | solution.py:368
  42.0 0.1 shard_map.117
  42.1 1.5 %collective-permute-start.9 = (bf16[64,1024]{1,0:T(8,128)(2,1)S(1)}, bf16[64,1024]{1,0:T(8,128)(2,1)S(1)}, u32[]{:S(2)}, u32[]{:S(2)}) collective-permute-start(bf16[64,1024]{1,0:T(8,128)(2,1)S(1)} %get-tuple-element.80), channel_id=1, source_target_pairs={{0,1},{1,0},{2,3},{3,2},{4,5},{5,4},{6,7},{7,6},{8,9},{9,8},{10,11... | collective-permute-start | bytes 393224 | tf_op jit(solution)/shard_map/ppermute | solution.py:375
  43.6 4.4 %collective-permute-start.10 = (bf16[64,1024]{1,0:T(8,128)(2,1)S(1)}, bf16[64,1024]{1,0:T(8,128)(2,1)S(1)}, u32[]{:S(2)}, u32[]{:S(2)}) collective-permute-start(bf16[64,1024]{1,0:T(8,128)(2,1)S(1)} %get-tuple-element.81), channel_id=1, source_target_pairs={{0,2},{1,3},{2,0},{3,1},{4,6},{5,7},{6,4},{7,5},{8,10},{9,11},{10,... | collective-permute-start | bytes 393224 | tf_op jit(solution)/shard_map/ppermute | solution.py:375
  48.0 2.0 %collective-permute-start.11 = (bf16[64,1024]{1,0:T(8,128)(2,1)S(1)}, bf16[64,1024]{1,0:T(8,128)(2,1)S(1)}, u32[]{:S(2)}, u32[]{:S(2)}) collective-permute-start(bf16[64,1024]{1,0:T(8,128)(2,1)S(1)} %get-tuple-element.82), channel_id=1, source_target_pairs={{0,3},{1,2},{2,1},{3,0},{4,7},{5,6},{6,5},{7,4},{8,11},{9,10},{10,... | collective-permute-start | bytes 393224 | tf_op jit(solution)/shard_map/ppermute | solution.py:375
  50.0 0.1 shard_map.121
  50.1 0.1 collective-permute-start.20
  50.2 2.3 %collective-permute-start.21 = (bf16[32,1152]{1,0:T(8,128)(2,1)S(1)}, bf16[32,1152]{1,0:T(8,128)(2,1)S(1)}, u32[]{:S(2)}, u32[]{:S(2)}) collective-permute-start(bf16[32,1152]{1,0:T(8,128)(2,1)S(1)} %get-tuple-element.96), channel_id=1, source_target_pairs={{0,2},{1,3},{2,0},{3,1},{4,6},{5,7},{6,4},{7,5},{8,10},{9,11},{10,... | collective-permute-start | bytes 221192 | tf_op jit(solution)/shard_map/ppermute | solution.py:375
  52.6 4.4 %collective-permute-done.10.refs_2_ = bf16[64,1024]{1,0:T(8,128)(2,1)S(1)} collective-permute-done((bf16[64,1024]{1,0:T(8,128)(2,1)S(1)}, bf16[64,1024]{1,0:T(8,128)(2,1)S(1)}, u32[]{:S(2)}, u32[]{:S(2)}) %collective-permute-start.10) | collective-permute-done | bytes 131104 | tf_op jit(solution)/shard_map/ppermute | solution.py:375
  56.9 0.1 shard_map.118
  57.0 2.8 %collective-permute-start.12 = (bf16[32,1024]{1,0:T(8,128)(2,1)S(1)}, bf16[32,1024]{1,0:T(8,128)(2,1)S(1)}, u32[]{:S(2)}, u32[]{:S(2)}) collective-permute-start(bf16[32,1024]{1,0:T(8,128)(2,1)S(1)} %get-tuple-element.84), channel_id=1, source_target_pairs={{0,16},{4,20},{8,24},{12,28},{16,0},{20,4},{24,8},{28,12},{1,17},{... | collective-permute-start | bytes 196616 | tf_op jit(solution)/shard_map/ppermute | solution.py:368
  59.8 2.1 %collective-permute-start.13 = (bf16[32,1024]{1,0:T(8,128)(2,1)S(1)}, bf16[32,1024]{1,0:T(8,128)(2,1)S(1)}, u32[]{:S(2)}, u32[]{:S(2)}) collective-permute-start(bf16[32,1024]{1,0:T(8,128)(2,1)S(1)} %get-tuple-element.85), channel_id=1, source_target_pairs={{0,8},{4,12},{8,0},{12,4},{16,24},{20,28},{24,16},{28,20},{1,9},{5... | collective-permute-start | bytes 196616 | tf_op jit(solution)/shard_map/ppermute | solution.py:368
  61.9 1.2 %shard_map.115 = (bf16[6,12,2,1024]{3,2,1,0:T(2,128)(2,1)}, bf16[6,12,2,1024]{3,2,1,0:T(2,128)(2,1)}) custom-call(bf16[3,6,2,1536]{3,2,1,0:T(2,128)(2,1)S(1)} %get-tuple-element.68.stay_ref, bf16[2,3,6,2,1536]{4,3,2,1,0:T(2,128)(2,1)S(1)} %collective-permute-done.3.east_ref, bf16[2,3,6,2,1536]{4,3,2,1,0:T(2,128)(2,1)S(1)} %collective-permute-done.4.both_ref, ...), custom_call_target="tpu_custom_call" | custom-call | tf_op jit(solution)/shard_map/pallas_call | solution.py:46
  63.1 1.0 %collective-permute-done.13.got_b = bf16[32,1024]{1,0:T(8,128)(2,1)S(1)} collective-permute-done((bf16[32,1024]{1,0:T(8,128)(2,1)S(1)}, bf16[32,1024]{1,0:T(8,128)(2,1)S(1)}, u32[]{:S(2)}, u32[]{:S(2)}) %collective-permute-start.13) | collective-permute-done | bytes 65568 | tf_op jit(solution)/shard_map/ppermute | solution.py:368
  64.2 0.8 %shard_map.122 = (f32[32,1536]{1,0:T(8,128)}, f32[32,512]{1,0:T(8,128)}, f32[1,32]{1,0:T(1,128)}, f32[1,32]{1,0:T(1,128)}) custom-call(f32[32,1024]{1,0:T(8,128)S(1)} %get-tuple-element.83.base, bf16[32,1024]{1,0:T(8,128)(2,1)S(1)} %collective-permute-done.12.got_a, bf16[32,1024]{1,0:T(8,128)(2,1)S(1)} %collective-permute-done.13.got_b, ...), custom_call_target="tpu_custom_call" | custom-call | tf_op jit(solution)/shard_map/pallas_call | solution.py:46
  (13 shorter events, 0.1 us)
Async XLA Ops:
  1.8 9.9 %collective-permute-start = (bf16[2,3,6,2,1024]{4,3,2,1,0:T(2,128)(2,1)S(1)}, bf16[2,3,6,2,1024]{4,3,2,1,0:T(2,128)(2,1)S(1)}, u32[]{:S(2)}, u32[]{:S(2)}) collective-permute-start(bf16[2,3,6,2,1024]{4,3,2,1,0:T(2,128)(2,1)S(1)} %get-tuple-element.55), channel_id=1, source_target_pairs={{0,3},{1,0},{2,1},{3,2},{4,7},{5,4},{6,5},{7,6},{8,11},{9,8},{10,9... | collective-permute-start | bytes 442376 | tf_op jit(solution)/shard_map/ppermute | solution.py:429
  7.0 4.8 %collective-permute-start.1 = (bf16[2,3,6,2,1024]{4,3,2,1,0:T(2,128)(2,1)S(1)}, bf16[2,3,6,2,1024]{4,3,2,1,0:T(2,128)(2,1)S(1)}, u32[]{:S(2)}, u32[]{:S(2)}) collective-permute-start(bf16[2,3,6,2,1024]{4,3,2,1,0:T(2,128)(2,1)S(1)} %get-tuple-element.56), channel_id=1, source_target_pairs={{0,28},{1,29},{2,30},{3,31},{4,0},{5,1},{6,2},{7,3},{8,4},{9,5},{1... | collective-permute-start | bytes 442376 | tf_op jit(solution)/shard_map/ppermute | solution.py:429
  8.6 5.2 %collective-permute-start.2 = (bf16[2,3,6,2,1024]{4,3,2,1,0:T(2,128)(2,1)S(1)}, bf16[2,3,6,2,1024]{4,3,2,1,0:T(2,128)(2,1)S(1)}, u32[]{:S(2)}, u32[]{:S(2)}) collective-permute-start(bf16[2,3,6,2,1024]{4,3,2,1,0:T(2,128)(2,1)S(1)} %get-tuple-element.57), channel_id=1, source_target_pairs={{0,31},{1,28},{2,29},{3,30},{4,3},{5,0},{6,1},{7,2},{8,7},{9,4},{1... | collective-permute-start | bytes 442376 | tf_op jit(solution)/shard_map/ppermute | solution.py:429
  19.1 4.4 %collective-permute-start.14 = (bf16[144,1024]{1,0:T(8,128)(2,1)S(1)}, bf16[144,1024]{1,0:T(8,128)(2,1)S(1)}, u32[]{:S(2)}, u32[]{:S(2)}) collective-permute-start(bf16[144,1024]{1,0:T(8,128)(2,1)S(1)} %shard_map.112.late_ref.refs_2_), channel_id=1, source_target_pairs={{0,4},{4,0},{8,12},{12,8},{16,20},{20,16},{24,28},{28,24},{1,5},{5... | collective-permute-start | bytes 884744 | tf_op jit(solution)/shard_map/ppermute | solution.py:368
  19.3 4.2 %collective-permute-start.6 = (bf16[144,1024]{1,0:T(8,128)(2,1)S(1)}, bf16[144,1024]{1,0:T(8,128)(2,1)S(1)}, u32[]{:S(2)}, u32[]{:S(2)}) collective-permute-start(bf16[144,1024]{1,0:T(8,128)(2,1)S(1)} %get-tuple-element.64.factor_ref.refs_0_), channel_id=1, source_target_pairs={{0,4},{4,0},{8,12},{12,8},{16,20},{20,16},{24,28},{28,24},{1,5},{5... | collective-permute-start | bytes 884744 | tf_op jit(solution)/shard_map/ppermute | solution.py:368
  19.7 3.8 %collective-permute-start.5 = (bf16[1024,144]{1,0:T(8,128)(2,1)S(1)}, bf16[1024,144]{1,0:T(8,128)(2,1)S(1)}, u32[]{:S(2)}, u32[]{:S(2)}) collective-permute-start(bf16[1024,144]{1,0:T(8,128)(2,1)S(1)} %get-tuple-element.75), channel_id=1, source_target_pairs={{0,4},{4,0},{8,12},{12,8},{16,20},{20,16},{24,28},{28,24},{1,5},{5... | collective-permute-start | bytes 884744 | tf_op jit(solution)/shard_map/ppermute | solution.py:368
  21.8 1.6 %collective-permute-start.15 = (f32[512,128]{1,0:T(8,128)S(1)}, f32[512,128]{1,0:T(8,128)S(1)}, u32[]{:S(2)}, u32[]{:S(2)}) collective-permute-start(f32[512,128]{1,0:T(8,128)S(1)} %get-tuple-element.87), channel_id=1, source_target_pairs={{0,4},{4,0},{8,12},{12,8},{16,20},{20,16},{24,28},{28,24},{1,5},{5... | collective-permute-start | bytes 786440 | tf_op jit(solution)/shard_map/ppermute | solution.py:368
  24.2 10.0 %collective-permute-start.16 = (bf16[128,1152]{1,0:T(8,128)(2,1)S(1)}, bf16[128,1152]{1,0:T(8,128)(2,1)S(1)}, u32[]{:S(2)}, u32[]{:S(2)}) collective-permute-start(bf16[128,1152]{1,0:T(8,128)(2,1)S(1)} %get-tuple-element.89), channel_id=1, source_target_pairs={{0,8},{4,12},{8,0},{12,4},{16,24},{20,28},{24,16},{28,20},{1,9},{5... | collective-permute-start | bytes 884744 | tf_op jit(solution)/shard_map/ppermute | solution.py:368
  26.3 9.9 %collective-permute-start.17 = (bf16[128,1152]{1,0:T(8,128)(2,1)S(1)}, bf16[128,1152]{1,0:T(8,128)(2,1)S(1)}, u32[]{:S(2)}, u32[]{:S(2)}) collective-permute-start(bf16[128,1152]{1,0:T(8,128)(2,1)S(1)} %get-tuple-element.90), channel_id=1, source_target_pairs={{0,16},{4,20},{8,24},{12,28},{16,0},{20,4},{24,8},{28,12},{1,17},{... | collective-permute-start | bytes 884744 | tf_op jit(solution)/shard_map/ppermute | solution.py:368
  27.8 10.1 %collective-permute-start.3 = (bf16[2,3,6,2,1536]{4,3,2,1,0:T(2,128)(2,1)S(1)}, bf16[2,3,6,2,1536]{4,3,2,1,0:T(2,128)(2,1)S(1)}, u32[]{:S(2)}, u32[]{:S(2)}) collective-permute-start(bf16[2,3,6,2,1536]{4,3,2,1,0:T(2,128)(2,1)S(1)} %get-tuple-element.69), channel_id=1, source_target_pairs={{0,1},{1,2},{2,3},{3,0},{4,5},{5,6},{6,7},{7,4},{8,9},{9,10},{10,1... | collective-permute-start | bytes 663560 | tf_op jit(solution)/shard_map/ppermute | solution.py:529
  28.5 10.7 %collective-permute-start.7 = (bf16[128,1024]{1,0:T(8,128)(2,1)S(1)}, bf16[128,1024]{1,0:T(8,128)(2,1)S(1)}, u32[]{:S(2)}, u32[]{:S(2)}) collective-permute-start(bf16[128,1024]{1,0:T(8,128)(2,1)S(1)} %get-tuple-element.77), channel_id=1, source_target_pairs={{0,8},{4,12},{8,0},{12,4},{16,24},{20,28},{24,16},{28,20},{1,9},{5... | collective-permute-start | bytes 786440 | tf_op jit(solution)/shard_map/ppermute | solution.py:368
  29.1 12.9 %collective-permute-start.8 = (bf16[128,1024]{1,0:T(8,128)(2,1)S(1)}, bf16[128,1024]{1,0:T(8,128)(2,1)S(1)}, u32[]{:S(2)}, u32[]{:S(2)}) collective-permute-start(bf16[128,1024]{1,0:T(8,128)(2,1)S(1)} %get-tuple-element.78), channel_id=1, source_target_pairs={{0,16},{4,20},{8,24},{12,28},{16,0},{20,4},{24,8},{28,12},{1,17},{... | collective-permute-start | bytes 786440 | tf_op jit(solution)/shard_map/ppermute | solution.py:368
  36.3 11.7 %collective-permute-start.18 = (bf16[64,1152]{1,0:T(8,128)(2,1)S(1)}, bf16[64,1152]{1,0:T(8,128)(2,1)S(1)}, u32[]{:S(2)}, u32[]{:S(2)}) collective-permute-start(bf16[64,1152]{1,0:T(8,128)(2,1)S(1)} %get-tuple-element.92), channel_id=1, source_target_pairs={{0,16},{4,20},{8,24},{12,28},{16,0},{20,4},{24,8},{28,12},{1,17},{... | collective-permute-start | bytes 442376 | tf_op jit(solution)/shard_map/ppermute | solution.py:368
  37.9 21.9 %collective-permute-start.4 = (bf16[2,3,6,2,1536]{4,3,2,1,0:T(2,128)(2,1)S(1)}, bf16[2,3,6,2,1536]{4,3,2,1,0:T(2,128)(2,1)S(1)}, u32[]{:S(2)}, u32[]{:S(2)}) collective-permute-start(bf16[2,3,6,2,1536]{4,3,2,1,0:T(2,128)(2,1)S(1)} %shard_map.114), channel_id=1, source_target_pairs={{0,4},{1,5},{2,6},{3,7},{4,8},{5,9},{6,10},{7,11},{8,12},{9,13},{1... | collective-permute-start | bytes 663560 | tf_op jit(solution)/shard_map/ppermute | solution.py:531
  38.0 12.0 %collective-permute-start.19 = (bf16[64,1152]{1,0:T(8,128)(2,1)S(1)}, bf16[64,1152]{1,0:T(8,128)(2,1)S(1)}, u32[]{:S(2)}, u32[]{:S(2)}) collective-permute-start(bf16[64,1152]{1,0:T(8,128)(2,1)S(1)} %get-tuple-element.93), channel_id=1, source_target_pairs={{0,8},{4,12},{8,0},{12,4},{16,24},{20,28},{24,16},{28,20},{1,9},{5... | collective-permute-start | bytes 442376 | tf_op jit(solution)/shard_map/ppermute | solution.py:368
  42.1 8.1 %collective-permute-start.9 = (bf16[64,1024]{1,0:T(8,128)(2,1)S(1)}, bf16[64,1024]{1,0:T(8,128)(2,1)S(1)}, u32[]{:S(2)}, u32[]{:S(2)}) collective-permute-start(bf16[64,1024]{1,0:T(8,128)(2,1)S(1)} %get-tuple-element.80), channel_id=1, source_target_pairs={{0,1},{1,0},{2,3},{3,2},{4,5},{5,4},{6,7},{7,6},{8,9},{9,8},{10,11... | collective-permute-start | bytes 393224 | tf_op jit(solution)/shard_map/ppermute | solution.py:375
  43.6 13.3 %collective-permute-start.10 = (bf16[64,1024]{1,0:T(8,128)(2,1)S(1)}, bf16[64,1024]{1,0:T(8,128)(2,1)S(1)}, u32[]{:S(2)}, u32[]{:S(2)}) collective-permute-start(bf16[64,1024]{1,0:T(8,128)(2,1)S(1)} %get-tuple-element.81), channel_id=1, source_target_pairs={{0,2},{1,3},{2,0},{3,1},{4,6},{5,7},{6,4},{7,5},{8,10},{9,11},{10,... | collective-permute-start | bytes 393224 | tf_op jit(solution)/shard_map/ppermute | solution.py:375
  48.0 8.9 %collective-permute-start.11 = (bf16[64,1024]{1,0:T(8,128)(2,1)S(1)}, bf16[64,1024]{1,0:T(8,128)(2,1)S(1)}, u32[]{:S(2)}, u32[]{:S(2)}) collective-permute-start(bf16[64,1024]{1,0:T(8,128)(2,1)S(1)} %get-tuple-element.82), channel_id=1, source_target_pairs={{0,3},{1,2},{2,1},{3,0},{4,7},{5,6},{6,5},{7,4},{8,11},{9,10},{10,... | collective-permute-start | bytes 393224 | tf_op jit(solution)/shard_map/ppermute | solution.py:375
  50.1 14.1 %collective-permute-start.20 = (bf16[32,1152]{1,0:T(8,128)(2,1)S(1)}, bf16[32,1152]{1,0:T(8,128)(2,1)S(1)}, u32[]{:S(2)}, u32[]{:S(2)}) collective-permute-start(bf16[32,1152]{1,0:T(8,128)(2,1)S(1)} %get-tuple-element.95), channel_id=1, source_target_pairs={{0,1},{1,0},{2,3},{3,2},{4,5},{5,4},{6,7},{7,6},{8,9},{9,8},{10,11... | collective-permute-start | bytes 221192 | tf_op jit(solution)/shard_map/ppermute | solution.py:375
  50.2 14.0 %collective-permute-start.21 = (bf16[32,1152]{1,0:T(8,128)(2,1)S(1)}, bf16[32,1152]{1,0:T(8,128)(2,1)S(1)}, u32[]{:S(2)}, u32[]{:S(2)}) collective-permute-start(bf16[32,1152]{1,0:T(8,128)(2,1)S(1)} %get-tuple-element.96), channel_id=1, source_target_pairs={{0,2},{1,3},{2,0},{3,1},{4,6},{5,7},{6,4},{7,5},{8,10},{9,11},{10,... | collective-permute-start | bytes 221192 | tf_op jit(solution)/shard_map/ppermute | solution.py:375
  56.9 7.2 %collective-permute-start.22 = (bf16[32,1152]{1,0:T(8,128)(2,1)S(1)}, bf16[32,1152]{1,0:T(8,128)(2,1)S(1)}, u32[]{:S(2)}, u32[]{:S(2)}) collective-permute-start(bf16[32,1152]{1,0:T(8,128)(2,1)S(1)} %get-tuple-element.97), channel_id=1, source_target_pairs={{0,3},{1,2},{2,1},{3,0},{4,7},{5,6},{6,5},{7,4},{8,11},{9,10},{10,... | collective-permute-start | bytes 221192 | tf_op jit(solution)/shard_map/ppermute | solution.py:375
  57.0 6.1 %collective-permute-start.12 = (bf16[32,1024]{1,0:T(8,128)(2,1)S(1)}, bf16[32,1024]{1,0:T(8,128)(2,1)S(1)}, u32[]{:S(2)}, u32[]{:S(2)}) collective-permute-start(bf16[32,1024]{1,0:T(8,128)(2,1)S(1)} %get-tuple-element.84), channel_id=1, source_target_pairs={{0,16},{4,20},{8,24},{12,28},{16,0},{20,4},{24,8},{28,12},{1,17},{... | collective-permute-start | bytes 196616 | tf_op jit(solution)/shard_map/ppermute | solution.py:368
  59.8 4.3 %collective-permute-start.13 = (bf16[32,1024]{1,0:T(8,128)(2,1)S(1)}, bf16[32,1024]{1,0:T(8,128)(2,1)S(1)}, u32[]{:S(2)}, u32[]{:S(2)}) collective-permute-start(bf16[32,1024]{1,0:T(8,128)(2,1)S(1)} %get-tuple-element.85), channel_id=1, source_target_pairs={{0,8},{4,12},{8,0},{12,4},{16,24},{20,28},{24,16},{28,20},{1,9},{5... | collective-permute-start | bytes 196616 | tf_op jit(solution)/shard_map/ppermute | solution.py:368
